TPU v7x, 32 devices: a whole 2x2x4 slice. The times are simulated.
32 devices in a mesh: dp: 8 (over y, x, core), tensor: 4 (over z).
Axes of the slice: x: 2, y: 2, z: 4, core: 2. Of those that a mesh axis runs over, the one named last changes fastest.
Arguments:
- gradient: float32 [5120, 27648], P('dp', 'tensor'), may hold values from -6 to 6
- momentum: float32 [5120, 27648], P('dp', 'tensor'), may hold values from -6 to 6
- right_factor: float32 [27648, 256], P('tensor'), may hold values from -6 to 6
Outputs:
- update: float32 [5120, 27648], P('dp', 'tensor')
- new_momentum: float32 [5120, 27648], P('dp', 'tensor')
- new_right: float32 [27648, 256], P('tensor')
All inputs are finite; a program needn't handle non-finite values.
Results may differ from a plain program's by a relative error of at most 0.000098.
Values sent between devices are 32-bit elements; how exact they have to be, the bound alone decides.
No kernel may reach another device: no remote copies, remote signals or barrier semaphores. Data moves between devices by JAX's collectives and lax.ppermute only.
A program may use at most 192 MiB of HBM per device.

v0:
```python
import jax
import jax.numpy as jnp
from jax import lax
from jax.sharding import PartitionSpec as P

ROWS = 5120
COLS = 27648
RANK = 256


def on_device(gradient, momentum, right_factor):
    high = lax.Precision.HIGHEST
    buffer = momentum + gradient
    partial_value = jnp.dot(
        buffer, right_factor, precision=high, preferred_element_type=jnp.float32
    )
    left = lax.psum(partial_value, "tensor")
    gram = lax.psum(jnp.dot(left.T, left, precision=high, preferred_element_type=jnp.float32), "dp")
    chol = jnp.linalg.cholesky(gram)
    ortho = jax.scipy.linalg.solve_triangular(chol, left.T, lower=True).T
    terms = jnp.dot(buffer.T, ortho, precision=high, preferred_element_type=jnp.float32)
    right = lax.psum(terms, "dp")
    squares = lax.psum(jnp.sum(right * right, axis=0), "tensor")
    scale_col = jnp.sqrt(squares / COLS + 1e-06)
    new_right = right / scale_col
    new_momentum = buffer - 0.05 * jnp.dot(
        ortho, right.T, precision=high, preferred_element_type=jnp.float32
    )
    factor = (ROWS / RANK) ** 0.5
    update = factor * jnp.dot(
        ortho, new_right.T, precision=high, preferred_element_type=jnp.float32
    )
    return (update, new_momentum, new_right)


def solution(mesh):
    return jax.shard_map(
        on_device,
        mesh=mesh,
        in_specs=(P("dp", "tensor"), P("dp", "tensor"), P("tensor", None)),
        out_specs=(P("dp", "tensor"), P("dp", "tensor"), P("tensor", None)),
        check_vma=False,
    )
```

profile of v0, /device:TPU:0, one launch (start us, length us, event | category | flops | bytes accessed | tf_op | source)
XLA Modules:
  0.0 446.9 jit_solution(4690855962468543818)
XLA Ops:
  7.2 0.0 all-reduce.5.cloned.1.call-start
  7.2 0.0 copy-start.1
  7.2 12.0 %add.40 = f32[640,6912]{1,0:T(8,128)S(1)} add(f32[640,6912]{1,0:T(8,128)} %param.4, f32[640,6912]{1,0:T(8,128)} %param.3) | non-fusion elementwise | flops 4423680 | bytes 53084160 | tf_op jit(solution)/shard_map/add | solution.py:13
  19.2 0.0 copy-start
  19.2 6.5 %copy-done = f32[640,6912]{1,0:T(8,128)} copy-done((f32[640,6912]{1,0:T(8,128)}, f32[640,6912]{1,0:T(8,128)S(1)}, u32[]{:S(2)}) %copy-start) | copy-done | bytes 17694744
  25.7 0.0 copy-done.1
  25.7 15.1 %fusion.13 = f32[640,256]{1,0:T(8,128)} fusion(f32[640,6912]{1,0:T(8,128)S(1)} %add.40, f32[6912,256]{1,0:T(8,128)S(1)} %copy-done.1), kind=kOutput, calls=%fused_computation.38 | convolution fusion | flops 13589544960 | bytes 25427968 | tf_op jit(solution)/shard_map/dot_general | solution.py:14
  40.8 0.0 all-reduce.5.cloned.1.call-update
  40.8 0.0 all-reduce.7.cloned.1.call-start
  40.9 43.2 %all-reduce.5.cloned.1.call-done = f32[640,256]{1,0:T(8,128)} async-done(((f32[640,256]{1,0:T(8,128)}), f32[640,256]{1,0:T(8,128)}) %all-reduce.5.cloned.1.call-update) | async-done | bytes 655376 | tf_op jit(solution)/shard_map/psum | solution.py:17
  84.1 3.2 fusion.14
  87.3 0.0 all-reduce.7.cloned.1.call-update
  87.3 0.5 all-reduce.9.cloned.1.call-start
  87.9 53.3 %all-reduce.7.cloned.1.call-done = f32[256,256]{0,1:T(8,128)} async-done(((f32[256,256]{0,1:T(8,128)}), f32[256,256]{0,1:T(8,128)}) %all-reduce.7.cloned.1.call-update) | async-done | bytes 262160 | tf_op jit(solution)/shard_map/psum | solution.py:18
  141.2 1.1 copy.7
  142.3 1.0 fusion.3
  143.3 11.7 %cholesky.50 = f32[128,128]{1,0:T(8,128)S(1)} custom-call(f32[128,128]{1,0:T(8,128)S(1)} %cholesky.118), custom_call_target="Cholesky" | custom-call | tf_op jit(solution)/shard_map/jit(cholesky)/cholesky | solution.py:19
  155.0 9.8 %custom-call.15 = f32[1,128,128]{1,2,0:T(8,128)S(1)} custom-call(f32[1,128,128]{2,1,0:T(8,128)S(1)} %get-tuple-element.24), custom_call_target="InvertDiagBlocksLowerTriangular" | custom-call | tf_op jit(solution)/shard_map/jit(cholesky)/cholesky | solution.py:19
  164.9 0.2 constant_dynamic-update-slice_fusion.1
  165.1 0.3 convolution_subtract_fusion.1
  165.3 11.7 %cholesky.105 = f32[128,128]{1,0:T(8,128)S(1)} custom-call(f32[128,128]{1,0:T(8,128)S(1)} %convolution_subtract_fusion.1), custom_call_target="Cholesky" | custom-call | tf_op jit(solution)/shard_map/jit(cholesky)/cholesky | solution.py:19
  177.1 0.7 compare_reduce_fusion
  179.1 0.1 triangular_solve.57
  179.2 3.9 while.1
  179.2 0.6 fusion.27
  179.8 1.4 bitcast_dynamic-update-slice_fusion.2
  181.2 0.6 fusion.27
  181.8 1.4 bitcast_dynamic-update-slice_fusion.2
  183.1 19.7 %custom-call.16 = f32[2,128,128]{1,2,0:T(8,128)S(1)} custom-call(f32[2,128,128]{2,1,0:T(8,128)S(1)} %get-tuple-element.10), custom_call_target="InvertDiagBlocksLowerTriangular" | custom-call | tf_op jit(solution)/shard_map/jit(_solve_triangular)/triangular_solve | solution.py:20
  202.8 1.5 fusion.1
  204.3 1.7 convolution_subtract_fusion
  206.0 0.5 fusion.5
  206.5 32.6 %fusion = f32[6912,256]{1,0:T(8,128)} fusion(f32[640,6912]{1,0:T(8,128)} %copy-done, f32[128,640]{1,0:T(8,128)S(1)} %fusion.5, f32[128,640]{1,0:T(8,128)S(1)} %fusion.1), kind=kOutput, calls=%fused_computation.9 | convolution fusion | flops 13589708800 | bytes 25427968 | tf_op jit(solution)/shard_map/dot_general | solution.py:21
  239.1 0.0 all-reduce.9.cloned.1.call-update
  239.1 112.1 %all-reduce.9.cloned.1.call-done = f32[6912,256]{1,0:T(8,128)} async-done(((f32[6912,256]{1,0:T(8,128)}), f32[6912,256]{1,0:T(8,128)}) %all-reduce.9.cloned.1.call-update) | async-done | bytes 7077904 | tf_op jit(solution)/shard_map/psum | solution.py:22
  351.2 3.9 multiply_reduce_fusion
  355.1 11.9 %psum.31 = f32[256]{0:T(256)S(1)} all-reduce(f32[256]{0:T(256)S(1)} %multiply_reduce_fusion), channel_id=1, replica_groups=mesh['dp'=8,'tensor'=4] {'tensor'}, use_global_device_ids=true, to_apply=%region_8.9 | all-reduce | flops 256 | bytes 2048 | tf_op jit(solution)/shard_map/psum | solution.py:23
  367.0 0.0 slice-start
  367.0 0.0 slice-start.1
  367.0 7.0 %broadcast_divide_fusion = f32[6912,256]{1,0:T(8,128)} fusion(f32[6912,256]{1,0:T(8,128)} %all-reduce.9.cloned.1.call-done, f32[256]{0:T(256)S(1)} %add_sqrt_fusion), kind=kLoop, calls=%fused_computation.5 | loop fusion | flops 1769472 | bytes 14156800 | tf_op jit(solution)/shard_map/div | solution.py:25
  374.0 0.0 slice-start.2
  374.0 0.0 slice-start.3
  374.0 0.0 slice-start.4
  374.0 32.6 %convolution_multiply_fusion = f32[640,6912]{1,0:T(8,128)} fusion(f32[6912,256]{1,0:T(8,128)} %broadcast_divide_fusion, f32[128,640]{1,0:T(8,128)S(1)} %fusion.5, f32[128,640]{1,0:T(8,128)S(1)} %fusion.1), kind=kOutput, calls=%fused_computation.3 | convolution fusion | flops 13594132480 | bytes 25427968 | tf_op jit(solution)/shard_map/dot_general | solution.py:30
  406.6 0.0 slice-done
  406.6 0.0 slice-done.1
  406.6 0.0 slice-done.2
  406.6 0.0 slice-done.3
  406.7 0.0 slice-done.4
  406.7 33.3 %multiply_subtract_fusion = f32[640,6912]{1,0:T(8,128)} fusion(f32[640,6912]{1,0:T(8,128)S(1)} %bitcast.40, f32[6912,256]{1,0:T(8,128)} %all-reduce.9.cloned.1.call-done, f32[128,640]{1,0:T(8,128)S(1)} %fusion.5, f32[128,640]{1,0:T(8,128)S(1)} %fusion.1), kind=kOutput, calls=%fused_computation.2 | convolution fusion | flops 13598556160 | bytes 43122688 | tf_op jit(solution)/shard_map/dot_general | solution.py:26
  (11 shorter events, 0.2 us)
Async XLA Ops:
  7.2 76.9 %all-reduce.5.cloned.1.call-start = ((), (), s32[]{:S(2)}) async-start(), calls=%async_computation | async-start | bytes 1310720 | tf_op jit(solution)/shard_map/psum | solution.py:17
  7.2 18.5 %copy-start.1 = (f32[6912,256]{1,0:T(8,128)S(1)}, f32[6912,256]{1,0:T(8,128)}, u32[]{:S(2)}) copy-start(f32[6912,256]{1,0:T(8,128)} %param.5) | copy-start | bytes 21233668
  19.2 6.5 %copy-start = (f32[640,6912]{1,0:T(8,128)}, f32[640,6912]{1,0:T(8,128)S(1)}, u32[]{:S(2)}) copy-start(f32[640,6912]{1,0:T(8,128)S(1)} %add.40) | copy-start | bytes 53084164
  40.8 100.3 %all-reduce.7.cloned.1.call-start = ((), (), s32[]{:S(2)}) async-start(), calls=%async_computation.1 | async-start | bytes 524288 | tf_op jit(solution)/shard_map/psum | solution.py:18
  87.3 263.9 %all-reduce.9.cloned.1.call-start = ((), (), s32[]{:S(2)}) async-start(), calls=%async_computation.2 | async-start | bytes 14155776 | tf_op jit(solution)/shard_map/psum | solution.py:22
  367.0 39.6 %slice-start = ((s8[17694720]{0:T(1024)(128)(4,1)}), s8[4194304]{0:T(1024)(128)(4,1)S(1)}, s32[]{:S(2)}) async-start(s8[17694720]{0:T(1024)(128)(4,1)} %bitcast.39), calls=%async_computation.3 | async-start | bytes 8388608
  367.0 39.6 %slice-start.1 = ((s8[17694720]{0:T(1024)(128)(4,1)}), s8[4194304]{0:T(1024)(128)(4,1)S(1)}, s32[]{:S(2)}) async-start(s8[17694720]{0:T(1024)(128)(4,1)} %bitcast.39), calls=%async_computation.4 | async-start | bytes 8388608
  374.0 32.6 %slice-start.2 = ((s8[17694720]{0:T(1024)(128)(4,1)}), s8[4194304]{0:T(1024)(128)(4,1)S(1)}, s32[]{:S(2)}) async-start(s8[17694720]{0:T(1024)(128)(4,1)} %bitcast.39), calls=%async_computation.5 | async-start | bytes 8388608
  374.0 32.6 %slice-start.3 = ((s8[17694720]{0:T(1024)(128)(4,1)}), s8[4194304]{0:T(1024)(128)(4,1)S(1)}, s32[]{:S(2)}) async-start(s8[17694720]{0:T(1024)(128)(4,1)} %bitcast.39), calls=%async_computation.6 | async-start | bytes 8388608
  374.0 32.6 %slice-start.4 = ((s8[17694720]{0:T(1024)(128)(4,1)}), s8[917504]{0:T(1024)(128)(4,1)S(1)}, s32[]{:S(2)}) async-start(s8[17694720]{0:T(1024)(128)(4,1)} %bitcast.39), calls=%async_computation.7 | async-start | bytes 1835008
Sparse Core Ops, SparseCore 0:
  41.0 43.0 all-reduce.4
  87.7 53.4 all-reduce.6
  239.2 111.9 all-reduce.8
where the time goes:
time: 453 us; the launch traced here: 447 us
  waiting for transfers between devices  209 us (46%)
  matrix products  121 us (27%)
  other arithmetic  77.6 us (17%)
  between operations  15.6 us (3%)
  blocking collectives  11.9 us (3%)
  local copies, waits for them, and re-layouts  11.6 us (3%)
    psum x1, waiting for transfers between devices, on_device(): right = lax.psum(terms, 'dp')  112 us
    psum x1, waiting for transfers between devices, on_device(): lax.psum(jnp.dot(left.T, left, precision=high, preferred_element_type=jnp...  53.3 us
    psum x1, waiting for transfers between devices, on_device(): left = lax.psum(partial_value, 'tensor')  43.2 us
    another operation x6, other arithmetic, on_device(): chol = jnp.linalg.cholesky(gram)  34 us
    dot_general x1, matrix products, on_device(): jnp.dot(ortho, right.T, precision=high, preferred_element_type=jnp.float32)  33.3 us
    dot_general x1, matrix products, on_device(): jnp.dot(ortho, new_right.T, precision=high, preferred_element_type=jnp.fl...  32.6 us
    dot_general x1, matrix products, on_device(): jnp.dot(buffer.T, ortho, precision=high, preferred_element_type=jnp.float32)  32.6 us
    another operation x3, other arithmetic, on_device(): ortho = jax.scipy.linalg.solve_triangular(chol, left.T, lower=True).T  19.7 us
  transfers between devices with their start and end apart: 3, of which 3 were waited for; matrix products, arithmetic and copies ran while one was open for 0% of the time, Pallas kernels for 0%

commit v1 on v0

v1 whole, which is shorter than its diff:
```python
import functools

import jax
import jax.numpy as jnp
from jax import lax
from jax.experimental import pallas as pl
from jax.experimental.pallas import tpu as pltpu
from jax.sharding import PartitionSpec as P

F32 = jnp.float32
BF16 = jnp.bfloat16
HIGH = lax.Precision.HIGHEST
LANES = 128
VMEM_LIMIT = 60 * 1024 * 1024

NN = (((1,), (0,)), ((), ()))
NT = (((1,), (1,)), ((), ()))
TN = (((0,), (0,)), ((), ()))


def params(**kw):
    return pltpu.CompilerParams(vmem_limit_bytes=VMEM_LIMIT, **kw)


def cost(flops, moved):
    return pl.CostEstimate(flops=int(flops), bytes_accessed=int(moved), transcendentals=0)


def split(x):
    hi = x.astype(BF16)
    lo = (x - hi.astype(F32)).astype(BF16)
    return hi, lo


def dot3(ah, al, bh, bl, dims):
    d = functools.partial(lax.dot_general, dimension_numbers=dims, preferred_element_type=F32)
    return d(ah, bh) + (d(ah, bl) + d(al, bh))


def dot_high(a, b, dims):
    return lax.dot_general(a, b, dims, precision=HIGH, preferred_element_type=F32)


def scalars(*values):
    return jnp.stack([jnp.asarray(v, jnp.int32) for v in values])


def column_block(cols):
    blocks = cols // LANES
    return LANES * max(k for k in range(1, 9) if blocks % k == 0)


def left_kernel(at, g, m, r, *rest):
    buffer, out = rest[-2:]
    step = pl.program_id(0)
    b = g[...] + m[...]
    buffer[...] = b
    bh, bl = split(b)
    rh, rl = split(r[...])
    term = dot3(bh, bl, rh, rl, NN)

    @pl.when(step == 0)
    def _():
        out[...] = term

    @pl.when(step > 0)
    def _():
        out[...] += term


def left_half(at, gradient, momentum, right_factor, buffer):
    rows, cols = gradient.shape
    rank = right_factor.shape[1]
    half, wide = rows // 2, column_block(cols)
    block = pl.BlockSpec((half, wide), lambda j, at: (at[0], j))
    first = buffer is None
    return pl.pallas_call(
        left_kernel,
        grid_spec=pltpu.PrefetchScalarGridSpec(
            num_scalar_prefetch=1,
            grid=(cols // wide,),
            in_specs=[block, block, pl.BlockSpec((wide, rank), lambda j, at: (j, 0))]
            + ([] if first else [pl.BlockSpec(memory_space=pl.ANY)]),
            out_specs=[block, pl.BlockSpec((half, rank), lambda j, at: (0, 0))],
        ),
        out_shape=[
            jax.ShapeDtypeStruct((rows, cols), F32),
            jax.ShapeDtypeStruct((half, rank), F32),
        ],
        input_output_aliases={} if first else {4: 0},
        compiler_params=params(),
        cost_estimate=cost(6 * half * cols * rank, 4 * (3 * half * cols + cols * rank)),
        name="left_half",
    )(scalars(at), gradient, momentum, right_factor, *([] if first else [buffer]))


def gram_kernel(*refs):
    pieces, (left, lh, ll, gram) = refs[:-4], refs[-4:]
    n = pieces[0].shape[0]
    for i, piece in enumerate(pieces):
        x = piece[...]
        at = pl.ds(i * n, n)
        left[at, :] = x
        h, l = split(x)
        lh[at, :] = h
        ll[at, :] = l
    half = left.shape[0] // 2
    own, other = left[:half, :], left[half:, :]
    gram[...] = dot_high(own, own, TN) + dot_high(other, other, TN)


def gram_of(pieces):
    rank = pieces[0].shape[1]
    rows = sum(p.shape[0] for p in pieces)
    return pl.pallas_call(
        gram_kernel,
        out_shape=[
            jax.ShapeDtypeStruct((rows, rank), F32),
            jax.ShapeDtypeStruct((rows, rank), BF16),
            jax.ShapeDtypeStruct((rows, rank), BF16),
            jax.ShapeDtypeStruct((rank, rank), F32),
        ],
        compiler_params=params(),
        cost_estimate=cost(12 * rows * rank * rank, 12 * rows * rank),
        name="gram_of",
    )(*pieces)


def w_term(own, other, lh, ll):
    half = own.shape[0]
    total = None
    for ref, at in ((own, 0), (other, half)):
        bh, bl = split(ref[...])
        term = dot3(bh, bl, lh[at : at + half, :], ll[at : at + half, :], TN)
        total = term if total is None else total + term
    return total


def w_send_kernel(at, own, other, lh, ll, out):
    out[...] = w_term(own, other, lh, ll)


def w_keep_kernel(at, own, other, lh, ll, got, send, keep):
    total = w_term(own, other, lh, ll) + got[...]

    @pl.when(pl.program_id(0) == 0)
    def _():
        send[...] = total

    @pl.when(pl.program_id(0) == 1)
    def _():
        keep[...] = total


def w_specs(buffer, rank, unit):
    half = buffer.shape[0] // 2
    whole = pl.BlockSpec((2 * half, rank), lambda i, at: (0, 0))
    return [
        pl.BlockSpec((half, unit), lambda i, at: (at[0], at[2 + i])),
        pl.BlockSpec((half, unit), lambda i, at: (at[1], at[2 + i])),
        whole,
        whole,
    ]


def w_cost(buffer, rank, unit):
    rows = buffer.shape[0]
    return cost(2 * 6 * rows * unit * rank, 2 * 4 * (rows * unit + unit * rank))


def w_send(s, units, buffer, lh, ll, unit):
    rank = lh.shape[1]
    return pl.pallas_call(
        w_send_kernel,
        grid_spec=pltpu.PrefetchScalarGridSpec(
            num_scalar_prefetch=1,
            grid=(2,),
            in_specs=w_specs(buffer, rank, unit),
            out_specs=pl.BlockSpec((unit, rank), lambda i, at: (i, 0)),
        ),
        out_shape=jax.ShapeDtypeStruct((2 * unit, rank), F32),
        compiler_params=params(),
        cost_estimate=w_cost(buffer, rank, unit),
        name="w_send",
    )(scalars(s, 1 - s, *units), buffer, buffer, lh, ll)


def w_keep(s, units, order, buffer, lh, ll, got, unit):
    rank = lh.shape[1]
    one = pl.BlockSpec((unit, rank), lambda i, at: (0, 0))
    return pl.pallas_call(
        w_keep_kernel,
        grid_spec=pltpu.PrefetchScalarGridSpec(
            num_scalar_prefetch=1,
            grid=(2,),
            in_specs=w_specs(buffer, rank, unit)
            + [pl.BlockSpec((unit, rank), lambda i, at: (at[4 + i], 0))],
            out_specs=[one, one],
        ),
        out_shape=[jax.ShapeDtypeStruct((unit, rank), F32)] * 2,
        compiler_params=params(),
        cost_estimate=w_cost(buffer, rank, unit),
        name="w_keep",
    )(scalars(s, 1 - s, *units, *order), buffer, buffer, lh, ll, got)


GROUP = 8


def factor_group(rows, at):
    full = (GROUP, LANES)
    columns = [jnp.broadcast_to(rows[:, at + j : at + j + 1], full) for j in range(GROUP)]
    a = {
        (i, j): jnp.broadcast_to(columns[j][i : i + 1, :], full)
        for j in range(GROUP)
        for i in range(j, GROUP)
    }
    low, c = {}, {}
    for k in range(GROUP):
        c[k, k] = lax.rsqrt(a[k, k])
        for i in range(k + 1, GROUP):
            low[i, k] = a[i, k] * c[k, k]
        for j in range(k + 1, GROUP):
            for i in range(j, GROUP):
                a[i, j] = a[i, j] - low[i, k] * low[j, k]
        for j in range(k):
            total = low[k, j] * c[j, j]
            for i in range(j + 1, k):
                total = total + low[k, i] * c[i, j]
            c[k, j] = -c[k, k] * total
    return c


def spread(x, width):
    return jnp.concatenate([x] * (width // LANES), axis=1)


def eliminate(block):
    size, width = block.shape
    sub = lax.broadcasted_iota(jnp.int32, (GROUP, LANES), 0)
    groups = [block[i : i + GROUP, :] for i in range(0, size, GROUP)]
    for p in range(len(groups)):
        at = p * GROUP
        rows = groups[p]
        c = factor_group(rows, at)
        done = None
        for j in range(GROUP):
            col = jnp.zeros((GROUP, LANES), F32)
            for i in range(j, GROUP):
                col = jnp.where(sub == i, c[i, j], col)
            term = spread(col, width) * jnp.broadcast_to(rows[j : j + 1, :], (GROUP, width))
            done = term if done is None else done + term
        groups[p] = done
        if p + 1 == len(groups):
            break
        solved = None
        for k in range(GROUP):
            col = jnp.zeros((GROUP, LANES), F32)
            for j in range(k + 1):
                col = jnp.where(sub == j, c[k, j], col)
            term = spread(col, width) * jnp.broadcast_to(done[k : k + 1, :], (GROUP, width))
            solved = term if solved is None else solved + term
        for q in range(p + 1, len(groups)):
            x = groups[q]
            total = None
            for j in range(GROUP):
                term = jnp.broadcast_to(x[:, at + j : at + j + 1], (GROUP, width)) * jnp.broadcast_to(
                    solved[j : j + 1, :], (GROUP, width)
                )
                total = term if total is None else total + term
            groups[q] = x - total
    return jnp.concatenate(groups, axis=0)


def chol_kernel(gram, left, x_out, oh, ol, work):
    rank = gram.shape[0]
    size = min(64, rank)
    work[:, :rank] = gram[...]
    r = lax.broadcasted_iota(jnp.int32, (rank, rank), 0)
    c = lax.broadcasted_iota(jnp.int32, (rank, rank), 1)
    work[:, rank:] = jnp.where(r == c, 1.0, 0.0).astype(F32)

    def step(b, _):
        at = pl.multiple_of(b * size, size)
        rows = pl.ds(at, size)
        width = 2 * rank
        block = pltpu.roll(work[rows, :], lax.rem(width - at, width), 1)
        block = pltpu.roll(eliminate(block), at, 1)
        x_out[rows, :] = block[:, rank:]

        @pl.when(b + 1 < rank // size)
        def _():
            work[...] -= dot_high(block[:, :rank], block, TN)

        return 0

    lax.fori_loop(0, rank // size, step, 0)
    h, l = split(dot_high(left[...], x_out[...], NT))
    oh[...] = h
    ol[...] = l


def chol_inverse(gram, left):
    rows, rank = left.shape
    return pl.pallas_call(
        chol_kernel,
        out_shape=[
            jax.ShapeDtypeStruct((rank, rank), F32),
            jax.ShapeDtypeStruct((rows, rank), BF16),
            jax.ShapeDtypeStruct((rows, rank), BF16),
        ],
        scratch_shapes=[pltpu.VMEM((rank, 2 * rank), F32)],
        compiler_params=params(),
        cost_estimate=cost(4e9, 4 * rows * rank),
        name="chol_inverse",
    )(gram, left)


def right_kernel(at, ka, ga, kb, gb, x, ra, rb, squares):
    rows, rank = ka.shape
    total = jnp.zeros((1, rank), F32)
    for i, (k, g, out) in enumerate(((ka, ga, ra), (kb, gb, rb))):
        value = dot_high(k[...] + g[...], x[...], NT)
        out[...] = value
        row = lax.broadcasted_iota(jnp.int32, (rows, rank), 0) + at[i]
        value = jnp.where(row < at[2], value, 0.0)
        total = total + jnp.sum(value * value, axis=0, keepdims=True)
    squares[...] = jnp.broadcast_to(total, squares.shape)


def right_rows(at_a, at_b, cols, ka, ga, kb, gb, x):
    rows, rank = ka.shape
    vm = pl.BlockSpec(memory_space=pltpu.VMEM)
    return pl.pallas_call(
        right_kernel,
        in_specs=[pl.BlockSpec(memory_space=pltpu.SMEM)] + [vm] * 5,
        out_specs=[vm] * 3,
        out_shape=[jax.ShapeDtypeStruct((rows, rank), F32)] * 2
        + [jax.ShapeDtypeStruct((GROUP, rank), F32)],
        compiler_params=params(),
        cost_estimate=cost(24 * rows * rank * rank, 24 * rows * rank),
        name="right_rows",
    )(scalars(at_a, at_b, cols), ka, ga, kb, gb, x)


def final_kernel(count, total_cols, factor, at, *refs):
    pieces = refs[:count]
    squares, oh, ol, buffer = refs[count : count + 4]
    update, momentum, new_right, rh, rl, nh, nl = refs[-7:]
    u, h = pl.program_id(0), pl.program_id(1)
    half = buffer.shape[0]
    for k in range(count):

        @pl.when((u == k) & (h == 0))
        def _(k=k):
            right = pieces[k][...]
            scale = jnp.sqrt(squares[0:1, :] / total_cols + 1e-06)
            scaled = right / scale
            new_right[...] = scaled
            rh[...], rl[...] = split(right)
            nh[...], nl[...] = split(scaled)

    rows = pl.ds(pl.multiple_of(h * half, half), half)
    a, b = oh[rows, :], ol[rows, :]
    momentum[...] = buffer[...] - 0.05 * dot3(a, b, rh[...], rl[...], NT)
    update[...] = factor * dot3(a, b, nh[...], nl[...], NT)


def final(s, units, pieces, squares, oh, ol, buffer, total_rows, total_cols, before):
    rows, cols = buffer.shape
    unit, rank = pieces[0].shape
    half, count = rows // 2, len(pieces)
    wide = pl.BlockSpec((half, unit), lambda u, h, at: (at[h], at[2 + u]))
    whole = lambda shape: pl.BlockSpec(shape, lambda u, h, at: (0, 0))
    n_in = count + 5
    factor = (total_rows / rank) ** 0.5
    return pl.pallas_call(
        functools.partial(final_kernel, count, total_cols, factor),
        grid_spec=pltpu.PrefetchScalarGridSpec(
            num_scalar_prefetch=1,
            grid=(count, 2),
            in_specs=[whole((unit, rank))] * count
            + [whole((GROUP, rank)), whole((rows, rank)), whole((rows, rank)), wide]
            + [pl.BlockSpec(memory_space=pl.ANY)] * len(before),
            out_specs=[wide, wide, pl.BlockSpec((unit, rank), lambda u, h, at: (at[2 + u], 0))],
            scratch_shapes=[pltpu.VMEM((unit, rank), BF16)] * 4,
        ),
        out_shape=[
            jax.ShapeDtypeStruct((rows, cols), F32),
            jax.ShapeDtypeStruct((rows, cols), F32),
            jax.ShapeDtypeStruct((cols, rank), F32),
        ],
        input_output_aliases={n_in + i: i for i in range(len(before))},
        compiler_params=params(),
        cost_estimate=cost(12 * count * rows * unit * rank, 4 * count * unit * (3 * rows + 2 * rank)),
        name="final",
    )(scalars(s, 1 - s, *units), *pieces, squares, oh, ol, buffer, *before)


def power_of_two(n):
    return n & (n - 1) == 0


def bits_of(n):
    return list(range(n.bit_length() - 1))


def swap(x, axis, bit):
    n = lax.axis_size(axis)
    return lax.ppermute(x, axis, [(i, i ^ (1 << bit)) for i in range(n)])


def sum_over(x, axis):
    n = lax.axis_size(axis)
    if not power_of_two(n):
        return lax.psum(x, axis)
    for bit in bits_of(n):
        x = x + swap(x, axis, bit)
    return x


def on_device(gradient, momentum, right_factor):
    rows, cols = gradient.shape
    rank = right_factor.shape[1]
    n_dp, n_tp = lax.axis_size("dp"), lax.axis_size("tensor")
    d, z = lax.axis_index("dp"), lax.axis_index("tensor")
    half = rows // 2

    s = lax.rem(z, 2)
    buffer, away = left_half(1 - s, gradient, momentum, right_factor, None)
    if power_of_two(n_tp) and n_tp > 1:
        got = swap(away, "tensor", 0)
        buffer, mine = left_half(s, gradient, momentum, right_factor, buffer)
        mine = mine + got
        own = [mine[: half // 2], mine[half // 2 :]]
        for bit in bits_of(n_tp)[1:]:
            own = [x + swap(x, "tensor", bit) for x in own]
        pieces = own + [swap(x, "tensor", 0) for x in own]
    else:
        buffer, mine = left_half(s, gradient, momentum, right_factor, buffer)
        both = lax.psum(jnp.where(s == 0, jnp.stack([mine, away]), jnp.stack([away, mine])), "tensor")
        pieces = [lax.dynamic_index_in_dim(both, i, 0, False) for i in (s, 1 - s)]

    left, lh, ll, gram = gram_of(pieces)
    gram = sum_over(gram, "dp")

    unit = LANES * (-(-cols // (8 * LANES)))
    bits = bits_of(n_dp)
    core = lax.rem(d, 2)
    orders = [bits[1:], bits[1:][::-1]]
    bit_of = lambda b: lax.rem(d // (1 << b), 2)
    sent = [
        w_send(s, [4 * h + 2 * (1 - core), 4 * h + 2 * (1 - core) + 1], buffer, lh, ll, unit)
        for h in range(2)
    ]
    got = [swap(x, "dp", 0) for x in sent]
    x_inv, oh, ol = chol_inverse(gram, left)
    kept, here = [], []
    for h, order in enumerate(orders):
        t = bit_of(order[0])
        base = 4 * h + 2 * core
        send, keep = w_keep(s, [base + 1 - t, base + t], [1 - t, t], buffer, lh, ll, got[h], unit)
        at = (base + t) * unit
        recv = swap(send, "dp", order[0])
        for b in order[1:]:
            x = keep + recv
            n = x.shape[0] // 2
            t = bit_of(b)
            recv = swap(lax.dynamic_slice_in_dim(x, (1 - t) * n, n, 0), "dp", b)
            keep = lax.dynamic_slice_in_dim(x, t * n, n, 0)
            at = at + t * n
        kept.append((keep, recv))
        here.append(at)

    ra, rb, squares = right_rows(here[0], here[1], cols, *kept[0], *kept[1], x_inv)

    near, far = [], []
    for h, (order, x) in enumerate(zip(orders, (ra, rb))):
        for b in order[:0:-1]:
            y = swap(x, "dp", b)
            x = jnp.where(bit_of(b) == 0, jnp.concatenate([x, y]), jnp.concatenate([y, x]))
        t = bit_of(order[0])
        y = swap(x, "dp", order[0])
        base, beside = 4 * h + 2 * core, 4 * h + 2 * (1 - core)
        near.append(((base + t, x), (beside + t, swap(x, "dp", 0))))
        far.append(((base + 1 - t, y), (beside + 1 - t, swap(y, "dp", 0))))

    squares = sum_over(sum_over(squares, "dp"), "tensor")
    outs = ()
    for group in (near, far):
        units = [u for part in group for u, _ in part]
        data = [x for part in group for _, x in part]
        outs = final(s, units, data, squares, oh, ol, buffer, rows * n_dp, cols * n_tp, outs)
    return tuple(outs)


def solution(mesh):
    return jax.shard_map(
        on_device,
        mesh=mesh,
        in_specs=(P("dp", "tensor"), P("dp", "tensor"), P("tensor", None)),
        out_specs=(P("dp", "tensor"), P("dp", "tensor"), P("tensor", None)),
        check_vma=False,
    )
```

time: 453 us -> 243 us (0.54); the launches traced: 447 us -> 242 us
  waiting for transfers between devices: 209 us -> 81.4 us
  matrix products: 121 us -> 0 us
  Pallas kernels: 0 us -> 119 us
  other arithmetic: 77.6 us -> 12 us
  starting transfers between devices: 0.59 us -> 21.6 us
  between operations: 15.6 us -> 0.78 us
  blocking collectives: 11.9 us -> 0 us
    psum x3 -> x0, waiting for transfers between devices: 209 us -> none  [the longest x1 112 us: on_device(): right = lax.psum(terms, 'dp')]
    pallas_call x0 -> x11, Pallas kernels: none -> 119 us  [the longest x2 37.5 us: final(): pl.pallas_call(functools.partial(final_kernel, count, total_cols, factor)...]
    dot_general x5 -> x0, matrix products: 117 us -> none  [the longest x1 33.3 us: on_device(): jnp.dot(ortho, right.T, precision=high, preferred_element_type=jnp.float32)]
    ppermute x0 -> x27, waiting for transfers between devices: none -> 81.4 us  [swap(): return lax.ppermute(x, axis, [(i, i ^ 1 << bit) for i in range(n)])]
    another operation x9 -> x3, other arithmetic: 53.7 us -> 1.85 us  [scalars(): return jnp.stack([jnp.asarray(v, jnp.int32) for v in values])]
    ppermute x0 -> x27, starting transfers between devices: none -> 21.6 us  [swap(): return lax.ppermute(x, axis, [(i, i ^ 1 << bit) for i in range(n)])]
    psum x1 -> x0, blocking collectives: 11.9 us -> none  [on_device(): squares = lax.psum(jnp.sum(right * right, axis=0), 'tensor')]
    div x2 -> x0, other arithmetic: 7.95 us -> none  [the longest x1 6.97 us: on_device(): new_right = right / scale_col]
  transfers between devices with their start and end apart: 3 -> 27, of which waited for: 3 -> 16; matrix products, arithmetic and copies ran while one was open for 0% -> 6% of each run, Pallas kernels for 0% -> 29%
where the time goes in v1:
time: 243 us; the launch traced here: 242 us
  Pallas kernels  119 us (49%)
  waiting for transfers between devices  81.4 us (33%)
  starting transfers between devices  21.6 us (9%)
  other arithmetic  12 us (5%)
  local copies, waits for them, and re-layouts  7.8 us (3%)
    ppermute x27, waiting for transfers between devices, swap(): return lax.ppermute(x, axis, [(i, i ^ 1 << bit) for i in range(n)])  81.4 us
    pallas_call x2, Pallas kernels, final(): pl.pallas_call(functools.partial(final_kernel, count, total_cols, factor)...  37.5 us
    pallas_call x2, Pallas kernels, left_half(): pl.pallas_call(left_kernel, grid_spec=pltpu.PrefetchScalarGridSpec(num_sc...  31.8 us
    ppermute x27, starting transfers between devices, swap(): return lax.ppermute(x, axis, [(i, i ^ 1 << bit) for i in range(n)])  21.6 us
    pallas_call x1, Pallas kernels, chol_inverse(): pl.pallas_call(chol_kernel, out_shape=[jax.ShapeDtypeStruct((rank, rank),...  14.9 us
    pallas_call x2, Pallas kernels, w_keep(): pl.pallas_call(w_keep_kernel, grid_spec=pltpu.PrefetchScalarGridSpec(num_...  14.9 us
    pallas_call x2, Pallas kernels, w_send(): pl.pallas_call(w_send_kernel, grid_spec=pltpu.PrefetchScalarGridSpec(num_...  13.4 us
  transfers between devices with their start and end apart: 27, of which 16 were waited for; matrix products, arithmetic and copies ran while one was open for 6% of the time, Pallas kernels for 29%

profile of v1, /device:TPU:0, one launch (start us, length us, event | category | flops | bytes accessed | tf_op | source)
XLA Modules:
  0.0 242.4 jit_solution(6313845992688134631)
XLA Ops:
  0.6 15.9 %left_half.2 = (f32[640,6912]{1,0:T(8,128)}, f32[320,256]{1,0:T(8,128)}) custom-call(s32[1]{0:T(128)} %bitcast.1.at, f32[640,6912]{1,0:T(8,128)} %g.3, f32[640,6912]{1,0:T(8,128)} %m.3, f32[6912,256]{1,0:T(8,128)} %r.3), custom_call_target="tpu_custom_call" | custom-call | flops 3397386240 | bytes 33619968 | tf_op jit(solution)/shard_map/left_half/pallas_call | solution.py:77
  16.6 3.0 %collective-permute-start = (f32[320,256]{1,0:T(8,128)}, f32[320,256]{1,0:T(8,128)S(1)}, u32[]{:S(2)}, u32[]{:S(2)}) collective-permute-start(f32[320,256]{1,0:T(8,128)} %get-tuple-element.27), channel_id=1, source_target_pairs={{0,1},{1,0},{2,3},{3,2},{4,5},{5,4},{6,7},{7,6},{8,9},{9,8},{10,11... | collective-permute-start | bytes 983048 | tf_op jit(solution)/shard_map/ppermute | solution.py:410
  19.6 15.9 %left_half.3 = (f32[640,6912]{1,0:T(8,128)}, f32[320,256]{1,0:T(8,128)}) custom-call(s32[1]{0:T(128)} %bitcast.at, f32[640,6912]{1,0:T(8,128)} %g.3, f32[640,6912]{1,0:T(8,128)} %m.3, f32[6912,256]{1,0:T(8,128)} %r.3, f32[640,6912]{1,0:T(8,128)} %get-tuple-element.24.rest_0_), custom_call_target="tpu_custom_call", output_to_operand_aliasing={{0}: (4, {})} | custom-call | flops 3397386240 | bytes 33619968 | tf_op jit(solution)/shard_map/left_half/pallas_call | solution.py:77
  35.5 1.0 add.113
  36.5 2.7 %collective-permute-start.2 = (f32[160,256]{1,0:T(8,128)S(1)}, f32[160,256]{1,0:T(8,128)S(1)}, u32[]{:S(2)}, u32[]{:S(2)}) collective-permute-start(f32[160,256]{1,0:T(8,128)S(1)} %get-tuple-element.51), channel_id=1, source_target_pairs={{0,2},{1,3},{2,0},{3,1},{4,6},{5,7},{6,4},{7,5},{8,10},{9,11},{10,... | collective-permute-start | bytes 491528 | tf_op jit(solution)/shard_map/ppermute | solution.py:410
  39.5 10.7 %collective-permute-done.2 = f32[160,256]{1,0:T(8,128)S(1)} collective-permute-done((f32[160,256]{1,0:T(8,128)S(1)}, f32[160,256]{1,0:T(8,128)S(1)}, u32[]{:S(2)}, u32[]{:S(2)}) %collective-permute-start.2) | collective-permute-done | bytes 163872 | tf_op jit(solution)/shard_map/ppermute | solution.py:410
  50.2 3.4 %collective-permute-done.1 = f32[160,256]{1,0:T(8,128)S(1)} collective-permute-done((f32[160,256]{1,0:T(8,128)S(1)}, f32[160,256]{1,0:T(8,128)S(1)}, u32[]{:S(2)}, u32[]{:S(2)}) %collective-permute-start.1) | collective-permute-done | bytes 163872 | tf_op jit(solution)/shard_map/ppermute | solution.py:410
  53.8 2.0 collective-permute-start.3
  55.8 0.7 pad_add_fusion.1.at
  56.4 4.4 %collective-permute-done.4.refs_3_ = f32[160,256]{1,0:T(8,128)S(1)} collective-permute-done((f32[160,256]{1,0:T(8,128)S(1)}, f32[160,256]{1,0:T(8,128)S(1)}, u32[]{:S(2)}, u32[]{:S(2)}) %collective-permute-start.4) | collective-permute-done | bytes 163872 | tf_op jit(solution)/shard_map/ppermute | solution.py:410
  60.8 2.6 %collective-permute-done.3.refs_2_ = f32[160,256]{1,0:T(8,128)S(1)} collective-permute-done((f32[160,256]{1,0:T(8,128)S(1)}, f32[160,256]{1,0:T(8,128)S(1)}, u32[]{:S(2)}, u32[]{:S(2)}) %collective-permute-start.3) | collective-permute-done | bytes 163872 | tf_op jit(solution)/shard_map/ppermute | solution.py:410
  63.4 0.7 copy-done.11
  64.0 3.0 %gram_of.1 = (f32[640,256]{1,0:T(8,128)}, bf16[640,256]{1,0:T(8,128)(2,1)}, bf16[640,256]{1,0:T(8,128)(2,1)}, f32[256,256]{1,0:T(8,128)}) custom-call(f32[160,256]{1,0:T(8,128)} %copy-done.7, f32[160,256]{1,0:T(8,128)} %copy-done.6, f32[160,256]{1,0:T(8,128)} %copy-done.11, f32[160,256]{1,0:T(8,128)} %copy-done.10), custom_call_target="tpu_custom_call" | custom-call | flops 503316480 | bytes 1966080 | tf_op jit(solution)/shard_map/gram_of/pallas_call | solution.py:115
  67.1 6.7 %w_send.2 = f32[1792,256]{1,0:T(8,128)} custom-call(s32[4]{0:T(128)} %pad_add_fusion.1.at, f32[640,6912]{1,0:T(8,128)} %get-tuple-element.25.own.other.refs_7_, f32[640,6912]{1,0:T(8,128)} %get-tuple-element.25.own.other.refs_7_, bf16[640,256]{1,0:T(8,128)(2,1)} %get-tuple-element.28.lh, bf16[640,256]{1,0:T(8,128)(2,1)} %get-tuple-element.29.ll), custom_call_target="tpu_custom_call" | custom-call | flops 1761607680 | bytes 6422528 | tf_op jit(solution)/shard_map/w_send/pallas_call | solution.py:173
  73.8 0.6 pad_add_fusion.3.at
  74.3 6.7 %w_send.3 = f32[1792,256]{1,0:T(8,128)} custom-call(s32[4]{0:T(128)} %pad_add_fusion.3.at, f32[640,6912]{1,0:T(8,128)} %get-tuple-element.25.own.other.refs_7_, f32[640,6912]{1,0:T(8,128)} %get-tuple-element.25.own.other.refs_7_, bf16[640,256]{1,0:T(8,128)(2,1)} %get-tuple-element.28.lh, bf16[640,256]{1,0:T(8,128)(2,1)} %get-tuple-element.29.ll), custom_call_target="tpu_custom_call" | custom-call | flops 1761607680 | bytes 6422528 | tf_op jit(solution)/shard_map/w_send/pallas_call | solution.py:173
  81.0 0.5 collective-permute-start.8
  81.5 0.6 stack.117.at
  82.2 0.6 stack.110.at
  82.8 7.4 %w_keep.2 = (f32[896,256]{1,0:T(8,128)}, f32[896,256]{1,0:T(8,128)}) custom-call(s32[6]{0:T(128)} %stack.110.at, f32[640,6912]{1,0:T(8,128)} %get-tuple-element.25.own.other.refs_7_, f32[640,6912]{1,0:T(8,128)} %get-tuple-element.25.own.other.refs_7_, bf16[640,256]{1,0:T(8,128)(2,1)} %get-tuple-element.28.lh, bf16[640,256]{1,0:T(8,128)(2,1)} %get-tuple-element.29.ll, ...), custom_call_target="tpu_custom_call" | custom-call | flops 1761607680 | bytes 6422528 | tf_op jit(solution)/shard_map/w_keep/pallas_call | solution.py:191
  90.2 1.6 collective-permute-start.6
  91.8 1.2 copy-done
  93.0 7.4 %w_keep.3 = (f32[896,256]{1,0:T(8,128)}, f32[896,256]{1,0:T(8,128)}) custom-call(s32[6]{0:T(128)} %stack.117.at, f32[640,6912]{1,0:T(8,128)} %get-tuple-element.25.own.other.refs_7_, f32[640,6912]{1,0:T(8,128)} %get-tuple-element.25.own.other.refs_7_, bf16[640,256]{1,0:T(8,128)(2,1)} %get-tuple-element.28.lh, bf16[640,256]{1,0:T(8,128)(2,1)} %get-tuple-element.29.ll, ...), custom_call_target="tpu_custom_call" | custom-call | flops 1761607680 | bytes 6422528 | tf_op jit(solution)/shard_map/w_keep/pallas_call | solution.py:191
  100.4 1.5 collective-permute-start.9
  102.0 1.5 collective-permute-done.11
  103.6 0.6 collective-permute-start.12
  104.2 14.2 %collective-permute-done.12 = f32[256,256]{1,0:T(8,128)S(1)} collective-permute-done((f32[256,256]{1,0:T(8,128)S(1)}, f32[256,256]{1,0:T(8,128)S(1)}, u32[]{:S(2)}, u32[]{:S(2)}) %collective-permute-start.12) | collective-permute-done | bytes 262176 | tf_op jit(solution)/shard_map/ppermute | solution.py:410
  118.4 1.6 collective-permute-start.13
  120.0 1.3 add.116
  121.3 0.8 constant_dynamic-slice_fusion.2
  122.2 0.5 collective-permute-start.7
  122.6 1.3 collective-permute-done.9
  123.9 1.3 add.120
  125.2 0.8 constant_dynamic-slice_fusion
  126.3 0.6 pad_add_fusion.at
  126.9 2.6 %collective-permute-done.13 = f32[256,256]{1,0:T(8,128)S(1)} collective-permute-done((f32[256,256]{1,0:T(8,128)S(1)}, f32[256,256]{1,0:T(8,128)S(1)}, u32[]{:S(2)}, u32[]{:S(2)}) %collective-permute-start.13) | collective-permute-done | bytes 262176 | tf_op jit(solution)/shard_map/ppermute | solution.py:410
  129.5 0.7 add.125.gram
  130.2 14.9 %chol_inverse.1 = (f32[256,256]{1,0:T(8,128)}, bf16[640,256]{1,0:T(8,128)(2,1)}, bf16[640,256]{1,0:T(8,128)(2,1)}) custom-call(f32[256,256]{1,0:T(8,128)} %add.125.gram, f32[640,256]{1,0:T(8,128)} %get-tuple-element.35.left), custom_call_target="tpu_custom_call" | custom-call | flops 4000000000 | bytes 655360 | tf_op jit(solution)/shard_map/chol_inverse/pallas_call | solution.py:305
  145.1 0.8 copy-done.8
  146.1 3.4 %right_rows.1 = (f32[448,256]{1,0:T(8,128)}, f32[448,256]{1,0:T(8,128)}, f32[8,256]{1,0:T(8,128)}) custom-call(s32[3]{0:T(128)} %pad_add_fusion.at, f32[448,256]{1,0:T(8,128)} %get-tuple-element.48.ka, f32[448,256]{1,0:T(8,128)} %copy-done.8, f32[448,256]{1,0:T(8,128)} %get-tuple-element.46.kb, f32[448,256]{1,0:T(8,128)} %copy-done.9, ...), custom_call_target="tpu_custom_call" | custom-call | flops 704643072 | bytes 2752512 | tf_op jit(solution)/shard_map/right_rows/pallas_call | solution.py:334
  149.7 1.8 collective-permute-start.14
  151.5 7.8 %collective-permute-done.17 = f32[448,256]{1,0:T(8,128)S(1)} collective-permute-done((f32[448,256]{1,0:T(8,128)}, f32[448,256]{1,0:T(8,128)S(1)}, u32[]{:S(2)}, u32[]{:S(2)}) %collective-permute-start.17) | collective-permute-done | bytes 458784 | tf_op jit(solution)/shard_map/ppermute | solution.py:410
  159.3 2.2 maximum_select_fusion.1.refs_2_
  161.5 1.9 collective-permute-start.18
  163.4 2.2 maximum_select_fusion.refs_0_
  165.6 0.5 collective-permute-start.15
  166.1 0.5 collective-permute-start.25
  166.6 14.3 %collective-permute-done.18.refs_2_ = f32[896,256]{1,0:T(8,128)S(1)} collective-permute-done((f32[896,256]{1,0:T(8,128)}, f32[896,256]{1,0:T(8,128)S(1)}, u32[]{:S(2)}, u32[]{:S(2)}) %collective-permute-start.18) | collective-permute-done | bytes 917536 | tf_op jit(solution)/shard_map/ppermute | solution.py:410
  180.9 3.7 %collective-permute-done.15.refs_0_ = f32[896,256]{1,0:T(8,128)S(1)} collective-permute-done((f32[896,256]{1,0:T(8,128)}, f32[896,256]{1,0:T(8,128)S(1)}, u32[]{:S(2)}, u32[]{:S(2)}) %collective-permute-start.15) | collective-permute-done | bytes 917536 | tf_op jit(solution)/shard_map/ppermute | solution.py:410
  184.6 0.5 collective-permute-start.20
  185.1 2.1 collective-permute-done.20
  187.2 0.7 add.126
  187.9 0.4 collective-permute-start.21
  188.3 3.2 %collective-permute-done.21 = f32[8,256]{1,0:T(8,128)S(1)} collective-permute-done((f32[8,256]{1,0:T(8,128)S(1)}, f32[8,256]{1,0:T(8,128)S(1)}, u32[]{:S(2)}, u32[]{:S(2)}) %collective-permute-start.21) | collective-permute-done | bytes 8224 | tf_op jit(solution)/shard_map/ppermute | solution.py:410
  191.8 3.4 %collective-permute-done.22 = f32[8,256]{1,0:T(8,128)S(1)} collective-permute-done((f32[8,256]{1,0:T(8,128)S(1)}, f32[8,256]{1,0:T(8,128)S(1)}, u32[]{:S(2)}, u32[]{:S(2)}) %collective-permute-start.22) | collective-permute-done | bytes 8224 | tf_op jit(solution)/shard_map/ppermute | solution.py:410
  195.4 3.4 %collective-permute-done.23 = f32[8,256]{1,0:T(8,128)S(1)} collective-permute-done((f32[8,256]{1,0:T(8,128)S(1)}, f32[8,256]{1,0:T(8,128)S(1)}, u32[]{:S(2)}, u32[]{:S(2)}) %collective-permute-start.23) | collective-permute-done | bytes 8224 | tf_op jit(solution)/shard_map/ppermute | solution.py:410
  198.8 0.5 collective-permute-start.24
  199.3 0.6 stack.123.at
  199.9 0.6 stack.103.at
  200.5 2.9 %collective-permute-done.24 = f32[8,256]{1,0:T(8,128)S(1)} collective-permute-done((f32[8,256]{1,0:T(8,128)S(1)}, f32[8,256]{1,0:T(8,128)S(1)}, u32[]{:S(2)}, u32[]{:S(2)}) %collective-permute-start.24) | collective-permute-done | bytes 8224 | tf_op jit(solution)/shard_map/ppermute | solution.py:410
  203.4 0.6 add.130.refs_4_
  204.0 19.0 %final.2 = (f32[640,6912]{1,0:T(8,128)}, f32[640,6912]{1,0:T(8,128)}, f32[6912,256]{1,0:T(8,128)}) custom-call(s32[6]{0:T(128)} %stack.123.at, f32[896,256]{1,0:T(8,128)} %maximum_select_fusion.refs_0_, f32[896,256]{1,0:T(8,128)} %collective-permute-done.25.refs_1_, f32[896,256]{1,0:T(8,128)} %maximum_select_fusion.1.refs_2_, ...), custom_call_target="tpu_custom_call" | custom-call | flops 7046430720 | bytes 34865152 | tf_op jit(solution)/shard_map/final/pallas_call | solution.py:377
  223.0 0.9 copy-done.3
  223.9 18.5 %final.3 = (f32[640,6912]{1,0:T(8,128)}, f32[640,6912]{1,0:T(8,128)}, f32[6912,256]{1,0:T(8,128)}) custom-call(s32[6]{0:T(128)} %stack.103.at, f32[896,256]{1,0:T(8,128)} %copy-done.2, f32[896,256]{1,0:T(8,128)} %collective-permute-done.16.refs_1_, f32[896,256]{1,0:T(8,128)} %copy-done.1, ...), custom_call_target="tpu_custom_call", output_to_operand_aliasing={{0}: (9, {}), {1}: (10, {}), {2}: (11, {})} | custom-call | flops 7046430720 | bytes 34865152 | tf_op jit(solution)/shard_map/final/pallas_call | solution.py:377
  (49 shorter events, 1.9 us)
Async XLA Ops:
  16.6 18.9 %collective-permute-start = (f32[320,256]{1,0:T(8,128)}, f32[320,256]{1,0:T(8,128)S(1)}, u32[]{:S(2)}, u32[]{:S(2)}) collective-permute-start(f32[320,256]{1,0:T(8,128)} %get-tuple-element.27), channel_id=1, source_target_pairs={{0,1},{1,0},{2,3},{3,2},{4,5},{5,4},{6,7},{7,6},{8,9},{9,8},{10,11... | collective-permute-start | bytes 983048 | tf_op jit(solution)/shard_map/ppermute | solution.py:410
  36.5 13.7 %collective-permute-start.2 = (f32[160,256]{1,0:T(8,128)S(1)}, f32[160,256]{1,0:T(8,128)S(1)}, u32[]{:S(2)}, u32[]{:S(2)}) collective-permute-start(f32[160,256]{1,0:T(8,128)S(1)} %get-tuple-element.51), channel_id=1, source_target_pairs={{0,2},{1,3},{2,0},{3,1},{4,6},{5,7},{6,4},{7,5},{8,10},{9,11},{10,... | collective-permute-start | bytes 491528 | tf_op jit(solution)/shard_map/ppermute | solution.py:410
  39.2 14.4 %collective-permute-start.1 = (f32[160,256]{1,0:T(8,128)S(1)}, f32[160,256]{1,0:T(8,128)S(1)}, u32[]{:S(2)}, u32[]{:S(2)}) collective-permute-start(f32[160,256]{1,0:T(8,128)S(1)} %get-tuple-element.52), channel_id=1, source_target_pairs={{0,2},{1,3},{2,0},{3,1},{4,6},{5,7},{6,4},{7,5},{8,10},{9,11},{10,... | collective-permute-start | bytes 491528 | tf_op jit(solution)/shard_map/ppermute | solution.py:410
  53.6 9.7 %copy-start.6 = (f32[160,256]{1,0:T(8,128)}, f32[160,256]{1,0:T(8,128)S(1)}, u32[]{:S(2)}) copy-start(f32[160,256]{1,0:T(8,128)S(1)} %get-tuple-element.49.refs_1_) | copy-start | bytes 491524
  53.7 9.7 %copy-start.7 = (f32[160,256]{1,0:T(8,128)}, f32[160,256]{1,0:T(8,128)S(1)}, u32[]{:S(2)}) copy-start(f32[160,256]{1,0:T(8,128)S(1)} %get-tuple-element.50.refs_0_) | copy-start | bytes 491524
  53.7 7.1 %collective-permute-start.4 = (f32[160,256]{1,0:T(8,128)S(1)}, f32[160,256]{1,0:T(8,128)S(1)}, u32[]{:S(2)}, u32[]{:S(2)}) collective-permute-start(f32[160,256]{1,0:T(8,128)S(1)} %get-tuple-element.49.refs_1_), channel_id=1, source_target_pairs={{0,1},{1,0},{2,3},{3,2},{4,5},{5,4},{6,7},{7,6},{8,9},{9,8},{10,11... | collective-permute-start | bytes 491528 | tf_op jit(solution)/shard_map/ppermute | solution.py:410
  53.8 9.6 %collective-permute-start.3 = (f32[160,256]{1,0:T(8,128)S(1)}, f32[160,256]{1,0:T(8,128)S(1)}, u32[]{:S(2)}, u32[]{:S(2)}) collective-permute-start(f32[160,256]{1,0:T(8,128)S(1)} %get-tuple-element.50.refs_0_), channel_id=1, source_target_pairs={{0,1},{1,0},{2,3},{3,2},{4,5},{5,4},{6,7},{7,6},{8,9},{9,8},{10,11... | collective-permute-start | bytes 491528 | tf_op jit(solution)/shard_map/ppermute | solution.py:410
  60.8 2.6 %copy-start.10 = (f32[160,256]{1,0:T(8,128)}, f32[160,256]{1,0:T(8,128)S(1)}, u32[]{:S(2)}) copy-start(f32[160,256]{1,0:T(8,128)S(1)} %collective-permute-done.4.refs_3_) | copy-start | bytes 491524
  63.4 0.7 copy-start.11
  73.8 9.0 %collective-permute-start.5 = (f32[1792,256]{1,0:T(8,128)}, f32[1792,256]{1,0:T(8,128)}, u32[]{:S(2)}, u32[]{:S(2)}) collective-permute-start(f32[1792,256]{1,0:T(8,128)} %w_send.2), channel_id=1, source_target_pairs={{0,4},{4,0},{8,12},{12,8},{16,20},{20,16},{24,28},{28,24},{1,5},{5... | collective-permute-start | bytes 5505032 | tf_op jit(solution)/shard_map/ppermute | solution.py:410
  81.0 10.8 %collective-permute-start.8 = (f32[1792,256]{1,0:T(8,128)}, f32[1792,256]{1,0:T(8,128)S(1)}, u32[]{:S(2)}, u32[]{:S(2)}) collective-permute-start(f32[1792,256]{1,0:T(8,128)} %w_send.3), channel_id=1, source_target_pairs={{0,4},{4,0},{8,12},{12,8},{16,20},{20,16},{24,28},{28,24},{1,5},{5... | collective-permute-start | bytes 5505032 | tf_op jit(solution)/shard_map/ppermute | solution.py:410
  90.2 11.8 %copy-start.5 = (f32[256,256]{1,0:T(8,128)S(1)}, f32[256,256]{1,0:T(8,128)}, u32[]{:S(2)}) copy-start(f32[256,256]{1,0:T(8,128)} %get-tuple-element.34) | copy-start | bytes 786436
  90.2 29.8 %copy-start.4 = (f32[896,256]{1,0:T(8,128)S(1)}, f32[896,256]{1,0:T(8,128)}, u32[]{:S(2)}) copy-start(f32[896,256]{1,0:T(8,128)} %get-tuple-element.30) | copy-start | bytes 2752516
  90.2 29.8 %collective-permute-start.6 = (f32[896,256]{1,0:T(8,128)}, f32[896,256]{1,0:T(8,128)}, u32[]{:S(2)}, u32[]{:S(2)}) collective-permute-start(f32[896,256]{1,0:T(8,128)} %get-tuple-element.31), channel_id=1, source_target_pairs={{0,8},{4,12},{8,0},{12,4},{16,24},{20,28},{24,16},{28,20},{1,9},{5... | collective-permute-start | bytes 2752520 | tf_op jit(solution)/shard_map/ppermute | solution.py:410
  91.8 1.2 copy-start
  100.4 23.4 %collective-permute-start.9 = (f32[896,256]{1,0:T(8,128)}, f32[896,256]{1,0:T(8,128)S(1)}, u32[]{:S(2)}, u32[]{:S(2)}) collective-permute-start(f32[896,256]{1,0:T(8,128)} %get-tuple-element.33), channel_id=1, source_target_pairs={{0,16},{4,20},{8,24},{12,28},{16,0},{20,4},{24,8},{28,12},{1,17},{... | collective-permute-start | bytes 2752520 | tf_op jit(solution)/shard_map/ppermute | solution.py:410
  102.0 1.5 collective-permute-start.11
  103.6 14.8 %collective-permute-start.12 = (f32[256,256]{1,0:T(8,128)S(1)}, f32[256,256]{1,0:T(8,128)S(1)}, u32[]{:S(2)}, u32[]{:S(2)}) collective-permute-start(f32[256,256]{1,0:T(8,128)S(1)} %add.123), channel_id=1, source_target_pairs={{0,8},{4,12},{8,0},{12,4},{16,24},{20,28},{24,16},{28,20},{1,9},{5... | collective-permute-start | bytes 786440 | tf_op jit(solution)/shard_map/ppermute | solution.py:410
  118.4 11.1 %collective-permute-start.13 = (f32[256,256]{1,0:T(8,128)S(1)}, f32[256,256]{1,0:T(8,128)S(1)}, u32[]{:S(2)}, u32[]{:S(2)}) collective-permute-start(f32[256,256]{1,0:T(8,128)S(1)} %add.124), channel_id=1, source_target_pairs={{0,16},{4,20},{8,24},{12,28},{16,0},{20,4},{24,8},{28,12},{1,17},{... | collective-permute-start | bytes 786440 | tf_op jit(solution)/shard_map/ppermute | solution.py:410
  122.2 23.0 %collective-permute-start.7 = (f32[448,256]{1,0:T(8,128)S(1)}, f32[448,256]{1,0:T(8,128)S(1)}, u32[]{:S(2)}, u32[]{:S(2)}) collective-permute-start(f32[448,256]{1,0:T(8,128)S(1)} %get-tuple-element.47), channel_id=1, source_target_pairs={{0,16},{4,20},{8,24},{12,28},{16,0},{20,4},{24,8},{28,12},{1,17},{... | collective-permute-start | bytes 1376264 | tf_op jit(solution)/shard_map/ppermute | solution.py:410
  126.0 19.1 %collective-permute-start.10 = (f32[448,256]{1,0:T(8,128)S(1)}, f32[448,256]{1,0:T(8,128)S(1)}, u32[]{:S(2)}, u32[]{:S(2)}) collective-permute-start(f32[448,256]{1,0:T(8,128)S(1)} %get-tuple-element.45), channel_id=1, source_target_pairs={{0,8},{4,12},{8,0},{12,4},{16,24},{20,28},{24,16},{28,20},{1,9},{5... | collective-permute-start | bytes 1376264 | tf_op jit(solution)/shard_map/ppermute | solution.py:410
  145.1 0.8 copy-start.8
  145.1 0.9 copy-start.9
  149.5 9.9 %collective-permute-start.17 = (f32[448,256]{1,0:T(8,128)}, f32[448,256]{1,0:T(8,128)S(1)}, u32[]{:S(2)}, u32[]{:S(2)}) collective-permute-start(f32[448,256]{1,0:T(8,128)} %get-tuple-element.38), channel_id=1, source_target_pairs={{0,8},{4,12},{8,0},{12,4},{16,24},{20,28},{24,16},{28,20},{1,9},{5... | collective-permute-start | bytes 1376264 | tf_op jit(solution)/shard_map/ppermute | solution.py:410
  149.7 13.7 %collective-permute-start.14 = (f32[448,256]{1,0:T(8,128)}, f32[448,256]{1,0:T(8,128)S(1)}, u32[]{:S(2)}, u32[]{:S(2)}) collective-permute-start(f32[448,256]{1,0:T(8,128)} %get-tuple-element.37), channel_id=1, source_target_pairs={{0,16},{4,20},{8,24},{12,28},{16,0},{20,4},{24,8},{28,12},{1,17},{... | collective-permute-start | bytes 1376264 | tf_op jit(solution)/shard_map/ppermute | solution.py:410
  161.5 19.4 %collective-permute-start.18 = (f32[896,256]{1,0:T(8,128)}, f32[896,256]{1,0:T(8,128)S(1)}, u32[]{:S(2)}, u32[]{:S(2)}) collective-permute-start(f32[896,256]{1,0:T(8,128)} %maximum_select_fusion.1.refs_2_), channel_id=1, source_target_pairs={{0,16},{4,20},{8,24},{12,28},{16,0},{20,4},{24,8},{28,12},{1,17},{... | collective-permute-start | bytes 2752520 | tf_op jit(solution)/shard_map/ppermute | solution.py:410
  165.6 18.9 %collective-permute-start.15 = (f32[896,256]{1,0:T(8,128)}, f32[896,256]{1,0:T(8,128)S(1)}, u32[]{:S(2)}, u32[]{:S(2)}) collective-permute-start(f32[896,256]{1,0:T(8,128)} %maximum_select_fusion.refs_0_), channel_id=1, source_target_pairs={{0,8},{4,12},{8,0},{12,4},{16,24},{20,28},{24,16},{28,20},{1,9},{5... | collective-permute-start | bytes 2752520 | tf_op jit(solution)/shard_map/ppermute | solution.py:410
  166.1 37.9 %collective-permute-start.26 = (f32[896,256]{1,0:T(8,128)}, f32[896,256]{1,0:T(8,128)}, u32[]{:S(2)}, u32[]{:S(2)}) collective-permute-start(f32[896,256]{1,0:T(8,128)} %maximum_select_fusion.1.refs_2_), channel_id=1, source_target_pairs={{0,4},{4,0},{8,12},{12,8},{16,20},{20,16},{24,28},{28,24},{1,5},{5... | collective-permute-start | bytes 2752520 | tf_op jit(solution)/shard_map/ppermute | solution.py:410
  166.1 37.9 %collective-permute-start.25 = (f32[896,256]{1,0:T(8,128)}, f32[896,256]{1,0:T(8,128)}, u32[]{:S(2)}, u32[]{:S(2)}) collective-permute-start(f32[896,256]{1,0:T(8,128)} %maximum_select_fusion.refs_0_), channel_id=1, source_target_pairs={{0,4},{4,0},{8,12},{12,8},{16,20},{20,16},{24,28},{28,24},{1,5},{5... | collective-permute-start | bytes 2752520 | tf_op jit(solution)/shard_map/ppermute | solution.py:410
  180.9 42.1 %copy-start.1 = (f32[896,256]{1,0:T(8,128)}, f32[896,256]{1,0:T(8,128)S(1)}, u32[]{:S(2)}) copy-start(f32[896,256]{1,0:T(8,128)S(1)} %collective-permute-done.18.refs_2_) | copy-start | bytes 2752516
  180.9 42.1 %collective-permute-start.19 = (f32[896,256]{1,0:T(8,128)S(1)}, f32[896,256]{1,0:T(8,128)S(1)}, u32[]{:S(2)}, u32[]{:S(2)}) collective-permute-start(f32[896,256]{1,0:T(8,128)S(1)} %collective-permute-done.18.refs_2_), channel_id=1, source_target_pairs={{0,4},{4,0},{8,12},{12,8},{16,20},{20,16},{24,28},{28,24},{1,5},{5... | collective-permute-start | bytes 2752520 | tf_op jit(solution)/shard_map/ppermute | solution.py:410
  184.6 38.5 %copy-start.2 = (f32[896,256]{1,0:T(8,128)}, f32[896,256]{1,0:T(8,128)S(1)}, u32[]{:S(2)}) copy-start(f32[896,256]{1,0:T(8,128)S(1)} %collective-permute-done.15.refs_0_) | copy-start | bytes 2752516
  184.6 38.5 %collective-permute-start.16 = (f32[896,256]{1,0:T(8,128)S(1)}, f32[896,256]{1,0:T(8,128)}, u32[]{:S(2)}, u32[]{:S(2)}) collective-permute-start(f32[896,256]{1,0:T(8,128)S(1)} %collective-permute-done.15.refs_0_), channel_id=1, source_target_pairs={{0,4},{4,0},{8,12},{12,8},{16,20},{20,16},{24,28},{28,24},{1,5},{5... | collective-permute-start | bytes 2752520 | tf_op jit(solution)/shard_map/ppermute | solution.py:410
  184.6 2.6 %collective-permute-start.20 = (f32[8,256]{1,0:T(8,128)}, f32[8,256]{1,0:T(8,128)S(1)}, u32[]{:S(2)}, u32[]{:S(2)}) collective-permute-start(f32[8,256]{1,0:T(8,128)} %get-tuple-element.39), channel_id=1, source_target_pairs={{0,4},{4,0},{8,12},{12,8},{16,20},{20,16},{24,28},{28,24},{1,5},{5... | collective-permute-start | bytes 24584 | tf_op jit(solution)/shard_map/ppermute | solution.py:410
  187.9 3.7 %collective-permute-start.21 = (f32[8,256]{1,0:T(8,128)S(1)}, f32[8,256]{1,0:T(8,128)S(1)}, u32[]{:S(2)}, u32[]{:S(2)}) collective-permute-start(f32[8,256]{1,0:T(8,128)S(1)} %add.126), channel_id=1, source_target_pairs={{0,8},{4,12},{8,0},{12,4},{16,24},{20,28},{24,16},{28,20},{1,9},{5... | collective-permute-start | bytes 24584 | tf_op jit(solution)/shard_map/ppermute | solution.py:410
  191.5 3.7 %collective-permute-start.22 = (f32[8,256]{1,0:T(8,128)S(1)}, f32[8,256]{1,0:T(8,128)S(1)}, u32[]{:S(2)}, u32[]{:S(2)}) collective-permute-start(f32[8,256]{1,0:T(8,128)S(1)} %add.127), channel_id=1, source_target_pairs={{0,16},{4,20},{8,24},{12,28},{16,0},{20,4},{24,8},{28,12},{1,17},{... | collective-permute-start | bytes 24584 | tf_op jit(solution)/shard_map/ppermute | solution.py:410
  195.2 3.7 %collective-permute-start.23 = (f32[8,256]{1,0:T(8,128)S(1)}, f32[8,256]{1,0:T(8,128)S(1)}, u32[]{:S(2)}, u32[]{:S(2)}) collective-permute-start(f32[8,256]{1,0:T(8,128)S(1)} %add.128), channel_id=1, source_target_pairs={{0,1},{1,0},{2,3},{3,2},{4,5},{5,4},{6,7},{7,6},{8,9},{9,8},{10,11... | collective-permute-start | bytes 24584 | tf_op jit(solution)/shard_map/ppermute | solution.py:410
  198.8 4.5 %collective-permute-start.24 = (f32[8,256]{1,0:T(8,128)S(1)}, f32[8,256]{1,0:T(8,128)S(1)}, u32[]{:S(2)}, u32[]{:S(2)}) collective-permute-start(f32[8,256]{1,0:T(8,128)S(1)} %add.129), channel_id=1, source_target_pairs={{0,2},{1,3},{2,0},{3,1},{4,6},{5,7},{6,4},{7,5},{8,10},{9,11},{10,... | collective-permute-start | bytes 24584 | tf_op jit(solution)/shard_map/ppermute | solution.py:410
  223.0 0.9 copy-start.3

commit v2 on v1

--- a/solution.py
+++ b/solution.py
@@ -7,6 +7,7 @@
 from jax.experimental.pallas import tpu as pltpu
 from jax.sharding import PartitionSpec as P
 
+
 F32 = jnp.float32
 BF16 = jnp.bfloat16
 HIGH = lax.Precision.HIGHEST
@@ -16,6 +17,9 @@
 NN = (((1,), (0,)), ((), ()))
 NT = (((1,), (1,)), ((), ()))
 TN = (((0,), (0,)), ((), ()))
+
+
+ANY = pl.BlockSpec(memory_space=pl.ANY)
 
 
 def params(**kw):
@@ -80,7 +84,7 @@
             num_scalar_prefetch=1,
             grid=(cols // wide,),
             in_specs=[block, block, pl.BlockSpec((wide, rank), lambda j, at: (j, 0))]
-            + ([] if first else [pl.BlockSpec(memory_space=pl.ANY)]),
+            + ([] if first else [ANY]),
             out_specs=[block, pl.BlockSpec((half, rank), lambda j, at: (0, 0))],
         ),
         out_shape=[
@@ -302,8 +306,11 @@
 
 def chol_inverse(gram, left):
     rows, rank = left.shape
+    vm = pl.BlockSpec(memory_space=pltpu.VMEM)
     return pl.pallas_call(
         chol_kernel,
+        in_specs=[vm, vm],
+        out_specs=[vm] * 3,
         out_shape=[
             jax.ShapeDtypeStruct((rank, rank), F32),
             jax.ShapeDtypeStruct((rows, rank), BF16),
@@ -343,6 +350,26 @@
     )(scalars(at_a, at_b, cols), ka, ga, kb, gb, x)
 
 
+def join_kernel(at, x, y, out):
+    n = x.shape[0]
+    out[pl.ds(pl.multiple_of(at[0] * n, GROUP), n), :] = x[...]
+    out[pl.ds(pl.multiple_of((1 - at[0]) * n, GROUP), n), :] = y[...]
+
+
+def join(t, x, y):
+    rows, rank = x.shape
+    vm = pl.BlockSpec(memory_space=pltpu.VMEM)
+    return pl.pallas_call(
+        join_kernel,
+        in_specs=[pl.BlockSpec(memory_space=pltpu.SMEM), vm, vm],
+        out_specs=vm,
+        out_shape=jax.ShapeDtypeStruct((2 * rows, rank), F32),
+        compiler_params=params(),
+        cost_estimate=cost(rows * rank, 16 * rows * rank),
+        name="join",
+    )(scalars(t), x, y)
+
+
 def final_kernel(count, total_cols, factor, at, *refs):
     pieces = refs[:count]
     squares, oh, ol, buffer = refs[count : count + 4]
@@ -381,7 +408,7 @@
             grid=(count, 2),
             in_specs=[whole((unit, rank))] * count
             + [whole((GROUP, rank)), whole((rows, rank)), whole((rows, rank)), wide]
-            + [pl.BlockSpec(memory_space=pl.ANY)] * len(before),
+            + [ANY] * len(before),
             out_specs=[wide, wide, pl.BlockSpec((unit, rank), lambda u, h, at: (at[2 + u], 0))],
             scratch_shapes=[pltpu.VMEM((unit, rank), BF16)] * 4,
         ),
@@ -415,13 +442,13 @@
     if not power_of_two(n):
         return lax.psum(x, axis)
     for bit in bits_of(n):
-        x = x + swap(x, axis, bit)
+        y = swap(x, axis, bit)
+        x = x + y
     return x
 
 
 def on_device(gradient, momentum, right_factor):
     rows, cols = gradient.shape
-    rank = right_factor.shape[1]
     n_dp, n_tp = lax.axis_size("dp"), lax.axis_size("tensor")
     d, z = lax.axis_index("dp"), lax.axis_index("tensor")
     half = rows // 2
@@ -449,12 +476,11 @@
     core = lax.rem(d, 2)
     orders = [bits[1:], bits[1:][::-1]]
     bit_of = lambda b: lax.rem(d // (1 << b), 2)
-    sent = [
-        w_send(s, [4 * h + 2 * (1 - core), 4 * h + 2 * (1 - core) + 1], buffer, lh, ll, unit)
-        for h in range(2)
-    ]
-    got = [swap(x, "dp", 0) for x in sent]
-    x_inv, oh, ol = chol_inverse(gram, left)
+    got = []
+    for h in range(2):
+        units = [4 * h + 2 * (1 - core), 4 * h + 2 * (1 - core) + 1]
+        sent = w_send(s, units, buffer, lh, ll, unit)
+        got.append(swap(sent, "dp", 0))
     kept, here = [], []
     for h, order in enumerate(orders):
         t = bit_of(order[0])
@@ -472,20 +498,21 @@
         kept.append((keep, recv))
         here.append(at)
 
+    x_inv, oh, ol = chol_inverse(gram, left)
     ra, rb, squares = right_rows(here[0], here[1], cols, *kept[0], *kept[1], x_inv)
+    squares = sum_over(sum_over(squares, "dp"), "tensor")
 
     near, far = [], []
     for h, (order, x) in enumerate(zip(orders, (ra, rb))):
         for b in order[:0:-1]:
             y = swap(x, "dp", b)
-            x = jnp.where(bit_of(b) == 0, jnp.concatenate([x, y]), jnp.concatenate([y, x]))
+            x = join(bit_of(b), x, y)
         t = bit_of(order[0])
         y = swap(x, "dp", order[0])
         base, beside = 4 * h + 2 * core, 4 * h + 2 * (1 - core)
         near.append(((base + t, x), (beside + t, swap(x, "dp", 0))))
         far.append(((base + 1 - t, y), (beside + 1 - t, swap(y, "dp", 0))))
 
-    squares = sum_over(sum_over(squares, "dp"), "tensor")
     outs = ()
     for group in (near, far):
         units = [u for part in group for u, _ in part]

time: 243 us -> 245 us (level)
  other arithmetic: 12 us -> 7.53 us
  Pallas kernels: 119 us -> 123 us
    select_n x2 -> x0, other arithmetic: 4.37 us -> none  [on_device(): jnp.where(bit_of(b) == 0, jnp.concatenate([x, y]), jnp.concatenate([y, x]))]
    pallas_call x1 -> x3, Pallas kernels: 14.9 us -> 19.2 us  [the longest x1 14.9 us: chol_inverse(): pl.pallas_call(chol_kernel, in_specs=[vm, vm], out_specs=[vm] * 3, out_sh...]
    unnamed x24 -> x28, local copies, waits for them, and re-layouts: 3.73 us -> 5.27 us
  transfers between devices with their start and end apart: 27 -> 27, of which waited for: 16 -> 16; matrix products, arithmetic and copies ran while one was open for 6% -> 4% of each run, Pallas kernels for 29% -> 31%
where the time goes in v2:
time: 245 us; the launch traced here: 244 us
  Pallas kernels  123 us (50%)
  waiting for transfers between devices  81.1 us (33%)
  starting transfers between devices  21.9 us (9%)
  local copies, waits for them, and re-layouts  9.55 us (4%)
  other arithmetic  7.53 us (3%)
    ppermute x27, waiting for transfers between devices, swap(): return lax.ppermute(x, axis, [(i, i ^ 1 << bit) for i in range(n)])  81.1 us
    pallas_call x2, Pallas kernels, final(): pl.pallas_call(functools.partial(final_kernel, count, total_cols, factor)...  37.5 us
    pallas_call x2, Pallas kernels, left_half(): pl.pallas_call(left_kernel, grid_spec=pltpu.PrefetchScalarGridSpec(num_sc...  31.8 us
    ppermute x27, starting transfers between devices, swap(): return lax.ppermute(x, axis, [(i, i ^ 1 << bit) for i in range(n)])  21.9 us
    pallas_call x1, Pallas kernels, chol_inverse(): pl.pallas_call(chol_kernel, in_specs=[vm, vm], out_specs=[vm] * 3, out_sh...  14.9 us
    pallas_call x2, Pallas kernels, w_keep(): pl.pallas_call(w_keep_kernel, grid_spec=pltpu.PrefetchScalarGridSpec(num_...  14.8 us
    pallas_call x2, Pallas kernels, w_send(): pl.pallas_call(w_send_kernel, grid_spec=pltpu.PrefetchScalarGridSpec(num_...  13.4 us
    unnamed x28, local copies, waits for them, and re-layouts  5.27 us
  transfers between devices with their start and end apart: 27, of which 16 were waited for; matrix products, arithmetic and copies ran while one was open for 4% of the time, Pallas kernels for 31%

profile of v2, /device:TPU:0, one launch (start us, length us, event | category | flops | bytes accessed | tf_op | source)
XLA Modules:
  0.0 244.0 jit_solution(8864596819197304899)
XLA Ops:
  0.6 16.0 %left_half.2 = (f32[640,6912]{1,0:T(8,128)}, f32[320,256]{1,0:T(8,128)}) custom-call(s32[1]{0:T(128)} %bitcast.1.at, f32[640,6912]{1,0:T(8,128)} %g.3, f32[640,6912]{1,0:T(8,128)} %m.3, f32[6912,256]{1,0:T(8,128)} %r.3), custom_call_target="tpu_custom_call" | custom-call | flops 3397386240 | bytes 33619968 | tf_op jit(solution)/shard_map/left_half/pallas_call | solution.py:81
  16.6 3.0 %collective-permute-start = (f32[320,256]{1,0:T(8,128)}, f32[320,256]{1,0:T(8,128)S(1)}, u32[]{:S(2)}, u32[]{:S(2)}) collective-permute-start(f32[320,256]{1,0:T(8,128)} %get-tuple-element.27), channel_id=1, source_target_pairs={{0,1},{1,0},{2,3},{3,2},{4,5},{5,4},{6,7},{7,6},{8,9},{9,8},{10,11... | collective-permute-start | bytes 983048 | tf_op jit(solution)/shard_map/ppermute | solution.py:437
  19.6 15.9 %left_half.3 = (f32[640,6912]{1,0:T(8,128)}, f32[320,256]{1,0:T(8,128)}) custom-call(s32[1]{0:T(128)} %bitcast.at, f32[640,6912]{1,0:T(8,128)} %g.3, f32[640,6912]{1,0:T(8,128)} %m.3, f32[6912,256]{1,0:T(8,128)} %r.3, f32[640,6912]{1,0:T(8,128)} %get-tuple-element.24.rest_0_), custom_call_target="tpu_custom_call", output_to_operand_aliasing={{0}: (4, {})} | custom-call | flops 3397386240 | bytes 33619968 | tf_op jit(solution)/shard_map/left_half/pallas_call | solution.py:81
  35.5 1.0 add.113
  36.5 2.7 %collective-permute-start.2 = (f32[160,256]{1,0:T(8,128)S(1)}, f32[160,256]{1,0:T(8,128)S(1)}, u32[]{:S(2)}, u32[]{:S(2)}) collective-permute-start(f32[160,256]{1,0:T(8,128)S(1)} %get-tuple-element.51), channel_id=1, source_target_pairs={{0,2},{1,3},{2,0},{3,1},{4,6},{5,7},{6,4},{7,5},{8,10},{9,11},{10,... | collective-permute-start | bytes 491528 | tf_op jit(solution)/shard_map/ppermute | solution.py:437
  39.5 10.7 %collective-permute-done.2 = f32[160,256]{1,0:T(8,128)S(1)} collective-permute-done((f32[160,256]{1,0:T(8,128)S(1)}, f32[160,256]{1,0:T(8,128)S(1)}, u32[]{:S(2)}, u32[]{:S(2)}) %collective-permute-start.2) | collective-permute-done | bytes 163872 | tf_op jit(solution)/shard_map/ppermute | solution.py:437
  50.2 3.4 %collective-permute-done.1 = f32[160,256]{1,0:T(8,128)S(1)} collective-permute-done((f32[160,256]{1,0:T(8,128)S(1)}, f32[160,256]{1,0:T(8,128)S(1)}, u32[]{:S(2)}, u32[]{:S(2)}) %collective-permute-start.1) | collective-permute-done | bytes 163872 | tf_op jit(solution)/shard_map/ppermute | solution.py:437
  53.8 2.0 collective-permute-start.3
  55.8 0.6 pad_add_fusion.1.at
  56.4 4.4 %collective-permute-done.4.refs_3_ = f32[160,256]{1,0:T(8,128)S(1)} collective-permute-done((f32[160,256]{1,0:T(8,128)S(1)}, f32[160,256]{1,0:T(8,128)S(1)}, u32[]{:S(2)}, u32[]{:S(2)}) %collective-permute-start.4) | collective-permute-done | bytes 163872 | tf_op jit(solution)/shard_map/ppermute | solution.py:437
  60.8 2.6 %collective-permute-done.3.refs_2_ = f32[160,256]{1,0:T(8,128)S(1)} collective-permute-done((f32[160,256]{1,0:T(8,128)S(1)}, f32[160,256]{1,0:T(8,128)S(1)}, u32[]{:S(2)}, u32[]{:S(2)}) %collective-permute-start.3) | collective-permute-done | bytes 163872 | tf_op jit(solution)/shard_map/ppermute | solution.py:437
  63.4 0.7 copy-done.13
  64.1 3.0 %gram_of.1 = (f32[640,256]{1,0:T(8,128)}, bf16[640,256]{1,0:T(8,128)(2,1)}, bf16[640,256]{1,0:T(8,128)(2,1)}, f32[256,256]{1,0:T(8,128)}) custom-call(f32[160,256]{1,0:T(8,128)} %copy-done.9, f32[160,256]{1,0:T(8,128)} %copy-done.8, f32[160,256]{1,0:T(8,128)} %copy-done.13, f32[160,256]{1,0:T(8,128)} %copy-done.12), custom_call_target="tpu_custom_call" | custom-call | flops 503316480 | bytes 1966080 | tf_op jit(solution)/shard_map/gram_of/pallas_call | solution.py:119
  67.1 6.7 %w_send.2 = f32[1792,256]{1,0:T(8,128)} custom-call(s32[4]{0:T(128)} %pad_add_fusion.1.at, f32[640,6912]{1,0:T(8,128)} %get-tuple-element.25.own.other.refs_7_, f32[640,6912]{1,0:T(8,128)} %get-tuple-element.25.own.other.refs_7_, bf16[640,256]{1,0:T(8,128)(2,1)} %get-tuple-element.28.lh, bf16[640,256]{1,0:T(8,128)(2,1)} %get-tuple-element.29.ll), custom_call_target="tpu_custom_call" | custom-call | flops 1761607680 | bytes 6422528 | tf_op jit(solution)/shard_map/w_send/pallas_call | solution.py:177
  73.8 0.6 pad_add_fusion.3.at
  74.4 6.7 %w_send.3 = f32[1792,256]{1,0:T(8,128)} custom-call(s32[4]{0:T(128)} %pad_add_fusion.3.at, f32[640,6912]{1,0:T(8,128)} %get-tuple-element.25.own.other.refs_7_, f32[640,6912]{1,0:T(8,128)} %get-tuple-element.25.own.other.refs_7_, bf16[640,256]{1,0:T(8,128)(2,1)} %get-tuple-element.28.lh, bf16[640,256]{1,0:T(8,128)(2,1)} %get-tuple-element.29.ll), custom_call_target="tpu_custom_call" | custom-call | flops 1761607680 | bytes 6422528 | tf_op jit(solution)/shard_map/w_send/pallas_call | solution.py:177
  81.0 0.5 collective-permute-start.8
  81.6 0.7 stack.119.at
  82.2 0.6 stack.113.at
  82.9 7.4 %w_keep.2 = (f32[896,256]{1,0:T(8,128)}, f32[896,256]{1,0:T(8,128)}) custom-call(s32[6]{0:T(128)} %stack.113.at, f32[640,6912]{1,0:T(8,128)} %get-tuple-element.25.own.other.refs_7_, f32[640,6912]{1,0:T(8,128)} %get-tuple-element.25.own.other.refs_7_, bf16[640,256]{1,0:T(8,128)(2,1)} %get-tuple-element.28.lh, bf16[640,256]{1,0:T(8,128)(2,1)} %get-tuple-element.29.ll, ...), custom_call_target="tpu_custom_call" | custom-call | flops 1761607680 | bytes 6422528 | tf_op jit(solution)/shard_map/w_keep/pallas_call | solution.py:195
  90.3 1.6 collective-permute-start.6
  91.9 1.2 copy-done
  93.1 7.4 %w_keep.3 = (f32[896,256]{1,0:T(8,128)}, f32[896,256]{1,0:T(8,128)}) custom-call(s32[6]{0:T(128)} %stack.119.at, f32[640,6912]{1,0:T(8,128)} %get-tuple-element.25.own.other.refs_7_, f32[640,6912]{1,0:T(8,128)} %get-tuple-element.25.own.other.refs_7_, bf16[640,256]{1,0:T(8,128)(2,1)} %get-tuple-element.28.lh, bf16[640,256]{1,0:T(8,128)(2,1)} %get-tuple-element.29.ll, ...), custom_call_target="tpu_custom_call" | custom-call | flops 1761607680 | bytes 6422528 | tf_op jit(solution)/shard_map/w_keep/pallas_call | solution.py:195
  100.5 1.5 collective-permute-start.9
  102.1 1.5 collective-permute-done.11
  103.6 0.6 collective-permute-start.12
  104.2 14.2 %collective-permute-done.12 = f32[256,256]{1,0:T(8,128)S(1)} collective-permute-done((f32[256,256]{1,0:T(8,128)S(1)}, f32[256,256]{1,0:T(8,128)S(1)}, u32[]{:S(2)}, u32[]{:S(2)}) %collective-permute-start.12) | collective-permute-done | bytes 262176 | tf_op jit(solution)/shard_map/ppermute | solution.py:437
  118.5 1.6 collective-permute-start.13
  120.1 1.3 add.116
  121.4 0.8 constant_dynamic-slice_fusion.2
  122.7 1.3 collective-permute-done.9
  124.0 1.3 add.120
  125.3 0.8 constant_dynamic-slice_fusion
  126.4 0.6 pad_add_fusion.at
  127.0 2.6 %collective-permute-done.13 = f32[256,256]{1,0:T(8,128)S(1)} collective-permute-done((f32[256,256]{1,0:T(8,128)S(1)}, f32[256,256]{1,0:T(8,128)S(1)}, u32[]{:S(2)}, u32[]{:S(2)}) %collective-permute-start.13) | collective-permute-done | bytes 262176 | tf_op jit(solution)/shard_map/ppermute | solution.py:437
  129.6 0.7 add.125.gram
  130.3 14.9 %chol_inverse.1 = (f32[256,256]{1,0:T(8,128)}, bf16[640,256]{1,0:T(8,128)(2,1)}, bf16[640,256]{1,0:T(8,128)(2,1)}) custom-call(f32[256,256]{1,0:T(8,128)} %add.125.gram, f32[640,256]{1,0:T(8,128)} %get-tuple-element.35.left), custom_call_target="tpu_custom_call" | custom-call | flops 4000000000 | bytes 655360 | tf_op jit(solution)/shard_map/chol_inverse/pallas_call | solution.py:310
  145.2 0.8 copy-done.10
  146.2 3.4 %right_rows.1 = (f32[448,256]{1,0:T(8,128)}, f32[448,256]{1,0:T(8,128)}, f32[8,256]{1,0:T(8,128)}) custom-call(s32[3]{0:T(128)} %pad_add_fusion.at, f32[448,256]{1,0:T(8,128)} %get-tuple-element.48.ka, f32[448,256]{1,0:T(8,128)} %copy-done.10, f32[448,256]{1,0:T(8,128)} %get-tuple-element.46.kb, f32[448,256]{1,0:T(8,128)} %copy-done.11, ...), custom_call_target="tpu_custom_call" | custom-call | flops 704643072 | bytes 2752512 | tf_op jit(solution)/shard_map/right_rows/pallas_call | solution.py:341
  149.9 1.8 collective-permute-start.14
  151.6 7.8 %collective-permute-done.17.y = f32[448,256]{1,0:T(8,128)S(1)} collective-permute-done((f32[448,256]{1,0:T(8,128)}, f32[448,256]{1,0:T(8,128)S(1)}, u32[]{:S(2)}, u32[]{:S(2)}) %collective-permute-start.17) | collective-permute-done | bytes 458784 | tf_op jit(solution)/shard_map/ppermute | solution.py:437
  159.4 0.8 copy-done.6
  160.2 2.1 join.3.refs_2_
  162.4 1.9 collective-permute-start.18
  164.3 0.8 copy-done.5
  165.0 2.2 join.2.refs_0_
  167.2 0.5 collective-permute-start.15
  167.8 0.5 collective-permute-start.25
  168.3 13.5 %collective-permute-done.18.refs_2_ = f32[896,256]{1,0:T(8,128)S(1)} collective-permute-done((f32[896,256]{1,0:T(8,128)}, f32[896,256]{1,0:T(8,128)S(1)}, u32[]{:S(2)}, u32[]{:S(2)}) %collective-permute-start.18) | collective-permute-done | bytes 917536 | tf_op jit(solution)/shard_map/ppermute | solution.py:437
  181.7 4.4 %collective-permute-done.15.refs_0_ = f32[896,256]{1,0:T(8,128)S(1)} collective-permute-done((f32[896,256]{1,0:T(8,128)}, f32[896,256]{1,0:T(8,128)S(1)}, u32[]{:S(2)}, u32[]{:S(2)}) %collective-permute-start.15) | collective-permute-done | bytes 917536 | tf_op jit(solution)/shard_map/ppermute | solution.py:437
  186.7 2.1 collective-permute-done.20
  188.8 0.7 add.126
  189.5 0.5 collective-permute-start.21
  190.0 3.1 %collective-permute-done.21 = f32[8,256]{1,0:T(8,128)S(1)} collective-permute-done((f32[8,256]{1,0:T(8,128)S(1)}, f32[8,256]{1,0:T(8,128)S(1)}, u32[]{:S(2)}, u32[]{:S(2)}) %collective-permute-start.21) | collective-permute-done | bytes 8224 | tf_op jit(solution)/shard_map/ppermute | solution.py:437
  193.4 3.4 %collective-permute-done.22 = f32[8,256]{1,0:T(8,128)S(1)} collective-permute-done((f32[8,256]{1,0:T(8,128)S(1)}, f32[8,256]{1,0:T(8,128)S(1)}, u32[]{:S(2)}, u32[]{:S(2)}) %collective-permute-start.22) | collective-permute-done | bytes 8224 | tf_op jit(solution)/shard_map/ppermute | solution.py:437
  197.1 3.3 %collective-permute-done.23 = f32[8,256]{1,0:T(8,128)S(1)} collective-permute-done((f32[8,256]{1,0:T(8,128)S(1)}, f32[8,256]{1,0:T(8,128)S(1)}, u32[]{:S(2)}, u32[]{:S(2)}) %collective-permute-start.23) | collective-permute-done | bytes 8224 | tf_op jit(solution)/shard_map/ppermute | solution.py:437
  200.4 0.5 collective-permute-start.24
  200.9 0.6 stack.125.at
  201.6 0.7 stack.105.at
  202.2 2.8 %collective-permute-done.24 = f32[8,256]{1,0:T(8,128)S(1)} collective-permute-done((f32[8,256]{1,0:T(8,128)S(1)}, f32[8,256]{1,0:T(8,128)S(1)}, u32[]{:S(2)}, u32[]{:S(2)}) %collective-permute-start.24) | collective-permute-done | bytes 8224 | tf_op jit(solution)/shard_map/ppermute | solution.py:437
  205.0 0.6 add.130.refs_4_
  205.6 19.0 %final.2 = (f32[640,6912]{1,0:T(8,128)}, f32[640,6912]{1,0:T(8,128)}, f32[6912,256]{1,0:T(8,128)}) custom-call(s32[6]{0:T(128)} %stack.125.at, f32[896,256]{1,0:T(8,128)} %join.2.refs_0_, f32[896,256]{1,0:T(8,128)} %collective-permute-done.25.refs_1_, f32[896,256]{1,0:T(8,128)} %join.3.refs_2_, f32[896,256]{1,0:T(8,128)} %collective-permute-done.26.refs_3_, ...), custom_call_target="tpu_custom_call" | custom-call | flops 7046430720 | bytes 34865152 | tf_op jit(solution)/shard_map/final/pallas_call | solution.py:404
  224.6 0.9 copy-done.3
  225.5 18.5 %final.3 = (f32[640,6912]{1,0:T(8,128)}, f32[640,6912]{1,0:T(8,128)}, f32[6912,256]{1,0:T(8,128)}) custom-call(s32[6]{0:T(128)} %stack.105.at, f32[896,256]{1,0:T(8,128)} %copy-done.2, f32[896,256]{1,0:T(8,128)} %collective-permute-done.16.refs_1_, f32[896,256]{1,0:T(8,128)} %copy-done.1, ...), custom_call_target="tpu_custom_call", output_to_operand_aliasing={{0}: (9, {}), {1}: (10, {}), {2}: (11, {})} | custom-call | flops 7046430720 | bytes 34865152 | tf_op jit(solution)/shard_map/final/pallas_call | solution.py:404
  (53 shorter events, 3.0 us)
Async XLA Ops:
  16.6 18.9 %collective-permute-start = (f32[320,256]{1,0:T(8,128)}, f32[320,256]{1,0:T(8,128)S(1)}, u32[]{:S(2)}, u32[]{:S(2)}) collective-permute-start(f32[320,256]{1,0:T(8,128)} %get-tuple-element.27), channel_id=1, source_target_pairs={{0,1},{1,0},{2,3},{3,2},{4,5},{5,4},{6,7},{7,6},{8,9},{9,8},{10,11... | collective-permute-start | bytes 983048 | tf_op jit(solution)/shard_map/ppermute | solution.py:437
  36.5 13.7 %collective-permute-start.2 = (f32[160,256]{1,0:T(8,128)S(1)}, f32[160,256]{1,0:T(8,128)S(1)}, u32[]{:S(2)}, u32[]{:S(2)}) collective-permute-start(f32[160,256]{1,0:T(8,128)S(1)} %get-tuple-element.51), channel_id=1, source_target_pairs={{0,2},{1,3},{2,0},{3,1},{4,6},{5,7},{6,4},{7,5},{8,10},{9,11},{10,... | collective-permute-start | bytes 491528 | tf_op jit(solution)/shard_map/ppermute | solution.py:437
  39.2 14.4 %collective-permute-start.1 = (f32[160,256]{1,0:T(8,128)S(1)}, f32[160,256]{1,0:T(8,128)S(1)}, u32[]{:S(2)}, u32[]{:S(2)}) collective-permute-start(f32[160,256]{1,0:T(8,128)S(1)} %get-tuple-element.52), channel_id=1, source_target_pairs={{0,2},{1,3},{2,0},{3,1},{4,6},{5,7},{6,4},{7,5},{8,10},{9,11},{10,... | collective-permute-start | bytes 491528 | tf_op jit(solution)/shard_map/ppermute | solution.py:437
  53.7 9.7 %copy-start.8 = (f32[160,256]{1,0:T(8,128)}, f32[160,256]{1,0:T(8,128)S(1)}, u32[]{:S(2)}) copy-start(f32[160,256]{1,0:T(8,128)S(1)} %get-tuple-element.49.refs_1_) | copy-start | bytes 491524
  53.7 9.7 %copy-start.9 = (f32[160,256]{1,0:T(8,128)}, f32[160,256]{1,0:T(8,128)S(1)}, u32[]{:S(2)}) copy-start(f32[160,256]{1,0:T(8,128)S(1)} %get-tuple-element.50.refs_0_) | copy-start | bytes 491524
  53.7 7.1 %collective-permute-start.4 = (f32[160,256]{1,0:T(8,128)S(1)}, f32[160,256]{1,0:T(8,128)S(1)}, u32[]{:S(2)}, u32[]{:S(2)}) collective-permute-start(f32[160,256]{1,0:T(8,128)S(1)} %get-tuple-element.49.refs_1_), channel_id=1, source_target_pairs={{0,1},{1,0},{2,3},{3,2},{4,5},{5,4},{6,7},{7,6},{8,9},{9,8},{10,11... | collective-permute-start | bytes 491528 | tf_op jit(solution)/shard_map/ppermute | solution.py:437
  53.8 9.6 %collective-permute-start.3 = (f32[160,256]{1,0:T(8,128)S(1)}, f32[160,256]{1,0:T(8,128)S(1)}, u32[]{:S(2)}, u32[]{:S(2)}) collective-permute-start(f32[160,256]{1,0:T(8,128)S(1)} %get-tuple-element.50.refs_0_), channel_id=1, source_target_pairs={{0,1},{1,0},{2,3},{3,2},{4,5},{5,4},{6,7},{7,6},{8,9},{9,8},{10,11... | collective-permute-start | bytes 491528 | tf_op jit(solution)/shard_map/ppermute | solution.py:437
  60.8 2.6 %copy-start.12 = (f32[160,256]{1,0:T(8,128)}, f32[160,256]{1,0:T(8,128)S(1)}, u32[]{:S(2)}) copy-start(f32[160,256]{1,0:T(8,128)S(1)} %collective-permute-done.4.refs_3_) | copy-start | bytes 491524
  63.4 0.7 copy-start.13
  73.8 9.1 %collective-permute-start.5 = (f32[1792,256]{1,0:T(8,128)}, f32[1792,256]{1,0:T(8,128)}, u32[]{:S(2)}, u32[]{:S(2)}) collective-permute-start(f32[1792,256]{1,0:T(8,128)} %w_send.2), channel_id=1, source_target_pairs={{0,4},{4,0},{8,12},{12,8},{16,20},{20,16},{24,28},{28,24},{1,5},{5... | collective-permute-start | bytes 5505032 | tf_op jit(solution)/shard_map/ppermute | solution.py:437
  81.0 10.8 %collective-permute-start.8 = (f32[1792,256]{1,0:T(8,128)}, f32[1792,256]{1,0:T(8,128)S(1)}, u32[]{:S(2)}, u32[]{:S(2)}) collective-permute-start(f32[1792,256]{1,0:T(8,128)} %w_send.3), channel_id=1, source_target_pairs={{0,4},{4,0},{8,12},{12,8},{16,20},{20,16},{24,28},{28,24},{1,5},{5... | collective-permute-start | bytes 5505032 | tf_op jit(solution)/shard_map/ppermute | solution.py:437
  90.3 11.8 %copy-start.7 = (f32[256,256]{1,0:T(8,128)S(1)}, f32[256,256]{1,0:T(8,128)}, u32[]{:S(2)}) copy-start(f32[256,256]{1,0:T(8,128)} %get-tuple-element.34) | copy-start | bytes 786436
  90.3 29.8 %copy-start.4 = (f32[896,256]{1,0:T(8,128)S(1)}, f32[896,256]{1,0:T(8,128)}, u32[]{:S(2)}) copy-start(f32[896,256]{1,0:T(8,128)} %get-tuple-element.30) | copy-start | bytes 2752516
  90.3 29.8 %collective-permute-start.6 = (f32[896,256]{1,0:T(8,128)}, f32[896,256]{1,0:T(8,128)}, u32[]{:S(2)}, u32[]{:S(2)}) collective-permute-start(f32[896,256]{1,0:T(8,128)} %get-tuple-element.31), channel_id=1, source_target_pairs={{0,8},{4,12},{8,0},{12,4},{16,24},{20,28},{24,16},{28,20},{1,9},{5... | collective-permute-start | bytes 2752520 | tf_op jit(solution)/shard_map/ppermute | solution.py:437
  91.9 1.2 copy-start
  100.5 23.4 %collective-permute-start.9 = (f32[896,256]{1,0:T(8,128)}, f32[896,256]{1,0:T(8,128)S(1)}, u32[]{:S(2)}, u32[]{:S(2)}) collective-permute-start(f32[896,256]{1,0:T(8,128)} %get-tuple-element.33), channel_id=1, source_target_pairs={{0,16},{4,20},{8,24},{12,28},{16,0},{20,4},{24,8},{28,12},{1,17},{... | collective-permute-start | bytes 2752520 | tf_op jit(solution)/shard_map/ppermute | solution.py:437
  102.1 1.5 collective-permute-start.11
  103.6 14.8 %collective-permute-start.12 = (f32[256,256]{1,0:T(8,128)S(1)}, f32[256,256]{1,0:T(8,128)S(1)}, u32[]{:S(2)}, u32[]{:S(2)}) collective-permute-start(f32[256,256]{1,0:T(8,128)S(1)} %add.123), channel_id=1, source_target_pairs={{0,8},{4,12},{8,0},{12,4},{16,24},{20,28},{24,16},{28,20},{1,9},{5... | collective-permute-start | bytes 786440 | tf_op jit(solution)/shard_map/ppermute | solution.py:437
  118.5 11.1 %collective-permute-start.13 = (f32[256,256]{1,0:T(8,128)S(1)}, f32[256,256]{1,0:T(8,128)S(1)}, u32[]{:S(2)}, u32[]{:S(2)}) collective-permute-start(f32[256,256]{1,0:T(8,128)S(1)} %add.124), channel_id=1, source_target_pairs={{0,16},{4,20},{8,24},{12,28},{16,0},{20,4},{24,8},{28,12},{1,17},{... | collective-permute-start | bytes 786440 | tf_op jit(solution)/shard_map/ppermute | solution.py:437
  122.2 23.0 %collective-permute-start.7 = (f32[448,256]{1,0:T(8,128)S(1)}, f32[448,256]{1,0:T(8,128)S(1)}, u32[]{:S(2)}, u32[]{:S(2)}) collective-permute-start(f32[448,256]{1,0:T(8,128)S(1)} %get-tuple-element.47), channel_id=1, source_target_pairs={{0,16},{4,20},{8,24},{12,28},{16,0},{20,4},{24,8},{28,12},{1,17},{... | collective-permute-start | bytes 1376264 | tf_op jit(solution)/shard_map/ppermute | solution.py:437
  126.1 19.1 %collective-permute-start.10 = (f32[448,256]{1,0:T(8,128)S(1)}, f32[448,256]{1,0:T(8,128)S(1)}, u32[]{:S(2)}, u32[]{:S(2)}) collective-permute-start(f32[448,256]{1,0:T(8,128)S(1)} %get-tuple-element.45), channel_id=1, source_target_pairs={{0,8},{4,12},{8,0},{12,4},{16,24},{20,28},{24,16},{28,20},{1,9},{5... | collective-permute-start | bytes 1376264 | tf_op jit(solution)/shard_map/ppermute | solution.py:437
  145.2 0.8 copy-start.10
  145.2 0.9 copy-start.11
  149.6 9.9 %collective-permute-start.17 = (f32[448,256]{1,0:T(8,128)}, f32[448,256]{1,0:T(8,128)S(1)}, u32[]{:S(2)}, u32[]{:S(2)}) collective-permute-start(f32[448,256]{1,0:T(8,128)} %get-tuple-element.38.x), channel_id=1, source_target_pairs={{0,8},{4,12},{8,0},{12,4},{16,24},{20,28},{24,16},{28,20},{1,9},{5... | collective-permute-start | bytes 1376264 | tf_op jit(solution)/shard_map/ppermute | solution.py:437
  149.9 14.4 %collective-permute-start.14 = (f32[448,256]{1,0:T(8,128)}, f32[448,256]{1,0:T(8,128)S(1)}, u32[]{:S(2)}, u32[]{:S(2)}) collective-permute-start(f32[448,256]{1,0:T(8,128)} %get-tuple-element.37.x), channel_id=1, source_target_pairs={{0,16},{4,20},{8,24},{12,28},{16,0},{20,4},{24,8},{28,12},{1,17},{... | collective-permute-start | bytes 1376264 | tf_op jit(solution)/shard_map/ppermute | solution.py:437
  159.4 0.8 copy-start.6
  162.4 19.4 %collective-permute-start.18 = (f32[896,256]{1,0:T(8,128)}, f32[896,256]{1,0:T(8,128)S(1)}, u32[]{:S(2)}, u32[]{:S(2)}) collective-permute-start(f32[896,256]{1,0:T(8,128)} %join.3.refs_2_), channel_id=1, source_target_pairs={{0,16},{4,20},{8,24},{12,28},{16,0},{20,4},{24,8},{28,12},{1,17},{... | collective-permute-start | bytes 2752520 | tf_op jit(solution)/shard_map/ppermute | solution.py:437
  164.3 0.8 copy-start.5
  167.2 18.9 %collective-permute-start.15 = (f32[896,256]{1,0:T(8,128)}, f32[896,256]{1,0:T(8,128)S(1)}, u32[]{:S(2)}, u32[]{:S(2)}) collective-permute-start(f32[896,256]{1,0:T(8,128)} %join.2.refs_0_), channel_id=1, source_target_pairs={{0,8},{4,12},{8,0},{12,4},{16,24},{20,28},{24,16},{28,20},{1,9},{5... | collective-permute-start | bytes 2752520 | tf_op jit(solution)/shard_map/ppermute | solution.py:437
  167.8 37.8 %collective-permute-start.26 = (f32[896,256]{1,0:T(8,128)}, f32[896,256]{1,0:T(8,128)}, u32[]{:S(2)}, u32[]{:S(2)}) collective-permute-start(f32[896,256]{1,0:T(8,128)} %join.3.refs_2_), channel_id=1, source_target_pairs={{0,4},{4,0},{8,12},{12,8},{16,20},{20,16},{24,28},{28,24},{1,5},{5... | collective-permute-start | bytes 2752520 | tf_op jit(solution)/shard_map/ppermute | solution.py:437
  167.8 37.8 %collective-permute-start.25 = (f32[896,256]{1,0:T(8,128)}, f32[896,256]{1,0:T(8,128)}, u32[]{:S(2)}, u32[]{:S(2)}) collective-permute-start(f32[896,256]{1,0:T(8,128)} %join.2.refs_0_), channel_id=1, source_target_pairs={{0,4},{4,0},{8,12},{12,8},{16,20},{20,16},{24,28},{28,24},{1,5},{5... | collective-permute-start | bytes 2752520 | tf_op jit(solution)/shard_map/ppermute | solution.py:437
  181.7 42.9 %copy-start.1 = (f32[896,256]{1,0:T(8,128)}, f32[896,256]{1,0:T(8,128)S(1)}, u32[]{:S(2)}) copy-start(f32[896,256]{1,0:T(8,128)S(1)} %collective-permute-done.18.refs_2_) | copy-start | bytes 2752516
  181.7 42.9 %collective-permute-start.19 = (f32[896,256]{1,0:T(8,128)S(1)}, f32[896,256]{1,0:T(8,128)S(1)}, u32[]{:S(2)}, u32[]{:S(2)}) collective-permute-start(f32[896,256]{1,0:T(8,128)S(1)} %collective-permute-done.18.refs_2_), channel_id=1, source_target_pairs={{0,4},{4,0},{8,12},{12,8},{16,20},{20,16},{24,28},{28,24},{1,5},{5... | collective-permute-start | bytes 2752520 | tf_op jit(solution)/shard_map/ppermute | solution.py:437
  186.2 38.5 %copy-start.2 = (f32[896,256]{1,0:T(8,128)}, f32[896,256]{1,0:T(8,128)S(1)}, u32[]{:S(2)}) copy-start(f32[896,256]{1,0:T(8,128)S(1)} %collective-permute-done.15.refs_0_) | copy-start | bytes 2752516
  186.2 38.5 %collective-permute-start.16 = (f32[896,256]{1,0:T(8,128)S(1)}, f32[896,256]{1,0:T(8,128)}, u32[]{:S(2)}, u32[]{:S(2)}) collective-permute-start(f32[896,256]{1,0:T(8,128)S(1)} %collective-permute-done.15.refs_0_), channel_id=1, source_target_pairs={{0,4},{4,0},{8,12},{12,8},{16,20},{20,16},{24,28},{28,24},{1,5},{5... | collective-permute-start | bytes 2752520 | tf_op jit(solution)/shard_map/ppermute | solution.py:437
  186.2 2.6 %collective-permute-start.20 = (f32[8,256]{1,0:T(8,128)}, f32[8,256]{1,0:T(8,128)S(1)}, u32[]{:S(2)}, u32[]{:S(2)}) collective-permute-start(f32[8,256]{1,0:T(8,128)} %get-tuple-element.39), channel_id=1, source_target_pairs={{0,4},{4,0},{8,12},{12,8},{16,20},{20,16},{24,28},{28,24},{1,5},{5... | collective-permute-start | bytes 24584 | tf_op jit(solution)/shard_map/ppermute | solution.py:437
  189.5 3.7 %collective-permute-start.21 = (f32[8,256]{1,0:T(8,128)S(1)}, f32[8,256]{1,0:T(8,128)S(1)}, u32[]{:S(2)}, u32[]{:S(2)}) collective-permute-start(f32[8,256]{1,0:T(8,128)S(1)} %add.126), channel_id=1, source_target_pairs={{0,8},{4,12},{8,0},{12,4},{16,24},{20,28},{24,16},{28,20},{1,9},{5... | collective-permute-start | bytes 24584 | tf_op jit(solution)/shard_map/ppermute | solution.py:437
  193.1 3.7 %collective-permute-start.22 = (f32[8,256]{1,0:T(8,128)S(1)}, f32[8,256]{1,0:T(8,128)S(1)}, u32[]{:S(2)}, u32[]{:S(2)}) collective-permute-start(f32[8,256]{1,0:T(8,128)S(1)} %add.127), channel_id=1, source_target_pairs={{0,16},{4,20},{8,24},{12,28},{16,0},{20,4},{24,8},{28,12},{1,17},{... | collective-permute-start | bytes 24584 | tf_op jit(solution)/shard_map/ppermute | solution.py:437
  196.8 3.7 %collective-permute-start.23 = (f32[8,256]{1,0:T(8,128)S(1)}, f32[8,256]{1,0:T(8,128)S(1)}, u32[]{:S(2)}, u32[]{:S(2)}) collective-permute-start(f32[8,256]{1,0:T(8,128)S(1)} %add.128), channel_id=1, source_target_pairs={{0,1},{1,0},{2,3},{3,2},{4,5},{5,4},{6,7},{7,6},{8,9},{9,8},{10,11... | collective-permute-start | bytes 24584 | tf_op jit(solution)/shard_map/ppermute | solution.py:437
  200.4 4.5 %collective-permute-start.24 = (f32[8,256]{1,0:T(8,128)S(1)}, f32[8,256]{1,0:T(8,128)S(1)}, u32[]{:S(2)}, u32[]{:S(2)}) collective-permute-start(f32[8,256]{1,0:T(8,128)S(1)} %add.129), channel_id=1, source_target_pairs={{0,2},{1,3},{2,0},{3,1},{4,6},{5,7},{6,4},{7,5},{8,10},{9,11},{10,... | collective-permute-start | bytes 24584 | tf_op jit(solution)/shard_map/ppermute | solution.py:437
  224.6 0.9 copy-start.3

commit v3 on v2

--- a/solution.py
+++ b/solution.py
@@ -12,7 +12,7 @@
 BF16 = jnp.bfloat16
 HIGH = lax.Precision.HIGHEST
 LANES = 128
-VMEM_LIMIT = 60 * 1024 * 1024
+VMEM_LIMIT = 40 * 1024 * 1024
 
 NN = (((1,), (0,)), ((), ()))
 NT = (((1,), (1,)), ((), ()))
@@ -20,6 +20,8 @@
 
 
 ANY = pl.BlockSpec(memory_space=pl.ANY)
+VMEM = pl.BlockSpec(memory_space=pltpu.VMEM)
+SMEM = pl.BlockSpec(memory_space=pltpu.SMEM)
 
 
 def params(**kw):
@@ -54,48 +56,63 @@
     return LANES * max(k for k in range(1, 9) if blocks % k == 0)
 
 
-def left_kernel(at, g, m, r, *rest):
-    buffer, out = rest[-2:]
-    step = pl.program_id(0)
-    b = g[...] + m[...]
-    buffer[...] = b
-    bh, bl = split(b)
-    rh, rl = split(r[...])
-    term = dot3(bh, bl, rh, rl, NN)
-
-    @pl.when(step == 0)
-    def _():
-        out[...] = term
-
-    @pl.when(step > 0)
-    def _():
-        out[...] += term
-
-
-def left_half(at, gradient, momentum, right_factor, buffer):
+def left_kernel(at, g, m, r, buffer, out, gs, ms, rs, sems):
+    depth, half, wide = gs.shape
+    steps = g.shape[1] // wide
+    rows = pl.ds(pl.multiple_of(at[0] * half, GROUP), half)
+
+    def copies(j, slot):
+        part = pl.ds(pl.multiple_of(j * wide, LANES), wide)
+        return (
+            pltpu.make_async_copy(g.at[rows, part], gs.at[slot], sems.at[0, slot]),
+            pltpu.make_async_copy(m.at[rows, part], ms.at[slot], sems.at[1, slot]),
+            pltpu.make_async_copy(r.at[part, :], rs.at[slot], sems.at[2, slot]),
+        )
+
+    for j in range(min(depth, steps)):
+        for copy in copies(j, j):
+            copy.start()
+    out[...] = jnp.zeros_like(out)
+
+    def body(j, _):
+        slot = lax.rem(j, depth)
+        for copy in copies(j, slot):
+            copy.wait()
+        b = gs[slot] + ms[slot]
+        buffer[:, pl.ds(pl.multiple_of(j * wide, LANES), wide)] = b
+        bh, bl = split(b)
+        rh, rl = split(rs[slot])
+        out[...] += dot3(bh, bl, rh, rl, NN)
+
+        @pl.when(j + depth < steps)
+        def _():
+            for copy in copies(j + depth, slot):
+                copy.start()
+
+        return 0
+
+    lax.fori_loop(0, steps, body, 0)
+
+
+def left_half(at, gradient, momentum, right_factor, padded):
     rows, cols = gradient.shape
     rank = right_factor.shape[1]
-    half, wide = rows // 2, column_block(cols)
-    block = pl.BlockSpec((half, wide), lambda j, at: (at[0], j))
-    first = buffer is None
+    half, wide, depth = rows // 2, column_block(cols), 4
     return pl.pallas_call(
         left_kernel,
-        grid_spec=pltpu.PrefetchScalarGridSpec(
-            num_scalar_prefetch=1,
-            grid=(cols // wide,),
-            in_specs=[block, block, pl.BlockSpec((wide, rank), lambda j, at: (j, 0))]
-            + ([] if first else [ANY]),
-            out_specs=[block, pl.BlockSpec((half, rank), lambda j, at: (0, 0))],
-        ),
-        out_shape=[
-            jax.ShapeDtypeStruct((rows, cols), F32),
-            jax.ShapeDtypeStruct((half, rank), F32),
+        in_specs=[SMEM, ANY, ANY, ANY],
+        out_specs=[VMEM, VMEM],
+        out_shape=[pltpu.VMEM((half, padded), F32), jax.ShapeDtypeStruct((half, rank), F32)],
+        scratch_shapes=[
+            pltpu.VMEM((depth, half, wide), F32),
+            pltpu.VMEM((depth, half, wide), F32),
+            pltpu.VMEM((depth, wide, rank), F32),
+            pltpu.SemaphoreType.DMA((3, depth)),
         ],
-        input_output_aliases={} if first else {4: 0},
-        compiler_params=params(),
-        cost_estimate=cost(6 * half * cols * rank, 4 * (3 * half * cols + cols * rank)),
+        compiler_params=params(),
+        cost_estimate=cost(6 * half * cols * rank, 4 * (2 * half * cols + cols * rank)),
         name="left_half",
-    )(scalars(at), gradient, momentum, right_factor, *([] if first else [buffer]))
+    )(scalars(at), gradient, momentum, right_factor)
 
 
 def gram_kernel(*refs):
@@ -130,82 +147,71 @@
     )(*pieces)
 
 
-def w_term(own, other, lh, ll):
+def w_term(unit, width, own, other, lh, ll):
     half = own.shape[0]
+    part = pl.ds(pl.multiple_of(unit * width, LANES), width)
     total = None
     for ref, at in ((own, 0), (other, half)):
-        bh, bl = split(ref[...])
+        bh, bl = split(ref[:, part])
         term = dot3(bh, bl, lh[at : at + half, :], ll[at : at + half, :], TN)
         total = term if total is None else total + term
     return total
 
 
 def w_send_kernel(at, own, other, lh, ll, out):
-    out[...] = w_term(own, other, lh, ll)
+    out[...] = w_term(at[pl.program_id(0)], out.shape[0], own, other, lh, ll)
 
 
 def w_keep_kernel(at, own, other, lh, ll, got, send, keep):
-    total = w_term(own, other, lh, ll) + got[...]
-
-    @pl.when(pl.program_id(0) == 0)
+    i, width = pl.program_id(0), send.shape[0]
+    total = w_term(at[i], width, own, other, lh, ll) + got[...]
+
+    @pl.when(i == 0)
     def _():
         send[...] = total
 
-    @pl.when(pl.program_id(0) == 1)
+    @pl.when(i == 1)
     def _():
         keep[...] = total
 
 
-def w_specs(buffer, rank, unit):
-    half = buffer.shape[0] // 2
-    whole = pl.BlockSpec((2 * half, rank), lambda i, at: (0, 0))
-    return [
-        pl.BlockSpec((half, unit), lambda i, at: (at[0], at[2 + i])),
-        pl.BlockSpec((half, unit), lambda i, at: (at[1], at[2 + i])),
-        whole,
-        whole,
-    ]
-
-
-def w_cost(buffer, rank, unit):
-    rows = buffer.shape[0]
-    return cost(2 * 6 * rows * unit * rank, 2 * 4 * (rows * unit + unit * rank))
-
-
-def w_send(s, units, buffer, lh, ll, unit):
-    rank = lh.shape[1]
+def w_cost(rows, rank, unit):
+    return cost(2 * 6 * rows * unit * rank, 2 * 4 * unit * rank)
+
+
+def w_send(units, own, other, lh, ll, unit):
+    rows, rank = lh.shape
     return pl.pallas_call(
         w_send_kernel,
         grid_spec=pltpu.PrefetchScalarGridSpec(
             num_scalar_prefetch=1,
             grid=(2,),
-            in_specs=w_specs(buffer, rank, unit),
+            in_specs=[VMEM] * 4,
             out_specs=pl.BlockSpec((unit, rank), lambda i, at: (i, 0)),
         ),
         out_shape=jax.ShapeDtypeStruct((2 * unit, rank), F32),
         compiler_params=params(),
-        cost_estimate=w_cost(buffer, rank, unit),
+        cost_estimate=w_cost(rows, rank, unit),
         name="w_send",
-    )(scalars(s, 1 - s, *units), buffer, buffer, lh, ll)
-
-
-def w_keep(s, units, order, buffer, lh, ll, got, unit):
-    rank = lh.shape[1]
+    )(scalars(*units), own, other, lh, ll)
+
+
+def w_keep(units, order, own, other, lh, ll, got, unit):
+    rows, rank = lh.shape
     one = pl.BlockSpec((unit, rank), lambda i, at: (0, 0))
     return pl.pallas_call(
         w_keep_kernel,
         grid_spec=pltpu.PrefetchScalarGridSpec(
             num_scalar_prefetch=1,
             grid=(2,),
-            in_specs=w_specs(buffer, rank, unit)
-            + [pl.BlockSpec((unit, rank), lambda i, at: (at[4 + i], 0))],
+            in_specs=[VMEM] * 4 + [pl.BlockSpec((unit, rank), lambda i, at: (at[2 + i], 0))],
             out_specs=[one, one],
         ),
         out_shape=[jax.ShapeDtypeStruct((unit, rank), F32)] * 2,
         compiler_params=params(),
-        cost_estimate=w_cost(buffer, rank, unit),
+        cost_estimate=w_cost(rows, rank, unit),
         name="w_keep",
-    )(scalars(s, 1 - s, *units, *order), buffer, buffer, lh, ll, got)
+    )(scalars(*units, *order), own, other, lh, ll, got)
 
 
 GROUP = 8
@@ -372,13 +378,13 @@
 
 def final_kernel(count, total_cols, factor, at, *refs):
     pieces = refs[:count]
-    squares, oh, ol, buffer = refs[count : count + 4]
+    squares, oh, ol, own, other = refs[count : count + 5]
     update, momentum, new_right, rh, rl, nh, nl = refs[-7:]
-    u, h = pl.program_id(0), pl.program_id(1)
-    half = buffer.shape[0]
+    u = pl.program_id(0)
+    half, width = own.shape[0], new_right.shape[0]
     for k in range(count):
 
-        @pl.when((u == k) & (h == 0))
+        @pl.when(u == k)
         def _(k=k):
             right = pieces[k][...]
             scale = jnp.sqrt(squares[0:1, :] / total_cols + 1e-06)
@@ -387,29 +393,27 @@
             rh[...], rl[...] = split(right)
             nh[...], nl[...] = split(scaled)
 
-    rows = pl.ds(pl.multiple_of(h * half, half), half)
-    a, b = oh[rows, :], ol[rows, :]
-    momentum[...] = buffer[...] - 0.05 * dot3(a, b, rh[...], rl[...], NT)
-    update[...] = factor * dot3(a, b, nh[...], nl[...], NT)
-
-
-def final(s, units, pieces, squares, oh, ol, buffer, total_rows, total_cols, before):
-    rows, cols = buffer.shape
+    part = pl.ds(pl.multiple_of(at[2 + u] * width, LANES), width)
+    for h, buffer in enumerate((own, other)):
+        rows = pl.ds(pl.multiple_of(at[h] * half, GROUP), half)
+        a, b = oh[h * half : (h + 1) * half, :], ol[h * half : (h + 1) * half, :]
+        momentum[rows, :] = buffer[:, part] - 0.05 * dot3(a, b, rh[...], rl[...], NT)
+        update[rows, :] = factor * dot3(a, b, nh[...], nl[...], NT)
+
+
+def final(s, units, pieces, squares, oh, ol, own, other, cols, total_rows, total_cols, before):
+    rows = oh.shape[0]
     unit, rank = pieces[0].shape
-    half, count = rows // 2, len(pieces)
-    wide = pl.BlockSpec((half, unit), lambda u, h, at: (at[h], at[2 + u]))
-    whole = lambda shape: pl.BlockSpec(shape, lambda u, h, at: (0, 0))
-    n_in = count + 5
+    count = len(pieces)
+    wide = pl.BlockSpec((rows, unit), lambda u, at: (0, at[2 + u]))
     factor = (total_rows / rank) ** 0.5
     return pl.pallas_call(
         functools.partial(final_kernel, count, total_cols, factor),
         grid_spec=pltpu.PrefetchScalarGridSpec(
             num_scalar_prefetch=1,
-            grid=(count, 2),
-            in_specs=[whole((unit, rank))] * count
-            + [whole((GROUP, rank)), whole((rows, rank)), whole((rows, rank)), wide]
-            + [ANY] * len(before),
-            out_specs=[wide, wide, pl.BlockSpec((unit, rank), lambda u, h, at: (at[2 + u], 0))],
+            grid=(count,),
+            in_specs=[VMEM] * (count + 5) + [ANY] * len(before),
+            out_specs=[wide, wide, pl.BlockSpec((unit, rank), lambda u, at: (at[2 + u], 0))],
             scratch_shapes=[pltpu.VMEM((unit, rank), BF16)] * 4,
         ),
         out_shape=[
@@ -417,11 +421,11 @@
             jax.ShapeDtypeStruct((rows, cols), F32),
             jax.ShapeDtypeStruct((cols, rank), F32),
         ],
-        input_output_aliases={n_in + i: i for i in range(len(before))},
-        compiler_params=params(),
-        cost_estimate=cost(12 * count * rows * unit * rank, 4 * count * unit * (3 * rows + 2 * rank)),
+        input_output_aliases={count + 6 + i: i for i in range(len(before))},
+        compiler_params=params(),
+        cost_estimate=cost(12 * count * rows * unit * rank, 4 * count * unit * (2 * rows + 2 * rank)),
         name="final",
-    )(scalars(s, 1 - s, *units), *pieces, squares, oh, ol, buffer, *before)
+    )(scalars(s, 1 - s, *units), *pieces, squares, oh, ol, own, other, *before)
 
 
 def power_of_two(n):
@@ -432,9 +436,10 @@
     return list(range(n.bit_length() - 1))
 
 
-def swap(x, axis, bit):
+def swap(x, axis, *places):
     n = lax.axis_size(axis)
-    return lax.ppermute(x, axis, [(i, i ^ (1 << bit)) for i in range(n)])
+    mask = sum(1 << bit for bit in places)
+    return lax.ppermute(x, axis, [(i, i ^ mask) for i in range(n)])
 
 
 def sum_over(x, axis):
@@ -451,27 +456,26 @@
     rows, cols = gradient.shape
     n_dp, n_tp = lax.axis_size("dp"), lax.axis_size("tensor")
     d, z = lax.axis_index("dp"), lax.axis_index("tensor")
-    half = rows // 2
 
     s = lax.rem(z, 2)
-    buffer, away = left_half(1 - s, gradient, momentum, right_factor, None)
+    unit = LANES * (-(-cols // (8 * LANES)))
+    buffer_other, away = left_half(1 - s, gradient, momentum, right_factor, 8 * unit)
     if power_of_two(n_tp) and n_tp > 1:
         got = swap(away, "tensor", 0)
-        buffer, mine = left_half(s, gradient, momentum, right_factor, buffer)
+        buffer_own, mine = left_half(s, gradient, momentum, right_factor, 8 * unit)
         mine = mine + got
-        own = [mine[: half // 2], mine[half // 2 :]]
+        own = [mine[: rows // 4], mine[rows // 4 :]]
         for bit in bits_of(n_tp)[1:]:
             own = [x + swap(x, "tensor", bit) for x in own]
         pieces = own + [swap(x, "tensor", 0) for x in own]
     else:
-        buffer, mine = left_half(s, gradient, momentum, right_factor, buffer)
+        buffer_own, mine = left_half(s, gradient, momentum, right_factor, 8 * unit)
         both = lax.psum(jnp.where(s == 0, jnp.stack([mine, away]), jnp.stack([away, mine])), "tensor")
         pieces = [lax.dynamic_index_in_dim(both, i, 0, False) for i in (s, 1 - s)]
 
     left, lh, ll, gram = gram_of(pieces)
     gram = sum_over(gram, "dp")
 
-    unit = LANES * (-(-cols // (8 * LANES)))
     bits = bits_of(n_dp)
     core = lax.rem(d, 2)
     orders = [bits[1:], bits[1:][::-1]]
@@ -479,13 +483,14 @@
     got = []
     for h in range(2):
         units = [4 * h + 2 * (1 - core), 4 * h + 2 * (1 - core) + 1]
-        sent = w_send(s, units, buffer, lh, ll, unit)
+        sent = w_send(units, buffer_own, buffer_other, lh, ll, unit)
         got.append(swap(sent, "dp", 0))
     kept, here = [], []
     for h, order in enumerate(orders):
         t = bit_of(order[0])
         base = 4 * h + 2 * core
-        send, keep = w_keep(s, [base + 1 - t, base + t], [1 - t, t], buffer, lh, ll, got[h], unit)
+        units, places = [base + 1 - t, base + t], [1 - t, t]
+        send, keep = w_keep(units, places, buffer_own, buffer_other, lh, ll, got[h], unit)
         at = (base + t) * unit
         recv = swap(send, "dp", order[0])
         for b in order[1:]:
@@ -500,7 +505,12 @@
 
     x_inv, oh, ol = chol_inverse(gram, left)
     ra, rb, squares = right_rows(here[0], here[1], cols, *kept[0], *kept[1], x_inv)
-    squares = sum_over(sum_over(squares, "dp"), "tensor")
+    squares = sum_over(squares, "tensor")
+    for b in bits[:1] + bits[3:]:
+        squares = squares + swap(squares, "dp", b)
+    first, second = bits[1:3]
+    others = [swap(squares, "dp", *m) for m in ((first,), (second,), (first, second))]
+    squares = (squares + others[0]) + (others[1] + others[2])
 
     near, far = [], []
     for h, (order, x) in enumerate(zip(orders, (ra, rb))):
@@ -517,7 +527,8 @@
     for group in (near, far):
         units = [u for part in group for u, _ in part]
         data = [x for part in group for _, x in part]
-        outs = final(s, units, data, squares, oh, ol, buffer, rows * n_dp, cols * n_tp, outs)
+        held = (squares, oh, ol, buffer_own, buffer_other)
+        outs = final(s, units, data, *held, cols, rows * n_dp, cols * n_tp, outs)
     return tuple(outs)
 
 

time: 245 us -> 229 us (0.935)
  Pallas kernels: 123 us -> 104 us
  local copies, waits for them, and re-layouts: 9.55 us -> 19.9 us
  waiting for transfers between devices: 81.1 us -> 75.1 us
  other arithmetic: 7.53 us -> 3.37 us
  starting transfers between devices: 21.9 us -> 25.4 us
    unnamed x28 -> x20, local copies, waits for them, and re-layouts: 5.27 us -> 19.6 us
    pallas_call x2, Pallas kernels: 31.8 us -> 18.1 us  [left_half(): pl.pallas_call(left_kernel, in_specs=[SMEM, ANY, ANY, ANY], out_specs=[VM...]
    ppermute x27 -> x28, waiting for transfers between devices: 81.1 us -> 75.1 us  [swap(): return lax.ppermute(x, axis, [(i, i ^ mask) for i in range(n)])]
    pallas_call x2, Pallas kernels: 4.33 us -> 0.12 us  [join(): pl.pallas_call(join_kernel, in_specs=[pl.BlockSpec(memory_space=pltpu.SME...]
    pallas_call x2, Pallas kernels: 13.4 us -> 16.9 us  [w_send(): pl.pallas_call(w_send_kernel, grid_spec=pltpu.PrefetchScalarGridSpec(num_...]
    ppermute x27 -> x28, starting transfers between devices: 21.9 us -> 25.4 us  [swap(): return lax.ppermute(x, axis, [(i, i ^ mask) for i in range(n)])]
    pallas_call x2, Pallas kernels: 14.8 us -> 17.3 us  [w_keep(): pl.pallas_call(w_keep_kernel, grid_spec=pltpu.PrefetchScalarGridSpec(num_...]
  transfers between devices with their start and end apart: 27 -> 28, of which waited for: 16 -> 16; matrix products, arithmetic and copies ran while one was open for 4% -> 2% of each run, Pallas kernels for 31% -> 29%
where the time goes in v3:
time: 229 us; the launch traced here: 228 us
  Pallas kernels  104 us (45%)
  waiting for transfers between devices  75.1 us (33%)
  starting transfers between devices  25.4 us (11%)
  local copies, waits for them, and re-layouts  19.9 us (9%)
  other arithmetic  3.37 us (1%)
    ppermute x28, waiting for transfers between devices, swap(): return lax.ppermute(x, axis, [(i, i ^ mask) for i in range(n)])  75.1 us
    pallas_call x2, Pallas kernels, final(): pl.pallas_call(functools.partial(final_kernel, count, total_cols, factor)...  35.6 us
    ppermute x28, starting transfers between devices, swap(): return lax.ppermute(x, axis, [(i, i ^ mask) for i in range(n)])  25.4 us
    unnamed x20, local copies, waits for them, and re-layouts  19.6 us
    pallas_call x2, Pallas kernels, left_half(): pl.pallas_call(left_kernel, in_specs=[SMEM, ANY, ANY, ANY], out_specs=[VM...  18.1 us
    pallas_call x2, Pallas kernels, w_keep(): pl.pallas_call(w_keep_kernel, grid_spec=pltpu.PrefetchScalarGridSpec(num_...  17.3 us
    pallas_call x2, Pallas kernels, w_send(): pl.pallas_call(w_send_kernel, grid_spec=pltpu.PrefetchScalarGridSpec(num_...  16.9 us
    pallas_call x1, Pallas kernels, chol_inverse(): pl.pallas_call(chol_kernel, in_specs=[vm, vm], out_specs=[vm] * 3, out_sh...  12.8 us
  transfers between devices with their start and end apart: 28, of which 16 were waited for; matrix products, arithmetic and copies ran while one was open for 2% of the time, Pallas kernels for 29%

profile of v3, /device:TPU:0, one launch (start us, length us, event | category | flops | bytes accessed | tf_op | source)
XLA Modules:
  0.0 228.1 jit_solution(8508299506234755152)
XLA Ops:
  0.6 9.1 %left_half.3 = (f32[320,7168]{1,0:T(8,128)S(1)}, f32[320,256]{1,0:T(8,128)S(1)}) custom-call(s32[1]{0:T(128)} %bitcast.1.at, f32[640,6912]{1,0:T(8,128)} %g.3, f32[640,6912]{1,0:T(8,128)} %m.3, f32[6912,256]{1,0:T(8,128)} %r.3), custom_call_target="tpu_custom_call" | custom-call | flops 3397386240 | bytes 24772608 | tf_op jit(solution)/shard_map/left_half/pallas_call | solution.py:101
  9.7 3.6 %copy-done = f32[320,7168]{1,0:T(8,128)} copy-done((f32[320,7168]{1,0:T(8,128)}, f32[320,7168]{1,0:T(8,128)S(1)}, u32[]{:S(2)}) %copy-start) | copy-done | bytes 9175064
  13.3 3.1 %collective-permute-start = (f32[320,256]{1,0:T(8,128)S(1)}, f32[320,256]{1,0:T(8,128)S(1)}, u32[]{:S(2)}, u32[]{:S(2)}) collective-permute-start(f32[320,256]{1,0:T(8,128)S(1)} %get-tuple-element.27), channel_id=1, source_target_pairs={{0,1},{1,0},{2,3},{3,2},{4,5},{5,4},{6,7},{7,6},{8,9},{9,8},{10,11... | collective-permute-start | bytes 983048 | tf_op jit(solution)/shard_map/ppermute | solution.py:442
  16.3 9.1 %left_half.2 = (f32[320,7168]{1,0:T(8,128)S(1)}, f32[320,256]{1,0:T(8,128)S(1)}) custom-call(s32[1]{0:T(128)} %bitcast.at, f32[640,6912]{1,0:T(8,128)} %g.3, f32[640,6912]{1,0:T(8,128)} %m.3, f32[6912,256]{1,0:T(8,128)} %r.3), custom_call_target="tpu_custom_call" | custom-call | flops 3397386240 | bytes 24772608 | tf_op jit(solution)/shard_map/left_half/pallas_call | solution.py:101
  25.4 3.6 %copy-done.1 = f32[320,7168]{1,0:T(8,128)} copy-done((f32[320,7168]{1,0:T(8,128)}, f32[320,7168]{1,0:T(8,128)S(1)}, u32[]{:S(2)}) %copy-start.1) | copy-done | bytes 9175064
  29.1 2.7 %collective-permute-start.2 = (f32[160,256]{1,0:T(8,128)S(1)}, f32[160,256]{1,0:T(8,128)S(1)}, u32[]{:S(2)}, u32[]{:S(2)}) collective-permute-start(f32[160,256]{1,0:T(8,128)S(1)} %get-tuple-element.51), channel_id=1, source_target_pairs={{0,2},{1,3},{2,0},{3,1},{4,6},{5,7},{6,4},{7,5},{8,10},{9,11},{10,... | collective-permute-start | bytes 491528 | tf_op jit(solution)/shard_map/ppermute | solution.py:442
  31.8 0.3 collective-permute-start.1
  32.1 10.6 %collective-permute-done.2 = f32[160,256]{1,0:T(8,128)S(1)} collective-permute-done((f32[160,256]{1,0:T(8,128)S(1)}, f32[160,256]{1,0:T(8,128)S(1)}, u32[]{:S(2)}, u32[]{:S(2)}) %collective-permute-start.2) | collective-permute-done | bytes 163872 | tf_op jit(solution)/shard_map/ppermute | solution.py:442
  42.7 3.4 %collective-permute-done.1 = f32[160,256]{1,0:T(8,128)S(1)} collective-permute-done((f32[160,256]{1,0:T(8,128)S(1)}, f32[160,256]{1,0:T(8,128)S(1)}, u32[]{:S(2)}, u32[]{:S(2)}) %collective-permute-start.1) | collective-permute-done | bytes 163872 | tf_op jit(solution)/shard_map/ppermute | solution.py:442
  46.2 0.1 collective-permute-start.4
  46.3 2.0 collective-permute-start.3
  48.3 0.1 pad_add_fusion.2
  48.3 5.0 %collective-permute-done.4.refs_3_ = f32[160,256]{1,0:T(8,128)S(1)} collective-permute-done((f32[160,256]{1,0:T(8,128)S(1)}, f32[160,256]{1,0:T(8,128)S(1)}, u32[]{:S(2)}, u32[]{:S(2)}) %collective-permute-start.4) | collective-permute-done | bytes 163872 | tf_op jit(solution)/shard_map/ppermute | solution.py:442
  53.3 2.6 %collective-permute-done.3.refs_2_ = f32[160,256]{1,0:T(8,128)S(1)} collective-permute-done((f32[160,256]{1,0:T(8,128)S(1)}, f32[160,256]{1,0:T(8,128)S(1)}, u32[]{:S(2)}, u32[]{:S(2)}) %collective-permute-start.3) | collective-permute-done | bytes 163872 | tf_op jit(solution)/shard_map/ppermute | solution.py:442
  55.9 1.2 gram_of.1
  57.0 0.7 copy-done.6
  57.7 0.9 copy-done.8
  58.6 3.6 %copy-done.2 = f32[320,7168]{1,0:T(8,128)S(1)} copy-done((f32[320,7168]{1,0:T(8,128)S(1)}, f32[320,7168]{1,0:T(8,128)}, u32[]{:S(2)}) %copy-start.2) | copy-done | bytes 9175064
  62.2 8.5 %w_send.2 = f32[1792,256]{1,0:T(8,128)} custom-call(s32[2]{0:T(128)S(1)} %get-tuple-element.53.at, f32[320,7168]{1,0:T(8,128)S(1)} %copy-done.2, f32[320,7168]{1,0:T(8,128)} %copy-done, bf16[640,256]{1,0:T(8,128)(2,1)S(1)} %get-tuple-element.28.lh, bf16[640,256]{1,0:T(8,128)(2,1)S(1)} %get-tuple-element.29.ll), custom_call_target="tpu_custom_call" | custom-call | flops 1761607680 | bytes 1835008 | tf_op jit(solution)/shard_map/w_send/pallas_call | solution.py:184
  70.7 8.5 %w_send.3 = f32[1792,256]{1,0:T(8,128)} custom-call(s32[2]{0:T(128)S(1)} %get-tuple-element.54.at, f32[320,7168]{1,0:T(8,128)S(1)} %copy-done.2, f32[320,7168]{1,0:T(8,128)} %copy-done, bf16[640,256]{1,0:T(8,128)(2,1)S(1)} %get-tuple-element.28.lh, bf16[640,256]{1,0:T(8,128)(2,1)S(1)} %get-tuple-element.29.ll), custom_call_target="tpu_custom_call" | custom-call | flops 1761607680 | bytes 1835008 | tf_op jit(solution)/shard_map/w_send/pallas_call | solution.py:184
  79.1 0.5 collective-permute-start.8
  79.6 0.1 pad_add_fusion.3.at
  79.7 0.1 pad_add_fusion.1.at
  79.8 3.6 %copy-done.3 = f32[320,7168]{1,0:T(8,128)S(1)} copy-done((f32[320,7168]{1,0:T(8,128)S(1)}, f32[320,7168]{1,0:T(8,128)}, u32[]{:S(2)}) %copy-start.3) | copy-done | bytes 9175064
  83.4 8.8 %w_keep.2 = (f32[896,256]{1,0:T(8,128)}, f32[896,256]{1,0:T(8,128)S(1)}) custom-call(s32[4]{0:T(128)S(1)} %pad_add_fusion.1.at, f32[320,7168]{1,0:T(8,128)S(1)} %copy-done.3, f32[320,7168]{1,0:T(8,128)} %copy-done, bf16[640,256]{1,0:T(8,128)(2,1)S(1)} %get-tuple-element.28.lh, bf16[640,256]{1,0:T(8,128)(2,1)S(1)} %get-tuple-element.29.ll, ...), custom_call_target="tpu_custom_call" | custom-call | flops 1761607680 | bytes 1835008 | tf_op jit(solution)/shard_map/w_keep/pallas_call | solution.py:202
  92.2 1.5 collective-permute-start.6
  93.7 8.5 %w_keep.3 = (f32[896,256]{1,0:T(8,128)}, f32[896,256]{1,0:T(8,128)S(1)}) custom-call(s32[4]{0:T(128)S(1)} %pad_add_fusion.3.at, f32[320,7168]{1,0:T(8,128)S(1)} %copy-done.3, f32[320,7168]{1,0:T(8,128)} %copy-done, bf16[640,256]{1,0:T(8,128)(2,1)S(1)} %get-tuple-element.28.lh, bf16[640,256]{1,0:T(8,128)(2,1)S(1)} %get-tuple-element.29.ll, ...), custom_call_target="tpu_custom_call" | custom-call | flops 1761607680 | bytes 1835008 | tf_op jit(solution)/shard_map/w_keep/pallas_call | solution.py:202
  102.3 1.5 collective-permute-start.9
  103.8 1.5 collective-permute-done.11
  105.4 0.6 collective-permute-start.12
  106.0 14.4 %collective-permute-done.12 = f32[256,256]{1,0:T(8,128)S(1)} collective-permute-done((f32[256,256]{1,0:T(8,128)S(1)}, f32[256,256]{1,0:T(8,128)S(1)}, u32[]{:S(2)}, u32[]{:S(2)}) %collective-permute-start.12) | collective-permute-done | bytes 262176 | tf_op jit(solution)/shard_map/ppermute | solution.py:442
  120.4 1.6 collective-permute-start.13
  122.1 1.6 add.119
  123.7 0.5 collective-permute-start.7
  124.2 1.6 collective-permute-done.9
  125.8 1.3 add.123
  127.2 0.6 collective-permute-start.10
  127.7 0.1 pad_add_fusion.at
  127.8 3.5 %collective-permute-done.13 = f32[256,256]{1,0:T(8,128)S(1)} collective-permute-done((f32[256,256]{1,0:T(8,128)S(1)}, f32[256,256]{1,0:T(8,128)S(1)}, u32[]{:S(2)}, u32[]{:S(2)}) %collective-permute-start.13) | collective-permute-done | bytes 262176 | tf_op jit(solution)/shard_map/ppermute | solution.py:442
  131.4 12.8 %chol_inverse.1 = (f32[256,256]{1,0:T(8,128)S(1)}, bf16[640,256]{1,0:T(8,128)(2,1)S(1)}, bf16[640,256]{1,0:T(8,128)(2,1)S(1)}) custom-call(f32[256,256]{1,0:T(8,128)S(1)} %add.128.gram, f32[640,256]{1,0:T(8,128)S(1)} %copy-done.9), custom_call_target="tpu_custom_call" | custom-call | flops 4000000000 | bytes 655360 | tf_op jit(solution)/shard_map/chol_inverse/pallas_call | solution.py:316
  144.2 1.5 right_rows.1
  145.7 0.6 collective-permute-start.17
  146.3 1.6 collective-permute-start.14
  147.8 8.3 %collective-permute-done.17.y = f32[448,256]{1,0:T(8,128)S(1)} collective-permute-done((f32[448,256]{1,0:T(8,128)S(1)}, f32[448,256]{1,0:T(8,128)S(1)}, u32[]{:S(2)}, u32[]{:S(2)}) %collective-permute-start.17) | collective-permute-done | bytes 458784 | tf_op jit(solution)/shard_map/ppermute | solution.py:442
  156.2 1.6 collective-permute-start.18
  157.8 1.7 collective-permute-start.15
  159.5 0.5 collective-permute-start.26
  160.0 0.3 collective-permute-start.20
  160.3 3.4 %collective-permute-done.20 = f32[8,256]{1,0:T(8,128)S(1)} collective-permute-done((f32[8,256]{1,0:T(8,128)S(1)}, f32[8,256]{1,0:T(8,128)S(1)}, u32[]{:S(2)}, u32[]{:S(2)}) %collective-permute-start.20) | collective-permute-done | bytes 8224 | tf_op jit(solution)/shard_map/ppermute | solution.py:442
  163.6 0.3 collective-permute-start.21
  164.0 4.2 %collective-permute-done.21 = f32[8,256]{1,0:T(8,128)S(1)} collective-permute-done((f32[8,256]{1,0:T(8,128)S(1)}, f32[8,256]{1,0:T(8,128)S(1)}, u32[]{:S(2)}, u32[]{:S(2)}) %collective-permute-start.21) | collective-permute-done | bytes 8224 | tf_op jit(solution)/shard_map/ppermute | solution.py:442
  168.2 7.8 %collective-permute-done.18.refs_2_ = f32[896,256]{1,0:T(8,128)S(1)} collective-permute-done((f32[896,256]{1,0:T(8,128)S(1)}, f32[896,256]{1,0:T(8,128)S(1)}, u32[]{:S(2)}, u32[]{:S(2)}) %collective-permute-start.18) | collective-permute-done | bytes 917536 | tf_op jit(solution)/shard_map/ppermute | solution.py:442
  176.0 1.0 collective-permute-done.15.refs_0_
  177.0 2.0 collective-permute-start.25
  179.0 2.6 %collective-permute-done.25 = f32[8,256]{1,0:T(8,128)S(1)} collective-permute-done((f32[8,256]{1,0:T(8,128)S(1)}, f32[8,256]{1,0:T(8,128)S(1)}, u32[]{:S(2)}, u32[]{:S(2)}) %collective-permute-start.25) | collective-permute-done | bytes 8224 | tf_op jit(solution)/shard_map/ppermute | solution.py:442
  181.6 1.0 collective-permute-start.24
  182.6 2.7 %collective-permute-done.24 = f32[8,256]{1,0:T(8,128)S(1)} collective-permute-done((f32[8,256]{1,0:T(8,128)S(1)}, f32[8,256]{1,0:T(8,128)S(1)}, u32[]{:S(2)}, u32[]{:S(2)}) %collective-permute-start.24) | collective-permute-done | bytes 8224 | tf_op jit(solution)/shard_map/ppermute | solution.py:442
  185.3 1.0 collective-permute-start.23
  186.2 0.1 stack.117.at
  186.3 0.1 stack.97.at
  186.4 2.5 %collective-permute-done.23 = f32[8,256]{1,0:T(8,128)S(1)} collective-permute-done((f32[8,256]{1,0:T(8,128)S(1)}, f32[8,256]{1,0:T(8,128)S(1)}, u32[]{:S(2)}, u32[]{:S(2)}) %collective-permute-start.23) | collective-permute-done | bytes 8224 | tf_op jit(solution)/shard_map/ppermute | solution.py:442
  188.9 3.6 %copy-done.4 = f32[320,7168]{1,0:T(8,128)S(1)} copy-done((f32[320,7168]{1,0:T(8,128)S(1)}, f32[320,7168]{1,0:T(8,128)}, u32[]{:S(2)}) %copy-start.4) | copy-done | bytes 9175064
  192.5 18.0 %final.2 = (f32[640,6912]{1,0:T(8,128)}, f32[640,6912]{1,0:T(8,128)}, f32[6912,256]{1,0:T(8,128)}) custom-call(s32[6]{0:T(128)S(1)} %stack.117.at, f32[896,256]{1,0:T(8,128)S(1)} %join.2.refs_0_, f32[896,256]{1,0:T(8,128)} %collective-permute-done.26.refs_1_, f32[896,256]{1,0:T(8,128)S(1)} %join.3.refs_2_, f32[896,256]{1,0:T(8,128)} %collective-permute-done.27.refs_3_, ...), custom_call_target="tpu_custom_call" | custom-call | flops 7046430720 | bytes 25690112 | tf_op jit(solution)/shard_map/final/pallas_call | solution.py:410
  210.5 17.6 %final.3 = (f32[640,6912]{1,0:T(8,128)}, f32[640,6912]{1,0:T(8,128)}, f32[6912,256]{1,0:T(8,128)}) custom-call(s32[6]{0:T(128)S(1)} %stack.97.at, f32[896,256]{1,0:T(8,128)} %collective-permute-done.15.refs_0_, f32[896,256]{1,0:T(8,128)} %collective-permute-done.16.refs_1_, ...), custom_call_target="tpu_custom_call", output_to_operand_aliasing={{0}: (10, {}), {1}: (11, {}), {2}: (12, {})} | custom-call | flops 7046430720 | bytes 25690112 | tf_op jit(solution)/shard_map/final/pallas_call | solution.py:410
  (45 shorter events, 0.6 us)
Async XLA Ops:
  9.7 3.6 %copy-start = (f32[320,7168]{1,0:T(8,128)}, f32[320,7168]{1,0:T(8,128)S(1)}, u32[]{:S(2)}) copy-start(f32[320,7168]{1,0:T(8,128)S(1)} %get-tuple-element.25.other.refs_8_) | copy-start | bytes 27525124
  13.3 15.8 %collective-permute-start = (f32[320,256]{1,0:T(8,128)S(1)}, f32[320,256]{1,0:T(8,128)S(1)}, u32[]{:S(2)}, u32[]{:S(2)}) collective-permute-start(f32[320,256]{1,0:T(8,128)S(1)} %get-tuple-element.27), channel_id=1, source_target_pairs={{0,1},{1,0},{2,3},{3,2},{4,5},{5,4},{6,7},{7,6},{8,9},{9,8},{10,11... | collective-permute-start | bytes 983048 | tf_op jit(solution)/shard_map/ppermute | solution.py:442
  25.4 3.7 %copy-start.1 = (f32[320,7168]{1,0:T(8,128)}, f32[320,7168]{1,0:T(8,128)S(1)}, u32[]{:S(2)}) copy-start(f32[320,7168]{1,0:T(8,128)S(1)} %get-tuple-element.24.own.refs_7_) | copy-start | bytes 27525124
  29.1 13.6 %collective-permute-start.2 = (f32[160,256]{1,0:T(8,128)S(1)}, f32[160,256]{1,0:T(8,128)S(1)}, u32[]{:S(2)}, u32[]{:S(2)}) collective-permute-start(f32[160,256]{1,0:T(8,128)S(1)} %get-tuple-element.51), channel_id=1, source_target_pairs={{0,2},{1,3},{2,0},{3,1},{4,6},{5,7},{6,4},{7,5},{8,10},{9,11},{10,... | collective-permute-start | bytes 491528 | tf_op jit(solution)/shard_map/ppermute | solution.py:442
  31.8 14.3 %collective-permute-start.1 = (f32[160,256]{1,0:T(8,128)S(1)}, f32[160,256]{1,0:T(8,128)S(1)}, u32[]{:S(2)}, u32[]{:S(2)}) collective-permute-start(f32[160,256]{1,0:T(8,128)S(1)} %get-tuple-element.52), channel_id=1, source_target_pairs={{0,2},{1,3},{2,0},{3,1},{4,6},{5,7},{6,4},{7,5},{8,10},{9,11},{10,... | collective-permute-start | bytes 491528 | tf_op jit(solution)/shard_map/ppermute | solution.py:442
  46.2 7.1 %collective-permute-start.4 = (f32[160,256]{1,0:T(8,128)S(1)}, f32[160,256]{1,0:T(8,128)S(1)}, u32[]{:S(2)}, u32[]{:S(2)}) collective-permute-start(f32[160,256]{1,0:T(8,128)S(1)} %get-tuple-element.49.refs_1_), channel_id=1, source_target_pairs={{0,1},{1,0},{2,3},{3,2},{4,5},{5,4},{6,7},{7,6},{8,9},{9,8},{10,11... | collective-permute-start | bytes 491528 | tf_op jit(solution)/shard_map/ppermute | solution.py:442
  46.3 9.6 %collective-permute-start.3 = (f32[160,256]{1,0:T(8,128)S(1)}, f32[160,256]{1,0:T(8,128)S(1)}, u32[]{:S(2)}, u32[]{:S(2)}) collective-permute-start(f32[160,256]{1,0:T(8,128)S(1)} %get-tuple-element.50.refs_0_), channel_id=1, source_target_pairs={{0,1},{1,0},{2,3},{3,2},{4,5},{5,4},{6,7},{7,6},{8,9},{9,8},{10,11... | collective-permute-start | bytes 491528 | tf_op jit(solution)/shard_map/ppermute | solution.py:442
  57.0 0.7 copy-start.6
  57.7 0.9 copy-start.8
  58.6 3.6 %copy-start.2 = (f32[320,7168]{1,0:T(8,128)S(1)}, f32[320,7168]{1,0:T(8,128)}, u32[]{:S(2)}) copy-start(f32[320,7168]{1,0:T(8,128)} %copy-done.1) | copy-start | bytes 27525124
  70.7 9.1 %collective-permute-start.5 = (f32[1792,256]{1,0:T(8,128)}, f32[1792,256]{1,0:T(8,128)}, u32[]{:S(2)}, u32[]{:S(2)}) collective-permute-start(f32[1792,256]{1,0:T(8,128)} %w_send.2), channel_id=1, source_target_pairs={{0,4},{4,0},{8,12},{12,8},{16,20},{20,16},{24,28},{28,24},{1,5},{5... | collective-permute-start | bytes 5505032 | tf_op jit(solution)/shard_map/ppermute | solution.py:442
  79.1 14.6 %collective-permute-start.8 = (f32[1792,256]{1,0:T(8,128)}, f32[1792,256]{1,0:T(8,128)S(1)}, u32[]{:S(2)}, u32[]{:S(2)}) collective-permute-start(f32[1792,256]{1,0:T(8,128)} %w_send.3), channel_id=1, source_target_pairs={{0,4},{4,0},{8,12},{12,8},{16,20},{20,16},{24,28},{28,24},{1,5},{5... | collective-permute-start | bytes 5505032 | tf_op jit(solution)/shard_map/ppermute | solution.py:442
  79.8 3.6 %copy-start.3 = (f32[320,7168]{1,0:T(8,128)S(1)}, f32[320,7168]{1,0:T(8,128)}, u32[]{:S(2)}) copy-start(f32[320,7168]{1,0:T(8,128)} %copy-done.1) | copy-start | bytes 27525124
  92.2 10.1 %copy-start.5 = (f32[896,256]{1,0:T(8,128)}, f32[896,256]{1,0:T(8,128)S(1)}, u32[]{:S(2)}) copy-start(f32[896,256]{1,0:T(8,128)S(1)} %get-tuple-element.30) | copy-start | bytes 2752516
  92.2 11.6 %copy-start.7 = (f32[256,256]{1,0:T(8,128)S(1)}, f32[256,256]{1,0:T(8,128)}, u32[]{:S(2)}) copy-start(f32[256,256]{1,0:T(8,128)} %copy-done.6) | copy-start | bytes 786436
  92.2 29.9 %collective-permute-start.6 = (f32[896,256]{1,0:T(8,128)}, f32[896,256]{1,0:T(8,128)}, u32[]{:S(2)}, u32[]{:S(2)}) collective-permute-start(f32[896,256]{1,0:T(8,128)} %get-tuple-element.31), channel_id=1, source_target_pairs={{0,8},{4,12},{8,0},{12,4},{16,24},{20,28},{24,16},{28,20},{1,9},{5... | collective-permute-start | bytes 2752520 | tf_op jit(solution)/shard_map/ppermute | solution.py:442
  102.3 29.1 %copy-start.9 = (f32[640,256]{1,0:T(8,128)S(1)}, f32[640,256]{1,0:T(8,128)}, u32[]{:S(2)}) copy-start(f32[640,256]{1,0:T(8,128)} %copy-done.8) | copy-start | bytes 1966084
  102.3 23.5 %collective-permute-start.9 = (f32[896,256]{1,0:T(8,128)}, f32[896,256]{1,0:T(8,128)}, u32[]{:S(2)}, u32[]{:S(2)}) collective-permute-start(f32[896,256]{1,0:T(8,128)} %get-tuple-element.33), channel_id=1, source_target_pairs={{0,16},{4,20},{8,24},{12,28},{16,0},{20,4},{24,8},{28,12},{1,17},{... | collective-permute-start | bytes 2752520 | tf_op jit(solution)/shard_map/ppermute | solution.py:442
  103.8 1.5 collective-permute-start.11
  105.4 15.0 %collective-permute-start.12 = (f32[256,256]{1,0:T(8,128)S(1)}, f32[256,256]{1,0:T(8,128)S(1)}, u32[]{:S(2)}, u32[]{:S(2)}) collective-permute-start(f32[256,256]{1,0:T(8,128)S(1)} %add.126), channel_id=1, source_target_pairs={{0,8},{4,12},{8,0},{12,4},{16,24},{20,28},{24,16},{28,20},{1,9},{5... | collective-permute-start | bytes 786440 | tf_op jit(solution)/shard_map/ppermute | solution.py:442
  120.4 10.9 %collective-permute-start.13 = (f32[256,256]{1,0:T(8,128)S(1)}, f32[256,256]{1,0:T(8,128)S(1)}, u32[]{:S(2)}, u32[]{:S(2)}) collective-permute-start(f32[256,256]{1,0:T(8,128)S(1)} %add.127), channel_id=1, source_target_pairs={{0,16},{4,20},{8,24},{12,28},{16,0},{20,4},{24,8},{28,12},{1,17},{... | collective-permute-start | bytes 786440 | tf_op jit(solution)/shard_map/ppermute | solution.py:442
  123.7 20.4 %collective-permute-start.7 = (f32[448,256]{1,0:T(8,128)S(1)}, f32[448,256]{1,0:T(8,128)S(1)}, u32[]{:S(2)}, u32[]{:S(2)}) collective-permute-start(f32[448,256]{1,0:T(8,128)S(1)} %get-tuple-element.47), channel_id=1, source_target_pairs={{0,16},{4,20},{8,24},{12,28},{16,0},{20,4},{24,8},{28,12},{1,17},{... | collective-permute-start | bytes 1376264 | tf_op jit(solution)/shard_map/ppermute | solution.py:442
  127.2 17.0 %collective-permute-start.10 = (f32[448,256]{1,0:T(8,128)S(1)}, f32[448,256]{1,0:T(8,128)S(1)}, u32[]{:S(2)}, u32[]{:S(2)}) collective-permute-start(f32[448,256]{1,0:T(8,128)S(1)} %get-tuple-element.45), channel_id=1, source_target_pairs={{0,8},{4,12},{8,0},{12,4},{16,24},{20,28},{24,16},{28,20},{1,9},{5... | collective-permute-start | bytes 1376264 | tf_op jit(solution)/shard_map/ppermute | solution.py:442
  145.7 10.4 %collective-permute-start.17 = (f32[448,256]{1,0:T(8,128)S(1)}, f32[448,256]{1,0:T(8,128)S(1)}, u32[]{:S(2)}, u32[]{:S(2)}) collective-permute-start(f32[448,256]{1,0:T(8,128)S(1)} %get-tuple-element.38.x), channel_id=1, source_target_pairs={{0,8},{4,12},{8,0},{12,4},{16,24},{20,28},{24,16},{28,20},{1,9},{5... | collective-permute-start | bytes 1376264 | tf_op jit(solution)/shard_map/ppermute | solution.py:442
  146.3 11.5 %collective-permute-start.14 = (f32[448,256]{1,0:T(8,128)S(1)}, f32[448,256]{1,0:T(8,128)S(1)}, u32[]{:S(2)}, u32[]{:S(2)}) collective-permute-start(f32[448,256]{1,0:T(8,128)S(1)} %get-tuple-element.37.x), channel_id=1, source_target_pairs={{0,16},{4,20},{8,24},{12,28},{16,0},{20,4},{24,8},{28,12},{1,17},{... | collective-permute-start | bytes 1376264 | tf_op jit(solution)/shard_map/ppermute | solution.py:442
  156.2 19.8 %collective-permute-start.18 = (f32[896,256]{1,0:T(8,128)S(1)}, f32[896,256]{1,0:T(8,128)S(1)}, u32[]{:S(2)}, u32[]{:S(2)}) collective-permute-start(f32[896,256]{1,0:T(8,128)S(1)} %join.3.refs_2_), channel_id=1, source_target_pairs={{0,16},{4,20},{8,24},{12,28},{16,0},{20,4},{24,8},{28,12},{1,17},{... | collective-permute-start | bytes 2752520 | tf_op jit(solution)/shard_map/ppermute | solution.py:442
  157.8 19.2 %collective-permute-start.15 = (f32[896,256]{1,0:T(8,128)S(1)}, f32[896,256]{1,0:T(8,128)}, u32[]{:S(2)}, u32[]{:S(2)}) collective-permute-start(f32[896,256]{1,0:T(8,128)S(1)} %join.2.refs_0_), channel_id=1, source_target_pairs={{0,8},{4,12},{8,0},{12,4},{16,24},{20,28},{24,16},{28,20},{1,9},{5... | collective-permute-start | bytes 2752520 | tf_op jit(solution)/shard_map/ppermute | solution.py:442
  159.5 29.5 %collective-permute-start.27 = (f32[896,256]{1,0:T(8,128)S(1)}, f32[896,256]{1,0:T(8,128)}, u32[]{:S(2)}, u32[]{:S(2)}) collective-permute-start(f32[896,256]{1,0:T(8,128)S(1)} %join.3.refs_2_), channel_id=1, source_target_pairs={{0,4},{4,0},{8,12},{12,8},{16,20},{20,16},{24,28},{28,24},{1,5},{5... | collective-permute-start | bytes 2752520 | tf_op jit(solution)/shard_map/ppermute | solution.py:442
  159.5 29.5 %collective-permute-start.26 = (f32[896,256]{1,0:T(8,128)S(1)}, f32[896,256]{1,0:T(8,128)}, u32[]{:S(2)}, u32[]{:S(2)}) collective-permute-start(f32[896,256]{1,0:T(8,128)S(1)} %join.2.refs_0_), channel_id=1, source_target_pairs={{0,4},{4,0},{8,12},{12,8},{16,20},{20,16},{24,28},{28,24},{1,5},{5... | collective-permute-start | bytes 2752520 | tf_op jit(solution)/shard_map/ppermute | solution.py:442
  160.0 3.7 %collective-permute-start.20 = (f32[8,256]{1,0:T(8,128)S(1)}, f32[8,256]{1,0:T(8,128)S(1)}, u32[]{:S(2)}, u32[]{:S(2)}) collective-permute-start(f32[8,256]{1,0:T(8,128)S(1)} %get-tuple-element.39), channel_id=1, source_target_pairs={{0,1},{1,0},{2,3},{3,2},{4,5},{5,4},{6,7},{7,6},{8,9},{9,8},{10,11... | collective-permute-start | bytes 24584 | tf_op jit(solution)/shard_map/ppermute | solution.py:442
  163.6 4.5 %collective-permute-start.21 = (f32[8,256]{1,0:T(8,128)S(1)}, f32[8,256]{1,0:T(8,128)S(1)}, u32[]{:S(2)}, u32[]{:S(2)}) collective-permute-start(f32[8,256]{1,0:T(8,128)S(1)} %add.129), channel_id=1, source_target_pairs={{0,2},{1,3},{2,0},{3,1},{4,6},{5,7},{6,4},{7,5},{8,10},{9,11},{10,... | collective-permute-start | bytes 24584 | tf_op jit(solution)/shard_map/ppermute | solution.py:442
  168.2 8.8 %collective-permute-start.22 = (f32[8,256]{1,0:T(8,128)S(1)}, f32[8,256]{1,0:T(8,128)S(1)}, u32[]{:S(2)}, u32[]{:S(2)}) collective-permute-start(f32[8,256]{1,0:T(8,128)S(1)} %add.130), channel_id=1, source_target_pairs={{0,4},{4,0},{8,12},{12,8},{16,20},{20,16},{24,28},{28,24},{1,5},{5... | collective-permute-start | bytes 24584 | tf_op jit(solution)/shard_map/ppermute | solution.py:442
  176.0 34.6 %collective-permute-start.19 = (f32[896,256]{1,0:T(8,128)S(1)}, f32[896,256]{1,0:T(8,128)}, u32[]{:S(2)}, u32[]{:S(2)}) collective-permute-start(f32[896,256]{1,0:T(8,128)S(1)} %collective-permute-done.18.refs_2_), channel_id=1, source_target_pairs={{0,4},{4,0},{8,12},{12,8},{16,20},{20,16},{24,28},{28,24},{1,5},{5... | collective-permute-start | bytes 2752520 | tf_op jit(solution)/shard_map/ppermute | solution.py:442
  177.0 33.5 %collective-permute-start.16 = (f32[896,256]{1,0:T(8,128)}, f32[896,256]{1,0:T(8,128)}, u32[]{:S(2)}, u32[]{:S(2)}) collective-permute-start(f32[896,256]{1,0:T(8,128)} %collective-permute-done.15.refs_0_), channel_id=1, source_target_pairs={{0,4},{4,0},{8,12},{12,8},{16,20},{20,16},{24,28},{28,24},{1,5},{5... | collective-permute-start | bytes 2752520 | tf_op jit(solution)/shard_map/ppermute | solution.py:442
  177.0 4.6 %collective-permute-start.25 = (f32[8,256]{1,0:T(8,128)S(1)}, f32[8,256]{1,0:T(8,128)S(1)}, u32[]{:S(2)}, u32[]{:S(2)}) collective-permute-start(f32[8,256]{1,0:T(8,128)S(1)} %add.131), channel_id=1, source_target_pairs={{0,24},{4,28},{8,16},{12,20},{16,8},{20,12},{24,0},{28,4},{1,25},{... | collective-permute-start | bytes 24584 | tf_op jit(solution)/shard_map/ppermute | solution.py:442
  181.6 3.7 %collective-permute-start.24 = (f32[8,256]{1,0:T(8,128)S(1)}, f32[8,256]{1,0:T(8,128)S(1)}, u32[]{:S(2)}, u32[]{:S(2)}) collective-permute-start(f32[8,256]{1,0:T(8,128)S(1)} %add.131), channel_id=1, source_target_pairs={{0,16},{4,20},{8,24},{12,28},{16,0},{20,4},{24,8},{28,12},{1,17},{... | collective-permute-start | bytes 24584 | tf_op jit(solution)/shard_map/ppermute | solution.py:442
  185.3 3.7 %collective-permute-start.23 = (f32[8,256]{1,0:T(8,128)S(1)}, f32[8,256]{1,0:T(8,128)S(1)}, u32[]{:S(2)}, u32[]{:S(2)}) collective-permute-start(f32[8,256]{1,0:T(8,128)S(1)} %add.131), channel_id=1, source_target_pairs={{0,8},{4,12},{8,0},{12,4},{16,24},{20,28},{24,16},{28,20},{1,9},{5... | collective-permute-start | bytes 24584 | tf_op jit(solution)/shard_map/ppermute | solution.py:442
  188.9 3.6 %copy-start.4 = (f32[320,7168]{1,0:T(8,128)S(1)}, f32[320,7168]{1,0:T(8,128)}, u32[]{:S(2)}) copy-start(f32[320,7168]{1,0:T(8,128)} %copy-done.1) | copy-start | bytes 27525124

commit v4 on v3

--- a/solution.py
+++ b/solution.py
@@ -12,20 +12,19 @@
 BF16 = jnp.bfloat16
 HIGH = lax.Precision.HIGHEST
 LANES = 128
-VMEM_LIMIT = 40 * 1024 * 1024
 
 NN = (((1,), (0,)), ((), ()))
 NT = (((1,), (1,)), ((), ()))
 TN = (((0,), (0,)), ((), ()))
 
 
-ANY = pl.BlockSpec(memory_space=pl.ANY)
+HBM = pl.BlockSpec(memory_space=pltpu.HBM)
 VMEM = pl.BlockSpec(memory_space=pltpu.VMEM)
 SMEM = pl.BlockSpec(memory_space=pltpu.SMEM)
 
 
-def params(**kw):
-    return pltpu.CompilerParams(vmem_limit_bytes=VMEM_LIMIT, **kw)
+def params(mib):
+    return pltpu.CompilerParams(vmem_limit_bytes=mib * 1024 * 1024)
 
 
 def cost(flops, moved):
@@ -47,19 +46,15 @@
     return lax.dot_general(a, b, dims, precision=HIGH, preferred_element_type=F32)
 
 
-def scalars(*values):
-    return jnp.stack([jnp.asarray(v, jnp.int32) for v in values])
-
-
 def column_block(cols):
     blocks = cols // LANES
     return LANES * max(k for k in range(1, 9) if blocks % k == 0)
 
 
-def left_kernel(at, g, m, r, buffer, out, gs, ms, rs, sems):
+def left_kernel(which, at, g, m, r, buffer, out, gs, ms, rs, sems):
     depth, half, wide = gs.shape
     steps = g.shape[1] // wide
-    rows = pl.ds(pl.multiple_of(at[0] * half, GROUP), half)
+    rows = pl.ds(pl.multiple_of(at[which] * half, GROUP), half)
 
     def copies(j, slot):
         part = pl.ds(pl.multiple_of(j * wide, LANES), wide)
@@ -94,13 +89,13 @@
     lax.fori_loop(0, steps, body, 0)
 
 
-def left_half(at, gradient, momentum, right_factor, padded):
+def left_half(at, which, gradient, momentum, right_factor, padded):
     rows, cols = gradient.shape
     rank = right_factor.shape[1]
     half, wide, depth = rows // 2, column_block(cols), 4
     return pl.pallas_call(
-        left_kernel,
-        in_specs=[SMEM, ANY, ANY, ANY],
+        functools.partial(left_kernel, which),
+        in_specs=[SMEM, HBM, HBM, HBM],
         out_specs=[VMEM, VMEM],
         out_shape=[pltpu.VMEM((half, padded), F32), jax.ShapeDtypeStruct((half, rank), F32)],
         scratch_shapes=[
@@ -109,10 +104,10 @@
             pltpu.VMEM((depth, wide, rank), F32),
             pltpu.SemaphoreType.DMA((3, depth)),
         ],
-        compiler_params=params(),
+        compiler_params=params(40),
         cost_estimate=cost(6 * half * cols * rank, 4 * (2 * half * cols + cols * rank)),
         name="left_half",
-    )(scalars(at), gradient, momentum, right_factor)
+    )(at, gradient, momentum, right_factor)
 
 
 def gram_kernel(*refs):
@@ -141,7 +136,7 @@
             jax.ShapeDtypeStruct((rows, rank), BF16),
             jax.ShapeDtypeStruct((rank, rank), F32),
         ],
-        compiler_params=params(),
+        compiler_params=params(8),
         cost_estimate=cost(12 * rows * rank * rank, 12 * rows * rank),
         name="gram_of",
     )(*pieces)
@@ -158,13 +153,13 @@
     return total
 
 
-def w_send_kernel(at, own, other, lh, ll, out):
-    out[...] = w_term(at[pl.program_id(0)], out.shape[0], own, other, lh, ll)
-
-
-def w_keep_kernel(at, own, other, lh, ll, got, send, keep):
+def w_send_kernel(place, at, own, other, lh, ll, out):
+    out[...] = w_term(at[place + pl.program_id(0)], out.shape[0], own, other, lh, ll)
+
+
+def w_keep_kernel(place, at, own, other, lh, ll, got, send, keep):
     i, width = pl.program_id(0), send.shape[0]
-    total = w_term(at[i], width, own, other, lh, ll) + got[...]
+    total = w_term(at[place + i], width, own, other, lh, ll) + got[...]
 
     @pl.when(i == 0)
     def _():
@@ -179,10 +174,10 @@
     return cost(2 * 6 * rows * unit * rank, 2 * 4 * unit * rank)
 
 
-def w_send(units, own, other, lh, ll, unit):
+def w_send(at, place, own, other, lh, ll, unit):
     rows, rank = lh.shape
     return pl.pallas_call(
-        w_send_kernel,
+        functools.partial(w_send_kernel, place),
         grid_spec=pltpu.PrefetchScalarGridSpec(
             num_scalar_prefetch=1,
             grid=(2,),
@@ -190,28 +185,28 @@
             out_specs=pl.BlockSpec((unit, rank), lambda i, at: (i, 0)),
         ),
         out_shape=jax.ShapeDtypeStruct((2 * unit, rank), F32),
-        compiler_params=params(),
+        compiler_params=params(8),
         cost_estimate=w_cost(rows, rank, unit),
         name="w_send",
-    )(scalars(*units), own, other, lh, ll)
-
-
-def w_keep(units, order, own, other, lh, ll, got, unit):
+    )(at, own, other, lh, ll)
+
+
+def w_keep(at, place, own, other, lh, ll, got, unit):
     rows, rank = lh.shape
     one = pl.BlockSpec((unit, rank), lambda i, at: (0, 0))
     return pl.pallas_call(
-        w_keep_kernel,
+        functools.partial(w_keep_kernel, place),
         grid_spec=pltpu.PrefetchScalarGridSpec(
             num_scalar_prefetch=1,
             grid=(2,),
-            in_specs=[VMEM] * 4 + [pl.BlockSpec((unit, rank), lambda i, at: (at[2 + i], 0))],
+            in_specs=[VMEM] * 4 + [pl.BlockSpec((unit, rank), lambda i, at: (at[place + 2 + i], 0))],
             out_specs=[one, one],
         ),
         out_shape=[jax.ShapeDtypeStruct((unit, rank), F32)] * 2,
-        compiler_params=params(),
+        compiler_params=params(10),
         cost_estimate=w_cost(rows, rank, unit),
         name="w_keep",
-    )(scalars(*units, *order), own, other, lh, ll, got)
+    )(at, own, other, lh, ll, got)
 
 
 GROUP = 8
@@ -323,60 +318,79 @@
             jax.ShapeDtypeStruct((rows, rank), BF16),
         ],
         scratch_shapes=[pltpu.VMEM((rank, 2 * rank), F32)],
-        compiler_params=params(),
+        compiler_params=params(8),
         cost_estimate=cost(4e9, 4 * rows * rank),
         name="chol_inverse",
     )(gram, left)
 
 
-def right_kernel(at, ka, ga, kb, gb, x, ra, rb, squares):
+def right_kernel(place, cols, at, ka, ga, kb, gb, x, ra, rb, squares):
     rows, rank = ka.shape
     total = jnp.zeros((1, rank), F32)
     for i, (k, g, out) in enumerate(((ka, ga, ra), (kb, gb, rb))):
         value = dot_high(k[...] + g[...], x[...], NT)
         out[...] = value
-        row = lax.broadcasted_iota(jnp.int32, (rows, rank), 0) + at[i]
-        value = jnp.where(row < at[2], value, 0.0)
+        row = lax.broadcasted_iota(jnp.int32, (rows, rank), 0) + at[place + i]
+        value = jnp.where(row < cols, value, 0.0)
         total = total + jnp.sum(value * value, axis=0, keepdims=True)
     squares[...] = jnp.broadcast_to(total, squares.shape)
 
 
-def right_rows(at_a, at_b, cols, ka, ga, kb, gb, x):
+def right_rows(at, place, cols, ka, ga, kb, gb, x):
     rows, rank = ka.shape
     vm = pl.BlockSpec(memory_space=pltpu.VMEM)
     return pl.pallas_call(
-        right_kernel,
+        functools.partial(right_kernel, place, cols),
         in_specs=[pl.BlockSpec(memory_space=pltpu.SMEM)] + [vm] * 5,
         out_specs=[vm] * 3,
         out_shape=[jax.ShapeDtypeStruct((rows, rank), F32)] * 2
         + [jax.ShapeDtypeStruct((GROUP, rank), F32)],
-        compiler_params=params(),
+        compiler_params=params(8),
         cost_estimate=cost(24 * rows * rank * rank, 24 * rows * rank),
         name="right_rows",
-    )(scalars(at_a, at_b, cols), ka, ga, kb, gb, x)
-
-
-def join_kernel(at, x, y, out):
-    n = x.shape[0]
-    out[pl.ds(pl.multiple_of(at[0] * n, GROUP), n), :] = x[...]
-    out[pl.ds(pl.multiple_of((1 - at[0]) * n, GROUP), n), :] = y[...]
-
-
-def join(t, x, y):
+    )(at, ka, ga, kb, gb, x)
+
+
+def join_kernel(place, at, x, y, out):
+    n, t = x.shape[0], at[place]
+    out[pl.ds(pl.multiple_of(t * n, GROUP), n), :] = x[...]
+    out[pl.ds(pl.multiple_of((1 - t) * n, GROUP), n), :] = y[...]
+
+
+def join(at, place, x, y):
     rows, rank = x.shape
-    vm = pl.BlockSpec(memory_space=pltpu.VMEM)
-    return pl.pallas_call(
-        join_kernel,
-        in_specs=[pl.BlockSpec(memory_space=pltpu.SMEM), vm, vm],
-        out_specs=vm,
+    return pl.pallas_call(
+        functools.partial(join_kernel, place),
+        in_specs=[SMEM, VMEM, VMEM],
+        out_specs=VMEM,
         out_shape=jax.ShapeDtypeStruct((2 * rows, rank), F32),
-        compiler_params=params(),
+        compiler_params=params(6),
         cost_estimate=cost(rows * rank, 16 * rows * rank),
         name="join",
-    )(scalars(t), x, y)
-
-
-def final_kernel(count, total_cols, factor, at, *refs):
+    )(at, x, y)
+
+
+def halve_kernel(place, at, x, y, send, keep):
+    n, t = send.shape[0], at[place]
+    for part, out in ((1 - t, send), (t, keep)):
+        rows = pl.ds(pl.multiple_of(part * n, GROUP), n)
+        out[...] = x[rows, :] + y[rows, :]
+
+
+def halve(at, place, x, y):
+    rows, rank = x.shape
+    return pl.pallas_call(
+        functools.partial(halve_kernel, place),
+        in_specs=[SMEM, VMEM, VMEM],
+        out_specs=[VMEM, VMEM],
+        out_shape=[jax.ShapeDtypeStruct((rows // 2, rank), F32)] * 2,
+        compiler_params=params(6),
+        cost_estimate=cost(rows * rank, 12 * rows * rank),
+        name="halve",
+    )(at, x, y)
+
+
+def final_kernel(place, count, total_cols, factor, at, *refs):
     pieces = refs[:count]
     squares, oh, ol, own, other = refs[count : count + 5]
     update, momentum, new_right, rh, rl, nh, nl = refs[-7:]
@@ -393,7 +407,7 @@
             rh[...], rl[...] = split(right)
             nh[...], nl[...] = split(scaled)
 
-    part = pl.ds(pl.multiple_of(at[2 + u] * width, LANES), width)
+    part = pl.ds(pl.multiple_of(at[place + u] * width, LANES), width)
     for h, buffer in enumerate((own, other)):
         rows = pl.ds(pl.multiple_of(at[h] * half, GROUP), half)
         a, b = oh[h * half : (h + 1) * half, :], ol[h * half : (h + 1) * half, :]
@@ -401,19 +415,19 @@
         update[rows, :] = factor * dot3(a, b, nh[...], nl[...], NT)
 
 
-def final(s, units, pieces, squares, oh, ol, own, other, cols, total_rows, total_cols, before):
+def final(at, place, pieces, squares, oh, ol, own, other, cols, total_rows, total_cols, before):
     rows = oh.shape[0]
     unit, rank = pieces[0].shape
     count = len(pieces)
-    wide = pl.BlockSpec((rows, unit), lambda u, at: (0, at[2 + u]))
+    wide = pl.BlockSpec((rows, unit), lambda u, at: (0, at[place + u]))
     factor = (total_rows / rank) ** 0.5
     return pl.pallas_call(
-        functools.partial(final_kernel, count, total_cols, factor),
+        functools.partial(final_kernel, place, count, total_cols, factor),
         grid_spec=pltpu.PrefetchScalarGridSpec(
             num_scalar_prefetch=1,
             grid=(count,),
-            in_specs=[VMEM] * (count + 5) + [ANY] * len(before),
-            out_specs=[wide, wide, pl.BlockSpec((unit, rank), lambda u, at: (at[2 + u], 0))],
+            in_specs=[VMEM] * (count + 5) + [HBM] * len(before),
+            out_specs=[wide, wide, pl.BlockSpec((unit, rank), lambda u, at: (at[place + u], 0))],
             scratch_shapes=[pltpu.VMEM((unit, rank), BF16)] * 4,
         ),
         out_shape=[
@@ -422,10 +436,10 @@
             jax.ShapeDtypeStruct((cols, rank), F32),
         ],
         input_output_aliases={count + 6 + i: i for i in range(len(before))},
-        compiler_params=params(),
+        compiler_params=params(20),
         cost_estimate=cost(12 * count * rows * unit * rank, 4 * count * unit * (2 * rows + 2 * rank)),
         name="final",
-    )(scalars(s, 1 - s, *units), *pieces, squares, oh, ol, own, other, *before)
+    )(at, *pieces, squares, oh, ol, own, other, *before)
 
 
 def power_of_two(n):
@@ -456,79 +470,89 @@
     rows, cols = gradient.shape
     n_dp, n_tp = lax.axis_size("dp"), lax.axis_size("tensor")
     d, z = lax.axis_index("dp"), lax.axis_index("tensor")
-
-    s = lax.rem(z, 2)
+    bits = bits_of(n_dp)
+
     unit = LANES * (-(-cols // (8 * LANES)))
-    buffer_other, away = left_half(1 - s, gradient, momentum, right_factor, 8 * unit)
+    orders = [bits[1:], bits[1:][::-1]]
+    table = []
+
+    def put(*values):
+        table.extend(values)
+        return len(table) - len(values)
+
+    bit_of = lambda b: (d >> b) & 1
+    s, core = z & 1, d & 1
+    put(s, 1 - s)
+    send_at, keep_at, bit_at, near, far, first = [], [], [], [], [], []
+    for h, order in enumerate(orders):
+        t = bit_of(order[0])
+        base, beside = 4 * h + 2 * core, 4 * h + 2 * (1 - core)
+        send_at.append(put(beside, beside + 1))
+        keep_at.append(put(base + 1 - t, base + t, 1 - t, t))
+        bit_at.append({b: put(bit_of(b)) for b in order[1:]})
+        near += [base + t, beside + t]
+        far += [base + 1 - t, beside + 1 - t]
+        at, n = (base + t) * unit, unit
+        for b in order[1:]:
+            n = n // 2
+            at = at + bit_of(b) * n
+        first.append(at)
+    near_at, far_at, first_at = put(*near), put(*far), put(*first)
+    at = jnp.stack([jnp.asarray(v, jnp.int32) for v in table])
+
+    inputs = (gradient, momentum, right_factor, 8 * unit)
+    buffer_other, away = left_half(at, 1, *inputs)
     if power_of_two(n_tp) and n_tp > 1:
         got = swap(away, "tensor", 0)
-        buffer_own, mine = left_half(s, gradient, momentum, right_factor, 8 * unit)
+        buffer_own, mine = left_half(at, 0, *inputs)
         mine = mine + got
         own = [mine[: rows // 4], mine[rows // 4 :]]
         for bit in bits_of(n_tp)[1:]:
             own = [x + swap(x, "tensor", bit) for x in own]
         pieces = own + [swap(x, "tensor", 0) for x in own]
     else:
-        buffer_own, mine = left_half(s, gradient, momentum, right_factor, 8 * unit)
+        buffer_own, mine = left_half(at, 0, *inputs)
         both = lax.psum(jnp.where(s == 0, jnp.stack([mine, away]), jnp.stack([away, mine])), "tensor")
         pieces = [lax.dynamic_index_in_dim(both, i, 0, False) for i in (s, 1 - s)]
 
     left, lh, ll, gram = gram_of(pieces)
     gram = sum_over(gram, "dp")
 
-    bits = bits_of(n_dp)
-    core = lax.rem(d, 2)
-    orders = [bits[1:], bits[1:][::-1]]
-    bit_of = lambda b: lax.rem(d // (1 << b), 2)
+    held = (buffer_own, buffer_other)
     got = []
     for h in range(2):
-        units = [4 * h + 2 * (1 - core), 4 * h + 2 * (1 - core) + 1]
-        sent = w_send(units, buffer_own, buffer_other, lh, ll, unit)
+        sent = w_send(at, send_at[h], *held, lh, ll, unit)
         got.append(swap(sent, "dp", 0))
-    kept, here = [], []
+    kept = []
     for h, order in enumerate(orders):
-        t = bit_of(order[0])
-        base = 4 * h + 2 * core
-        units, places = [base + 1 - t, base + t], [1 - t, t]
-        send, keep = w_keep(units, places, buffer_own, buffer_other, lh, ll, got[h], unit)
-        at = (base + t) * unit
+        send, keep = w_keep(at, keep_at[h], *held, lh, ll, got[h], unit)
         recv = swap(send, "dp", order[0])
         for b in order[1:]:
-            x = keep + recv
-            n = x.shape[0] // 2
-            t = bit_of(b)
-            recv = swap(lax.dynamic_slice_in_dim(x, (1 - t) * n, n, 0), "dp", b)
-            keep = lax.dynamic_slice_in_dim(x, t * n, n, 0)
-            at = at + t * n
-        kept.append((keep, recv))
-        here.append(at)
+            send, keep = halve(at, bit_at[h][b], keep, recv)
+            recv = swap(send, "dp", b)
+        kept += [keep, recv]
 
     x_inv, oh, ol = chol_inverse(gram, left)
-    ra, rb, squares = right_rows(here[0], here[1], cols, *kept[0], *kept[1], x_inv)
+    *right, squares = right_rows(at, first_at, cols, *kept, x_inv)
     squares = sum_over(squares, "tensor")
     for b in bits[:1] + bits[3:]:
         squares = squares + swap(squares, "dp", b)
-    first, second = bits[1:3]
-    others = [swap(squares, "dp", *m) for m in ((first,), (second,), (first, second))]
+    b, c = bits[1:3]
+    others = [swap(squares, "dp", *m) for m in ((b,), (c,), (b, c))]
     squares = (squares + others[0]) + (others[1] + others[2])
 
     near, far = [], []
-    for h, (order, x) in enumerate(zip(orders, (ra, rb))):
+    for h, (order, x) in enumerate(zip(orders, right)):
         for b in order[:0:-1]:
-            y = swap(x, "dp", b)
-            x = join(bit_of(b), x, y)
-        t = bit_of(order[0])
+            x = join(at, bit_at[h][b], x, swap(x, "dp", b))
         y = swap(x, "dp", order[0])
-        base, beside = 4 * h + 2 * core, 4 * h + 2 * (1 - core)
-        near.append(((base + t, x), (beside + t, swap(x, "dp", 0))))
-        far.append(((base + 1 - t, y), (beside + 1 - t, swap(y, "dp", 0))))
+        near += [x, swap(x, "dp", 0)]
+        far += [y, swap(y, "dp", 0)]
 
     outs = ()
-    for group in (near, far):
-        units = [u for part in group for u, _ in part]
-        data = [x for part in group for _, x in part]
-        held = (squares, oh, ol, buffer_own, buffer_other)
-        outs = final(s, units, data, *held, cols, rows * n_dp, cols * n_tp, outs)
+    for place, data in ((near_at, near), (far_at, far)):
+        sizes = (cols, rows * n_dp, cols * n_tp)
+        outs = final(at, place, data, squares, oh, ol, *held, *sizes, outs)
     return tuple(outs)
 
 

time: 229 us -> 185 us (0.81)
  Pallas kernels: 104 us -> 80.1 us
  local copies, waits for them, and re-layouts: 19.9 us -> 0.15 us
  other arithmetic: 3.37 us -> 0.2 us
    pallas_call x11 -> x13, Pallas kernels: 89.6 us -> 66.2 us  [the longest x2 27.1 us: final(): pl.pallas_call(functools.partial(final_kernel, place, count, total_cols,...]
    unnamed x20 -> x8, local copies, waits for them, and re-layouts: 19.6 us -> 0.02 us
    add x2 -> x0, other arithmetic: 2.87 us -> none  [on_device(): x = keep + recv]
  transfers between devices with their start and end apart: 28 -> 28, of which waited for: 16 -> 15; matrix products, arithmetic and copies ran while one was open for 2% -> 0% of each run, Pallas kernels for 29% -> 27%
where the time goes in v4:
time: 185 us
  Pallas kernels  80.1 us (43%)
  waiting for transfers between devices  76.5 us (41%)
  starting transfers between devices  27 us (15%)
    ppermute x28, waiting for transfers between devices, swap(): return lax.ppermute(x, axis, [(i, i ^ mask) for i in range(n)])  76.5 us
    pallas_call x2, Pallas kernels, final(): pl.pallas_call(functools.partial(final_kernel, place, count, total_cols,...  27.1 us
    ppermute x28, starting transfers between devices, swap(): return lax.ppermute(x, axis, [(i, i ^ mask) for i in range(n)])  27 us
    pallas_call x2, Pallas kernels, left_half(): pl.pallas_call(functools.partial(left_kernel, which), in_specs=[SMEM, HBM...  19.2 us
    pallas_call x1, Pallas kernels, chol_inverse(): pl.pallas_call(chol_kernel, in_specs=[vm, vm], out_specs=[vm] * 3, out_sh...  12.7 us
    pallas_call x2, Pallas kernels, w_keep(): pl.pallas_call(functools.partial(w_keep_kernel, place), grid_spec=pltpu.P...  8.02 us
    pallas_call x2, Pallas kernels, w_send(): pl.pallas_call(functools.partial(w_send_kernel, place), grid_spec=pltpu.P...  7.87 us
  transfers between devices with their start and end apart: 28, of which 15 were waited for; matrix products, arithmetic and copies ran while one was open for 0% of the time, Pallas kernels for 27%

profile of v4, /device:TPU:0, one launch (start us, length us, event | category | flops | bytes accessed | tf_op | source)
XLA Modules:
  0.0 184.9 jit_solution(400759355256513822)
XLA Ops:
  0.7 0.1 stack.89.at
  0.8 9.6 %left_half.3 = (f32[320,7168]{1,0:T(8,128)S(1)}, f32[320,256]{1,0:T(8,128)S(1)}) custom-call(s32[26]{0:T(128)S(1)} %stack.89.at, f32[640,6912]{1,0:T(8,128)} %g.3, f32[640,6912]{1,0:T(8,128)} %m.3, f32[6912,256]{1,0:T(8,128)} %r.3), custom_call_target="tpu_custom_call" | custom-call | flops 3397386240 | bytes 24772608 | tf_op jit(solution)/shard_map/left_half/pallas_call | solution.py:96
  10.4 3.1 %collective-permute-start = (f32[320,256]{1,0:T(8,128)S(1)}, f32[320,256]{1,0:T(8,128)S(1)}, u32[]{:S(2)}, u32[]{:S(2)}) collective-permute-start(f32[320,256]{1,0:T(8,128)S(1)} %get-tuple-element.31), channel_id=1, source_target_pairs={{0,1},{1,0},{2,3},{3,2},{4,5},{5,4},{6,7},{7,6},{8,9},{9,8},{10,11... | collective-permute-start | bytes 983048 | tf_op jit(solution)/shard_map/ppermute | solution.py:456
  13.5 9.6 %left_half.2 = (f32[320,7168]{1,0:T(8,128)S(1)}, f32[320,256]{1,0:T(8,128)S(1)}) custom-call(s32[26]{0:T(128)S(1)} %stack.89.at, f32[640,6912]{1,0:T(8,128)} %g.3, f32[640,6912]{1,0:T(8,128)} %m.3, f32[6912,256]{1,0:T(8,128)} %r.3), custom_call_target="tpu_custom_call" | custom-call | flops 3397386240 | bytes 24772608 | tf_op jit(solution)/shard_map/left_half/pallas_call | solution.py:96
  23.1 0.0 copy-start
  23.2 2.7 %collective-permute-start.2 = (f32[160,256]{1,0:T(8,128)S(1)}, f32[160,256]{1,0:T(8,128)S(1)}, u32[]{:S(2)}, u32[]{:S(2)}) collective-permute-start(f32[160,256]{1,0:T(8,128)S(1)} %get-tuple-element.55), channel_id=1, source_target_pairs={{0,2},{1,3},{2,0},{3,1},{4,6},{5,7},{6,4},{7,5},{8,10},{9,11},{10,... | collective-permute-start | bytes 491528 | tf_op jit(solution)/shard_map/ppermute | solution.py:456
  25.9 0.3 collective-permute-start.1
  26.2 10.6 %collective-permute-done.2 = f32[160,256]{1,0:T(8,128)S(1)} collective-permute-done((f32[160,256]{1,0:T(8,128)S(1)}, f32[160,256]{1,0:T(8,128)S(1)}, u32[]{:S(2)}, u32[]{:S(2)}) %collective-permute-start.2) | collective-permute-done | bytes 163872 | tf_op jit(solution)/shard_map/ppermute | solution.py:456
  36.8 3.4 %collective-permute-done.1 = f32[160,256]{1,0:T(8,128)S(1)} collective-permute-done((f32[160,256]{1,0:T(8,128)S(1)}, f32[160,256]{1,0:T(8,128)S(1)}, u32[]{:S(2)}, u32[]{:S(2)}) %collective-permute-start.1) | collective-permute-done | bytes 163872 | tf_op jit(solution)/shard_map/ppermute | solution.py:456
  40.2 0.1 collective-permute-start.4
  40.3 2.0 %collective-permute-start.3 = (f32[160,256]{1,0:T(8,128)S(1)}, f32[160,256]{1,0:T(8,128)S(1)}, u32[]{:S(2)}, u32[]{:S(2)}) collective-permute-start(f32[160,256]{1,0:T(8,128)S(1)} %get-tuple-element.54.refs_0_), channel_id=1, source_target_pairs={{0,1},{1,0},{2,3},{3,2},{4,5},{5,4},{6,7},{7,6},{8,9},{9,8},{10,11... | collective-permute-start | bytes 491528 | tf_op jit(solution)/shard_map/ppermute | solution.py:456
  42.3 5.0 %collective-permute-done.4.refs_3_ = f32[160,256]{1,0:T(8,128)S(1)} collective-permute-done((f32[160,256]{1,0:T(8,128)S(1)}, f32[160,256]{1,0:T(8,128)S(1)}, u32[]{:S(2)}, u32[]{:S(2)}) %collective-permute-start.4) | collective-permute-done | bytes 163872 | tf_op jit(solution)/shard_map/ppermute | solution.py:456
  47.4 2.6 %collective-permute-done.3.refs_2_ = f32[160,256]{1,0:T(8,128)S(1)} collective-permute-done((f32[160,256]{1,0:T(8,128)S(1)}, f32[160,256]{1,0:T(8,128)S(1)}, u32[]{:S(2)}, u32[]{:S(2)}) %collective-permute-start.3) | collective-permute-done | bytes 163872 | tf_op jit(solution)/shard_map/ppermute | solution.py:456
  49.9 1.2 gram_of.1
  51.1 3.9 %w_send.2 = f32[1792,256]{1,0:T(8,128)S(1)} custom-call(s32[26]{0:T(128)S(1)} %stack.89.at, f32[320,7168]{1,0:T(8,128)S(1)} %get-tuple-element.28.own.refs_7_, f32[320,7168]{1,0:T(8,128)S(1)} %get-tuple-element.29.other.refs_8_, bf16[640,256]{1,0:T(8,128)(2,1)S(1)} %get-tuple-element.32.lh, bf16[640,256]{1,0:T(8,128)(2,1)S(1)} %get-tuple-element.33.ll), custom_call_target="tpu_custom_call" | custom-call | flops 1761607680 | bytes 1835008 | tf_op jit(solution)/shard_map/w_send/pallas_call | solution.py:179
  55.0 0.1 collective-permute-start.5
  55.1 3.9 %w_send.3 = f32[1792,256]{1,0:T(8,128)S(1)} custom-call(s32[26]{0:T(128)S(1)} %stack.89.at, f32[320,7168]{1,0:T(8,128)S(1)} %get-tuple-element.28.own.refs_7_, f32[320,7168]{1,0:T(8,128)S(1)} %get-tuple-element.29.other.refs_8_, bf16[640,256]{1,0:T(8,128)(2,1)S(1)} %get-tuple-element.32.lh, bf16[640,256]{1,0:T(8,128)(2,1)S(1)} %get-tuple-element.33.ll), custom_call_target="tpu_custom_call" | custom-call | flops 1761607680 | bytes 1835008 | tf_op jit(solution)/shard_map/w_send/pallas_call | solution.py:179
  59.1 0.5 collective-permute-start.8
  59.6 4.0 %w_keep.2 = (f32[896,256]{1,0:T(8,128)S(1)}, f32[896,256]{1,0:T(8,128)S(1)}) custom-call(s32[26]{0:T(128)S(1)} %stack.89.at, f32[320,7168]{1,0:T(8,128)S(1)} %get-tuple-element.28.own.refs_7_, f32[320,7168]{1,0:T(8,128)S(1)} %get-tuple-element.29.other.refs_8_, bf16[640,256]{1,0:T(8,128)(2,1)S(1)} %get-tuple-element.32.lh, ...), custom_call_target="tpu_custom_call" | custom-call | flops 1761607680 | bytes 1835008 | tf_op jit(solution)/shard_map/w_keep/pallas_call | solution.py:197
  63.6 1.6 collective-permute-start.6
  65.2 4.0 %w_keep.3 = (f32[896,256]{1,0:T(8,128)S(1)}, f32[896,256]{1,0:T(8,128)S(1)}) custom-call(s32[26]{0:T(128)S(1)} %stack.89.at, f32[320,7168]{1,0:T(8,128)S(1)} %get-tuple-element.28.own.refs_7_, f32[320,7168]{1,0:T(8,128)S(1)} %get-tuple-element.29.other.refs_8_, bf16[640,256]{1,0:T(8,128)(2,1)S(1)} %get-tuple-element.32.lh, ...), custom_call_target="tpu_custom_call" | custom-call | flops 1761607680 | bytes 1835008 | tf_op jit(solution)/shard_map/w_keep/pallas_call | solution.py:197
  69.2 1.6 collective-permute-start.9
  70.8 0.0 collective-permute-start.11
  70.8 1.5 collective-permute-done.11
  72.4 0.6 collective-permute-start.12
  73.0 18.6 %collective-permute-done.12 = f32[256,256]{1,0:T(8,128)S(1)} collective-permute-done((f32[256,256]{1,0:T(8,128)S(1)}, f32[256,256]{1,0:T(8,128)S(1)}, u32[]{:S(2)}, u32[]{:S(2)}) %collective-permute-start.12) | collective-permute-done | bytes 262176 | tf_op jit(solution)/shard_map/ppermute | solution.py:456
  91.7 1.6 collective-permute-start.13
  93.3 0.0 collective-permute-done.6.y
  93.3 0.6 halve.2
  94.0 0.5 collective-permute-start.7
  94.5 0.0 collective-permute-done.9.y
  94.5 0.6 halve.3
  95.1 1.6 collective-permute-start.10
  96.7 4.2 %collective-permute-done.13 = f32[256,256]{1,0:T(8,128)S(1)} collective-permute-done((f32[256,256]{1,0:T(8,128)S(1)}, f32[256,256]{1,0:T(8,128)S(1)}, u32[]{:S(2)}, u32[]{:S(2)}) %collective-permute-start.13) | collective-permute-done | bytes 262176 | tf_op jit(solution)/shard_map/ppermute | solution.py:456
  101.0 0.0 slice-start.1
  101.0 0.0 slice-start.2
  101.0 12.7 %chol_inverse.1 = (f32[256,256]{1,0:T(8,128)S(1)}, bf16[640,256]{1,0:T(8,128)(2,1)S(1)}, bf16[640,256]{1,0:T(8,128)(2,1)S(1)}) custom-call(f32[256,256]{1,0:T(8,128)S(1)} %add.101.gram, f32[640,256]{1,0:T(8,128)S(1)} %get-tuple-element.43.left), custom_call_target="tpu_custom_call" | custom-call | flops 4000000000 | bytes 655360 | tf_op jit(solution)/shard_map/chol_inverse/pallas_call | solution.py:311
  113.7 0.0 collective-permute-done.7.ga
  113.7 0.0 collective-permute-done.10.gb
  113.7 1.5 right_rows.1
  115.3 1.6 collective-permute-start.17
  116.9 1.5 collective-permute-start.14
  118.4 6.0 %collective-permute-done.17.y = f32[448,256]{1,0:T(8,128)S(1)} collective-permute-done((f32[448,256]{1,0:T(8,128)S(1)}, f32[448,256]{1,0:T(8,128)S(1)}, u32[]{:S(2)}, u32[]{:S(2)}) %collective-permute-start.17) | collective-permute-done | bytes 458784 | tf_op jit(solution)/shard_map/ppermute | solution.py:456
  124.4 0.6 join.3.refs_2_
  125.0 1.6 collective-permute-start.18
  126.7 1.2 collective-permute-done.14.y
  127.8 0.6 join.2.refs_0_
  128.5 0.4 collective-permute-start.15
  128.8 0.5 collective-permute-start.26
  129.4 0.3 collective-permute-start.20
  129.6 3.4 %collective-permute-done.20 = f32[8,256]{1,0:T(8,128)S(1)} collective-permute-done((f32[8,256]{1,0:T(8,128)S(1)}, f32[8,256]{1,0:T(8,128)S(1)}, u32[]{:S(2)}, u32[]{:S(2)}) %collective-permute-start.20) | collective-permute-done | bytes 8224 | tf_op jit(solution)/shard_map/ppermute | solution.py:456
  133.0 0.4 collective-permute-start.21
  133.4 4.2 %collective-permute-done.21 = f32[8,256]{1,0:T(8,128)S(1)} collective-permute-done((f32[8,256]{1,0:T(8,128)S(1)}, f32[8,256]{1,0:T(8,128)S(1)}, u32[]{:S(2)}, u32[]{:S(2)}) %collective-permute-start.21) | collective-permute-done | bytes 8224 | tf_op jit(solution)/shard_map/ppermute | solution.py:456
  137.6 0.0 collective-permute-start.22
  137.6 7.8 %collective-permute-done.18.refs_2_ = f32[896,256]{1,0:T(8,128)S(1)} collective-permute-done((f32[896,256]{1,0:T(8,128)S(1)}, f32[896,256]{1,0:T(8,128)S(1)}, u32[]{:S(2)}, u32[]{:S(2)}) %collective-permute-start.18) | collective-permute-done | bytes 917536 | tf_op jit(solution)/shard_map/ppermute | solution.py:456
  145.3 0.5 collective-permute-start.16
  145.9 1.5 collective-permute-start.25
  147.4 3.1 %collective-permute-done.25 = f32[8,256]{1,0:T(8,128)S(1)} collective-permute-done((f32[8,256]{1,0:T(8,128)S(1)}, f32[8,256]{1,0:T(8,128)S(1)}, u32[]{:S(2)}, u32[]{:S(2)}) %collective-permute-start.25) | collective-permute-done | bytes 8224 | tf_op jit(solution)/shard_map/ppermute | solution.py:456
  150.4 1.5 collective-permute-start.24
  151.9 2.1 %collective-permute-done.24 = f32[8,256]{1,0:T(8,128)S(1)} collective-permute-done((f32[8,256]{1,0:T(8,128)S(1)}, f32[8,256]{1,0:T(8,128)S(1)}, u32[]{:S(2)}, u32[]{:S(2)}) %collective-permute-start.24) | collective-permute-done | bytes 8224 | tf_op jit(solution)/shard_map/ppermute | solution.py:456
  154.1 0.8 collective-permute-start.23
  154.9 2.8 %collective-permute-done.23 = f32[8,256]{1,0:T(8,128)S(1)} collective-permute-done((f32[8,256]{1,0:T(8,128)S(1)}, f32[8,256]{1,0:T(8,128)S(1)}, u32[]{:S(2)}, u32[]{:S(2)}) %collective-permute-start.23) | collective-permute-done | bytes 8224 | tf_op jit(solution)/shard_map/ppermute | solution.py:456
  157.8 13.8 %final.2 = (f32[640,6912]{1,0:T(8,128)}, f32[640,6912]{1,0:T(8,128)}, f32[6912,256]{1,0:T(8,128)}) custom-call(s32[26]{0:T(128)S(1)} %stack.89.at, f32[896,256]{1,0:T(8,128)S(1)} %join.2.refs_0_, f32[896,256]{1,0:T(8,128)S(1)} %collective-permute-done.26.refs_1_, f32[896,256]{1,0:T(8,128)S(1)} %join.3.refs_2_, ...), custom_call_target="tpu_custom_call" | custom-call | flops 7046430720 | bytes 25690112 | tf_op jit(solution)/shard_map/final/pallas_call | solution.py:424
  171.6 13.3 %final.3 = (f32[640,6912]{1,0:T(8,128)}, f32[640,6912]{1,0:T(8,128)}, f32[6912,256]{1,0:T(8,128)}) custom-call(s32[26]{0:T(128)S(1)} %stack.89.at, f32[896,256]{1,0:T(8,128)S(1)} %collective-permute-done.15.refs_0_, f32[896,256]{1,0:T(8,128)S(1)} %collective-permute-done.16.refs_1_, ...), custom_call_target="tpu_custom_call", output_to_operand_aliasing={{0}: (10, {}), {1}: (11, {}), {2}: (12, {})} | custom-call | flops 7046430720 | bytes 25690112 | tf_op jit(solution)/shard_map/final/pallas_call | solution.py:424
  (27 shorter events, 0.3 us)
Async XLA Ops:
  10.4 12.7 %collective-permute-start = (f32[320,256]{1,0:T(8,128)S(1)}, f32[320,256]{1,0:T(8,128)S(1)}, u32[]{:S(2)}, u32[]{:S(2)}) collective-permute-start(f32[320,256]{1,0:T(8,128)S(1)} %get-tuple-element.31), channel_id=1, source_target_pairs={{0,1},{1,0},{2,3},{3,2},{4,5},{5,4},{6,7},{7,6},{8,9},{9,8},{10,11... | collective-permute-start | bytes 983048 | tf_op jit(solution)/shard_map/ppermute | solution.py:456
  23.1 42.1 %copy-start = (f32[320,7168]{1,0:T(8,128)}, f32[320,7168]{1,0:T(8,128)S(1)}, u32[]{:S(2)}) copy-start(f32[320,7168]{1,0:T(8,128)S(1)} %get-tuple-element.28.own.refs_7_) | copy-start | bytes 27525124
  23.2 13.6 %collective-permute-start.2 = (f32[160,256]{1,0:T(8,128)S(1)}, f32[160,256]{1,0:T(8,128)S(1)}, u32[]{:S(2)}, u32[]{:S(2)}) collective-permute-start(f32[160,256]{1,0:T(8,128)S(1)} %get-tuple-element.55), channel_id=1, source_target_pairs={{0,2},{1,3},{2,0},{3,1},{4,6},{5,7},{6,4},{7,5},{8,10},{9,11},{10,... | collective-permute-start | bytes 491528 | tf_op jit(solution)/shard_map/ppermute | solution.py:456
  25.9 14.3 %collective-permute-start.1 = (f32[160,256]{1,0:T(8,128)S(1)}, f32[160,256]{1,0:T(8,128)S(1)}, u32[]{:S(2)}, u32[]{:S(2)}) collective-permute-start(f32[160,256]{1,0:T(8,128)S(1)} %get-tuple-element.56), channel_id=1, source_target_pairs={{0,2},{1,3},{2,0},{3,1},{4,6},{5,7},{6,4},{7,5},{8,10},{9,11},{10,... | collective-permute-start | bytes 491528 | tf_op jit(solution)/shard_map/ppermute | solution.py:456
  40.2 7.1 %collective-permute-start.4 = (f32[160,256]{1,0:T(8,128)S(1)}, f32[160,256]{1,0:T(8,128)S(1)}, u32[]{:S(2)}, u32[]{:S(2)}) collective-permute-start(f32[160,256]{1,0:T(8,128)S(1)} %get-tuple-element.53.refs_1_), channel_id=1, source_target_pairs={{0,1},{1,0},{2,3},{3,2},{4,5},{5,4},{6,7},{7,6},{8,9},{9,8},{10,11... | collective-permute-start | bytes 491528 | tf_op jit(solution)/shard_map/ppermute | solution.py:456
  40.3 9.6 %collective-permute-start.3 = (f32[160,256]{1,0:T(8,128)S(1)}, f32[160,256]{1,0:T(8,128)S(1)}, u32[]{:S(2)}, u32[]{:S(2)}) collective-permute-start(f32[160,256]{1,0:T(8,128)S(1)} %get-tuple-element.54.refs_0_), channel_id=1, source_target_pairs={{0,1},{1,0},{2,3},{3,2},{4,5},{5,4},{6,7},{7,6},{8,9},{9,8},{10,11... | collective-permute-start | bytes 491528 | tf_op jit(solution)/shard_map/ppermute | solution.py:456
  55.0 4.5 %collective-permute-start.5 = (f32[1792,256]{1,0:T(8,128)S(1)}, f32[1792,256]{1,0:T(8,128)S(1)}, u32[]{:S(2)}, u32[]{:S(2)}) collective-permute-start(f32[1792,256]{1,0:T(8,128)S(1)} %w_send.2), channel_id=1, source_target_pairs={{0,4},{4,0},{8,12},{12,8},{16,20},{20,16},{24,28},{28,24},{1,5},{5... | collective-permute-start | bytes 5505032 | tf_op jit(solution)/shard_map/ppermute | solution.py:456
  59.1 6.1 %collective-permute-start.8 = (f32[1792,256]{1,0:T(8,128)S(1)}, f32[1792,256]{1,0:T(8,128)S(1)}, u32[]{:S(2)}, u32[]{:S(2)}) collective-permute-start(f32[1792,256]{1,0:T(8,128)S(1)} %w_send.3), channel_id=1, source_target_pairs={{0,4},{4,0},{8,12},{12,8},{16,20},{20,16},{24,28},{28,24},{1,5},{5... | collective-permute-start | bytes 5505032 | tf_op jit(solution)/shard_map/ppermute | solution.py:456
  63.6 29.7 %collective-permute-start.6 = (f32[896,256]{1,0:T(8,128)S(1)}, f32[896,256]{1,0:T(8,128)S(1)}, u32[]{:S(2)}, u32[]{:S(2)}) collective-permute-start(f32[896,256]{1,0:T(8,128)S(1)} %get-tuple-element.35), channel_id=1, source_target_pairs={{0,8},{4,12},{8,0},{12,4},{16,24},{20,28},{24,16},{28,20},{1,9},{5... | collective-permute-start | bytes 2752520 | tf_op jit(solution)/shard_map/ppermute | solution.py:456
  69.2 25.3 %collective-permute-start.9 = (f32[896,256]{1,0:T(8,128)S(1)}, f32[896,256]{1,0:T(8,128)S(1)}, u32[]{:S(2)}, u32[]{:S(2)}) collective-permute-start(f32[896,256]{1,0:T(8,128)S(1)} %get-tuple-element.39), channel_id=1, source_target_pairs={{0,16},{4,20},{8,24},{12,28},{16,0},{20,4},{24,8},{28,12},{1,17},{... | collective-permute-start | bytes 2752520 | tf_op jit(solution)/shard_map/ppermute | solution.py:456
  70.8 1.5 collective-permute-start.11
  72.4 19.3 %collective-permute-start.12 = (f32[256,256]{1,0:T(8,128)S(1)}, f32[256,256]{1,0:T(8,128)S(1)}, u32[]{:S(2)}, u32[]{:S(2)}) collective-permute-start(f32[256,256]{1,0:T(8,128)S(1)} %add.99), channel_id=1, source_target_pairs={{0,8},{4,12},{8,0},{12,4},{16,24},{20,28},{24,16},{28,20},{1,9},{5... | collective-permute-start | bytes 786440 | tf_op jit(solution)/shard_map/ppermute | solution.py:456
  91.7 9.2 %collective-permute-start.13 = (f32[256,256]{1,0:T(8,128)S(1)}, f32[256,256]{1,0:T(8,128)S(1)}, u32[]{:S(2)}, u32[]{:S(2)}) collective-permute-start(f32[256,256]{1,0:T(8,128)S(1)} %add.100), channel_id=1, source_target_pairs={{0,16},{4,20},{8,24},{12,28},{16,0},{20,4},{24,8},{28,12},{1,17},{... | collective-permute-start | bytes 786440 | tf_op jit(solution)/shard_map/ppermute | solution.py:456
  94.0 19.7 %collective-permute-start.7 = (f32[448,256]{1,0:T(8,128)S(1)}, f32[448,256]{1,0:T(8,128)S(1)}, u32[]{:S(2)}, u32[]{:S(2)}) collective-permute-start(f32[448,256]{1,0:T(8,128)S(1)} %get-tuple-element.37), channel_id=1, source_target_pairs={{0,16},{4,20},{8,24},{12,28},{16,0},{20,4},{24,8},{28,12},{1,17},{... | collective-permute-start | bytes 1376264 | tf_op jit(solution)/shard_map/ppermute | solution.py:456
  95.1 18.6 %collective-permute-start.10 = (f32[448,256]{1,0:T(8,128)S(1)}, f32[448,256]{1,0:T(8,128)S(1)}, u32[]{:S(2)}, u32[]{:S(2)}) collective-permute-start(f32[448,256]{1,0:T(8,128)S(1)} %get-tuple-element.41), channel_id=1, source_target_pairs={{0,8},{4,12},{8,0},{12,4},{16,24},{20,28},{24,16},{28,20},{1,9},{5... | collective-permute-start | bytes 1376264 | tf_op jit(solution)/shard_map/ppermute | solution.py:456
  100.9 56.8 %slice-start = ((s8[9175040]{0:T(1024)(128)(4,1)}), s8[4194304]{0:T(1024)(128)(4,1)S(1)}, s32[]{:S(2)}) async-start(s8[9175040]{0:T(1024)(128)(4,1)} %bitcast.20), calls=%async_computation | async-start | bytes 8388608
  101.0 56.8 %slice-start.1 = ((s8[9175040]{0:T(1024)(128)(4,1)}), s8[4194304]{0:T(1024)(128)(4,1)S(1)}, s32[]{:S(2)}) async-start(s8[9175040]{0:T(1024)(128)(4,1)} %bitcast.20), calls=%async_computation.1 | async-start | bytes 8388608
  101.0 56.8 %slice-start.2 = ((s8[9175040]{0:T(1024)(128)(4,1)}), s8[786432]{0:T(1024)(128)(4,1)S(1)}, s32[]{:S(2)}) async-start(s8[9175040]{0:T(1024)(128)(4,1)} %bitcast.20), calls=%async_computation.2 | async-start | bytes 1572864
  115.3 9.2 %collective-permute-start.17 = (f32[448,256]{1,0:T(8,128)S(1)}, f32[448,256]{1,0:T(8,128)S(1)}, u32[]{:S(2)}, u32[]{:S(2)}) collective-permute-start(f32[448,256]{1,0:T(8,128)S(1)} %get-tuple-element.46.x), channel_id=1, source_target_pairs={{0,8},{4,12},{8,0},{12,4},{16,24},{20,28},{24,16},{28,20},{1,9},{5... | collective-permute-start | bytes 1376264 | tf_op jit(solution)/shard_map/ppermute | solution.py:456
  116.9 11.0 %collective-permute-start.14 = (f32[448,256]{1,0:T(8,128)S(1)}, f32[448,256]{1,0:T(8,128)S(1)}, u32[]{:S(2)}, u32[]{:S(2)}) collective-permute-start(f32[448,256]{1,0:T(8,128)S(1)} %get-tuple-element.45.x), channel_id=1, source_target_pairs={{0,16},{4,20},{8,24},{12,28},{16,0},{20,4},{24,8},{28,12},{1,17},{... | collective-permute-start | bytes 1376264 | tf_op jit(solution)/shard_map/ppermute | solution.py:456
  125.0 20.3 %collective-permute-start.18 = (f32[896,256]{1,0:T(8,128)S(1)}, f32[896,256]{1,0:T(8,128)S(1)}, u32[]{:S(2)}, u32[]{:S(2)}) collective-permute-start(f32[896,256]{1,0:T(8,128)S(1)} %join.3.refs_2_), channel_id=1, source_target_pairs={{0,16},{4,20},{8,24},{12,28},{16,0},{20,4},{24,8},{28,12},{1,17},{... | collective-permute-start | bytes 2752520 | tf_op jit(solution)/shard_map/ppermute | solution.py:456
  128.5 16.9 %collective-permute-start.15 = (f32[896,256]{1,0:T(8,128)S(1)}, f32[896,256]{1,0:T(8,128)S(1)}, u32[]{:S(2)}, u32[]{:S(2)}) collective-permute-start(f32[896,256]{1,0:T(8,128)S(1)} %join.2.refs_0_), channel_id=1, source_target_pairs={{0,8},{4,12},{8,0},{12,4},{16,24},{20,28},{24,16},{28,20},{1,9},{5... | collective-permute-start | bytes 2752520 | tf_op jit(solution)/shard_map/ppermute | solution.py:456
  128.8 28.9 %collective-permute-start.27 = (f32[896,256]{1,0:T(8,128)S(1)}, f32[896,256]{1,0:T(8,128)S(1)}, u32[]{:S(2)}, u32[]{:S(2)}) collective-permute-start(f32[896,256]{1,0:T(8,128)S(1)} %join.3.refs_2_), channel_id=1, source_target_pairs={{0,4},{4,0},{8,12},{12,8},{16,20},{20,16},{24,28},{28,24},{1,5},{5... | collective-permute-start | bytes 2752520 | tf_op jit(solution)/shard_map/ppermute | solution.py:456
  128.8 28.9 %collective-permute-start.26 = (f32[896,256]{1,0:T(8,128)S(1)}, f32[896,256]{1,0:T(8,128)S(1)}, u32[]{:S(2)}, u32[]{:S(2)}) collective-permute-start(f32[896,256]{1,0:T(8,128)S(1)} %join.2.refs_0_), channel_id=1, source_target_pairs={{0,4},{4,0},{8,12},{12,8},{16,20},{20,16},{24,28},{28,24},{1,5},{5... | collective-permute-start | bytes 2752520 | tf_op jit(solution)/shard_map/ppermute | solution.py:456
  129.4 3.7 %collective-permute-start.20 = (f32[8,256]{1,0:T(8,128)S(1)}, f32[8,256]{1,0:T(8,128)S(1)}, u32[]{:S(2)}, u32[]{:S(2)}) collective-permute-start(f32[8,256]{1,0:T(8,128)S(1)} %get-tuple-element.47), channel_id=1, source_target_pairs={{0,1},{1,0},{2,3},{3,2},{4,5},{5,4},{6,7},{7,6},{8,9},{9,8},{10,11... | collective-permute-start | bytes 24584 | tf_op jit(solution)/shard_map/ppermute | solution.py:456
  133.0 4.5 %collective-permute-start.21 = (f32[8,256]{1,0:T(8,128)S(1)}, f32[8,256]{1,0:T(8,128)S(1)}, u32[]{:S(2)}, u32[]{:S(2)}) collective-permute-start(f32[8,256]{1,0:T(8,128)S(1)} %add.102), channel_id=1, source_target_pairs={{0,2},{1,3},{2,0},{3,1},{4,6},{5,7},{6,4},{7,5},{8,10},{9,11},{10,... | collective-permute-start | bytes 24584 | tf_op jit(solution)/shard_map/ppermute | solution.py:456
  137.6 8.3 %collective-permute-start.22 = (f32[8,256]{1,0:T(8,128)S(1)}, f32[8,256]{1,0:T(8,128)S(1)}, u32[]{:S(2)}, u32[]{:S(2)}) collective-permute-start(f32[8,256]{1,0:T(8,128)S(1)} %add.103), channel_id=1, source_target_pairs={{0,4},{4,0},{8,12},{12,8},{16,20},{20,16},{24,28},{28,24},{1,5},{5... | collective-permute-start | bytes 24584 | tf_op jit(solution)/shard_map/ppermute | solution.py:456
  145.3 26.3 %collective-permute-start.19 = (f32[896,256]{1,0:T(8,128)S(1)}, f32[896,256]{1,0:T(8,128)S(1)}, u32[]{:S(2)}, u32[]{:S(2)}) collective-permute-start(f32[896,256]{1,0:T(8,128)S(1)} %collective-permute-done.18.refs_2_), channel_id=1, source_target_pairs={{0,4},{4,0},{8,12},{12,8},{16,20},{20,16},{24,28},{28,24},{1,5},{5... | collective-permute-start | bytes 2752520 | tf_op jit(solution)/shard_map/ppermute | solution.py:456
  145.3 26.3 %collective-permute-start.16 = (f32[896,256]{1,0:T(8,128)S(1)}, f32[896,256]{1,0:T(8,128)S(1)}, u32[]{:S(2)}, u32[]{:S(2)}) collective-permute-start(f32[896,256]{1,0:T(8,128)S(1)} %collective-permute-done.15.refs_0_), channel_id=1, source_target_pairs={{0,4},{4,0},{8,12},{12,8},{16,20},{20,16},{24,28},{28,24},{1,5},{5... | collective-permute-start | bytes 2752520 | tf_op jit(solution)/shard_map/ppermute | solution.py:456
  145.9 4.6 %collective-permute-start.25 = (f32[8,256]{1,0:T(8,128)S(1)}, f32[8,256]{1,0:T(8,128)S(1)}, u32[]{:S(2)}, u32[]{:S(2)}) collective-permute-start(f32[8,256]{1,0:T(8,128)S(1)} %add.104), channel_id=1, source_target_pairs={{0,24},{4,28},{8,16},{12,20},{16,8},{20,12},{24,0},{28,4},{1,25},{... | collective-permute-start | bytes 24584 | tf_op jit(solution)/shard_map/ppermute | solution.py:456
  150.4 3.7 %collective-permute-start.24 = (f32[8,256]{1,0:T(8,128)S(1)}, f32[8,256]{1,0:T(8,128)S(1)}, u32[]{:S(2)}, u32[]{:S(2)}) collective-permute-start(f32[8,256]{1,0:T(8,128)S(1)} %add.104), channel_id=1, source_target_pairs={{0,16},{4,20},{8,24},{12,28},{16,0},{20,4},{24,8},{28,12},{1,17},{... | collective-permute-start | bytes 24584 | tf_op jit(solution)/shard_map/ppermute | solution.py:456
  154.1 3.7 %collective-permute-start.23 = (f32[8,256]{1,0:T(8,128)S(1)}, f32[8,256]{1,0:T(8,128)S(1)}, u32[]{:S(2)}, u32[]{:S(2)}) collective-permute-start(f32[8,256]{1,0:T(8,128)S(1)} %add.104), channel_id=1, source_target_pairs={{0,8},{4,12},{8,0},{12,4},{16,24},{20,28},{24,16},{28,20},{1,9},{5... | collective-permute-start | bytes 24584 | tf_op jit(solution)/shard_map/ppermute | solution.py:456

commit v5 on v4

--- a/solution.py
+++ b/solution.py
@@ -110,47 +110,71 @@
     )(at, gradient, momentum, right_factor)
 
 
-def gram_kernel(*refs):
-    pieces, (left, lh, ll, gram) = refs[:-4], refs[-4:]
+def total_kernel(count, *refs):
+    ins, outs = refs[:count], refs[count:]
+    n = outs[0].shape[0]
+    for i, out in enumerate(outs):
+        terms = [x[i * n : (i + 1) * n, :] for x in ins]
+        while len(terms) > 1:
+            terms = [terms[k] + terms[k + 1] for k in range(0, len(terms), 2)]
+        out[...] = terms[0]
+
+
+def total(*blocks, parts=1):
+    rows, rank = blocks[0].shape
+    outs = pl.pallas_call(
+        functools.partial(total_kernel, len(blocks)),
+        in_specs=[VMEM] * len(blocks),
+        out_specs=[VMEM] * parts,
+        out_shape=[jax.ShapeDtypeStruct((rows // parts, rank), F32)] * parts,
+        compiler_params=params(6),
+        cost_estimate=cost(rows * rank, 4 * (len(blocks) + 1) * rows * rank),
+        name="total",
+    )(*blocks)
+    return outs[0] if parts == 1 else outs
+
+
+def gram_kernel(place, at, *refs):
+    pieces, (left, lh, ll, send, keep, gram) = refs[:-6], refs[-6:]
     n = pieces[0].shape[0]
     for i, piece in enumerate(pieces):
         x = piece[...]
-        at = pl.ds(i * n, n)
-        left[at, :] = x
-        h, l = split(x)
-        lh[at, :] = h
-        ll[at, :] = l
+        rows = pl.ds(i * n, n)
+        left[rows, :] = x
+        lh[rows, :], ll[rows, :] = split(x)
     half = left.shape[0] // 2
     own, other = left[:half, :], left[half:, :]
     gram[...] = dot_high(own, own, TN) + dot_high(other, other, TN)
-
-
-def gram_of(pieces):
+    n, core = send.shape[0], at[place]
+    send[...] = gram[pl.ds(pl.multiple_of((1 - core) * n, GROUP), n), :]
+    keep[...] = gram[pl.ds(pl.multiple_of(core * n, GROUP), n), :]
+
+
+def gram_of(at, place, pieces):
     rank = pieces[0].shape[1]
     rows = sum(p.shape[0] for p in pieces)
     return pl.pallas_call(
-        gram_kernel,
+        functools.partial(gram_kernel, place),
+        in_specs=[SMEM] + [VMEM] * len(pieces),
+        out_specs=[VMEM] * 5,
         out_shape=[
             jax.ShapeDtypeStruct((rows, rank), F32),
             jax.ShapeDtypeStruct((rows, rank), BF16),
             jax.ShapeDtypeStruct((rows, rank), BF16),
-            jax.ShapeDtypeStruct((rank, rank), F32),
+            jax.ShapeDtypeStruct((rank // 2, rank), F32),
+            jax.ShapeDtypeStruct((rank // 2, rank), F32),
         ],
+        scratch_shapes=[pltpu.VMEM((rank, rank), F32)],
         compiler_params=params(8),
         cost_estimate=cost(12 * rows * rank * rank, 12 * rows * rank),
         name="gram_of",
-    )(*pieces)
+    )(at, *pieces)
 
 
 def w_term(unit, width, own, other, lh, ll):
-    half = own.shape[0]
     part = pl.ds(pl.multiple_of(unit * width, LANES), width)
-    total = None
-    for ref, at in ((own, 0), (other, half)):
-        bh, bl = split(ref[:, part])
-        term = dot3(bh, bl, lh[at : at + half, :], ll[at : at + half, :], TN)
-        total = term if total is None else total + term
-    return total
+    bh, bl = split(jnp.concatenate([own[:, part], other[:, part]], axis=0))
+    return dot3(bh, bl, lh[...], ll[...], TN)
 
 
 def w_send_kernel(place, at, own, other, lh, ll, out):
@@ -185,7 +209,7 @@
             out_specs=pl.BlockSpec((unit, rank), lambda i, at: (i, 0)),
         ),
         out_shape=jax.ShapeDtypeStruct((2 * unit, rank), F32),
-        compiler_params=params(8),
+        compiler_params=params(12),
         cost_estimate=w_cost(rows, rank, unit),
         name="w_send",
     )(at, own, other, lh, ll)
@@ -203,7 +227,7 @@
             out_specs=[one, one],
         ),
         out_shape=[jax.ShapeDtypeStruct((unit, rank), F32)] * 2,
-        compiler_params=params(10),
+        compiler_params=params(14),
         cost_estimate=w_cost(rows, rank, unit),
         name="w_keep",
     )(at, own, other, lh, ll, got)
@@ -277,20 +301,22 @@
     return jnp.concatenate(groups, axis=0)
 
 
-def chol_kernel(gram, left, x_out, oh, ol, work):
-    rank = gram.shape[0]
+def chol_kernel(place, at, mine, beside, left, x_out, oh, ol, work):
+    n, rank = mine.shape
     size = min(64, rank)
-    work[:, :rank] = gram[...]
+    core = at[place]
+    work[pl.ds(pl.multiple_of(core * n, GROUP), n), :rank] = mine[...]
+    work[pl.ds(pl.multiple_of((1 - core) * n, GROUP), n), :rank] = beside[...]
     r = lax.broadcasted_iota(jnp.int32, (rank, rank), 0)
     c = lax.broadcasted_iota(jnp.int32, (rank, rank), 1)
     work[:, rank:] = jnp.where(r == c, 1.0, 0.0).astype(F32)
 
     def step(b, _):
-        at = pl.multiple_of(b * size, size)
-        rows = pl.ds(at, size)
+        top = pl.multiple_of(b * size, size)
+        rows = pl.ds(top, size)
         width = 2 * rank
-        block = pltpu.roll(work[rows, :], lax.rem(width - at, width), 1)
-        block = pltpu.roll(eliminate(block), at, 1)
+        block = pltpu.roll(work[rows, :], lax.rem(width - top, width), 1)
+        block = pltpu.roll(eliminate(block), top, 1)
         x_out[rows, :] = block[:, rank:]
 
         @pl.when(b + 1 < rank // size)
@@ -305,13 +331,12 @@
     ol[...] = l
 
 
-def chol_inverse(gram, left):
+def chol_inverse(at, place, mine, beside, left):
     rows, rank = left.shape
-    vm = pl.BlockSpec(memory_space=pltpu.VMEM)
-    return pl.pallas_call(
-        chol_kernel,
-        in_specs=[vm, vm],
-        out_specs=[vm] * 3,
+    return pl.pallas_call(
+        functools.partial(chol_kernel, place),
+        in_specs=[SMEM] + [VMEM] * 3,
+        out_specs=[VMEM] * 3,
         out_shape=[
             jax.ShapeDtypeStruct((rank, rank), F32),
             jax.ShapeDtypeStruct((rows, rank), BF16),
@@ -321,7 +346,7 @@
         compiler_params=params(8),
         cost_estimate=cost(4e9, 4 * rows * rank),
         name="chol_inverse",
-    )(gram, left)
+    )(at, mine, beside, left)
 
 
 def right_kernel(place, cols, at, ka, ga, kb, gb, x, ra, rb, squares):
@@ -456,14 +481,12 @@
     return lax.ppermute(x, axis, [(i, i ^ mask) for i in range(n)])
 
 
-def sum_over(x, axis):
-    n = lax.axis_size(axis)
-    if not power_of_two(n):
-        return lax.psum(x, axis)
-    for bit in bits_of(n):
-        y = swap(x, axis, bit)
-        x = x + y
-    return x
+def spread_sum(x, bits):
+    for b in bits[3:]:
+        x = total(x, swap(x, "dp", b))
+    b, c = bits[1:3]
+    others = [swap(x, "dp", *m) for m in ((b,), (c,), (b, c))]
+    return total(x, *others)
 
 
 def on_device(gradient, momentum, right_factor):
@@ -483,6 +506,7 @@
     bit_of = lambda b: (d >> b) & 1
     s, core = z & 1, d & 1
     put(s, 1 - s)
+    core_at = put(core)
     send_at, keep_at, bit_at, near, far, first = [], [], [], [], [], []
     for h, order in enumerate(orders):
         t = bit_of(order[0])
@@ -505,18 +529,23 @@
     if power_of_two(n_tp) and n_tp > 1:
         got = swap(away, "tensor", 0)
         buffer_own, mine = left_half(at, 0, *inputs)
-        mine = mine + got
-        own = [mine[: rows // 4], mine[rows // 4 :]]
+        own = list(total(mine, got, parts=2))
         for bit in bits_of(n_tp)[1:]:
-            own = [x + swap(x, "tensor", bit) for x in own]
-        pieces = own + [swap(x, "tensor", 0) for x in own]
+            for i in range(2):
+                got = swap(own[i], "tensor", bit)
+                own[i] = total(own[i], got)
+        pieces = own[:]
+        for i in range(2):
+            pieces.append(swap(own[i], "tensor", 0))
     else:
         buffer_own, mine = left_half(at, 0, *inputs)
         both = lax.psum(jnp.where(s == 0, jnp.stack([mine, away]), jnp.stack([away, mine])), "tensor")
         pieces = [lax.dynamic_index_in_dim(both, i, 0, False) for i in (s, 1 - s)]
 
-    left, lh, ll, gram = gram_of(pieces)
-    gram = sum_over(gram, "dp")
+    left, lh, ll, send, gram = gram_of(at, core_at, pieces)
+    got = swap(send, "dp", 0)
+    gram = spread_sum(total(gram, got), bits)
+    gram_beside = swap(gram, "dp", 0)
 
     held = (buffer_own, buffer_other)
     got = []
@@ -532,19 +561,22 @@
             recv = swap(send, "dp", b)
         kept += [keep, recv]
 
-    x_inv, oh, ol = chol_inverse(gram, left)
+    x_inv, oh, ol = chol_inverse(at, core_at, gram, gram_beside, left)
     *right, squares = right_rows(at, first_at, cols, *kept, x_inv)
-    squares = sum_over(squares, "tensor")
-    for b in bits[:1] + bits[3:]:
-        squares = squares + swap(squares, "dp", b)
-    b, c = bits[1:3]
-    others = [swap(squares, "dp", *m) for m in ((b,), (c,), (b, c))]
-    squares = (squares + others[0]) + (others[1] + others[2])
+    if power_of_two(n_tp):
+        for b in bits_of(n_tp):
+            squares = total(squares, swap(squares, "tensor", b))
+    else:
+        squares = lax.psum(squares, "tensor")
+    got = swap(squares, "dp", 0)
+    squares = total(squares, got)
+    squares = spread_sum(squares, bits)
 
     near, far = [], []
     for h, (order, x) in enumerate(zip(orders, right)):
         for b in order[:0:-1]:
-            x = join(at, bit_at[h][b], x, swap(x, "dp", b))
+            y = swap(x, "dp", b)
+            x = join(at, bit_at[h][b], x, y)
         y = swap(x, "dp", order[0])
         near += [x, swap(x, "dp", 0)]
         far += [y, swap(y, "dp", 0)]

time: 185 us -> 194 us (1.049)
  waiting for transfers between devices: 76.5 us -> 86.8 us
    ppermute x28 -> x30, waiting for transfers between devices: 76.5 us -> 86.8 us  [swap(): return lax.ppermute(x, axis, [(i, i ^ mask) for i in range(n)])]
    pallas_call x2 -> x11, Pallas kernels: 13.9 us -> 15.1 us  [the longest x1 13.3 us: chol_inverse(): pl.pallas_call(functools.partial(chol_kernel, place), in_specs=[SMEM] + [...]
    ppermute x28 -> x30, starting transfers between devices: 27 us -> 27.9 us  [swap(): return lax.ppermute(x, axis, [(i, i ^ mask) for i in range(n)])]
  transfers between devices with their start and end apart: 28 -> 30, of which waited for: 15 -> 16; matrix products, arithmetic and copies ran while one was open for 0% -> 0% of each run, Pallas kernels for 27% -> 25%
where the time goes in v5:
time: 194 us
  waiting for transfers between devices  86.8 us (45%)
  Pallas kernels  78.4 us (40%)
  starting transfers between devices  27.9 us (14%)
    ppermute x30, waiting for transfers between devices, swap(): return lax.ppermute(x, axis, [(i, i ^ mask) for i in range(n)])  86.8 us
    ppermute x30, starting transfers between devices, swap(): return lax.ppermute(x, axis, [(i, i ^ mask) for i in range(n)])  27.9 us
    pallas_call x2, Pallas kernels, final(): pl.pallas_call(functools.partial(final_kernel, place, count, total_cols,...  27.1 us
    pallas_call x2, Pallas kernels, left_half(): pl.pallas_call(functools.partial(left_kernel, which), in_specs=[SMEM, HBM...  19.2 us
    pallas_call x1, Pallas kernels, chol_inverse(): pl.pallas_call(functools.partial(chol_kernel, place), in_specs=[SMEM] + [...  13.3 us
    pallas_call x2, Pallas kernels, w_keep(): pl.pallas_call(functools.partial(w_keep_kernel, place), grid_spec=pltpu.P...  6.57 us
    pallas_call x2, Pallas kernels, w_send(): pl.pallas_call(functools.partial(w_send_kernel, place), grid_spec=pltpu.P...  6.36 us
  transfers between devices with their start and end apart: 30, of which 16 were waited for; matrix products, arithmetic and copies ran while one was open for 0% of the time, Pallas kernels for 25%

profile of v5, /device:TPU:0, one launch (start us, length us, event | category | flops | bytes accessed | tf_op | source)
XLA Modules:
  0.0 194.2 jit_solution(3105317811578984885)
XLA Ops:
  0.7 0.1 stack.93.at
  0.8 9.6 %left_half.3 = (f32[320,7168]{1,0:T(8,128)S(1)}, f32[320,256]{1,0:T(8,128)S(1)}) custom-call(s32[27]{0:T(128)S(1)} %stack.93.at, f32[640,6912]{1,0:T(8,128)} %g.3, f32[640,6912]{1,0:T(8,128)} %m.3, f32[6912,256]{1,0:T(8,128)} %r.3), custom_call_target="tpu_custom_call" | custom-call | flops 3397386240 | bytes 24772608 | tf_op jit(solution)/shard_map/left_half/pallas_call | solution.py:96
  10.4 3.1 %collective-permute-start = (f32[320,256]{1,0:T(8,128)S(1)}, f32[320,256]{1,0:T(8,128)S(1)}, u32[]{:S(2)}, u32[]{:S(2)}) collective-permute-start(f32[320,256]{1,0:T(8,128)S(1)} %get-tuple-element.34), channel_id=1, source_target_pairs={{0,1},{1,0},{2,3},{3,2},{4,5},{5,4},{6,7},{7,6},{8,9},{9,8},{10,11... | collective-permute-start | bytes 983048 | tf_op jit(solution)/shard_map/ppermute | solution.py:481
  13.5 9.6 %left_half.2 = (f32[320,7168]{1,0:T(8,128)S(1)}, f32[320,256]{1,0:T(8,128)S(1)}) custom-call(s32[27]{0:T(128)S(1)} %stack.93.at, f32[640,6912]{1,0:T(8,128)} %g.3, f32[640,6912]{1,0:T(8,128)} %m.3, f32[6912,256]{1,0:T(8,128)} %r.3), custom_call_target="tpu_custom_call" | custom-call | flops 3397386240 | bytes 24772608 | tf_op jit(solution)/shard_map/left_half/pallas_call | solution.py:96
  23.1 0.0 copy-start
  23.1 0.0 collective-permute-done.refs_1_
  23.2 2.7 %collective-permute-start.1 = (f32[160,256]{1,0:T(8,128)S(1)}, f32[160,256]{1,0:T(8,128)S(1)}, u32[]{:S(2)}, u32[]{:S(2)}) collective-permute-start(f32[160,256]{1,0:T(8,128)S(1)} %get-tuple-element.35.refs_0_), channel_id=1, source_target_pairs={{0,2},{1,3},{2,0},{3,1},{4,6},{5,7},{6,4},{7,5},{8,10},{9,11},{10,... | collective-permute-start | bytes 491528 | tf_op jit(solution)/shard_map/ppermute | solution.py:481
  25.8 0.3 collective-permute-start.2
  26.1 10.6 %collective-permute-done.1.refs_1_ = f32[160,256]{1,0:T(8,128)S(1)} collective-permute-done((f32[160,256]{1,0:T(8,128)S(1)}, f32[160,256]{1,0:T(8,128)S(1)}, u32[]{:S(2)}, u32[]{:S(2)}) %collective-permute-start.1) | collective-permute-done | bytes 163872 | tf_op jit(solution)/shard_map/ppermute | solution.py:481
  36.8 0.9 collective-permute-start.3
  37.7 2.6 %collective-permute-done.2.refs_1_ = f32[160,256]{1,0:T(8,128)S(1)} collective-permute-done((f32[160,256]{1,0:T(8,128)S(1)}, f32[160,256]{1,0:T(8,128)S(1)}, u32[]{:S(2)}, u32[]{:S(2)}) %collective-permute-start.2) | collective-permute-done | bytes 163872 | tf_op jit(solution)/shard_map/ppermute | solution.py:481
  40.3 0.1 collective-permute-start.4
  40.3 3.6 %collective-permute-done.3.refs_2_ = f32[160,256]{1,0:T(8,128)S(1)} collective-permute-done((f32[160,256]{1,0:T(8,128)S(1)}, f32[160,256]{1,0:T(8,128)S(1)}, u32[]{:S(2)}, u32[]{:S(2)}) %collective-permute-start.3) | collective-permute-done | bytes 163872 | tf_op jit(solution)/shard_map/ppermute | solution.py:481
  43.9 3.3 %collective-permute-done.4.refs_3_ = f32[160,256]{1,0:T(8,128)S(1)} collective-permute-done((f32[160,256]{1,0:T(8,128)S(1)}, f32[160,256]{1,0:T(8,128)S(1)}, u32[]{:S(2)}, u32[]{:S(2)}) %collective-permute-start.4) | collective-permute-done | bytes 163872 | tf_op jit(solution)/shard_map/ppermute | solution.py:481
  47.2 1.7 gram_of.1
  48.9 3.2 %w_send.2 = f32[1792,256]{1,0:T(8,128)S(1)} custom-call(s32[27]{0:T(128)S(1)} %stack.93.at, f32[320,7168]{1,0:T(8,128)S(1)} %get-tuple-element.31.own.refs_7_, f32[320,7168]{1,0:T(8,128)S(1)} %get-tuple-element.32.other.refs_8_, bf16[640,256]{1,0:T(8,128)(2,1)S(1)} %get-tuple-element.37.lh, bf16[640,256]{1,0:T(8,128)(2,1)S(1)} %get-tuple-element.38.ll), custom_call_target="tpu_custom_call" | custom-call | flops 1761607680 | bytes 1835008 | tf_op jit(solution)/shard_map/w_send/pallas_call | solution.py:203
  52.1 0.1 collective-permute-start.5
  52.2 3.2 %w_send.3 = f32[1792,256]{1,0:T(8,128)S(1)} custom-call(s32[27]{0:T(128)S(1)} %stack.93.at, f32[320,7168]{1,0:T(8,128)S(1)} %get-tuple-element.31.own.refs_7_, f32[320,7168]{1,0:T(8,128)S(1)} %get-tuple-element.32.other.refs_8_, bf16[640,256]{1,0:T(8,128)(2,1)S(1)} %get-tuple-element.37.lh, bf16[640,256]{1,0:T(8,128)(2,1)S(1)} %get-tuple-element.38.ll), custom_call_target="tpu_custom_call" | custom-call | flops 1761607680 | bytes 1835008 | tf_op jit(solution)/shard_map/w_send/pallas_call | solution.py:203
  55.4 0.5 collective-permute-start.8
  55.9 0.0 collective-permute-done.5.got
  55.9 3.3 %w_keep.2 = (f32[896,256]{1,0:T(8,128)S(1)}, f32[896,256]{1,0:T(8,128)S(1)}) custom-call(s32[27]{0:T(128)S(1)} %stack.93.at, f32[320,7168]{1,0:T(8,128)S(1)} %get-tuple-element.31.own.refs_7_, f32[320,7168]{1,0:T(8,128)S(1)} %get-tuple-element.32.other.refs_8_, bf16[640,256]{1,0:T(8,128)(2,1)S(1)} %get-tuple-element.37.lh, ...), custom_call_target="tpu_custom_call" | custom-call | flops 1761607680 | bytes 1835008 | tf_op jit(solution)/shard_map/w_keep/pallas_call | solution.py:221
  59.2 1.6 collective-permute-start.6
  60.8 0.0 collective-permute-done.8.got
  60.8 3.3 %w_keep.3 = (f32[896,256]{1,0:T(8,128)S(1)}, f32[896,256]{1,0:T(8,128)S(1)}) custom-call(s32[27]{0:T(128)S(1)} %stack.93.at, f32[320,7168]{1,0:T(8,128)S(1)} %get-tuple-element.31.own.refs_7_, f32[320,7168]{1,0:T(8,128)S(1)} %get-tuple-element.32.other.refs_8_, bf16[640,256]{1,0:T(8,128)(2,1)S(1)} %get-tuple-element.37.lh, ...), custom_call_target="tpu_custom_call" | custom-call | flops 1761607680 | bytes 1835008 | tf_op jit(solution)/shard_map/w_keep/pallas_call | solution.py:221
  64.1 1.6 collective-permute-start.9
  65.7 1.3 collective-permute-done.11.refs_1_
  67.1 0.5 collective-permute-start.14
  67.6 1.6 collective-permute-start.13
  69.2 1.5 collective-permute-start.12
  70.6 15.7 %collective-permute-done.14.refs_3_ = f32[128,256]{1,0:T(8,128)S(1)} collective-permute-done((f32[128,256]{1,0:T(8,128)S(1)}, f32[128,256]{1,0:T(8,128)S(1)}, u32[]{:S(2)}, u32[]{:S(2)}) %collective-permute-start.14) | collective-permute-done | bytes 131104 | tf_op jit(solution)/shard_map/ppermute | solution.py:481
  86.4 5.6 %collective-permute-done.13.refs_2_ = f32[128,256]{1,0:T(8,128)S(1)} collective-permute-done((f32[128,256]{1,0:T(8,128)S(1)}, f32[128,256]{1,0:T(8,128)S(1)}, u32[]{:S(2)}, u32[]{:S(2)}) %collective-permute-start.13) | collective-permute-done | bytes 131104 | tf_op jit(solution)/shard_map/ppermute | solution.py:481
  92.0 0.1 collective-permute-start.15
  92.1 0.0 collective-permute-done.6.y
  92.1 0.6 halve.2
  92.7 1.6 collective-permute-start.7
  94.3 0.6 halve.3
  95.0 0.6 collective-permute-start.10
  95.6 0.0 collective-permute-done.15.beside
  95.6 13.3 %chol_inverse.1 = (f32[256,256]{1,0:T(8,128)S(1)}, bf16[640,256]{1,0:T(8,128)(2,1)S(1)}, bf16[640,256]{1,0:T(8,128)(2,1)S(1)}) custom-call(s32[27]{0:T(128)S(1)} %stack.93.at, f32[128,256]{1,0:T(8,128)S(1)} %total.13.mine, f32[128,256]{1,0:T(8,128)S(1)} %collective-permute-done.15.beside, f32[640,256]{1,0:T(8,128)S(1)} %get-tuple-element.49.left), custom_call_target="tpu_custom_call" | custom-call | flops 4000000000 | bytes 655360 | tf_op jit(solution)/shard_map/chol_inverse/pallas_call | solution.py:336
  108.9 0.0 collective-permute-done.7.ga
  108.9 1.5 right_rows.1
  110.4 1.6 collective-permute-start.19
  112.0 0.5 collective-permute-start.16
  112.5 10.4 %collective-permute-done.19.y = f32[448,256]{1,0:T(8,128)S(1)} collective-permute-done((f32[448,256]{1,0:T(8,128)S(1)}, f32[448,256]{1,0:T(8,128)S(1)}, u32[]{:S(2)}, u32[]{:S(2)}) %collective-permute-start.19) | collective-permute-done | bytes 458784 | tf_op jit(solution)/shard_map/ppermute | solution.py:481
  122.8 0.6 join.3.refs_2_
  123.4 0.5 collective-permute-start.20
  124.0 0.0 collective-permute-done.16.y
  124.0 0.6 join.2.refs_0_
  124.6 1.5 collective-permute-start.17
  126.2 0.5 collective-permute-start.28
  126.7 18.1 %collective-permute-done.20.refs_2_ = f32[896,256]{1,0:T(8,128)S(1)} collective-permute-done((f32[896,256]{1,0:T(8,128)S(1)}, f32[896,256]{1,0:T(8,128)S(1)}, u32[]{:S(2)}, u32[]{:S(2)}) %collective-permute-start.20) | collective-permute-done | bytes 917536 | tf_op jit(solution)/shard_map/ppermute | solution.py:481
  144.8 0.9 collective-permute-done.17.refs_0_
  145.8 3.6 %collective-permute-done.22.refs_1_ = f32[8,256]{1,0:T(8,128)S(1)} collective-permute-done((f32[8,256]{1,0:T(8,128)S(1)}, f32[8,256]{1,0:T(8,128)S(1)}, u32[]{:S(2)}, u32[]{:S(2)}) %collective-permute-start.22) | collective-permute-done | bytes 8224 | tf_op jit(solution)/shard_map/ppermute | solution.py:481
  149.4 1.2 collective-permute-start.23
  150.6 3.4 %collective-permute-done.23.refs_1_ = f32[8,256]{1,0:T(8,128)S(1)} collective-permute-done((f32[8,256]{1,0:T(8,128)S(1)}, f32[8,256]{1,0:T(8,128)S(1)}, u32[]{:S(2)}, u32[]{:S(2)}) %collective-permute-start.23) | collective-permute-done | bytes 8224 | tf_op jit(solution)/shard_map/ppermute | solution.py:481
  154.0 1.2 collective-permute-done.24.refs_1_
  155.1 2.4 %collective-permute-start.27 = (f32[8,256]{1,0:T(8,128)S(1)}, f32[8,256]{1,0:T(8,128)S(1)}, u32[]{:S(2)}, u32[]{:S(2)}) collective-permute-start(f32[8,256]{1,0:T(8,128)S(1)} %total.16.refs_0_), channel_id=1, source_target_pairs={{0,24},{4,28},{8,16},{12,20},{16,8},{20,12},{24,0},{28,4},{1,25},{... | collective-permute-start | bytes 24584 | tf_op jit(solution)/shard_map/ppermute | solution.py:481
  157.6 2.1 %collective-permute-done.27.refs_3_ = f32[8,256]{1,0:T(8,128)S(1)} collective-permute-done((f32[8,256]{1,0:T(8,128)S(1)}, f32[8,256]{1,0:T(8,128)S(1)}, u32[]{:S(2)}, u32[]{:S(2)}) %collective-permute-start.27) | collective-permute-done | bytes 8224 | tf_op jit(solution)/shard_map/ppermute | solution.py:481
  159.7 1.5 collective-permute-start.26
  161.2 2.1 %collective-permute-done.26.refs_2_ = f32[8,256]{1,0:T(8,128)S(1)} collective-permute-done((f32[8,256]{1,0:T(8,128)S(1)}, f32[8,256]{1,0:T(8,128)S(1)}, u32[]{:S(2)}, u32[]{:S(2)}) %collective-permute-start.26) | collective-permute-done | bytes 8224 | tf_op jit(solution)/shard_map/ppermute | solution.py:481
  163.3 1.5 collective-permute-start.25
  164.8 2.2 %collective-permute-done.25.refs_1_ = f32[8,256]{1,0:T(8,128)S(1)} collective-permute-done((f32[8,256]{1,0:T(8,128)S(1)}, f32[8,256]{1,0:T(8,128)S(1)}, u32[]{:S(2)}, u32[]{:S(2)}) %collective-permute-start.25) | collective-permute-done | bytes 8224 | tf_op jit(solution)/shard_map/ppermute | solution.py:481
  167.1 13.8 %final.2 = (f32[640,6912]{1,0:T(8,128)}, f32[640,6912]{1,0:T(8,128)}, f32[6912,256]{1,0:T(8,128)}) custom-call(s32[27]{0:T(128)S(1)} %stack.93.at, f32[896,256]{1,0:T(8,128)S(1)} %join.2.refs_0_, f32[896,256]{1,0:T(8,128)S(1)} %collective-permute-done.28.refs_1_, f32[896,256]{1,0:T(8,128)S(1)} %join.3.refs_2_, ...), custom_call_target="tpu_custom_call" | custom-call | flops 7046430720 | bytes 25690112 | tf_op jit(solution)/shard_map/final/pallas_call | solution.py:449
  180.9 13.3 %final.3 = (f32[640,6912]{1,0:T(8,128)}, f32[640,6912]{1,0:T(8,128)}, f32[6912,256]{1,0:T(8,128)}) custom-call(s32[27]{0:T(128)S(1)} %stack.93.at, f32[896,256]{1,0:T(8,128)S(1)} %collective-permute-done.17.refs_0_, f32[896,256]{1,0:T(8,128)S(1)} %collective-permute-done.18.refs_1_, ...), custom_call_target="tpu_custom_call", output_to_operand_aliasing={{0}: (10, {}), {1}: (11, {}), {2}: (12, {})} | custom-call | flops 7046430720 | bytes 25690112 | tf_op jit(solution)/shard_map/final/pallas_call | solution.py:449
  (30 shorter events, 0.2 us)
Async XLA Ops:
  10.4 12.7 %collective-permute-start = (f32[320,256]{1,0:T(8,128)S(1)}, f32[320,256]{1,0:T(8,128)S(1)}, u32[]{:S(2)}, u32[]{:S(2)}) collective-permute-start(f32[320,256]{1,0:T(8,128)S(1)} %get-tuple-element.34), channel_id=1, source_target_pairs={{0,1},{1,0},{2,3},{3,2},{4,5},{5,4},{6,7},{7,6},{8,9},{9,8},{10,11... | collective-permute-start | bytes 983048 | tf_op jit(solution)/shard_map/ppermute | solution.py:481
  23.1 37.7 %copy-start = (f32[320,7168]{1,0:T(8,128)}, f32[320,7168]{1,0:T(8,128)S(1)}, u32[]{:S(2)}) copy-start(f32[320,7168]{1,0:T(8,128)S(1)} %get-tuple-element.31.own.refs_7_) | copy-start | bytes 27525124
  23.2 13.6 %collective-permute-start.1 = (f32[160,256]{1,0:T(8,128)S(1)}, f32[160,256]{1,0:T(8,128)S(1)}, u32[]{:S(2)}, u32[]{:S(2)}) collective-permute-start(f32[160,256]{1,0:T(8,128)S(1)} %get-tuple-element.35.refs_0_), channel_id=1, source_target_pairs={{0,2},{1,3},{2,0},{3,1},{4,6},{5,7},{6,4},{7,5},{8,10},{9,11},{10,... | collective-permute-start | bytes 491528 | tf_op jit(solution)/shard_map/ppermute | solution.py:481
  25.8 14.4 %collective-permute-start.2 = (f32[160,256]{1,0:T(8,128)S(1)}, f32[160,256]{1,0:T(8,128)S(1)}, u32[]{:S(2)}, u32[]{:S(2)}) collective-permute-start(f32[160,256]{1,0:T(8,128)S(1)} %get-tuple-element.36.refs_0_), channel_id=1, source_target_pairs={{0,2},{1,3},{2,0},{3,1},{4,6},{5,7},{6,4},{7,5},{8,10},{9,11},{10,... | collective-permute-start | bytes 491528 | tf_op jit(solution)/shard_map/ppermute | solution.py:481
  36.8 7.1 %collective-permute-start.3 = (f32[160,256]{1,0:T(8,128)S(1)}, f32[160,256]{1,0:T(8,128)S(1)}, u32[]{:S(2)}, u32[]{:S(2)}) collective-permute-start(f32[160,256]{1,0:T(8,128)S(1)} %total.10.refs_0_), channel_id=1, source_target_pairs={{0,1},{1,0},{2,3},{3,2},{4,5},{5,4},{6,7},{7,6},{8,9},{9,8},{10,11... | collective-permute-start | bytes 491528 | tf_op jit(solution)/shard_map/ppermute | solution.py:481
  40.3 6.9 %collective-permute-start.4 = (f32[160,256]{1,0:T(8,128)S(1)}, f32[160,256]{1,0:T(8,128)S(1)}, u32[]{:S(2)}, u32[]{:S(2)}) collective-permute-start(f32[160,256]{1,0:T(8,128)S(1)} %total.11.refs_1_), channel_id=1, source_target_pairs={{0,1},{1,0},{2,3},{3,2},{4,5},{5,4},{6,7},{7,6},{8,9},{9,8},{10,11... | collective-permute-start | bytes 491528 | tf_op jit(solution)/shard_map/ppermute | solution.py:481
  52.1 3.9 %collective-permute-start.5 = (f32[1792,256]{1,0:T(8,128)S(1)}, f32[1792,256]{1,0:T(8,128)S(1)}, u32[]{:S(2)}, u32[]{:S(2)}) collective-permute-start(f32[1792,256]{1,0:T(8,128)S(1)} %w_send.2), channel_id=1, source_target_pairs={{0,4},{4,0},{8,12},{12,8},{16,20},{20,16},{24,28},{28,24},{1,5},{5... | collective-permute-start | bytes 5505032 | tf_op jit(solution)/shard_map/ppermute | solution.py:481
  55.4 5.5 %collective-permute-start.8 = (f32[1792,256]{1,0:T(8,128)S(1)}, f32[1792,256]{1,0:T(8,128)S(1)}, u32[]{:S(2)}, u32[]{:S(2)}) collective-permute-start(f32[1792,256]{1,0:T(8,128)S(1)} %w_send.3), channel_id=1, source_target_pairs={{0,4},{4,0},{8,12},{12,8},{16,20},{20,16},{24,28},{28,24},{1,5},{5... | collective-permute-start | bytes 5505032 | tf_op jit(solution)/shard_map/ppermute | solution.py:481
  59.2 32.8 %collective-permute-start.6 = (f32[896,256]{1,0:T(8,128)S(1)}, f32[896,256]{1,0:T(8,128)S(1)}, u32[]{:S(2)}, u32[]{:S(2)}) collective-permute-start(f32[896,256]{1,0:T(8,128)S(1)} %get-tuple-element.40), channel_id=1, source_target_pairs={{0,8},{4,12},{8,0},{12,4},{16,24},{20,28},{24,16},{28,20},{1,9},{5... | collective-permute-start | bytes 2752520 | tf_op jit(solution)/shard_map/ppermute | solution.py:481
  64.1 30.2 %collective-permute-start.9 = (f32[896,256]{1,0:T(8,128)S(1)}, f32[896,256]{1,0:T(8,128)S(1)}, u32[]{:S(2)}, u32[]{:S(2)}) collective-permute-start(f32[896,256]{1,0:T(8,128)S(1)} %get-tuple-element.44), channel_id=1, source_target_pairs={{0,16},{4,20},{8,24},{12,28},{16,0},{20,4},{24,8},{28,12},{1,17},{... | collective-permute-start | bytes 2752520 | tf_op jit(solution)/shard_map/ppermute | solution.py:481
  65.7 1.3 collective-permute-start.11
  67.1 19.3 %collective-permute-start.14 = (f32[128,256]{1,0:T(8,128)S(1)}, f32[128,256]{1,0:T(8,128)S(1)}, u32[]{:S(2)}, u32[]{:S(2)}) collective-permute-start(f32[128,256]{1,0:T(8,128)S(1)} %total.12.refs_0_), channel_id=1, source_target_pairs={{0,24},{4,28},{8,16},{12,20},{16,8},{20,12},{24,0},{28,4},{1,25},{... | collective-permute-start | bytes 393224 | tf_op jit(solution)/shard_map/ppermute | solution.py:481
  67.6 24.4 %collective-permute-start.13 = (f32[128,256]{1,0:T(8,128)S(1)}, f32[128,256]{1,0:T(8,128)S(1)}, u32[]{:S(2)}, u32[]{:S(2)}) collective-permute-start(f32[128,256]{1,0:T(8,128)S(1)} %total.12.refs_0_), channel_id=1, source_target_pairs={{0,16},{4,20},{8,24},{12,28},{16,0},{20,4},{24,8},{28,12},{1,17},{... | collective-permute-start | bytes 393224 | tf_op jit(solution)/shard_map/ppermute | solution.py:481
  69.2 22.8 %collective-permute-start.12 = (f32[128,256]{1,0:T(8,128)S(1)}, f32[128,256]{1,0:T(8,128)S(1)}, u32[]{:S(2)}, u32[]{:S(2)}) collective-permute-start(f32[128,256]{1,0:T(8,128)S(1)} %total.12.refs_0_), channel_id=1, source_target_pairs={{0,8},{4,12},{8,0},{12,4},{16,24},{20,28},{24,16},{28,20},{1,9},{5... | collective-permute-start | bytes 393224 | tf_op jit(solution)/shard_map/ppermute | solution.py:481
  92.0 3.6 %collective-permute-start.15 = (f32[128,256]{1,0:T(8,128)S(1)}, f32[128,256]{1,0:T(8,128)S(1)}, u32[]{:S(2)}, u32[]{:S(2)}) collective-permute-start(f32[128,256]{1,0:T(8,128)S(1)} %total.13.mine), channel_id=1, source_target_pairs={{0,4},{4,0},{8,12},{12,8},{16,20},{20,16},{24,28},{28,24},{1,5},{5... | collective-permute-start | bytes 393224 | tf_op jit(solution)/shard_map/ppermute | solution.py:481
  92.7 16.1 %collective-permute-start.7 = (f32[448,256]{1,0:T(8,128)S(1)}, f32[448,256]{1,0:T(8,128)S(1)}, u32[]{:S(2)}, u32[]{:S(2)}) collective-permute-start(f32[448,256]{1,0:T(8,128)S(1)} %get-tuple-element.42), channel_id=1, source_target_pairs={{0,16},{4,20},{8,24},{12,28},{16,0},{20,4},{24,8},{28,12},{1,17},{... | collective-permute-start | bytes 1376264 | tf_op jit(solution)/shard_map/ppermute | solution.py:481
  94.3 72.7 %slice-start = ((s8[9175040]{0:T(1024)(128)(4,1)}), s8[4194304]{0:T(1024)(128)(4,1)S(1)}, s32[]{:S(2)}) async-start(s8[9175040]{0:T(1024)(128)(4,1)} %bitcast.21), calls=%async_computation | async-start | bytes 8388608
  95.0 13.9 %collective-permute-start.10 = (f32[448,256]{1,0:T(8,128)S(1)}, f32[448,256]{1,0:T(8,128)S(1)}, u32[]{:S(2)}, u32[]{:S(2)}) collective-permute-start(f32[448,256]{1,0:T(8,128)S(1)} %get-tuple-element.46), channel_id=1, source_target_pairs={{0,8},{4,12},{8,0},{12,4},{16,24},{20,28},{24,16},{28,20},{1,9},{5... | collective-permute-start | bytes 1376264 | tf_op jit(solution)/shard_map/ppermute | solution.py:481
  95.6 71.5 %slice-start.1 = ((s8[9175040]{0:T(1024)(128)(4,1)}), s8[4194304]{0:T(1024)(128)(4,1)S(1)}, s32[]{:S(2)}) async-start(s8[9175040]{0:T(1024)(128)(4,1)} %bitcast.21), calls=%async_computation.1 | async-start | bytes 8388608
  95.6 71.5 %slice-start.2 = ((s8[9175040]{0:T(1024)(128)(4,1)}), s8[786432]{0:T(1024)(128)(4,1)S(1)}, s32[]{:S(2)}) async-start(s8[9175040]{0:T(1024)(128)(4,1)} %bitcast.21), calls=%async_computation.2 | async-start | bytes 1572864
  110.4 12.4 %collective-permute-start.19 = (f32[448,256]{1,0:T(8,128)S(1)}, f32[448,256]{1,0:T(8,128)S(1)}, u32[]{:S(2)}, u32[]{:S(2)}) collective-permute-start(f32[448,256]{1,0:T(8,128)S(1)} %get-tuple-element.52.x), channel_id=1, source_target_pairs={{0,8},{4,12},{8,0},{12,4},{16,24},{20,28},{24,16},{28,20},{1,9},{5... | collective-permute-start | bytes 1376264 | tf_op jit(solution)/shard_map/ppermute | solution.py:481
  112.0 12.1 %collective-permute-start.16 = (f32[448,256]{1,0:T(8,128)S(1)}, f32[448,256]{1,0:T(8,128)S(1)}, u32[]{:S(2)}, u32[]{:S(2)}) collective-permute-start(f32[448,256]{1,0:T(8,128)S(1)} %get-tuple-element.51.x), channel_id=1, source_target_pairs={{0,16},{4,20},{8,24},{12,28},{16,0},{20,4},{24,8},{28,12},{1,17},{... | collective-permute-start | bytes 1376264 | tf_op jit(solution)/shard_map/ppermute | solution.py:481
  123.4 21.4 %collective-permute-start.20 = (f32[896,256]{1,0:T(8,128)S(1)}, f32[896,256]{1,0:T(8,128)S(1)}, u32[]{:S(2)}, u32[]{:S(2)}) collective-permute-start(f32[896,256]{1,0:T(8,128)S(1)} %join.3.refs_2_), channel_id=1, source_target_pairs={{0,16},{4,20},{8,24},{12,28},{16,0},{20,4},{24,8},{28,12},{1,17},{... | collective-permute-start | bytes 2752520 | tf_op jit(solution)/shard_map/ppermute | solution.py:481
  124.6 21.1 %collective-permute-start.17 = (f32[896,256]{1,0:T(8,128)S(1)}, f32[896,256]{1,0:T(8,128)S(1)}, u32[]{:S(2)}, u32[]{:S(2)}) collective-permute-start(f32[896,256]{1,0:T(8,128)S(1)} %join.2.refs_0_), channel_id=1, source_target_pairs={{0,8},{4,12},{8,0},{12,4},{16,24},{20,28},{24,16},{28,20},{1,9},{5... | collective-permute-start | bytes 2752520 | tf_op jit(solution)/shard_map/ppermute | solution.py:481
  126.2 40.8 %collective-permute-start.29 = (f32[896,256]{1,0:T(8,128)S(1)}, f32[896,256]{1,0:T(8,128)S(1)}, u32[]{:S(2)}, u32[]{:S(2)}) collective-permute-start(f32[896,256]{1,0:T(8,128)S(1)} %join.3.refs_2_), channel_id=1, source_target_pairs={{0,4},{4,0},{8,12},{12,8},{16,20},{20,16},{24,28},{28,24},{1,5},{5... | collective-permute-start | bytes 2752520 | tf_op jit(solution)/shard_map/ppermute | solution.py:481
  126.2 40.8 %collective-permute-start.28 = (f32[896,256]{1,0:T(8,128)S(1)}, f32[896,256]{1,0:T(8,128)S(1)}, u32[]{:S(2)}, u32[]{:S(2)}) collective-permute-start(f32[896,256]{1,0:T(8,128)S(1)} %join.2.refs_0_), channel_id=1, source_target_pairs={{0,4},{4,0},{8,12},{12,8},{16,20},{20,16},{24,28},{28,24},{1,5},{5... | collective-permute-start | bytes 2752520 | tf_op jit(solution)/shard_map/ppermute | solution.py:481
  144.8 36.1 %collective-permute-start.21 = (f32[896,256]{1,0:T(8,128)S(1)}, f32[896,256]{1,0:T(8,128)S(1)}, u32[]{:S(2)}, u32[]{:S(2)}) collective-permute-start(f32[896,256]{1,0:T(8,128)S(1)} %collective-permute-done.20.refs_2_), channel_id=1, source_target_pairs={{0,4},{4,0},{8,12},{12,8},{16,20},{20,16},{24,28},{28,24},{1,5},{5... | collective-permute-start | bytes 2752520 | tf_op jit(solution)/shard_map/ppermute | solution.py:481
  145.8 35.1 %collective-permute-start.18 = (f32[896,256]{1,0:T(8,128)S(1)}, f32[896,256]{1,0:T(8,128)S(1)}, u32[]{:S(2)}, u32[]{:S(2)}) collective-permute-start(f32[896,256]{1,0:T(8,128)S(1)} %collective-permute-done.17.refs_0_), channel_id=1, source_target_pairs={{0,4},{4,0},{8,12},{12,8},{16,20},{20,16},{24,28},{28,24},{1,5},{5... | collective-permute-start | bytes 2752520 | tf_op jit(solution)/shard_map/ppermute | solution.py:481
  145.8 3.7 %collective-permute-start.22 = (f32[8,256]{1,0:T(8,128)S(1)}, f32[8,256]{1,0:T(8,128)S(1)}, u32[]{:S(2)}, u32[]{:S(2)}) collective-permute-start(f32[8,256]{1,0:T(8,128)S(1)} %get-tuple-element.53.refs_0_), channel_id=1, source_target_pairs={{0,1},{1,0},{2,3},{3,2},{4,5},{5,4},{6,7},{7,6},{8,9},{9,8},{10,11... | collective-permute-start | bytes 24584 | tf_op jit(solution)/shard_map/ppermute | solution.py:481
  149.4 4.5 %collective-permute-start.23 = (f32[8,256]{1,0:T(8,128)S(1)}, f32[8,256]{1,0:T(8,128)S(1)}, u32[]{:S(2)}, u32[]{:S(2)}) collective-permute-start(f32[8,256]{1,0:T(8,128)S(1)} %total.14.refs_0_), channel_id=1, source_target_pairs={{0,2},{1,3},{2,0},{3,1},{4,6},{5,7},{6,4},{7,5},{8,10},{9,11},{10,... | collective-permute-start | bytes 24584 | tf_op jit(solution)/shard_map/ppermute | solution.py:481
  154.0 1.2 collective-permute-start.24
  155.1 4.5 %collective-permute-start.27 = (f32[8,256]{1,0:T(8,128)S(1)}, f32[8,256]{1,0:T(8,128)S(1)}, u32[]{:S(2)}, u32[]{:S(2)}) collective-permute-start(f32[8,256]{1,0:T(8,128)S(1)} %total.16.refs_0_), channel_id=1, source_target_pairs={{0,24},{4,28},{8,16},{12,20},{16,8},{20,12},{24,0},{28,4},{1,25},{... | collective-permute-start | bytes 24584 | tf_op jit(solution)/shard_map/ppermute | solution.py:481
  159.7 3.7 %collective-permute-start.26 = (f32[8,256]{1,0:T(8,128)S(1)}, f32[8,256]{1,0:T(8,128)S(1)}, u32[]{:S(2)}, u32[]{:S(2)}) collective-permute-start(f32[8,256]{1,0:T(8,128)S(1)} %total.16.refs_0_), channel_id=1, source_target_pairs={{0,16},{4,20},{8,24},{12,28},{16,0},{20,4},{24,8},{28,12},{1,17},{... | collective-permute-start | bytes 24584 | tf_op jit(solution)/shard_map/ppermute | solution.py:481
  163.3 3.7 %collective-permute-start.25 = (f32[8,256]{1,0:T(8,128)S(1)}, f32[8,256]{1,0:T(8,128)S(1)}, u32[]{:S(2)}, u32[]{:S(2)}) collective-permute-start(f32[8,256]{1,0:T(8,128)S(1)} %total.16.refs_0_), channel_id=1, source_target_pairs={{0,8},{4,12},{8,0},{12,4},{16,24},{20,28},{24,16},{28,20},{1,9},{5... | collective-permute-start | bytes 24584 | tf_op jit(solution)/shard_map/ppermute | solution.py:481

commit v6 on v5

--- a/solution.py
+++ b/solution.py
@@ -376,19 +376,25 @@
     )(at, ka, ga, kb, gb, x)
 
 
-def join_kernel(place, at, x, y, out):
+def join_kernel(place, at, x, y, *rest):
+    outs, both = rest[:-1], rest[-1]
     n, t = x.shape[0], at[place]
-    out[pl.ds(pl.multiple_of(t * n, GROUP), n), :] = x[...]
-    out[pl.ds(pl.multiple_of((1 - t) * n, GROUP), n), :] = y[...]
-
-
-def join(at, place, x, y):
+    both[pl.ds(pl.multiple_of(t * n, GROUP), n), :] = x[...]
+    both[pl.ds(pl.multiple_of((1 - t) * n, GROUP), n), :] = y[...]
+    top = 0
+    for out in outs:
+        out[...] = both[top : top + out.shape[0], :]
+        top += out.shape[0]
+
+
+def join(at, place, x, y, sizes):
     rows, rank = x.shape
     return pl.pallas_call(
         functools.partial(join_kernel, place),
         in_specs=[SMEM, VMEM, VMEM],
-        out_specs=VMEM,
-        out_shape=jax.ShapeDtypeStruct((2 * rows, rank), F32),
+        out_specs=[VMEM] * len(sizes),
+        out_shape=[jax.ShapeDtypeStruct((n, rank), F32) for n in sizes],
+        scratch_shapes=[pltpu.VMEM((2 * rows, rank), F32)],
         compiler_params=params(6),
         cost_estimate=cost(rows * rank, 16 * rows * rank),
         name="join",
@@ -415,54 +421,120 @@
     )(at, x, y)
 
 
-def final_kernel(place, count, total_cols, factor, at, *refs):
-    pieces = refs[:count]
-    squares, oh, ol, own, other = refs[count : count + 5]
-    update, momentum, new_right, rh, rl, nh, nl = refs[-7:]
-    u = pl.program_id(0)
-    half, width = own.shape[0], new_right.shape[0]
-    for k in range(count):
-
-        @pl.when(u == k)
-        def _(k=k):
-            right = pieces[k][...]
-            scale = jnp.sqrt(squares[0:1, :] / total_cols + 1e-06)
-            scaled = right / scale
-            new_right[...] = scaled
-            rh[...], rl[...] = split(right)
-            nh[...], nl[...] = split(scaled)
-
-    part = pl.ds(pl.multiple_of(at[place + u] * width, LANES), width)
-    for h, buffer in enumerate((own, other)):
-        rows = pl.ds(pl.multiple_of(at[h] * half, GROUP), half)
-        a, b = oh[h * half : (h + 1) * half, :], ol[h * half : (h + 1) * half, :]
-        momentum[rows, :] = buffer[:, part] - 0.05 * dot3(a, b, rh[...], rl[...], NT)
-        update[rows, :] = factor * dot3(a, b, nh[...], nl[...], NT)
-
-
-def final(at, place, pieces, squares, oh, ol, own, other, cols, total_rows, total_cols, before):
-    rows = oh.shape[0]
-    unit, rank = pieces[0].shape
-    count = len(pieces)
-    wide = pl.BlockSpec((rows, unit), lambda u, at: (0, at[place + u]))
+def final_kernel(place, groups, unit, parts, total_cols, factor, at, *refs):
+    refs = list(refs)
+    take = lambda n: [refs.pop(0) for _ in range(n)]
+    pieces = [take(4) for _ in groups]
+    squares, oh, ol, own, other = take(5)
+    del refs[: len(refs) - 3 - 6 * len(groups)]
+    update, momentum, new_right = take(3)
+    half = own.shape[0]
+    blocks = update.shape[1] // LANES
+    halves = [pl.ds(pl.multiple_of(at[h] * half, GROUP), half) for h in range(2)]
+
+    def copies(group, k, stage_m, stage_u, stage_r, sems):
+        start, count = group
+        first = at[place + k] * (unit // LANES) + start
+        for j in range(count):
+            here = pl.ds(j * LANES, LANES)
+            there = pl.ds(pl.multiple_of((first + j) * LANES, LANES), LANES)
+            both = []
+            if "m" in parts:
+                both.append((stage_m.at[k, :, here], momentum.at[:, there]))
+            if "u" in parts:
+                both.append((stage_u.at[k, :, here], update.at[:, there]))
+                both.append((stage_r.at[k, here, :], new_right.at[there, :]))
+            yield first + j < blocks, [
+                pltpu.make_async_copy(a, b, sems.at[i, k, j]) for i, (a, b) in enumerate(both)
+            ]
+
+    stages = []
+    for group, data in zip(groups, pieces):
+        stage_m, stage_u, stage_r, high, low, sems = take(6)
+        stages.append((stage_m, stage_u, stage_r, sems))
+        start, count = group
+        n = count * LANES
+
+        def body(k, _):
+            def load(scaled):
+                for i, piece in enumerate(data):
+
+                    @pl.when(k == i)
+                    def _(piece=piece):
+                        x = piece[...]
+                        if scaled:
+                            x = x / jnp.sqrt(squares[0:1, :] / total_cols + 1e-06)
+                            stage_r[k] = x
+                        high[...], low[...] = split(x)
+
+            if "m" in parts:
+                load(False)
+                value = 0.05 * dot3(oh[...], ol[...], high[...], low[...], NT)
+                part = pl.ds(pl.multiple_of(at[place + k] * unit + start * LANES, LANES), n)
+                stage_m[k, halves[0], :] = own[:, part] - value[:half]
+                stage_m[k, halves[1], :] = other[:, part] - value[half:]
+            if "u" in parts:
+                load(True)
+                value = factor * dot3(oh[...], ol[...], high[...], low[...], NT)
+                stage_u[k, halves[0], :] = value[:half]
+                stage_u[k, halves[1], :] = value[half:]
+            for inside, some in copies(group, k, stage_m, stage_u, stage_r, sems):
+
+                @pl.when(inside)
+                def _(some=some):
+                    for copy in some:
+                        copy.start()
+
+            return 0
+
+        lax.fori_loop(0, 4, body, 0)
+
+    for group, stage in zip(groups, stages):
+
+        def finish(k, _):
+            for inside, some in copies(group, k, *stage):
+
+                @pl.when(inside)
+                def _(some=some):
+                    for copy in some:
+                        copy.wait()
+
+            return 0
+
+        lax.fori_loop(0, 4, finish, 0)
+
+
+def final(at, place, groups, unit, parts, pieces, squares, oh, ol, own, other, sizes, before):
+    rows, rank = oh.shape
+    cols, total_rows, total_cols = sizes
     factor = (total_rows / rank) ** 0.5
-    return pl.pallas_call(
-        functools.partial(final_kernel, place, count, total_cols, factor),
-        grid_spec=pltpu.PrefetchScalarGridSpec(
-            num_scalar_prefetch=1,
-            grid=(count,),
-            in_specs=[VMEM] * (count + 5) + [HBM] * len(before),
-            out_specs=[wide, wide, pl.BlockSpec((unit, rank), lambda u, at: (at[place + u], 0))],
-            scratch_shapes=[pltpu.VMEM((unit, rank), BF16)] * 4,
-        ),
+    m, u = "m" in parts, "u" in parts
+    scratch = []
+    for _, count in groups:
+        n = count * LANES
+        tiny = (4, GROUP, LANES)
+        scratch += [
+            pltpu.VMEM((4, rows, n) if m else tiny, F32),
+            pltpu.VMEM((4, rows, n) if u else tiny, F32),
+            pltpu.VMEM((4, n, rank) if u else tiny, F32),
+            pltpu.VMEM((n, rank), BF16),
+            pltpu.VMEM((n, rank), BF16),
+            pltpu.SemaphoreType.DMA((3, 4, count)),
+        ]
+    width = 4 * sum(count for _, count in groups) * LANES
+    return pl.pallas_call(
+        functools.partial(final_kernel, place, groups, unit, parts, total_cols, factor),
+        in_specs=[SMEM] + [VMEM] * (len(pieces) + 5) + [HBM] * len(before),
+        out_specs=[HBM] * 3,
         out_shape=[
             jax.ShapeDtypeStruct((rows, cols), F32),
             jax.ShapeDtypeStruct((rows, cols), F32),
             jax.ShapeDtypeStruct((cols, rank), F32),
         ],
-        input_output_aliases={count + 6 + i: i for i in range(len(before))},
+        scratch_shapes=scratch,
+        input_output_aliases={len(pieces) + 6 + i: i for i in range(len(before))},
         compiler_params=params(20),
-        cost_estimate=cost(12 * count * rows * unit * rank, 4 * count * unit * (2 * rows + 2 * rank)),
+        cost_estimate=cost(6 * len(parts) * rows * width * rank, 4 * len(parts) * rows * width),
         name="final",
     )(at, *pieces, squares, oh, ol, own, other, *before)
 
@@ -569,22 +641,31 @@
     else:
         squares = lax.psum(squares, "tensor")
     got = swap(squares, "dp", 0)
-    squares = total(squares, got)
-    squares = spread_sum(squares, bits)
-
-    near, far = [], []
+    squares_part = total(squares, got)
+    squares = spread_sum(squares_part, bits)
+
+    blocks = unit // LANES
+    groups = ((0, blocks - blocks // 2), (blocks - blocks // 2, blocks // 2))
+    near, far = ([], []), ([], [])
     for h, (order, x) in enumerate(zip(orders, right)):
         for b in order[:0:-1]:
             y = swap(x, "dp", b)
-            x = join(at, bit_at[h][b], x, y)
-        y = swap(x, "dp", order[0])
-        near += [x, swap(x, "dp", 0)]
-        far += [y, swap(y, "dp", 0)]
-
-    outs = ()
-    for place, data in ((near_at, near), (far_at, far)):
-        sizes = (cols, rows * n_dp, cols * n_tp)
-        outs = final(at, place, data, squares, oh, ol, *held, *sizes, outs)
+            whole = 2 * x.shape[0]
+            cut = [count * LANES for _, count in groups] if whole == unit else [whole]
+            x, *rest = join(at, bit_at[h][b], x, y, cut)
+        for g, part in enumerate([x] + rest):
+            y = swap(part, "dp", order[0])
+            beside = swap(part, "dp", 0)
+            near[g].extend([part, beside])
+            far[g].extend([y, swap(y, "dp", 0)])
+
+    sizes = (cols, rows * n_dp, cols * n_tp)
+    same = (oh, ol, *held, sizes)
+    both = near[0] + near[1]
+    outs = final(at, near_at, groups, unit, "m", both, squares_part, *same, ())
+    outs = final(at, near_at, groups, unit, "u", both, squares, *same, outs)
+    for g in range(2):
+        outs = final(at, far_at, groups[g : g + 1], unit, "mu", far[g], squares, *same, outs)
     return tuple(outs)
 
 

time: 194 us -> 202 us (1.041)
  Pallas kernels: 78.4 us -> 86.6 us
  waiting for transfers between devices: 86.8 us -> 84.5 us
    pallas_call x2 -> x4, Pallas kernels: 27.1 us -> 35.2 us  [final(): pl.pallas_call(functools.partial(final_kernel, place, groups, unit, parts...]
    ppermute x30 -> x36, waiting for transfers between devices: 86.8 us -> 84.5 us  [swap(): return lax.ppermute(x, axis, [(i, i ^ mask) for i in range(n)])]
    ppermute x30 -> x36, starting transfers between devices: 27.9 us -> 29.3 us  [swap(): return lax.ppermute(x, axis, [(i, i ^ mask) for i in range(n)])]
  transfers between devices with their start and end apart: 30 -> 36, of which waited for: 16 -> 14; matrix products, arithmetic and copies ran while one was open for 0% -> 0% of each run, Pallas kernels for 25% -> 31%
where the time goes in v6:
time: 202 us
  Pallas kernels  86.6 us (43%)
  waiting for transfers between devices  84.5 us (42%)
  starting transfers between devices  29.3 us (15%)
    ppermute x36, waiting for transfers between devices, swap(): return lax.ppermute(x, axis, [(i, i ^ mask) for i in range(n)])  84.5 us
    pallas_call x4, Pallas kernels, final(): pl.pallas_call(functools.partial(final_kernel, place, groups, unit, parts...  35.2 us
    ppermute x36, starting transfers between devices, swap(): return lax.ppermute(x, axis, [(i, i ^ mask) for i in range(n)])  29.3 us
    pallas_call x2, Pallas kernels, left_half(): pl.pallas_call(functools.partial(left_kernel, which), in_specs=[SMEM, HBM...  19.2 us
    pallas_call x1, Pallas kernels, chol_inverse(): pl.pallas_call(functools.partial(chol_kernel, place), in_specs=[SMEM] + [...  13.3 us
    pallas_call x2, Pallas kernels, w_keep(): pl.pallas_call(functools.partial(w_keep_kernel, place), grid_spec=pltpu.P...  6.56 us
    pallas_call x2, Pallas kernels, w_send(): pl.pallas_call(functools.partial(w_send_kernel, place), grid_spec=pltpu.P...  6.36 us
  transfers between devices with their start and end apart: 36, of which 14 were waited for; matrix products, arithmetic and copies ran while one was open for 0% of the time, Pallas kernels for 31%

profile of v6, /device:TPU:0, one launch (start us, length us, event | category | flops | bytes accessed | tf_op | source)
XLA Modules:
  0.0 201.7 jit_solution(5261562924669155397)
XLA Ops:
  0.7 0.1 stack.93.at
  0.8 9.6 %left_half.3 = (f32[320,7168]{1,0:T(8,128)S(1)}, f32[320,256]{1,0:T(8,128)S(1)}) custom-call(s32[27]{0:T(128)S(1)} %stack.93.at, f32[640,6912]{1,0:T(8,128)} %g.3, f32[640,6912]{1,0:T(8,128)} %m.3, f32[6912,256]{1,0:T(8,128)} %r.3), custom_call_target="tpu_custom_call" | custom-call | flops 3397386240 | bytes 24772608 | tf_op jit(solution)/shard_map/left_half/pallas_call | solution.py:96
  10.4 3.1 %collective-permute-start = (f32[320,256]{1,0:T(8,128)S(1)}, f32[320,256]{1,0:T(8,128)S(1)}, u32[]{:S(2)}, u32[]{:S(2)}) collective-permute-start(f32[320,256]{1,0:T(8,128)S(1)} %get-tuple-element.44), channel_id=1, source_target_pairs={{0,1},{1,0},{2,3},{3,2},{4,5},{5,4},{6,7},{7,6},{8,9},{9,8},{10,11... | collective-permute-start | bytes 983048 | tf_op jit(solution)/shard_map/ppermute | solution.py:553
  13.5 9.6 %left_half.2 = (f32[320,7168]{1,0:T(8,128)S(1)}, f32[320,256]{1,0:T(8,128)S(1)}) custom-call(s32[27]{0:T(128)S(1)} %stack.93.at, f32[640,6912]{1,0:T(8,128)} %g.3, f32[640,6912]{1,0:T(8,128)} %m.3, f32[6912,256]{1,0:T(8,128)} %r.3), custom_call_target="tpu_custom_call" | custom-call | flops 3397386240 | bytes 24772608 | tf_op jit(solution)/shard_map/left_half/pallas_call | solution.py:96
  23.1 0.0 copy-start
  23.2 2.7 %collective-permute-start.2 = (f32[160,256]{1,0:T(8,128)S(1)}, f32[160,256]{1,0:T(8,128)S(1)}, u32[]{:S(2)}, u32[]{:S(2)}) collective-permute-start(f32[160,256]{1,0:T(8,128)S(1)} %get-tuple-element.46.refs_0_), channel_id=1, source_target_pairs={{0,2},{1,3},{2,0},{3,1},{4,6},{5,7},{6,4},{7,5},{8,10},{9,11},{10,... | collective-permute-start | bytes 491528 | tf_op jit(solution)/shard_map/ppermute | solution.py:553
  25.8 0.3 collective-permute-start.1
  26.1 10.6 %collective-permute-done.2.refs_1_ = f32[160,256]{1,0:T(8,128)S(1)} collective-permute-done((f32[160,256]{1,0:T(8,128)S(1)}, f32[160,256]{1,0:T(8,128)S(1)}, u32[]{:S(2)}, u32[]{:S(2)}) %collective-permute-start.2) | collective-permute-done | bytes 163872 | tf_op jit(solution)/shard_map/ppermute | solution.py:553
  36.8 0.9 collective-permute-start.4
  37.7 2.6 %collective-permute-done.1.refs_1_ = f32[160,256]{1,0:T(8,128)S(1)} collective-permute-done((f32[160,256]{1,0:T(8,128)S(1)}, f32[160,256]{1,0:T(8,128)S(1)}, u32[]{:S(2)}, u32[]{:S(2)}) %collective-permute-start.1) | collective-permute-done | bytes 163872 | tf_op jit(solution)/shard_map/ppermute | solution.py:553
  40.3 0.1 collective-permute-start.3
  40.3 3.6 %collective-permute-done.4.refs_3_ = f32[160,256]{1,0:T(8,128)S(1)} collective-permute-done((f32[160,256]{1,0:T(8,128)S(1)}, f32[160,256]{1,0:T(8,128)S(1)}, u32[]{:S(2)}, u32[]{:S(2)}) %collective-permute-start.4) | collective-permute-done | bytes 163872 | tf_op jit(solution)/shard_map/ppermute | solution.py:553
  43.9 3.3 %collective-permute-done.3.refs_2_ = f32[160,256]{1,0:T(8,128)S(1)} collective-permute-done((f32[160,256]{1,0:T(8,128)S(1)}, f32[160,256]{1,0:T(8,128)S(1)}, u32[]{:S(2)}, u32[]{:S(2)}) %collective-permute-start.3) | collective-permute-done | bytes 163872 | tf_op jit(solution)/shard_map/ppermute | solution.py:553
  47.2 1.7 gram_of.1
  48.9 3.2 %w_send.3 = f32[1792,256]{1,0:T(8,128)S(1)} custom-call(s32[27]{0:T(128)S(1)} %stack.93.at, f32[320,7168]{1,0:T(8,128)S(1)} %get-tuple-element.41.own.refs_11_.refs_7_, f32[320,7168]{1,0:T(8,128)S(1)} %get-tuple-element.42.other.refs_12_.refs_8_, bf16[640,256]{1,0:T(8,128)(2,1)S(1)} %get-tuple-element.47.lh, bf16[640,256]{1,0:T(8,128)(2,1)S(1)} %get-tuple-element.48.ll), custom_call_target="tpu_custom_call" | custom-call | flops 1761607680 | bytes 1835008 | tf_op jit(solution)/shard_map/w_send/pallas_call | solution.py:203
  52.1 0.1 collective-permute-start.8
  52.2 3.2 %w_send.2 = f32[1792,256]{1,0:T(8,128)S(1)} custom-call(s32[27]{0:T(128)S(1)} %stack.93.at, f32[320,7168]{1,0:T(8,128)S(1)} %get-tuple-element.41.own.refs_11_.refs_7_, f32[320,7168]{1,0:T(8,128)S(1)} %get-tuple-element.42.other.refs_12_.refs_8_, bf16[640,256]{1,0:T(8,128)(2,1)S(1)} %get-tuple-element.47.lh, bf16[640,256]{1,0:T(8,128)(2,1)S(1)} %get-tuple-element.48.ll), custom_call_target="tpu_custom_call" | custom-call | flops 1761607680 | bytes 1835008 | tf_op jit(solution)/shard_map/w_send/pallas_call | solution.py:203
  55.4 0.6 collective-permute-start.5
  55.9 0.0 collective-permute-done.8.got
  55.9 3.3 %w_keep.3 = (f32[896,256]{1,0:T(8,128)S(1)}, f32[896,256]{1,0:T(8,128)S(1)}) custom-call(s32[27]{0:T(128)S(1)} %stack.93.at, f32[320,7168]{1,0:T(8,128)S(1)} %get-tuple-element.41.own.refs_11_.refs_7_, f32[320,7168]{1,0:T(8,128)S(1)} %get-tuple-element.42.other.refs_12_.refs_8_, bf16[640,256]{1,0:T(8,128)(2,1)S(1)} %get-tuple-element.47.lh, ...), custom_call_target="tpu_custom_call" | custom-call | flops 1761607680 | bytes 1835008 | tf_op jit(solution)/shard_map/w_keep/pallas_call | solution.py:221
  59.2 1.6 collective-permute-start.9
  60.9 3.3 %w_keep.2 = (f32[896,256]{1,0:T(8,128)S(1)}, f32[896,256]{1,0:T(8,128)S(1)}) custom-call(s32[27]{0:T(128)S(1)} %stack.93.at, f32[320,7168]{1,0:T(8,128)S(1)} %get-tuple-element.41.own.refs_11_.refs_7_, f32[320,7168]{1,0:T(8,128)S(1)} %get-tuple-element.42.other.refs_12_.refs_8_, bf16[640,256]{1,0:T(8,128)(2,1)S(1)} %get-tuple-element.47.lh, ...), custom_call_target="tpu_custom_call" | custom-call | flops 1761607680 | bytes 1835008 | tf_op jit(solution)/shard_map/w_keep/pallas_call | solution.py:221
  64.1 1.6 collective-permute-start.6
  65.7 1.3 collective-permute-done.11.refs_1_
  67.1 0.6 collective-permute-start.12
  67.7 0.5 collective-permute-start.13
  68.1 2.5 %collective-permute-start.14 = (f32[128,256]{1,0:T(8,128)S(1)}, f32[128,256]{1,0:T(8,128)S(1)}, u32[]{:S(2)}, u32[]{:S(2)}) collective-permute-start(f32[128,256]{1,0:T(8,128)S(1)} %total.12.refs_0_), channel_id=1, source_target_pairs={{0,24},{4,28},{8,16},{12,20},{16,8},{20,12},{24,0},{28,4},{1,25},{... | collective-permute-start | bytes 393224 | tf_op jit(solution)/shard_map/ppermute | solution.py:553
  70.6 19.6 %collective-permute-done.12.refs_1_ = f32[128,256]{1,0:T(8,128)S(1)} collective-permute-done((f32[128,256]{1,0:T(8,128)S(1)}, f32[128,256]{1,0:T(8,128)S(1)}, u32[]{:S(2)}, u32[]{:S(2)}) %collective-permute-start.12) | collective-permute-done | bytes 131104 | tf_op jit(solution)/shard_map/ppermute | solution.py:553
  90.2 1.7 collective-permute-done.14.refs_3_
  92.0 0.1 collective-permute-start.15
  92.1 0.6 halve.3
  92.7 1.5 collective-permute-start.10
  94.3 0.6 halve.2
  94.9 1.6 collective-permute-start.7
  96.5 13.3 %chol_inverse.1 = (f32[256,256]{1,0:T(8,128)S(1)}, bf16[640,256]{1,0:T(8,128)(2,1)S(1)}, bf16[640,256]{1,0:T(8,128)(2,1)S(1)}) custom-call(s32[27]{0:T(128)S(1)} %stack.93.at, f32[128,256]{1,0:T(8,128)S(1)} %total.13.mine, f32[128,256]{1,0:T(8,128)S(1)} %collective-permute-done.15.beside, f32[640,256]{1,0:T(8,128)S(1)} %get-tuple-element.59.left), custom_call_target="tpu_custom_call" | custom-call | flops 4000000000 | bytes 655360 | tf_op jit(solution)/shard_map/chol_inverse/pallas_call | solution.py:336
  109.8 1.5 right_rows.1
  111.3 0.6 collective-permute-start.19
  111.9 0.5 collective-permute-start.16
  112.5 11.3 %collective-permute-done.19.y = f32[448,256]{1,0:T(8,128)S(1)} collective-permute-done((f32[448,256]{1,0:T(8,128)S(1)}, f32[448,256]{1,0:T(8,128)S(1)}, u32[]{:S(2)}, u32[]{:S(2)}) %collective-permute-start.19) | collective-permute-done | bytes 458784 | tf_op jit(solution)/shard_map/ppermute | solution.py:553
  123.7 0.7 join.3
  124.4 0.1 collective-permute-start.35
  124.5 0.7 join.2
  125.2 0.6 collective-permute-start.34
  125.7 0.5 collective-permute-start.20
  126.2 3.6 %collective-permute-done.22.refs_1_ = f32[8,256]{1,0:T(8,128)S(1)} collective-permute-done((f32[8,256]{1,0:T(8,128)S(1)}, f32[8,256]{1,0:T(8,128)S(1)}, u32[]{:S(2)}, u32[]{:S(2)}) %collective-permute-start.22) | collective-permute-done | bytes 8224 | tf_op jit(solution)/shard_map/ppermute | solution.py:553
  129.9 1.1 collective-permute-start.23
  131.0 3.4 %collective-permute-done.23.refs_1_ = f32[8,256]{1,0:T(8,128)S(1)} collective-permute-done((f32[8,256]{1,0:T(8,128)S(1)}, f32[8,256]{1,0:T(8,128)S(1)}, u32[]{:S(2)}, u32[]{:S(2)}) %collective-permute-start.23) | collective-permute-done | bytes 8224 | tf_op jit(solution)/shard_map/ppermute | solution.py:553
  134.5 1.2 collective-permute-done.24.refs_1_
  135.6 0.6 collective-permute-start.25
  136.2 1.5 collective-permute-start.26
  137.7 1.6 collective-permute-done.25.refs_1_
  139.3 1.5 collective-permute-start.27
  140.8 3.0 %collective-permute-done.27.refs_3_ = f32[8,256]{1,0:T(8,128)S(1)} collective-permute-done((f32[8,256]{1,0:T(8,128)S(1)}, f32[8,256]{1,0:T(8,128)S(1)}, u32[]{:S(2)}, u32[]{:S(2)}) %collective-permute-start.27) | collective-permute-done | bytes 8224 | tf_op jit(solution)/shard_map/ppermute | solution.py:553
  143.8 1.5 collective-permute-start.30
  145.4 0.6 collective-permute-start.28
  145.9 1.5 collective-permute-start.17
  147.5 17.7 %collective-permute-done.17.refs_0_ = f32[384,256]{1,0:T(8,128)S(1)} collective-permute-done((f32[384,256]{1,0:T(8,128)S(1)}, f32[384,256]{1,0:T(8,128)S(1)}, u32[]{:S(2)}, u32[]{:S(2)}) %collective-permute-start.17) | collective-permute-done | bytes 393248 | tf_op jit(solution)/shard_map/ppermute | solution.py:553
  165.2 0.5 collective-permute-start.18
  165.7 0.1 collective-permute-start.31
  165.8 0.4 collective-permute-start.29
  166.3 8.6 %final.4 = (f32[640,6912]{1,0:T(8,128)}, f32[640,6912]{1,0:T(8,128)}, f32[6912,256]{1,0:T(8,128)}) custom-call(s32[27]{0:T(128)S(1)} %stack.93.at, f32[512,256]{1,0:T(8,128)S(1)} %get-tuple-element.68.refs_0_, f32[512,256]{1,0:T(8,128)S(1)} %collective-permute-done.32.refs_1_, f32[512,256]{1,0:T(8,128)S(1)} %get-tuple-element.69.refs_2_, ...), custom_call_target="tpu_custom_call" | custom-call | flops 3523215360 | bytes 9175040 | tf_op jit(solution)/shard_map/final/pallas_call | solution.py:525
  174.9 9.2 %final.5 = (f32[640,6912]{1,0:T(8,128)}, f32[640,6912]{1,0:T(8,128)}, f32[6912,256]{1,0:T(8,128)}) custom-call(s32[27]{0:T(128)S(1)} %stack.93.at, f32[512,256]{1,0:T(8,128)S(1)} %get-tuple-element.68.refs_0_, f32[512,256]{1,0:T(8,128)S(1)} %collective-permute-done.32.refs_1_, ...), custom_call_target="tpu_custom_call", output_to_operand_aliasing={{0}: (14, {}), {1}: (15, {}), {2}: (16, {})} | custom-call | flops 3523215360 | bytes 9175040 | tf_op jit(solution)/shard_map/final/pallas_call | solution.py:525
  184.1 9.3 %final.6 = (f32[640,6912]{1,0:T(8,128)}, f32[640,6912]{1,0:T(8,128)}, f32[6912,256]{1,0:T(8,128)}) custom-call(s32[27]{0:T(128)S(1)} %stack.93.at, f32[512,256]{1,0:T(8,128)S(1)} %collective-permute-done.28.refs_0_, f32[512,256]{1,0:T(8,128)S(1)} %collective-permute-done.29.refs_1_, ...), custom_call_target="tpu_custom_call", output_to_operand_aliasing={{0}: (10, {}), {1}: (11, {}), {2}: (12, {})} | custom-call | flops 4026531840 | bytes 10485760 | tf_op jit(solution)/shard_map/final/pallas_call | solution.py:525
  193.4 8.2 %final.7 = (f32[640,6912]{1,0:T(8,128)}, f32[640,6912]{1,0:T(8,128)}, f32[6912,256]{1,0:T(8,128)}) custom-call(s32[27]{0:T(128)S(1)} %stack.93.at, f32[384,256]{1,0:T(8,128)S(1)} %collective-permute-done.17.refs_0_, f32[384,256]{1,0:T(8,128)S(1)} %collective-permute-done.18.refs_1_, ...), custom_call_target="tpu_custom_call", output_to_operand_aliasing={{0}: (10, {}), {1}: (11, {}), {2}: (12, {})} | custom-call | flops 3019898880 | bytes 7864320 | tf_op jit(solution)/shard_map/final/pallas_call | solution.py:525
  (44 shorter events, 0.2 us)
Async XLA Ops:
  10.4 12.7 %collective-permute-start = (f32[320,256]{1,0:T(8,128)S(1)}, f32[320,256]{1,0:T(8,128)S(1)}, u32[]{:S(2)}, u32[]{:S(2)}) collective-permute-start(f32[320,256]{1,0:T(8,128)S(1)} %get-tuple-element.44), channel_id=1, source_target_pairs={{0,1},{1,0},{2,3},{3,2},{4,5},{5,4},{6,7},{7,6},{8,9},{9,8},{10,11... | collective-permute-start | bytes 983048 | tf_op jit(solution)/shard_map/ppermute | solution.py:553
  23.1 37.8 %copy-start = (f32[320,7168]{1,0:T(8,128)}, f32[320,7168]{1,0:T(8,128)S(1)}, u32[]{:S(2)}) copy-start(f32[320,7168]{1,0:T(8,128)S(1)} %get-tuple-element.41.own.refs_11_.refs_7_) | copy-start | bytes 27525124
  23.2 13.6 %collective-permute-start.2 = (f32[160,256]{1,0:T(8,128)S(1)}, f32[160,256]{1,0:T(8,128)S(1)}, u32[]{:S(2)}, u32[]{:S(2)}) collective-permute-start(f32[160,256]{1,0:T(8,128)S(1)} %get-tuple-element.46.refs_0_), channel_id=1, source_target_pairs={{0,2},{1,3},{2,0},{3,1},{4,6},{5,7},{6,4},{7,5},{8,10},{9,11},{10,... | collective-permute-start | bytes 491528 | tf_op jit(solution)/shard_map/ppermute | solution.py:553
  25.8 14.4 %collective-permute-start.1 = (f32[160,256]{1,0:T(8,128)S(1)}, f32[160,256]{1,0:T(8,128)S(1)}, u32[]{:S(2)}, u32[]{:S(2)}) collective-permute-start(f32[160,256]{1,0:T(8,128)S(1)} %get-tuple-element.45.refs_0_), channel_id=1, source_target_pairs={{0,2},{1,3},{2,0},{3,1},{4,6},{5,7},{6,4},{7,5},{8,10},{9,11},{10,... | collective-permute-start | bytes 491528 | tf_op jit(solution)/shard_map/ppermute | solution.py:553
  36.8 7.1 %collective-permute-start.4 = (f32[160,256]{1,0:T(8,128)S(1)}, f32[160,256]{1,0:T(8,128)S(1)}, u32[]{:S(2)}, u32[]{:S(2)}) collective-permute-start(f32[160,256]{1,0:T(8,128)S(1)} %total.11.refs_1_), channel_id=1, source_target_pairs={{0,1},{1,0},{2,3},{3,2},{4,5},{5,4},{6,7},{7,6},{8,9},{9,8},{10,11... | collective-permute-start | bytes 491528 | tf_op jit(solution)/shard_map/ppermute | solution.py:553
  40.3 6.9 %collective-permute-start.3 = (f32[160,256]{1,0:T(8,128)S(1)}, f32[160,256]{1,0:T(8,128)S(1)}, u32[]{:S(2)}, u32[]{:S(2)}) collective-permute-start(f32[160,256]{1,0:T(8,128)S(1)} %total.10.refs_0_), channel_id=1, source_target_pairs={{0,1},{1,0},{2,3},{3,2},{4,5},{5,4},{6,7},{7,6},{8,9},{9,8},{10,11... | collective-permute-start | bytes 491528 | tf_op jit(solution)/shard_map/ppermute | solution.py:553
  52.1 3.9 %collective-permute-start.8 = (f32[1792,256]{1,0:T(8,128)S(1)}, f32[1792,256]{1,0:T(8,128)S(1)}, u32[]{:S(2)}, u32[]{:S(2)}) collective-permute-start(f32[1792,256]{1,0:T(8,128)S(1)} %w_send.3), channel_id=1, source_target_pairs={{0,4},{4,0},{8,12},{12,8},{16,20},{20,16},{24,28},{28,24},{1,5},{5... | collective-permute-start | bytes 5505032 | tf_op jit(solution)/shard_map/ppermute | solution.py:553
  55.4 5.5 %collective-permute-start.5 = (f32[1792,256]{1,0:T(8,128)S(1)}, f32[1792,256]{1,0:T(8,128)S(1)}, u32[]{:S(2)}, u32[]{:S(2)}) collective-permute-start(f32[1792,256]{1,0:T(8,128)S(1)} %w_send.2), channel_id=1, source_target_pairs={{0,4},{4,0},{8,12},{12,8},{16,20},{20,16},{24,28},{28,24},{1,5},{5... | collective-permute-start | bytes 5505032 | tf_op jit(solution)/shard_map/ppermute | solution.py:553
  59.2 32.8 %collective-permute-start.9 = (f32[896,256]{1,0:T(8,128)S(1)}, f32[896,256]{1,0:T(8,128)S(1)}, u32[]{:S(2)}, u32[]{:S(2)}) collective-permute-start(f32[896,256]{1,0:T(8,128)S(1)} %get-tuple-element.54), channel_id=1, source_target_pairs={{0,16},{4,20},{8,24},{12,28},{16,0},{20,4},{24,8},{28,12},{1,17},{... | collective-permute-start | bytes 2752520 | tf_op jit(solution)/shard_map/ppermute | solution.py:553
  64.1 30.1 %collective-permute-start.6 = (f32[896,256]{1,0:T(8,128)S(1)}, f32[896,256]{1,0:T(8,128)S(1)}, u32[]{:S(2)}, u32[]{:S(2)}) collective-permute-start(f32[896,256]{1,0:T(8,128)S(1)} %get-tuple-element.50), channel_id=1, source_target_pairs={{0,8},{4,12},{8,0},{12,4},{16,24},{20,28},{24,16},{28,20},{1,9},{5... | collective-permute-start | bytes 2752520 | tf_op jit(solution)/shard_map/ppermute | solution.py:553
  65.7 1.3 collective-permute-start.11
  67.1 23.2 %collective-permute-start.12 = (f32[128,256]{1,0:T(8,128)S(1)}, f32[128,256]{1,0:T(8,128)S(1)}, u32[]{:S(2)}, u32[]{:S(2)}) collective-permute-start(f32[128,256]{1,0:T(8,128)S(1)} %total.12.refs_0_), channel_id=1, source_target_pairs={{0,8},{4,12},{8,0},{12,4},{16,24},{20,28},{24,16},{28,20},{1,9},{5... | collective-permute-start | bytes 393224 | tf_op jit(solution)/shard_map/ppermute | solution.py:553
  67.7 22.6 %collective-permute-start.13 = (f32[128,256]{1,0:T(8,128)S(1)}, f32[128,256]{1,0:T(8,128)S(1)}, u32[]{:S(2)}, u32[]{:S(2)}) collective-permute-start(f32[128,256]{1,0:T(8,128)S(1)} %total.12.refs_0_), channel_id=1, source_target_pairs={{0,16},{4,20},{8,24},{12,28},{16,0},{20,4},{24,8},{28,12},{1,17},{... | collective-permute-start | bytes 393224 | tf_op jit(solution)/shard_map/ppermute | solution.py:553
  68.1 23.8 %collective-permute-start.14 = (f32[128,256]{1,0:T(8,128)S(1)}, f32[128,256]{1,0:T(8,128)S(1)}, u32[]{:S(2)}, u32[]{:S(2)}) collective-permute-start(f32[128,256]{1,0:T(8,128)S(1)} %total.12.refs_0_), channel_id=1, source_target_pairs={{0,24},{4,28},{8,16},{12,20},{16,8},{20,12},{24,0},{28,4},{1,25},{... | collective-permute-start | bytes 393224 | tf_op jit(solution)/shard_map/ppermute | solution.py:553
  92.0 4.5 %collective-permute-start.15 = (f32[128,256]{1,0:T(8,128)S(1)}, f32[128,256]{1,0:T(8,128)S(1)}, u32[]{:S(2)}, u32[]{:S(2)}) collective-permute-start(f32[128,256]{1,0:T(8,128)S(1)} %total.13.mine), channel_id=1, source_target_pairs={{0,4},{4,0},{8,12},{12,8},{16,20},{20,16},{24,28},{28,24},{1,5},{5... | collective-permute-start | bytes 393224 | tf_op jit(solution)/shard_map/ppermute | solution.py:553
  92.7 17.1 %collective-permute-start.10 = (f32[448,256]{1,0:T(8,128)S(1)}, f32[448,256]{1,0:T(8,128)S(1)}, u32[]{:S(2)}, u32[]{:S(2)}) collective-permute-start(f32[448,256]{1,0:T(8,128)S(1)} %get-tuple-element.56), channel_id=1, source_target_pairs={{0,8},{4,12},{8,0},{12,4},{16,24},{20,28},{24,16},{28,20},{1,9},{5... | collective-permute-start | bytes 1376264 | tf_op jit(solution)/shard_map/ppermute | solution.py:553
  94.9 14.9 %collective-permute-start.7 = (f32[448,256]{1,0:T(8,128)S(1)}, f32[448,256]{1,0:T(8,128)S(1)}, u32[]{:S(2)}, u32[]{:S(2)}) collective-permute-start(f32[448,256]{1,0:T(8,128)S(1)} %get-tuple-element.52), channel_id=1, source_target_pairs={{0,16},{4,20},{8,24},{12,28},{16,0},{20,4},{24,8},{28,12},{1,17},{... | collective-permute-start | bytes 1376264 | tf_op jit(solution)/shard_map/ppermute | solution.py:553
  96.5 69.7 %slice-start = ((s8[9175040]{0:T(1024)(128)(4,1)}), s8[4194304]{0:T(1024)(128)(4,1)S(1)}, s32[]{:S(2)}) async-start(s8[9175040]{0:T(1024)(128)(4,1)} %bitcast.21), calls=%async_computation | async-start | bytes 8388608
  96.5 69.7 %slice-start.1 = ((s8[9175040]{0:T(1024)(128)(4,1)}), s8[4194304]{0:T(1024)(128)(4,1)S(1)}, s32[]{:S(2)}) async-start(s8[9175040]{0:T(1024)(128)(4,1)} %bitcast.21), calls=%async_computation.1 | async-start | bytes 8388608
  96.5 69.7 %slice-start.2 = ((s8[9175040]{0:T(1024)(128)(4,1)}), s8[786432]{0:T(1024)(128)(4,1)S(1)}, s32[]{:S(2)}) async-start(s8[9175040]{0:T(1024)(128)(4,1)} %bitcast.21), calls=%async_computation.2 | async-start | bytes 1572864
  111.3 12.4 %collective-permute-start.19 = (f32[448,256]{1,0:T(8,128)S(1)}, f32[448,256]{1,0:T(8,128)S(1)}, u32[]{:S(2)}, u32[]{:S(2)}) collective-permute-start(f32[448,256]{1,0:T(8,128)S(1)} %get-tuple-element.63.x), channel_id=1, source_target_pairs={{0,8},{4,12},{8,0},{12,4},{16,24},{20,28},{24,16},{28,20},{1,9},{5... | collective-permute-start | bytes 1376264 | tf_op jit(solution)/shard_map/ppermute | solution.py:553
  111.9 12.6 %collective-permute-start.16 = (f32[448,256]{1,0:T(8,128)S(1)}, f32[448,256]{1,0:T(8,128)S(1)}, u32[]{:S(2)}, u32[]{:S(2)}) collective-permute-start(f32[448,256]{1,0:T(8,128)S(1)} %get-tuple-element.61.x), channel_id=1, source_target_pairs={{0,16},{4,20},{8,24},{12,28},{16,0},{20,4},{24,8},{28,12},{1,17},{... | collective-permute-start | bytes 1376264 | tf_op jit(solution)/shard_map/ppermute | solution.py:553
  124.4 20.9 %collective-permute-start.35 = (f32[384,256]{1,0:T(8,128)S(1)}, f32[384,256]{1,0:T(8,128)S(1)}, u32[]{:S(2)}, u32[]{:S(2)}) collective-permute-start(f32[384,256]{1,0:T(8,128)S(1)} %get-tuple-element.64.refs_6_), channel_id=1, source_target_pairs={{0,4},{4,0},{8,12},{12,8},{16,20},{20,16},{24,28},{28,24},{1,5},{5... | collective-permute-start | bytes 1179656 | tf_op jit(solution)/shard_map/ppermute | solution.py:553
  125.2 20.7 %collective-permute-start.34 = (f32[384,256]{1,0:T(8,128)S(1)}, f32[384,256]{1,0:T(8,128)S(1)}, u32[]{:S(2)}, u32[]{:S(2)}) collective-permute-start(f32[384,256]{1,0:T(8,128)S(1)} %get-tuple-element.62.refs_4_), channel_id=1, source_target_pairs={{0,4},{4,0},{8,12},{12,8},{16,20},{20,16},{24,28},{28,24},{1,5},{5... | collective-permute-start | bytes 1179656 | tf_op jit(solution)/shard_map/ppermute | solution.py:553
  125.7 20.2 %collective-permute-start.20 = (f32[384,256]{1,0:T(8,128)S(1)}, f32[384,256]{1,0:T(8,128)S(1)}, u32[]{:S(2)}, u32[]{:S(2)}) collective-permute-start(f32[384,256]{1,0:T(8,128)S(1)} %get-tuple-element.64.refs_6_), channel_id=1, source_target_pairs={{0,16},{4,20},{8,24},{12,28},{16,0},{20,4},{24,8},{28,12},{1,17},{... | collective-permute-start | bytes 1179656 | tf_op jit(solution)/shard_map/ppermute | solution.py:553
  126.2 3.7 %collective-permute-start.22 = (f32[8,256]{1,0:T(8,128)S(1)}, f32[8,256]{1,0:T(8,128)S(1)}, u32[]{:S(2)}, u32[]{:S(2)}) collective-permute-start(f32[8,256]{1,0:T(8,128)S(1)} %get-tuple-element.65.refs_0_), channel_id=1, source_target_pairs={{0,1},{1,0},{2,3},{3,2},{4,5},{5,4},{6,7},{7,6},{8,9},{9,8},{10,11... | collective-permute-start | bytes 24584 | tf_op jit(solution)/shard_map/ppermute | solution.py:553
  129.9 4.5 %collective-permute-start.23 = (f32[8,256]{1,0:T(8,128)S(1)}, f32[8,256]{1,0:T(8,128)S(1)}, u32[]{:S(2)}, u32[]{:S(2)}) collective-permute-start(f32[8,256]{1,0:T(8,128)S(1)} %total.14.refs_0_), channel_id=1, source_target_pairs={{0,2},{1,3},{2,0},{3,1},{4,6},{5,7},{6,4},{7,5},{8,10},{9,11},{10,... | collective-permute-start | bytes 24584 | tf_op jit(solution)/shard_map/ppermute | solution.py:553
  134.5 1.2 collective-permute-start.24
  135.6 3.7 %collective-permute-start.25 = (f32[8,256]{1,0:T(8,128)S(1)}, f32[8,256]{1,0:T(8,128)S(1)}, u32[]{:S(2)}, u32[]{:S(2)}) collective-permute-start(f32[8,256]{1,0:T(8,128)S(1)} %total.16.refs_0_.refs_8_), channel_id=1, source_target_pairs={{0,8},{4,12},{8,0},{12,4},{16,24},{20,28},{24,16},{28,20},{1,9},{5... | collective-permute-start | bytes 24584 | tf_op jit(solution)/shard_map/ppermute | solution.py:553
  136.2 4.6 %collective-permute-start.26 = (f32[8,256]{1,0:T(8,128)S(1)}, f32[8,256]{1,0:T(8,128)S(1)}, u32[]{:S(2)}, u32[]{:S(2)}) collective-permute-start(f32[8,256]{1,0:T(8,128)S(1)} %total.16.refs_0_.refs_8_), channel_id=1, source_target_pairs={{0,16},{4,20},{8,24},{12,28},{16,0},{20,4},{24,8},{28,12},{1,17},{... | collective-permute-start | bytes 24584 | tf_op jit(solution)/shard_map/ppermute | solution.py:553
  139.3 4.5 %collective-permute-start.27 = (f32[8,256]{1,0:T(8,128)S(1)}, f32[8,256]{1,0:T(8,128)S(1)}, u32[]{:S(2)}, u32[]{:S(2)}) collective-permute-start(f32[8,256]{1,0:T(8,128)S(1)} %total.16.refs_0_.refs_8_), channel_id=1, source_target_pairs={{0,24},{4,28},{8,16},{12,20},{16,8},{20,12},{24,0},{28,4},{1,25},{... | collective-permute-start | bytes 24584 | tf_op jit(solution)/shard_map/ppermute | solution.py:553
  140.8 24.4 %collective-permute-start.33 = (f32[512,256]{1,0:T(8,128)S(1)}, f32[512,256]{1,0:T(8,128)S(1)}, u32[]{:S(2)}, u32[]{:S(2)}) collective-permute-start(f32[512,256]{1,0:T(8,128)S(1)} %get-tuple-element.69.refs_2_), channel_id=1, source_target_pairs={{0,4},{4,0},{8,12},{12,8},{16,20},{20,16},{24,28},{28,24},{1,5},{5... | collective-permute-start | bytes 1572872 | tf_op jit(solution)/shard_map/ppermute | solution.py:553
  143.8 21.9 %collective-permute-start.30 = (f32[512,256]{1,0:T(8,128)S(1)}, f32[512,256]{1,0:T(8,128)S(1)}, u32[]{:S(2)}, u32[]{:S(2)}) collective-permute-start(f32[512,256]{1,0:T(8,128)S(1)} %get-tuple-element.69.refs_2_), channel_id=1, source_target_pairs={{0,16},{4,20},{8,24},{12,28},{16,0},{20,4},{24,8},{28,12},{1,17},{... | collective-permute-start | bytes 1572872 | tf_op jit(solution)/shard_map/ppermute | solution.py:553
  145.4 20.4 %collective-permute-start.28 = (f32[512,256]{1,0:T(8,128)S(1)}, f32[512,256]{1,0:T(8,128)S(1)}, u32[]{:S(2)}, u32[]{:S(2)}) collective-permute-start(f32[512,256]{1,0:T(8,128)S(1)} %get-tuple-element.68.refs_0_), channel_id=1, source_target_pairs={{0,8},{4,12},{8,0},{12,4},{16,24},{20,28},{24,16},{28,20},{1,9},{5... | collective-permute-start | bytes 1572872 | tf_op jit(solution)/shard_map/ppermute | solution.py:553
  145.9 20.3 %collective-permute-start.32 = (f32[512,256]{1,0:T(8,128)S(1)}, f32[512,256]{1,0:T(8,128)S(1)}, u32[]{:S(2)}, u32[]{:S(2)}) collective-permute-start(f32[512,256]{1,0:T(8,128)S(1)} %get-tuple-element.68.refs_0_), channel_id=1, source_target_pairs={{0,4},{4,0},{8,12},{12,8},{16,20},{20,16},{24,28},{28,24},{1,5},{5... | collective-permute-start | bytes 1572872 | tf_op jit(solution)/shard_map/ppermute | solution.py:553
  145.9 19.3 %collective-permute-start.17 = (f32[384,256]{1,0:T(8,128)S(1)}, f32[384,256]{1,0:T(8,128)S(1)}, u32[]{:S(2)}, u32[]{:S(2)}) collective-permute-start(f32[384,256]{1,0:T(8,128)S(1)} %get-tuple-element.62.refs_4_), channel_id=1, source_target_pairs={{0,8},{4,12},{8,0},{12,4},{16,24},{20,28},{24,16},{28,20},{1,9},{5... | collective-permute-start | bytes 1179656 | tf_op jit(solution)/shard_map/ppermute | solution.py:553
  165.2 28.2 %collective-permute-start.21 = (f32[384,256]{1,0:T(8,128)S(1)}, f32[384,256]{1,0:T(8,128)S(1)}, u32[]{:S(2)}, u32[]{:S(2)}) collective-permute-start(f32[384,256]{1,0:T(8,128)S(1)} %collective-permute-done.20.refs_2_), channel_id=1, source_target_pairs={{0,4},{4,0},{8,12},{12,8},{16,20},{20,16},{24,28},{28,24},{1,5},{5... | collective-permute-start | bytes 1179656 | tf_op jit(solution)/shard_map/ppermute | solution.py:553
  165.2 28.2 %collective-permute-start.18 = (f32[384,256]{1,0:T(8,128)S(1)}, f32[384,256]{1,0:T(8,128)S(1)}, u32[]{:S(2)}, u32[]{:S(2)}) collective-permute-start(f32[384,256]{1,0:T(8,128)S(1)} %collective-permute-done.17.refs_0_), channel_id=1, source_target_pairs={{0,4},{4,0},{8,12},{12,8},{16,20},{20,16},{24,28},{28,24},{1,5},{5... | collective-permute-start | bytes 1179656 | tf_op jit(solution)/shard_map/ppermute | solution.py:553
  165.7 18.4 %collective-permute-start.31 = (f32[512,256]{1,0:T(8,128)S(1)}, f32[512,256]{1,0:T(8,128)S(1)}, u32[]{:S(2)}, u32[]{:S(2)}) collective-permute-start(f32[512,256]{1,0:T(8,128)S(1)} %collective-permute-done.30.refs_2_), channel_id=1, source_target_pairs={{0,4},{4,0},{8,12},{12,8},{16,20},{20,16},{24,28},{28,24},{1,5},{5... | collective-permute-start | bytes 1572872 | tf_op jit(solution)/shard_map/ppermute | solution.py:553
  165.8 18.3 %collective-permute-start.29 = (f32[512,256]{1,0:T(8,128)S(1)}, f32[512,256]{1,0:T(8,128)S(1)}, u32[]{:S(2)}, u32[]{:S(2)}) collective-permute-start(f32[512,256]{1,0:T(8,128)S(1)} %collective-permute-done.28.refs_0_), channel_id=1, source_target_pairs={{0,4},{4,0},{8,12},{12,8},{16,20},{20,16},{24,28},{28,24},{1,5},{5... | collective-permute-start | bytes 1572872 | tf_op jit(solution)/shard_map/ppermute | solution.py:553

commit v7 on v5

--- a/solution.py
+++ b/solution.py
@@ -37,9 +37,12 @@
     return hi, lo
 
 
+def dot(a, b, dims):
+    return lax.dot_general(a, b, dims, preferred_element_type=F32)
+
+
 def dot3(ah, al, bh, bl, dims):
-    d = functools.partial(lax.dot_general, dimension_numbers=dims, preferred_element_type=F32)
-    return d(ah, bh) + (d(ah, bl) + d(al, bh))
+    return dot(ah, bh, dims) + (dot(ah, bl, dims) + dot(al, bh, dims))
 
 
 def dot_high(a, b, dims):
@@ -376,19 +379,23 @@
     )(at, ka, ga, kb, gb, x)
 
 
-def join_kernel(place, at, x, y, out):
+def join_kernel(place, at, x, y, both, *parts):
     n, t = x.shape[0], at[place]
-    out[pl.ds(pl.multiple_of(t * n, GROUP), n), :] = x[...]
-    out[pl.ds(pl.multiple_of((1 - t) * n, GROUP), n), :] = y[...]
-
-
-def join(at, place, x, y):
+    both[pl.ds(pl.multiple_of(t * n, GROUP), n), :] = x[...]
+    both[pl.ds(pl.multiple_of((1 - t) * n, GROUP), n), :] = y[...]
+    top = 0
+    for out in parts:
+        out[...] = both[top : top + out.shape[0], :]
+        top += out.shape[0]
+
+
+def join(at, place, x, y, sizes):
     rows, rank = x.shape
     return pl.pallas_call(
         functools.partial(join_kernel, place),
         in_specs=[SMEM, VMEM, VMEM],
-        out_specs=VMEM,
-        out_shape=jax.ShapeDtypeStruct((2 * rows, rank), F32),
+        out_specs=[VMEM] * (1 + len(sizes)),
+        out_shape=[jax.ShapeDtypeStruct((n, rank), F32) for n in [2 * rows, *sizes]],
         compiler_params=params(6),
         cost_estimate=cost(rows * rank, 16 * rows * rank),
         name="join",
@@ -415,54 +422,97 @@
     )(at, x, y)
 
 
-def final_kernel(place, count, total_cols, factor, at, *refs):
-    pieces = refs[:count]
-    squares, oh, ol, own, other = refs[count : count + 5]
-    update, momentum, new_right, rh, rl, nh, nl = refs[-7:]
-    u = pl.program_id(0)
-    half, width = own.shape[0], new_right.shape[0]
-    for k in range(count):
-
-        @pl.when(u == k)
-        def _(k=k):
-            right = pieces[k][...]
-            scale = jnp.sqrt(squares[0:1, :] / total_cols + 1e-06)
-            scaled = right / scale
-            new_right[...] = scaled
-            rh[...], rl[...] = split(right)
-            nh[...], nl[...] = split(scaled)
-
-    part = pl.ds(pl.multiple_of(at[place + u] * width, LANES), width)
-    for h, buffer in enumerate((own, other)):
-        rows = pl.ds(pl.multiple_of(at[h] * half, GROUP), half)
-        a, b = oh[h * half : (h + 1) * half, :], ol[h * half : (h + 1) * half, :]
-        momentum[rows, :] = buffer[:, part] - 0.05 * dot3(a, b, rh[...], rl[...], NT)
-        update[rows, :] = factor * dot3(a, b, nh[...], nl[...], NT)
-
-
-def final(at, place, pieces, squares, oh, ol, own, other, cols, total_rows, total_cols, before):
-    rows = oh.shape[0]
-    unit, rank = pieces[0].shape
-    count = len(pieces)
-    wide = pl.BlockSpec((rows, unit), lambda u, at: (0, at[place + u]))
+SLOTS = 2
+
+
+def final_kernel(place, group, unit, total_cols, factor, at, *refs):
+    pieces = refs[:4]
+    squares, oh, ol, own, other = refs[4:9]
+    update, momentum, new_right, stage_m, stage_u, stage_r, lh, ll, high, low, sems = refs[-11:]
+    start, count = group
+    n, rows, half = count * LANES, oh.shape[0], own.shape[0]
+    blocks = update.shape[1] // LANES
+    halves = [pl.ds(pl.multiple_of(at[h] * half, GROUP), half) for h in range(2)]
+    scale = jnp.sqrt(squares[0:1, :] / total_cols + 1e-06)
+    lh[:rows, :] = oh[...]
+    ll[:rows, :] = ol[...]
+    lh[rows:, :], ll[rows:, :] = split((oh[...].astype(F32) + ol[...].astype(F32)) * (factor / scale))
+
+    def each_copy(k, act):
+        slot = lax.rem(k, SLOTS)
+        first = at[place + k] * (unit // LANES) + start
+        for j in range(count):
+
+            @pl.when(first + j < blocks)
+            def _(j=j):
+                here = pl.ds(j * LANES, LANES)
+                there = pl.ds(pl.multiple_of((first + j) * LANES, LANES), LANES)
+                for i, (a, b) in enumerate(
+                    (
+                        (stage_m.at[slot, :, here], momentum.at[:, there]),
+                        (stage_u.at[slot, :, here], update.at[:, there]),
+                        (stage_r.at[slot, here, :], new_right.at[there, :]),
+                    )
+                ):
+                    act(pltpu.make_async_copy(a, b, sems.at[i, slot, j]))
+
+    def body(k, _):
+        slot = lax.rem(k, SLOTS)
+
+        @pl.when(k >= SLOTS)
+        def _():
+            each_copy(k - SLOTS, lambda copy: copy.wait())
+
+        for i, piece in enumerate(pieces):
+
+            @pl.when(k == i)
+            def _(piece=piece):
+                right = piece[...]
+                high[...], low[...] = split(right)
+                stage_r[slot] = right / scale
+
+        part = pl.ds(pl.multiple_of(at[place + k] * unit + start * LANES, LANES), n)
+        value = dot(lh[...], high[...], NT) + dot(ll[...], high[...], NT)
+        rest = dot(lh[rows:, :], low[...], NT)
+        for h, buffer in enumerate((own, other)):
+            top = h * half
+            stage_m[slot, halves[h], :] = buffer[:, part] - 0.05 * value[top : top + half]
+            stage_u[slot, halves[h], :] = value[rows + top : rows + top + half] + rest[top : top + half]
+        each_copy(k, lambda copy: copy.start())
+        return 0
+
+    lax.fori_loop(0, 4, body, 0)
+    for k in range(4 - SLOTS, 4):
+        each_copy(k, lambda copy: copy.wait())
+
+
+def final(at, place, group, unit, pieces, squares, oh, ol, own, other, sizes, before):
+    rows, rank = oh.shape
+    cols, total_rows, total_cols = sizes
     factor = (total_rows / rank) ** 0.5
-    return pl.pallas_call(
-        functools.partial(final_kernel, place, count, total_cols, factor),
-        grid_spec=pltpu.PrefetchScalarGridSpec(
-            num_scalar_prefetch=1,
-            grid=(count,),
-            in_specs=[VMEM] * (count + 5) + [HBM] * len(before),
-            out_specs=[wide, wide, pl.BlockSpec((unit, rank), lambda u, at: (at[place + u], 0))],
-            scratch_shapes=[pltpu.VMEM((unit, rank), BF16)] * 4,
-        ),
+    n = group[1] * LANES
+    return pl.pallas_call(
+        functools.partial(final_kernel, place, group, unit, total_cols, factor),
+        in_specs=[SMEM] + [VMEM] * 9 + [HBM] * len(before),
+        out_specs=[HBM] * 3,
         out_shape=[
             jax.ShapeDtypeStruct((rows, cols), F32),
             jax.ShapeDtypeStruct((rows, cols), F32),
             jax.ShapeDtypeStruct((cols, rank), F32),
         ],
-        input_output_aliases={count + 6 + i: i for i in range(len(before))},
-        compiler_params=params(20),
-        cost_estimate=cost(12 * count * rows * unit * rank, 4 * count * unit * (2 * rows + 2 * rank)),
+        scratch_shapes=[
+            pltpu.VMEM((SLOTS, rows, n), F32),
+            pltpu.VMEM((SLOTS, rows, n), F32),
+            pltpu.VMEM((SLOTS, n, rank), F32),
+            pltpu.VMEM((2 * rows, rank), BF16),
+            pltpu.VMEM((2 * rows, rank), BF16),
+            pltpu.VMEM((n, rank), BF16),
+            pltpu.VMEM((n, rank), BF16),
+            pltpu.SemaphoreType.DMA((3, SLOTS, group[1])),
+        ],
+        input_output_aliases={10 + i: i for i in range(len(before))},
+        compiler_params=params(28),
+        cost_estimate=cost(48 * rows * n * rank, 32 * rows * n),
         name="final",
     )(at, *pieces, squares, oh, ol, own, other, *before)
 
@@ -572,19 +622,26 @@
     squares = total(squares, got)
     squares = spread_sum(squares, bits)
 
-    near, far = [], []
+    blocks = unit // LANES
+    groups = ((0, blocks - blocks // 2), (blocks - blocks // 2, blocks // 2))
+    near, far = [], ([], [])
     for h, (order, x) in enumerate(zip(orders, right)):
+        parts = [x]
         for b in order[:0:-1]:
             y = swap(x, "dp", b)
-            x = join(at, bit_at[h][b], x, y)
-        y = swap(x, "dp", order[0])
-        near += [x, swap(x, "dp", 0)]
-        far += [y, swap(y, "dp", 0)]
-
-    outs = ()
-    for place, data in ((near_at, near), (far_at, far)):
-        sizes = (cols, rows * n_dp, cols * n_tp)
-        outs = final(at, place, data, squares, oh, ol, *held, *sizes, outs)
+            last = 2 * x.shape[0] == unit
+            x, *parts = join(
+                at, bit_at[h][b], x, y, [count * LANES for _, count in groups] if last else []
+            )
+        for g, part in enumerate(parts):
+            y = swap(part, "dp", order[0])
+            far[g].extend([y, swap(y, "dp", 0)])
+        near.extend([x, swap(x, "dp", 0)])
+
+    same = (squares, oh, ol, *held, (cols, rows * n_dp, cols * n_tp))
+    outs = final(at, near_at, (0, blocks), unit, near, *same, ())
+    for g in range(2):
+        outs = final(at, far_at, groups[g], unit, far[g], *same, outs)
     return tuple(outs)
 
 

time: 194 us -> 192 us (0.990)
  waiting for transfers between devices: 86.8 us -> 84.4 us
    ppermute x30 -> x34, waiting for transfers between devices: 86.8 us -> 84.4 us  [swap(): return lax.ppermute(x, axis, [(i, i ^ mask) for i in range(n)])]
    pallas_call x2 -> x3, Pallas kernels: 27.1 us -> 26.9 us  [final(): pl.pallas_call(functools.partial(final_kernel, place, group, unit, total_...]
    ppermute x30 -> x34, starting transfers between devices: 27.9 us -> 28.2 us  [swap(): return lax.ppermute(x, axis, [(i, i ^ mask) for i in range(n)])]
  transfers between devices with their start and end apart: 30 -> 34, of which waited for: 16 -> 14; matrix products, arithmetic and copies ran while one was open for 0% -> 0% of each run, Pallas kernels for 25% -> 29%
where the time goes in v7:
time: 192 us
  waiting for transfers between devices  84.4 us (44%)
  Pallas kernels  78.3 us (41%)
  starting transfers between devices  28.2 us (15%)
    ppermute x34, waiting for transfers between devices, swap(): return lax.ppermute(x, axis, [(i, i ^ mask) for i in range(n)])  84.4 us
    ppermute x34, starting transfers between devices, swap(): return lax.ppermute(x, axis, [(i, i ^ mask) for i in range(n)])  28.2 us
    pallas_call x3, Pallas kernels, final(): pl.pallas_call(functools.partial(final_kernel, place, group, unit, total_...  26.9 us
    pallas_call x2, Pallas kernels, left_half(): pl.pallas_call(functools.partial(left_kernel, which), in_specs=[SMEM, HBM...  19.2 us
    pallas_call x1, Pallas kernels, chol_inverse(): pl.pallas_call(functools.partial(chol_kernel, place), in_specs=[SMEM] + [...  13.3 us
    pallas_call x2, Pallas kernels, w_keep(): pl.pallas_call(functools.partial(w_keep_kernel, place), grid_spec=pltpu.P...  6.62 us
    pallas_call x2, Pallas kernels, w_send(): pl.pallas_call(functools.partial(w_send_kernel, place), grid_spec=pltpu.P...  6.33 us
  transfers between devices with their start and end apart: 34, of which 14 were waited for; matrix products, arithmetic and copies ran while one was open for 0% of the time, Pallas kernels for 29%

profile of v7, /device:TPU:0, one launch (start us, length us, event | category | flops | bytes accessed | tf_op | source)
XLA Modules:
  0.0 192.1 jit_solution(2660248426375448261)
XLA Ops:
  0.7 0.1 stack.93.at
  0.8 9.6 %left_half.3 = (f32[320,7168]{1,0:T(8,128)S(1)}, f32[320,256]{1,0:T(8,128)S(1)}) custom-call(s32[27]{0:T(128)S(1)} %stack.93.at, f32[640,6912]{1,0:T(8,128)} %g.3, f32[640,6912]{1,0:T(8,128)} %m.3, f32[6912,256]{1,0:T(8,128)} %r.3), custom_call_target="tpu_custom_call" | custom-call | flops 3397386240 | bytes 24772608 | tf_op jit(solution)/shard_map/left_half/pallas_call | solution.py:99
  10.4 3.1 %collective-permute-start = (f32[320,256]{1,0:T(8,128)S(1)}, f32[320,256]{1,0:T(8,128)S(1)}, u32[]{:S(2)}, u32[]{:S(2)}) collective-permute-start(f32[320,256]{1,0:T(8,128)S(1)} %get-tuple-element.43), channel_id=1, source_target_pairs={{0,1},{1,0},{2,3},{3,2},{4,5},{5,4},{6,7},{7,6},{8,9},{9,8},{10,11... | collective-permute-start | bytes 983048 | tf_op jit(solution)/shard_map/ppermute | solution.py:531
  13.5 9.6 %left_half.2 = (f32[320,7168]{1,0:T(8,128)S(1)}, f32[320,256]{1,0:T(8,128)S(1)}) custom-call(s32[27]{0:T(128)S(1)} %stack.93.at, f32[640,6912]{1,0:T(8,128)} %g.3, f32[640,6912]{1,0:T(8,128)} %m.3, f32[6912,256]{1,0:T(8,128)} %r.3), custom_call_target="tpu_custom_call" | custom-call | flops 3397386240 | bytes 24772608 | tf_op jit(solution)/shard_map/left_half/pallas_call | solution.py:99
  23.1 0.0 copy-start
  23.1 0.0 collective-permute-done.refs_1_
  23.2 2.7 %collective-permute-start.2 = (f32[160,256]{1,0:T(8,128)S(1)}, f32[160,256]{1,0:T(8,128)S(1)}, u32[]{:S(2)}, u32[]{:S(2)}) collective-permute-start(f32[160,256]{1,0:T(8,128)S(1)} %get-tuple-element.45.refs_0_), channel_id=1, source_target_pairs={{0,2},{1,3},{2,0},{3,1},{4,6},{5,7},{6,4},{7,5},{8,10},{9,11},{10,... | collective-permute-start | bytes 491528 | tf_op jit(solution)/shard_map/ppermute | solution.py:531
  25.8 0.3 collective-permute-start.1
  26.2 10.6 %collective-permute-done.2.refs_1_ = f32[160,256]{1,0:T(8,128)S(1)} collective-permute-done((f32[160,256]{1,0:T(8,128)S(1)}, f32[160,256]{1,0:T(8,128)S(1)}, u32[]{:S(2)}, u32[]{:S(2)}) %collective-permute-start.2) | collective-permute-done | bytes 163872 | tf_op jit(solution)/shard_map/ppermute | solution.py:531
  36.8 0.9 collective-permute-start.4
  37.7 2.6 %collective-permute-done.1.refs_1_ = f32[160,256]{1,0:T(8,128)S(1)} collective-permute-done((f32[160,256]{1,0:T(8,128)S(1)}, f32[160,256]{1,0:T(8,128)S(1)}, u32[]{:S(2)}, u32[]{:S(2)}) %collective-permute-start.1) | collective-permute-done | bytes 163872 | tf_op jit(solution)/shard_map/ppermute | solution.py:531
  40.3 0.1 collective-permute-start.3
  40.3 3.6 %collective-permute-done.4.refs_3_ = f32[160,256]{1,0:T(8,128)S(1)} collective-permute-done((f32[160,256]{1,0:T(8,128)S(1)}, f32[160,256]{1,0:T(8,128)S(1)}, u32[]{:S(2)}, u32[]{:S(2)}) %collective-permute-start.4) | collective-permute-done | bytes 163872 | tf_op jit(solution)/shard_map/ppermute | solution.py:531
  43.9 3.3 %collective-permute-done.3.refs_2_ = f32[160,256]{1,0:T(8,128)S(1)} collective-permute-done((f32[160,256]{1,0:T(8,128)S(1)}, f32[160,256]{1,0:T(8,128)S(1)}, u32[]{:S(2)}, u32[]{:S(2)}) %collective-permute-start.3) | collective-permute-done | bytes 163872 | tf_op jit(solution)/shard_map/ppermute | solution.py:531
  47.2 1.7 gram_of.1
  48.9 3.2 %w_send.3 = f32[1792,256]{1,0:T(8,128)S(1)} custom-call(s32[27]{0:T(128)S(1)} %stack.93.at, f32[320,7168]{1,0:T(8,128)S(1)} %get-tuple-element.40.own.refs_7_, f32[320,7168]{1,0:T(8,128)S(1)} %get-tuple-element.41.other.refs_8_, bf16[640,256]{1,0:T(8,128)(2,1)S(1)} %get-tuple-element.46.lh, bf16[640,256]{1,0:T(8,128)(2,1)S(1)} %get-tuple-element.47.ll), custom_call_target="tpu_custom_call" | custom-call | flops 1761607680 | bytes 1835008 | tf_op jit(solution)/shard_map/w_send/pallas_call | solution.py:206
  52.1 0.1 collective-permute-start.8
  52.1 3.2 %w_send.2 = f32[1792,256]{1,0:T(8,128)S(1)} custom-call(s32[27]{0:T(128)S(1)} %stack.93.at, f32[320,7168]{1,0:T(8,128)S(1)} %get-tuple-element.40.own.refs_7_, f32[320,7168]{1,0:T(8,128)S(1)} %get-tuple-element.41.other.refs_8_, bf16[640,256]{1,0:T(8,128)(2,1)S(1)} %get-tuple-element.46.lh, bf16[640,256]{1,0:T(8,128)(2,1)S(1)} %get-tuple-element.47.ll), custom_call_target="tpu_custom_call" | custom-call | flops 1761607680 | bytes 1835008 | tf_op jit(solution)/shard_map/w_send/pallas_call | solution.py:206
  55.3 0.6 collective-permute-start.5
  55.9 0.0 collective-permute-done.8.got
  55.9 3.3 %w_keep.3 = (f32[896,256]{1,0:T(8,128)S(1)}, f32[896,256]{1,0:T(8,128)S(1)}) custom-call(s32[27]{0:T(128)S(1)} %stack.93.at, f32[320,7168]{1,0:T(8,128)S(1)} %get-tuple-element.40.own.refs_7_, f32[320,7168]{1,0:T(8,128)S(1)} %get-tuple-element.41.other.refs_8_, bf16[640,256]{1,0:T(8,128)(2,1)S(1)} %get-tuple-element.46.lh, ...), custom_call_target="tpu_custom_call" | custom-call | flops 1761607680 | bytes 1835008 | tf_op jit(solution)/shard_map/w_keep/pallas_call | solution.py:224
  59.2 1.6 collective-permute-start.9
  60.9 3.3 %w_keep.2 = (f32[896,256]{1,0:T(8,128)S(1)}, f32[896,256]{1,0:T(8,128)S(1)}) custom-call(s32[27]{0:T(128)S(1)} %stack.93.at, f32[320,7168]{1,0:T(8,128)S(1)} %get-tuple-element.40.own.refs_7_, f32[320,7168]{1,0:T(8,128)S(1)} %get-tuple-element.41.other.refs_8_, bf16[640,256]{1,0:T(8,128)(2,1)S(1)} %get-tuple-element.46.lh, ...), custom_call_target="tpu_custom_call" | custom-call | flops 1761607680 | bytes 1835008 | tf_op jit(solution)/shard_map/w_keep/pallas_call | solution.py:224
  64.2 1.6 collective-permute-start.6
  65.8 1.3 collective-permute-done.11.refs_1_
  67.1 0.6 collective-permute-start.12
  67.7 0.5 collective-permute-start.13
  68.2 2.5 %collective-permute-start.14 = (f32[128,256]{1,0:T(8,128)S(1)}, f32[128,256]{1,0:T(8,128)S(1)}, u32[]{:S(2)}, u32[]{:S(2)}) collective-permute-start(f32[128,256]{1,0:T(8,128)S(1)} %total.12.refs_0_), channel_id=1, source_target_pairs={{0,24},{4,28},{8,16},{12,20},{16,8},{20,12},{24,0},{28,4},{1,25},{... | collective-permute-start | bytes 393224 | tf_op jit(solution)/shard_map/ppermute | solution.py:531
  70.7 19.6 %collective-permute-done.12.refs_1_ = f32[128,256]{1,0:T(8,128)S(1)} collective-permute-done((f32[128,256]{1,0:T(8,128)S(1)}, f32[128,256]{1,0:T(8,128)S(1)}, u32[]{:S(2)}, u32[]{:S(2)}) %collective-permute-start.12) | collective-permute-done | bytes 131104 | tf_op jit(solution)/shard_map/ppermute | solution.py:531
  90.3 1.7 collective-permute-done.14.refs_3_
  92.0 0.1 collective-permute-start.15
  92.1 0.6 halve.3
  92.7 1.6 collective-permute-start.10
  94.3 0.6 halve.2
  94.9 1.5 collective-permute-start.7
  96.4 13.3 %chol_inverse.1 = (f32[256,256]{1,0:T(8,128)S(1)}, bf16[640,256]{1,0:T(8,128)(2,1)S(1)}, bf16[640,256]{1,0:T(8,128)(2,1)S(1)}) custom-call(s32[27]{0:T(128)S(1)} %stack.93.at, f32[128,256]{1,0:T(8,128)S(1)} %total.13.mine, f32[128,256]{1,0:T(8,128)S(1)} %collective-permute-done.15.beside, f32[640,256]{1,0:T(8,128)S(1)} %get-tuple-element.58.left), custom_call_target="tpu_custom_call" | custom-call | flops 4000000000 | bytes 655360 | tf_op jit(solution)/shard_map/chol_inverse/pallas_call | solution.py:339
  109.7 1.5 right_rows.1
  111.3 0.6 collective-permute-start.19
  111.9 0.6 collective-permute-start.16
  112.5 11.2 %collective-permute-done.19.y = f32[448,256]{1,0:T(8,128)S(1)} collective-permute-done((f32[448,256]{1,0:T(8,128)S(1)}, f32[448,256]{1,0:T(8,128)S(1)}, u32[]{:S(2)}, u32[]{:S(2)}) %collective-permute-start.19) | collective-permute-done | bytes 458784 | tf_op jit(solution)/shard_map/ppermute | solution.py:531
  123.7 0.7 join.3
  124.4 0.1 collective-permute-start.33
  124.5 0.7 join.2
  125.1 0.6 collective-permute-start.32
  125.7 0.6 collective-permute-start.20
  126.3 3.6 %collective-permute-done.22.refs_1_ = f32[8,256]{1,0:T(8,128)S(1)} collective-permute-done((f32[8,256]{1,0:T(8,128)S(1)}, f32[8,256]{1,0:T(8,128)S(1)}, u32[]{:S(2)}, u32[]{:S(2)}) %collective-permute-start.22) | collective-permute-done | bytes 8224 | tf_op jit(solution)/shard_map/ppermute | solution.py:531
  129.9 1.1 collective-permute-start.23
  131.0 3.4 %collective-permute-done.23.refs_1_ = f32[8,256]{1,0:T(8,128)S(1)} collective-permute-done((f32[8,256]{1,0:T(8,128)S(1)}, f32[8,256]{1,0:T(8,128)S(1)}, u32[]{:S(2)}, u32[]{:S(2)}) %collective-permute-start.23) | collective-permute-done | bytes 8224 | tf_op jit(solution)/shard_map/ppermute | solution.py:531
  134.5 1.2 collective-permute-done.24.refs_1_
  135.7 0.6 collective-permute-start.25
  136.2 1.4 collective-permute-start.26
  137.7 1.6 collective-permute-done.25.refs_1_
  139.3 1.4 collective-permute-start.27
  140.8 0.6 collective-permute-start.30
  141.3 2.6 %collective-permute-done.27.refs_3_ = f32[8,256]{1,0:T(8,128)S(1)} collective-permute-done((f32[8,256]{1,0:T(8,128)S(1)}, f32[8,256]{1,0:T(8,128)S(1)}, u32[]{:S(2)}, u32[]{:S(2)}) %collective-permute-start.27) | collective-permute-done | bytes 8224 | tf_op jit(solution)/shard_map/ppermute | solution.py:531
  144.0 0.6 collective-permute-start.28
  144.5 1.5 collective-permute-start.17
  146.0 18.0 %collective-permute-done.17.refs_0_ = f32[384,256]{1,0:T(8,128)S(1)} collective-permute-done((f32[384,256]{1,0:T(8,128)S(1)}, f32[384,256]{1,0:T(8,128)S(1)}, u32[]{:S(2)}, u32[]{:S(2)}) %collective-permute-start.17) | collective-permute-done | bytes 393248 | tf_op jit(solution)/shard_map/ppermute | solution.py:531
  164.0 0.5 collective-permute-start.18
  164.5 0.1 collective-permute-start.31
  164.6 0.4 collective-permute-start.29
  165.0 12.8 %final.3 = (f32[640,6912]{1,0:T(8,128)}, f32[640,6912]{1,0:T(8,128)}, f32[6912,256]{1,0:T(8,128)}) custom-call(s32[27]{0:T(128)S(1)} %stack.93.at, f32[896,256]{1,0:T(8,128)S(1)} %get-tuple-element.69.refs_0_, f32[896,256]{1,0:T(8,128)S(1)} %collective-permute-done.32.refs_1_, f32[896,256]{1,0:T(8,128)S(1)} %get-tuple-element.70.refs_2_, ...), custom_call_target="tpu_custom_call" | custom-call | flops 7046430720 | bytes 18350080 | tf_op jit(solution)/shard_map/final/pallas_call | solution.py:494
  177.8 7.6 %final.4 = (f32[640,6912]{1,0:T(8,128)}, f32[640,6912]{1,0:T(8,128)}, f32[6912,256]{1,0:T(8,128)}) custom-call(s32[27]{0:T(128)S(1)} %stack.93.at, f32[512,256]{1,0:T(8,128)S(1)} %collective-permute-done.28.refs_0_, f32[512,256]{1,0:T(8,128)S(1)} %collective-permute-done.29.refs_1_, ...), custom_call_target="tpu_custom_call", output_to_operand_aliasing={{0}: (10, {}), {1}: (11, {}), {2}: (12, {})} | custom-call | flops 4026531840 | bytes 10485760 | tf_op jit(solution)/shard_map/final/pallas_call | solution.py:494
  185.5 6.5 %final.5 = (f32[640,6912]{1,0:T(8,128)}, f32[640,6912]{1,0:T(8,128)}, f32[6912,256]{1,0:T(8,128)}) custom-call(s32[27]{0:T(128)S(1)} %stack.93.at, f32[384,256]{1,0:T(8,128)S(1)} %collective-permute-done.17.refs_0_, f32[384,256]{1,0:T(8,128)S(1)} %collective-permute-done.18.refs_1_, ...), custom_call_target="tpu_custom_call", output_to_operand_aliasing={{0}: (10, {}), {1}: (11, {}), {2}: (12, {})} | custom-call | flops 3019898880 | bytes 7864320 | tf_op jit(solution)/shard_map/final/pallas_call | solution.py:494
  (39 shorter events, 0.2 us)
Async XLA Ops:
  10.4 12.7 %collective-permute-start = (f32[320,256]{1,0:T(8,128)S(1)}, f32[320,256]{1,0:T(8,128)S(1)}, u32[]{:S(2)}, u32[]{:S(2)}) collective-permute-start(f32[320,256]{1,0:T(8,128)S(1)} %get-tuple-element.43), channel_id=1, source_target_pairs={{0,1},{1,0},{2,3},{3,2},{4,5},{5,4},{6,7},{7,6},{8,9},{9,8},{10,11... | collective-permute-start | bytes 983048 | tf_op jit(solution)/shard_map/ppermute | solution.py:531
  23.1 37.8 %copy-start = (f32[320,7168]{1,0:T(8,128)}, f32[320,7168]{1,0:T(8,128)S(1)}, u32[]{:S(2)}) copy-start(f32[320,7168]{1,0:T(8,128)S(1)} %get-tuple-element.40.own.refs_7_) | copy-start | bytes 27525124
  23.2 13.6 %collective-permute-start.2 = (f32[160,256]{1,0:T(8,128)S(1)}, f32[160,256]{1,0:T(8,128)S(1)}, u32[]{:S(2)}, u32[]{:S(2)}) collective-permute-start(f32[160,256]{1,0:T(8,128)S(1)} %get-tuple-element.45.refs_0_), channel_id=1, source_target_pairs={{0,2},{1,3},{2,0},{3,1},{4,6},{5,7},{6,4},{7,5},{8,10},{9,11},{10,... | collective-permute-start | bytes 491528 | tf_op jit(solution)/shard_map/ppermute | solution.py:531
  25.8 14.4 %collective-permute-start.1 = (f32[160,256]{1,0:T(8,128)S(1)}, f32[160,256]{1,0:T(8,128)S(1)}, u32[]{:S(2)}, u32[]{:S(2)}) collective-permute-start(f32[160,256]{1,0:T(8,128)S(1)} %get-tuple-element.44.refs_0_), channel_id=1, source_target_pairs={{0,2},{1,3},{2,0},{3,1},{4,6},{5,7},{6,4},{7,5},{8,10},{9,11},{10,... | collective-permute-start | bytes 491528 | tf_op jit(solution)/shard_map/ppermute | solution.py:531
  36.8 7.1 %collective-permute-start.4 = (f32[160,256]{1,0:T(8,128)S(1)}, f32[160,256]{1,0:T(8,128)S(1)}, u32[]{:S(2)}, u32[]{:S(2)}) collective-permute-start(f32[160,256]{1,0:T(8,128)S(1)} %total.11.refs_1_), channel_id=1, source_target_pairs={{0,1},{1,0},{2,3},{3,2},{4,5},{5,4},{6,7},{7,6},{8,9},{9,8},{10,11... | collective-permute-start | bytes 491528 | tf_op jit(solution)/shard_map/ppermute | solution.py:531
  40.3 6.9 %collective-permute-start.3 = (f32[160,256]{1,0:T(8,128)S(1)}, f32[160,256]{1,0:T(8,128)S(1)}, u32[]{:S(2)}, u32[]{:S(2)}) collective-permute-start(f32[160,256]{1,0:T(8,128)S(1)} %total.10.refs_0_), channel_id=1, source_target_pairs={{0,1},{1,0},{2,3},{3,2},{4,5},{5,4},{6,7},{7,6},{8,9},{9,8},{10,11... | collective-permute-start | bytes 491528 | tf_op jit(solution)/shard_map/ppermute | solution.py:531
  52.1 3.9 %collective-permute-start.8 = (f32[1792,256]{1,0:T(8,128)S(1)}, f32[1792,256]{1,0:T(8,128)S(1)}, u32[]{:S(2)}, u32[]{:S(2)}) collective-permute-start(f32[1792,256]{1,0:T(8,128)S(1)} %w_send.3), channel_id=1, source_target_pairs={{0,4},{4,0},{8,12},{12,8},{16,20},{20,16},{24,28},{28,24},{1,5},{5... | collective-permute-start | bytes 5505032 | tf_op jit(solution)/shard_map/ppermute | solution.py:531
  55.3 5.5 %collective-permute-start.5 = (f32[1792,256]{1,0:T(8,128)S(1)}, f32[1792,256]{1,0:T(8,128)S(1)}, u32[]{:S(2)}, u32[]{:S(2)}) collective-permute-start(f32[1792,256]{1,0:T(8,128)S(1)} %w_send.2), channel_id=1, source_target_pairs={{0,4},{4,0},{8,12},{12,8},{16,20},{20,16},{24,28},{28,24},{1,5},{5... | collective-permute-start | bytes 5505032 | tf_op jit(solution)/shard_map/ppermute | solution.py:531
  59.2 32.8 %collective-permute-start.9 = (f32[896,256]{1,0:T(8,128)S(1)}, f32[896,256]{1,0:T(8,128)S(1)}, u32[]{:S(2)}, u32[]{:S(2)}) collective-permute-start(f32[896,256]{1,0:T(8,128)S(1)} %get-tuple-element.53), channel_id=1, source_target_pairs={{0,16},{4,20},{8,24},{12,28},{16,0},{20,4},{24,8},{28,12},{1,17},{... | collective-permute-start | bytes 2752520 | tf_op jit(solution)/shard_map/ppermute | solution.py:531
  64.2 30.1 %collective-permute-start.6 = (f32[896,256]{1,0:T(8,128)S(1)}, f32[896,256]{1,0:T(8,128)S(1)}, u32[]{:S(2)}, u32[]{:S(2)}) collective-permute-start(f32[896,256]{1,0:T(8,128)S(1)} %get-tuple-element.49), channel_id=1, source_target_pairs={{0,8},{4,12},{8,0},{12,4},{16,24},{20,28},{24,16},{28,20},{1,9},{5... | collective-permute-start | bytes 2752520 | tf_op jit(solution)/shard_map/ppermute | solution.py:531
  65.7 1.3 collective-permute-start.11
  67.1 23.2 %collective-permute-start.12 = (f32[128,256]{1,0:T(8,128)S(1)}, f32[128,256]{1,0:T(8,128)S(1)}, u32[]{:S(2)}, u32[]{:S(2)}) collective-permute-start(f32[128,256]{1,0:T(8,128)S(1)} %total.12.refs_0_), channel_id=1, source_target_pairs={{0,8},{4,12},{8,0},{12,4},{16,24},{20,28},{24,16},{28,20},{1,9},{5... | collective-permute-start | bytes 393224 | tf_op jit(solution)/shard_map/ppermute | solution.py:531
  67.7 22.6 %collective-permute-start.13 = (f32[128,256]{1,0:T(8,128)S(1)}, f32[128,256]{1,0:T(8,128)S(1)}, u32[]{:S(2)}, u32[]{:S(2)}) collective-permute-start(f32[128,256]{1,0:T(8,128)S(1)} %total.12.refs_0_), channel_id=1, source_target_pairs={{0,16},{4,20},{8,24},{12,28},{16,0},{20,4},{24,8},{28,12},{1,17},{... | collective-permute-start | bytes 393224 | tf_op jit(solution)/shard_map/ppermute | solution.py:531
  68.2 23.8 %collective-permute-start.14 = (f32[128,256]{1,0:T(8,128)S(1)}, f32[128,256]{1,0:T(8,128)S(1)}, u32[]{:S(2)}, u32[]{:S(2)}) collective-permute-start(f32[128,256]{1,0:T(8,128)S(1)} %total.12.refs_0_), channel_id=1, source_target_pairs={{0,24},{4,28},{8,16},{12,20},{16,8},{20,12},{24,0},{28,4},{1,25},{... | collective-permute-start | bytes 393224 | tf_op jit(solution)/shard_map/ppermute | solution.py:531
  92.0 4.5 %collective-permute-start.15 = (f32[128,256]{1,0:T(8,128)S(1)}, f32[128,256]{1,0:T(8,128)S(1)}, u32[]{:S(2)}, u32[]{:S(2)}) collective-permute-start(f32[128,256]{1,0:T(8,128)S(1)} %total.13.mine), channel_id=1, source_target_pairs={{0,4},{4,0},{8,12},{12,8},{16,20},{20,16},{24,28},{28,24},{1,5},{5... | collective-permute-start | bytes 393224 | tf_op jit(solution)/shard_map/ppermute | solution.py:531
  92.7 17.0 %collective-permute-start.10 = (f32[448,256]{1,0:T(8,128)S(1)}, f32[448,256]{1,0:T(8,128)S(1)}, u32[]{:S(2)}, u32[]{:S(2)}) collective-permute-start(f32[448,256]{1,0:T(8,128)S(1)} %get-tuple-element.55), channel_id=1, source_target_pairs={{0,8},{4,12},{8,0},{12,4},{16,24},{20,28},{24,16},{28,20},{1,9},{5... | collective-permute-start | bytes 1376264 | tf_op jit(solution)/shard_map/ppermute | solution.py:531
  94.3 70.7 %slice-start = ((s8[9175040]{0:T(1024)(128)(4,1)}), s8[4194304]{0:T(1024)(128)(4,1)S(1)}, s32[]{:S(2)}) async-start(s8[9175040]{0:T(1024)(128)(4,1)} %bitcast.21), calls=%async_computation | async-start | bytes 8388608
  94.9 14.8 %collective-permute-start.7 = (f32[448,256]{1,0:T(8,128)S(1)}, f32[448,256]{1,0:T(8,128)S(1)}, u32[]{:S(2)}, u32[]{:S(2)}) collective-permute-start(f32[448,256]{1,0:T(8,128)S(1)} %get-tuple-element.51), channel_id=1, source_target_pairs={{0,16},{4,20},{8,24},{12,28},{16,0},{20,4},{24,8},{28,12},{1,17},{... | collective-permute-start | bytes 1376264 | tf_op jit(solution)/shard_map/ppermute | solution.py:531
  96.4 68.6 %slice-start.1 = ((s8[9175040]{0:T(1024)(128)(4,1)}), s8[4194304]{0:T(1024)(128)(4,1)S(1)}, s32[]{:S(2)}) async-start(s8[9175040]{0:T(1024)(128)(4,1)} %bitcast.21), calls=%async_computation.1 | async-start | bytes 8388608
  96.4 68.6 %slice-start.2 = ((s8[9175040]{0:T(1024)(128)(4,1)}), s8[786432]{0:T(1024)(128)(4,1)S(1)}, s32[]{:S(2)}) async-start(s8[9175040]{0:T(1024)(128)(4,1)} %bitcast.21), calls=%async_computation.2 | async-start | bytes 1572864
  111.3 12.4 %collective-permute-start.19 = (f32[448,256]{1,0:T(8,128)S(1)}, f32[448,256]{1,0:T(8,128)S(1)}, u32[]{:S(2)}, u32[]{:S(2)}) collective-permute-start(f32[448,256]{1,0:T(8,128)S(1)} %get-tuple-element.62.x), channel_id=1, source_target_pairs={{0,8},{4,12},{8,0},{12,4},{16,24},{20,28},{24,16},{28,20},{1,9},{5... | collective-permute-start | bytes 1376264 | tf_op jit(solution)/shard_map/ppermute | solution.py:531
  111.9 12.5 %collective-permute-start.16 = (f32[448,256]{1,0:T(8,128)S(1)}, f32[448,256]{1,0:T(8,128)S(1)}, u32[]{:S(2)}, u32[]{:S(2)}) collective-permute-start(f32[448,256]{1,0:T(8,128)S(1)} %get-tuple-element.60.x), channel_id=1, source_target_pairs={{0,16},{4,20},{8,24},{12,28},{16,0},{20,4},{24,8},{28,12},{1,17},{... | collective-permute-start | bytes 1376264 | tf_op jit(solution)/shard_map/ppermute | solution.py:531
  124.4 40.2 %collective-permute-start.33 = (f32[896,256]{1,0:T(8,128)S(1)}, f32[896,256]{1,0:T(8,128)S(1)}, u32[]{:S(2)}, u32[]{:S(2)}) collective-permute-start(f32[896,256]{1,0:T(8,128)S(1)} %get-tuple-element.70.refs_2_), channel_id=1, source_target_pairs={{0,4},{4,0},{8,12},{12,8},{16,20},{20,16},{24,28},{28,24},{1,5},{5... | collective-permute-start | bytes 2752520 | tf_op jit(solution)/shard_map/ppermute | solution.py:531
  125.1 39.9 %collective-permute-start.32 = (f32[896,256]{1,0:T(8,128)S(1)}, f32[896,256]{1,0:T(8,128)S(1)}, u32[]{:S(2)}, u32[]{:S(2)}) collective-permute-start(f32[896,256]{1,0:T(8,128)S(1)} %get-tuple-element.69.refs_0_), channel_id=1, source_target_pairs={{0,4},{4,0},{8,12},{12,8},{16,20},{20,16},{24,28},{28,24},{1,5},{5... | collective-permute-start | bytes 2752520 | tf_op jit(solution)/shard_map/ppermute | solution.py:531
  125.7 18.9 %collective-permute-start.20 = (f32[384,256]{1,0:T(8,128)S(1)}, f32[384,256]{1,0:T(8,128)S(1)}, u32[]{:S(2)}, u32[]{:S(2)}) collective-permute-start(f32[384,256]{1,0:T(8,128)S(1)} %get-tuple-element.63), channel_id=1, source_target_pairs={{0,16},{4,20},{8,24},{12,28},{16,0},{20,4},{24,8},{28,12},{1,17},{... | collective-permute-start | bytes 1179656 | tf_op jit(solution)/shard_map/ppermute | solution.py:531
  126.3 3.7 %collective-permute-start.22 = (f32[8,256]{1,0:T(8,128)S(1)}, f32[8,256]{1,0:T(8,128)S(1)}, u32[]{:S(2)}, u32[]{:S(2)}) collective-permute-start(f32[8,256]{1,0:T(8,128)S(1)} %get-tuple-element.64.refs_0_), channel_id=1, source_target_pairs={{0,1},{1,0},{2,3},{3,2},{4,5},{5,4},{6,7},{7,6},{8,9},{9,8},{10,11... | collective-permute-start | bytes 24584 | tf_op jit(solution)/shard_map/ppermute | solution.py:531
  129.9 4.5 %collective-permute-start.23 = (f32[8,256]{1,0:T(8,128)S(1)}, f32[8,256]{1,0:T(8,128)S(1)}, u32[]{:S(2)}, u32[]{:S(2)}) collective-permute-start(f32[8,256]{1,0:T(8,128)S(1)} %total.14.refs_0_), channel_id=1, source_target_pairs={{0,2},{1,3},{2,0},{3,1},{4,6},{5,7},{6,4},{7,5},{8,10},{9,11},{10,... | collective-permute-start | bytes 24584 | tf_op jit(solution)/shard_map/ppermute | solution.py:531
  134.5 1.2 collective-permute-start.24
  135.7 3.7 %collective-permute-start.25 = (f32[8,256]{1,0:T(8,128)S(1)}, f32[8,256]{1,0:T(8,128)S(1)}, u32[]{:S(2)}, u32[]{:S(2)}) collective-permute-start(f32[8,256]{1,0:T(8,128)S(1)} %total.16.refs_0_), channel_id=1, source_target_pairs={{0,8},{4,12},{8,0},{12,4},{16,24},{20,28},{24,16},{28,20},{1,9},{5... | collective-permute-start | bytes 24584 | tf_op jit(solution)/shard_map/ppermute | solution.py:531
  136.2 4.5 %collective-permute-start.26 = (f32[8,256]{1,0:T(8,128)S(1)}, f32[8,256]{1,0:T(8,128)S(1)}, u32[]{:S(2)}, u32[]{:S(2)}) collective-permute-start(f32[8,256]{1,0:T(8,128)S(1)} %total.16.refs_0_), channel_id=1, source_target_pairs={{0,16},{4,20},{8,24},{12,28},{16,0},{20,4},{24,8},{28,12},{1,17},{... | collective-permute-start | bytes 24584 | tf_op jit(solution)/shard_map/ppermute | solution.py:531
  139.3 4.7 %collective-permute-start.27 = (f32[8,256]{1,0:T(8,128)S(1)}, f32[8,256]{1,0:T(8,128)S(1)}, u32[]{:S(2)}, u32[]{:S(2)}) collective-permute-start(f32[8,256]{1,0:T(8,128)S(1)} %total.16.refs_0_), channel_id=1, source_target_pairs={{0,24},{4,28},{8,16},{12,20},{16,8},{20,12},{24,0},{28,4},{1,25},{... | collective-permute-start | bytes 24584 | tf_op jit(solution)/shard_map/ppermute | solution.py:531
  140.8 23.2 %collective-permute-start.30 = (f32[512,256]{1,0:T(8,128)S(1)}, f32[512,256]{1,0:T(8,128)S(1)}, u32[]{:S(2)}, u32[]{:S(2)}) collective-permute-start(f32[512,256]{1,0:T(8,128)S(1)} %get-tuple-element.68), channel_id=1, source_target_pairs={{0,16},{4,20},{8,24},{12,28},{16,0},{20,4},{24,8},{28,12},{1,17},{... | collective-permute-start | bytes 1572872 | tf_op jit(solution)/shard_map/ppermute | solution.py:531
  144.0 20.5 %collective-permute-start.28 = (f32[512,256]{1,0:T(8,128)S(1)}, f32[512,256]{1,0:T(8,128)S(1)}, u32[]{:S(2)}, u32[]{:S(2)}) collective-permute-start(f32[512,256]{1,0:T(8,128)S(1)} %get-tuple-element.67), channel_id=1, source_target_pairs={{0,8},{4,12},{8,0},{12,4},{16,24},{20,28},{24,16},{28,20},{1,9},{5... | collective-permute-start | bytes 1572872 | tf_op jit(solution)/shard_map/ppermute | solution.py:531
  144.5 19.4 %collective-permute-start.17 = (f32[384,256]{1,0:T(8,128)S(1)}, f32[384,256]{1,0:T(8,128)S(1)}, u32[]{:S(2)}, u32[]{:S(2)}) collective-permute-start(f32[384,256]{1,0:T(8,128)S(1)} %get-tuple-element.61), channel_id=1, source_target_pairs={{0,8},{4,12},{8,0},{12,4},{16,24},{20,28},{24,16},{28,20},{1,9},{5... | collective-permute-start | bytes 1179656 | tf_op jit(solution)/shard_map/ppermute | solution.py:531
  164.0 21.5 %collective-permute-start.21 = (f32[384,256]{1,0:T(8,128)S(1)}, f32[384,256]{1,0:T(8,128)S(1)}, u32[]{:S(2)}, u32[]{:S(2)}) collective-permute-start(f32[384,256]{1,0:T(8,128)S(1)} %collective-permute-done.20.refs_2_), channel_id=1, source_target_pairs={{0,4},{4,0},{8,12},{12,8},{16,20},{20,16},{24,28},{28,24},{1,5},{5... | collective-permute-start | bytes 1179656 | tf_op jit(solution)/shard_map/ppermute | solution.py:531
  164.0 21.5 %collective-permute-start.18 = (f32[384,256]{1,0:T(8,128)S(1)}, f32[384,256]{1,0:T(8,128)S(1)}, u32[]{:S(2)}, u32[]{:S(2)}) collective-permute-start(f32[384,256]{1,0:T(8,128)S(1)} %collective-permute-done.17.refs_0_), channel_id=1, source_target_pairs={{0,4},{4,0},{8,12},{12,8},{16,20},{20,16},{24,28},{28,24},{1,5},{5... | collective-permute-start | bytes 1179656 | tf_op jit(solution)/shard_map/ppermute | solution.py:531
  164.5 13.3 %collective-permute-start.31 = (f32[512,256]{1,0:T(8,128)S(1)}, f32[512,256]{1,0:T(8,128)S(1)}, u32[]{:S(2)}, u32[]{:S(2)}) collective-permute-start(f32[512,256]{1,0:T(8,128)S(1)} %collective-permute-done.30.refs_2_), channel_id=1, source_target_pairs={{0,4},{4,0},{8,12},{12,8},{16,20},{20,16},{24,28},{28,24},{1,5},{5... | collective-permute-start | bytes 1572872 | tf_op jit(solution)/shard_map/ppermute | solution.py:531
  164.6 13.3 %collective-permute-start.29 = (f32[512,256]{1,0:T(8,128)S(1)}, f32[512,256]{1,0:T(8,128)S(1)}, u32[]{:S(2)}, u32[]{:S(2)}) collective-permute-start(f32[512,256]{1,0:T(8,128)S(1)} %collective-permute-done.28.refs_0_), channel_id=1, source_target_pairs={{0,4},{4,0},{8,12},{12,8},{16,20},{20,16},{24,28},{28,24},{1,5},{5... | collective-permute-start | bytes 1572872 | tf_op jit(solution)/shard_map/ppermute | solution.py:531

commit v8 on v7

--- a/solution.py
+++ b/solution.py
@@ -425,9 +425,9 @@
 SLOTS = 2
 
 
-def final_kernel(place, group, unit, total_cols, factor, at, *refs):
-    pieces = refs[:4]
-    squares, oh, ol, own, other = refs[4:9]
+def final_kernel(units, place, group, unit, total_cols, factor, at, *refs):
+    pieces = refs[:units]
+    squares, oh, ol, own, other = refs[units : units + 5]
     update, momentum, new_right, stage_m, stage_u, stage_r, lh, ll, high, low, sems = refs[-11:]
     start, count = group
     n, rows, half = count * LANES, oh.shape[0], own.shape[0]
@@ -481,8 +481,8 @@
         each_copy(k, lambda copy: copy.start())
         return 0
 
-    lax.fori_loop(0, 4, body, 0)
-    for k in range(4 - SLOTS, 4):
+    lax.fori_loop(0, units, body, 0)
+    for k in range(units - SLOTS, units):
         each_copy(k, lambda copy: copy.wait())
 
 
@@ -492,8 +492,8 @@
     factor = (total_rows / rank) ** 0.5
     n = group[1] * LANES
     return pl.pallas_call(
-        functools.partial(final_kernel, place, group, unit, total_cols, factor),
-        in_specs=[SMEM] + [VMEM] * 9 + [HBM] * len(before),
+        functools.partial(final_kernel, len(pieces), place, group, unit, total_cols, factor),
+        in_specs=[SMEM] + [VMEM] * (len(pieces) + 5) + [HBM] * len(before),
         out_specs=[HBM] * 3,
         out_shape=[
             jax.ShapeDtypeStruct((rows, cols), F32),
@@ -510,9 +510,9 @@
             pltpu.VMEM((n, rank), BF16),
             pltpu.SemaphoreType.DMA((3, SLOTS, group[1])),
         ],
-        input_output_aliases={10 + i: i for i in range(len(before))},
+        input_output_aliases={len(pieces) + 6 + i: i for i in range(len(before))},
         compiler_params=params(28),
-        cost_estimate=cost(48 * rows * n * rank, 32 * rows * n),
+        cost_estimate=cost(12 * len(pieces) * rows * n * rank, 8 * len(pieces) * rows * n),
         name="final",
     )(at, *pieces, squares, oh, ol, own, other, *before)
 
@@ -557,21 +557,25 @@
     s, core = z & 1, d & 1
     put(s, 1 - s)
     core_at = put(core)
-    send_at, keep_at, bit_at, near, far, first = [], [], [], [], [], []
+    send_at, keep_at, bit_at, first = [], [], [], []
+    near, near_beside, far, far_beside = [], [], [], []
     for h, order in enumerate(orders):
         t = bit_of(order[0])
         base, beside = 4 * h + 2 * core, 4 * h + 2 * (1 - core)
         send_at.append(put(beside, beside + 1))
         keep_at.append(put(base + 1 - t, base + t, 1 - t, t))
         bit_at.append({b: put(bit_of(b)) for b in order[1:]})
-        near += [base + t, beside + t]
-        far += [base + 1 - t, beside + 1 - t]
+        near.append(base + t)
+        near_beside.append(beside + t)
+        far.append(base + 1 - t)
+        far_beside.append(beside + 1 - t)
         at, n = (base + t) * unit, unit
         for b in order[1:]:
             n = n // 2
             at = at + bit_of(b) * n
         first.append(at)
-    near_at, far_at, first_at = put(*near), put(*far), put(*first)
+    near_at, beside_at = put(*near), put(*near_beside)
+    far_at, first_at = put(*far, *far_beside), put(*first)
     at = jnp.stack([jnp.asarray(v, jnp.int32) for v in table])
 
     inputs = (gradient, momentum, right_factor, 8 * unit)
@@ -613,9 +617,8 @@
 
     x_inv, oh, ol = chol_inverse(at, core_at, gram, gram_beside, left)
     *right, squares = right_rows(at, first_at, cols, *kept, x_inv)
-    if power_of_two(n_tp):
-        for b in bits_of(n_tp):
-            squares = total(squares, swap(squares, "tensor", b))
+    if n_tp == 4:
+        squares = total(squares, *(swap(squares, "tensor", *m) for m in ((0,), (1,), (0, 1))))
     else:
         squares = lax.psum(squares, "tensor")
     got = swap(squares, "dp", 0)
@@ -624,7 +627,7 @@
 
     blocks = unit // LANES
     groups = ((0, blocks - blocks // 2), (blocks - blocks // 2, blocks // 2))
-    near, far = [], ([], [])
+    near, near_beside, far, far_beside = [], [], ([], []), ([], [])
     for h, (order, x) in enumerate(zip(orders, right)):
         parts = [x]
         for b in order[:0:-1]:
@@ -635,13 +638,16 @@
             )
         for g, part in enumerate(parts):
             y = swap(part, "dp", order[0])
-            far[g].extend([y, swap(y, "dp", 0)])
-        near.extend([x, swap(x, "dp", 0)])
+            far_beside[g].append(swap(y, "dp", 0))
+            far[g].append(y)
+        near.append(x)
+        near_beside.append(swap(x, "dp", 0))
 
     same = (squares, oh, ol, *held, (cols, rows * n_dp, cols * n_tp))
     outs = final(at, near_at, (0, blocks), unit, near, *same, ())
+    outs = final(at, beside_at, (0, blocks), unit, near_beside, *same, outs)
     for g in range(2):
-        outs = final(at, far_at, groups[g], unit, far[g], *same, outs)
+        outs = final(at, far_at, groups[g], unit, far[g] + far_beside[g], *same, outs)
     return tuple(outs)
 
 

time: 192 us -> 195 us (1.016)
  waiting for transfers between devices: 84.4 us -> 77.9 us
  starting transfers between devices: 28.2 us -> 33.7 us
  Pallas kernels: 78.3 us -> 81.4 us
    ppermute x34 -> x35, waiting for transfers between devices: 84.4 us -> 77.9 us  [swap(): return lax.ppermute(x, axis, [(i, i ^ mask) for i in range(n)])]
    ppermute x34 -> x35, starting transfers between devices: 28.2 us -> 33.7 us  [swap(): return lax.ppermute(x, axis, [(i, i ^ mask) for i in range(n)])]
    pallas_call x3 -> x4, Pallas kernels: 26.9 us -> 30 us  [final(): pl.pallas_call(functools.partial(final_kernel, len(pieces), place, group,...]
  transfers between devices with their start and end apart: 34 -> 35, of which waited for: 14 -> 16; matrix products, arithmetic and copies ran while one was open for 0% -> 0% of each run, Pallas kernels for 29% -> 30%
where the time goes in v8:
time: 195 us; the launch traced here: 194 us
  Pallas kernels  81.4 us (42%)
  waiting for transfers between devices  77.9 us (40%)
  starting transfers between devices  33.7 us (17%)
    ppermute x35, waiting for transfers between devices, swap(): return lax.ppermute(x, axis, [(i, i ^ mask) for i in range(n)])  77.9 us
    ppermute x35, starting transfers between devices, swap(): return lax.ppermute(x, axis, [(i, i ^ mask) for i in range(n)])  33.7 us
    pallas_call x4, Pallas kernels, final(): pl.pallas_call(functools.partial(final_kernel, len(pieces), place, group,...  30 us
    pallas_call x2, Pallas kernels, left_half(): pl.pallas_call(functools.partial(left_kernel, which), in_specs=[SMEM, HBM...  19.2 us
    pallas_call x1, Pallas kernels, chol_inverse(): pl.pallas_call(functools.partial(chol_kernel, place), in_specs=[SMEM] + [...  13.3 us
    pallas_call x2, Pallas kernels, w_keep(): pl.pallas_call(functools.partial(w_keep_kernel, place), grid_spec=pltpu.P...  6.56 us
    pallas_call x2, Pallas kernels, w_send(): pl.pallas_call(functools.partial(w_send_kernel, place), grid_spec=pltpu.P...  6.36 us
  transfers between devices with their start and end apart: 35, of which 16 were waited for; matrix products, arithmetic and copies ran while one was open for 0% of the time, Pallas kernels for 30%

profile of v8, /device:TPU:0, one launch (start us, length us, event | category | flops | bytes accessed | tf_op | source)
XLA Modules:
  0.0 194.3 jit_solution(6434379383036785839)
XLA Ops:
  0.7 0.1 stack.93.at
  0.8 9.6 %left_half.3 = (f32[320,7168]{1,0:T(8,128)S(1)}, f32[320,256]{1,0:T(8,128)S(1)}) custom-call(s32[27]{0:T(128)S(1)} %stack.93.at, f32[640,6912]{1,0:T(8,128)} %g.3, f32[640,6912]{1,0:T(8,128)} %m.3, f32[6912,256]{1,0:T(8,128)} %r.3), custom_call_target="tpu_custom_call" | custom-call | flops 3397386240 | bytes 24772608 | tf_op jit(solution)/shard_map/left_half/pallas_call | solution.py:99
  10.4 3.1 %collective-permute-start = (f32[320,256]{1,0:T(8,128)S(1)}, f32[320,256]{1,0:T(8,128)S(1)}, u32[]{:S(2)}, u32[]{:S(2)}) collective-permute-start(f32[320,256]{1,0:T(8,128)S(1)} %get-tuple-element.46), channel_id=1, source_target_pairs={{0,1},{1,0},{2,3},{3,2},{4,5},{5,4},{6,7},{7,6},{8,9},{9,8},{10,11... | collective-permute-start | bytes 983048 | tf_op jit(solution)/shard_map/ppermute | solution.py:531
  13.5 9.6 %left_half.2 = (f32[320,7168]{1,0:T(8,128)S(1)}, f32[320,256]{1,0:T(8,128)S(1)}) custom-call(s32[27]{0:T(128)S(1)} %stack.93.at, f32[640,6912]{1,0:T(8,128)} %g.3, f32[640,6912]{1,0:T(8,128)} %m.3, f32[6912,256]{1,0:T(8,128)} %r.3), custom_call_target="tpu_custom_call" | custom-call | flops 3397386240 | bytes 24772608 | tf_op jit(solution)/shard_map/left_half/pallas_call | solution.py:99
  23.2 2.7 %collective-permute-start.2 = (f32[160,256]{1,0:T(8,128)S(1)}, f32[160,256]{1,0:T(8,128)S(1)}, u32[]{:S(2)}, u32[]{:S(2)}) collective-permute-start(f32[160,256]{1,0:T(8,128)S(1)} %get-tuple-element.48.refs_0_), channel_id=1, source_target_pairs={{0,2},{1,3},{2,0},{3,1},{4,6},{5,7},{6,4},{7,5},{8,10},{9,11},{10,... | collective-permute-start | bytes 491528 | tf_op jit(solution)/shard_map/ppermute | solution.py:531
  25.8 0.3 collective-permute-start.1
  26.1 10.6 %collective-permute-done.2.refs_1_ = f32[160,256]{1,0:T(8,128)S(1)} collective-permute-done((f32[160,256]{1,0:T(8,128)S(1)}, f32[160,256]{1,0:T(8,128)S(1)}, u32[]{:S(2)}, u32[]{:S(2)}) %collective-permute-start.2) | collective-permute-done | bytes 163872 | tf_op jit(solution)/shard_map/ppermute | solution.py:531
  36.8 0.9 collective-permute-start.4
  37.7 2.6 %collective-permute-done.1.refs_1_ = f32[160,256]{1,0:T(8,128)S(1)} collective-permute-done((f32[160,256]{1,0:T(8,128)S(1)}, f32[160,256]{1,0:T(8,128)S(1)}, u32[]{:S(2)}, u32[]{:S(2)}) %collective-permute-start.1) | collective-permute-done | bytes 163872 | tf_op jit(solution)/shard_map/ppermute | solution.py:531
  40.3 0.1 collective-permute-start.3
  40.3 3.6 %collective-permute-done.4.refs_3_ = f32[160,256]{1,0:T(8,128)S(1)} collective-permute-done((f32[160,256]{1,0:T(8,128)S(1)}, f32[160,256]{1,0:T(8,128)S(1)}, u32[]{:S(2)}, u32[]{:S(2)}) %collective-permute-start.4) | collective-permute-done | bytes 163872 | tf_op jit(solution)/shard_map/ppermute | solution.py:531
  43.9 3.3 %collective-permute-done.3.refs_2_ = f32[160,256]{1,0:T(8,128)S(1)} collective-permute-done((f32[160,256]{1,0:T(8,128)S(1)}, f32[160,256]{1,0:T(8,128)S(1)}, u32[]{:S(2)}, u32[]{:S(2)}) %collective-permute-start.3) | collective-permute-done | bytes 163872 | tf_op jit(solution)/shard_map/ppermute | solution.py:531
  47.2 1.7 gram_of.1
  48.9 3.2 %w_send.3 = f32[1792,256]{1,0:T(8,128)S(1)} custom-call(s32[27]{0:T(128)S(1)} %stack.93.at, f32[320,7168]{1,0:T(8,128)S(1)} %get-tuple-element.43.own.refs_5_.refs_7_, f32[320,7168]{1,0:T(8,128)S(1)} %get-tuple-element.44.other.refs_6_.refs_8_, bf16[640,256]{1,0:T(8,128)(2,1)S(1)} %get-tuple-element.49.lh, bf16[640,256]{1,0:T(8,128)(2,1)S(1)} %get-tuple-element.50.ll), custom_call_target="tpu_custom_call" | custom-call | flops 1761607680 | bytes 1835008 | tf_op jit(solution)/shard_map/w_send/pallas_call | solution.py:206
  52.1 0.1 collective-permute-start.8
  52.2 3.2 %w_send.2 = f32[1792,256]{1,0:T(8,128)S(1)} custom-call(s32[27]{0:T(128)S(1)} %stack.93.at, f32[320,7168]{1,0:T(8,128)S(1)} %get-tuple-element.43.own.refs_5_.refs_7_, f32[320,7168]{1,0:T(8,128)S(1)} %get-tuple-element.44.other.refs_6_.refs_8_, bf16[640,256]{1,0:T(8,128)(2,1)S(1)} %get-tuple-element.49.lh, bf16[640,256]{1,0:T(8,128)(2,1)S(1)} %get-tuple-element.50.ll), custom_call_target="tpu_custom_call" | custom-call | flops 1761607680 | bytes 1835008 | tf_op jit(solution)/shard_map/w_send/pallas_call | solution.py:206
  55.4 0.6 collective-permute-start.5
  55.9 3.3 %w_keep.3 = (f32[896,256]{1,0:T(8,128)S(1)}, f32[896,256]{1,0:T(8,128)S(1)}) custom-call(s32[27]{0:T(128)S(1)} %stack.93.at, f32[320,7168]{1,0:T(8,128)S(1)} %get-tuple-element.43.own.refs_5_.refs_7_, f32[320,7168]{1,0:T(8,128)S(1)} %get-tuple-element.44.other.refs_6_.refs_8_, bf16[640,256]{1,0:T(8,128)(2,1)S(1)} %get-tuple-element.49.lh, ...), custom_call_target="tpu_custom_call" | custom-call | flops 1761607680 | bytes 1835008 | tf_op jit(solution)/shard_map/w_keep/pallas_call | solution.py:224
  59.2 1.6 collective-permute-start.9
  60.9 3.3 %w_keep.2 = (f32[896,256]{1,0:T(8,128)S(1)}, f32[896,256]{1,0:T(8,128)S(1)}) custom-call(s32[27]{0:T(128)S(1)} %stack.93.at, f32[320,7168]{1,0:T(8,128)S(1)} %get-tuple-element.43.own.refs_5_.refs_7_, f32[320,7168]{1,0:T(8,128)S(1)} %get-tuple-element.44.other.refs_6_.refs_8_, bf16[640,256]{1,0:T(8,128)(2,1)S(1)} %get-tuple-element.49.lh, ...), custom_call_target="tpu_custom_call" | custom-call | flops 1761607680 | bytes 1835008 | tf_op jit(solution)/shard_map/w_keep/pallas_call | solution.py:224
  64.1 1.6 collective-permute-start.6
  65.7 1.3 collective-permute-done.11.refs_1_
  67.1 0.6 collective-permute-start.12
  67.7 0.5 collective-permute-start.13
  68.1 2.5 %collective-permute-start.14 = (f32[128,256]{1,0:T(8,128)S(1)}, f32[128,256]{1,0:T(8,128)S(1)}, u32[]{:S(2)}, u32[]{:S(2)}) collective-permute-start(f32[128,256]{1,0:T(8,128)S(1)} %total.11.refs_0_), channel_id=1, source_target_pairs={{0,24},{4,28},{8,16},{12,20},{16,8},{20,12},{24,0},{28,4},{1,25},{... | collective-permute-start | bytes 393224 | tf_op jit(solution)/shard_map/ppermute | solution.py:531
  70.6 19.6 %collective-permute-done.12.refs_1_ = f32[128,256]{1,0:T(8,128)S(1)} collective-permute-done((f32[128,256]{1,0:T(8,128)S(1)}, f32[128,256]{1,0:T(8,128)S(1)}, u32[]{:S(2)}, u32[]{:S(2)}) %collective-permute-start.12) | collective-permute-done | bytes 131104 | tf_op jit(solution)/shard_map/ppermute | solution.py:531
  90.2 1.7 collective-permute-done.14.refs_3_
  92.0 0.1 collective-permute-start.15
  92.1 0.6 halve.3
  92.7 1.5 collective-permute-start.10
  94.3 0.6 halve.2
  94.9 1.6 collective-permute-start.7
  96.5 13.3 %chol_inverse.1 = (f32[256,256]{1,0:T(8,128)S(1)}, bf16[640,256]{1,0:T(8,128)(2,1)S(1)}, bf16[640,256]{1,0:T(8,128)(2,1)S(1)}) custom-call(s32[27]{0:T(128)S(1)} %stack.93.at, f32[128,256]{1,0:T(8,128)S(1)} %total.12.mine, f32[128,256]{1,0:T(8,128)S(1)} %collective-permute-done.15.beside, f32[640,256]{1,0:T(8,128)S(1)} %get-tuple-element.61.left), custom_call_target="tpu_custom_call" | custom-call | flops 4000000000 | bytes 655360 | tf_op jit(solution)/shard_map/chol_inverse/pallas_call | solution.py:339
  109.8 1.5 right_rows.1
  111.3 0.6 collective-permute-start.18
  111.9 0.5 collective-permute-start.16
  112.5 11.3 %collective-permute-done.18.y = f32[448,256]{1,0:T(8,128)S(1)} collective-permute-done((f32[448,256]{1,0:T(8,128)S(1)}, f32[448,256]{1,0:T(8,128)S(1)}, u32[]{:S(2)}, u32[]{:S(2)}) %collective-permute-start.18) | collective-permute-done | bytes 458784 | tf_op jit(solution)/shard_map/ppermute | solution.py:531
  123.7 0.7 join.3
  124.5 0.7 join.2
  125.2 0.6 collective-permute-start.33
  125.7 0.5 collective-permute-start.30
  126.2 0.6 collective-permute-start.29
  126.8 3.6 %collective-permute-done.22.refs_1_ = f32[8,256]{1,0:T(8,128)S(1)} collective-permute-done((f32[8,256]{1,0:T(8,128)S(1)}, f32[8,256]{1,0:T(8,128)S(1)}, u32[]{:S(2)}, u32[]{:S(2)}) %collective-permute-start.22) | collective-permute-done | bytes 8224 | tf_op jit(solution)/shard_map/ppermute | solution.py:531
  130.5 1.1 collective-permute-start.23
  131.6 3.4 %collective-permute-done.23.refs_2_ = f32[8,256]{1,0:T(8,128)S(1)} collective-permute-done((f32[8,256]{1,0:T(8,128)S(1)}, f32[8,256]{1,0:T(8,128)S(1)}, u32[]{:S(2)}, u32[]{:S(2)}) %collective-permute-start.23) | collective-permute-done | bytes 8224 | tf_op jit(solution)/shard_map/ppermute | solution.py:531
  135.0 2.6 %collective-permute-start.24 = (f32[8,256]{1,0:T(8,128)S(1)}, f32[8,256]{1,0:T(8,128)S(1)}, u32[]{:S(2)}, u32[]{:S(2)}) collective-permute-start(f32[8,256]{1,0:T(8,128)S(1)} %get-tuple-element.67.refs_0_), channel_id=1, source_target_pairs={{0,3},{1,2},{2,1},{3,0},{4,7},{5,6},{6,5},{7,4},{8,11},{9,10},{10,... | collective-permute-start | bytes 24584 | tf_op jit(solution)/shard_map/ppermute | solution.py:531
  137.6 2.9 %collective-permute-done.24.refs_3_ = f32[8,256]{1,0:T(8,128)S(1)} collective-permute-done((f32[8,256]{1,0:T(8,128)S(1)}, f32[8,256]{1,0:T(8,128)S(1)}, u32[]{:S(2)}, u32[]{:S(2)}) %collective-permute-start.24) | collective-permute-done | bytes 8224 | tf_op jit(solution)/shard_map/ppermute | solution.py:531
  140.5 1.2 collective-permute-done.25.refs_1_
  141.6 1.5 collective-permute-start.26
  143.1 2.2 %collective-permute-done.26.refs_1_ = f32[8,256]{1,0:T(8,128)S(1)} collective-permute-done((f32[8,256]{1,0:T(8,128)S(1)}, f32[8,256]{1,0:T(8,128)S(1)}, u32[]{:S(2)}, u32[]{:S(2)}) %collective-permute-start.26) | collective-permute-done | bytes 8224 | tf_op jit(solution)/shard_map/ppermute | solution.py:531
  145.3 1.5 collective-permute-start.27
  146.8 2.1 %collective-permute-done.27.refs_2_ = f32[8,256]{1,0:T(8,128)S(1)} collective-permute-done((f32[8,256]{1,0:T(8,128)S(1)}, f32[8,256]{1,0:T(8,128)S(1)}, u32[]{:S(2)}, u32[]{:S(2)}) %collective-permute-start.27) | collective-permute-done | bytes 8224 | tf_op jit(solution)/shard_map/ppermute | solution.py:531
  149.0 2.4 %collective-permute-start.28 = (f32[8,256]{1,0:T(8,128)S(1)}, f32[8,256]{1,0:T(8,128)S(1)}, u32[]{:S(2)}, u32[]{:S(2)}) collective-permute-start(f32[8,256]{1,0:T(8,128)S(1)} %total.14.refs_0_), channel_id=1, source_target_pairs={{0,24},{4,28},{8,16},{12,20},{16,8},{20,12},{24,0},{28,4},{1,25},{... | collective-permute-start | bytes 24584 | tf_op jit(solution)/shard_map/ppermute | solution.py:531
  151.4 2.2 %collective-permute-done.28.refs_3_ = f32[8,256]{1,0:T(8,128)S(1)} collective-permute-done((f32[8,256]{1,0:T(8,128)S(1)}, f32[8,256]{1,0:T(8,128)S(1)}, u32[]{:S(2)}, u32[]{:S(2)}) %collective-permute-start.28) | collective-permute-done | bytes 8224 | tf_op jit(solution)/shard_map/ppermute | solution.py:531
  153.6 1.5 collective-permute-start.19
  155.1 6.3 %collective-permute-done.19.refs_1_ = f32[384,256]{1,0:T(8,128)S(1)} collective-permute-done((f32[384,256]{1,0:T(8,128)S(1)}, f32[384,256]{1,0:T(8,128)S(1)}, u32[]{:S(2)}, u32[]{:S(2)}) %collective-permute-start.19) | collective-permute-done | bytes 393248 | tf_op jit(solution)/shard_map/ppermute | solution.py:531
  161.4 1.5 collective-permute-start.17
  162.9 0.5 collective-permute-start.31
  163.4 8.0 %final.4 = (f32[640,6912]{1,0:T(8,128)}, f32[640,6912]{1,0:T(8,128)}, f32[6912,256]{1,0:T(8,128)}) custom-call(s32[27]{0:T(128)S(1)} %stack.93.at, f32[896,256]{1,0:T(8,128)S(1)} %get-tuple-element.72.refs_0_, f32[896,256]{1,0:T(8,128)S(1)} %get-tuple-element.73.refs_1_, f32[8,256]{1,0:T(8,128)S(1)} %total.15.refs_2_.refs_4_, ...), custom_call_target="tpu_custom_call" | custom-call | flops 3523215360 | bytes 9175040 | tf_op jit(solution)/shard_map/final/pallas_call | solution.py:494
  171.4 0.1 collective-permute-start.21
  171.5 0.5 collective-permute-start.20
  172.0 7.9 %final.5 = (f32[640,6912]{1,0:T(8,128)}, f32[640,6912]{1,0:T(8,128)}, f32[6912,256]{1,0:T(8,128)}) custom-call(s32[27]{0:T(128)S(1)} %stack.93.at, f32[896,256]{1,0:T(8,128)S(1)} %collective-permute-done.33.refs_0_, f32[896,256]{1,0:T(8,128)S(1)} %collective-permute-done.34.refs_1_, ...), custom_call_target="tpu_custom_call", output_to_operand_aliasing={{0}: (8, {}), {1}: (9, {}), {2}: (10, {})} | custom-call | flops 3523215360 | bytes 9175040 | tf_op jit(solution)/shard_map/final/pallas_call | solution.py:494
  180.0 7.6 %final.6 = (f32[640,6912]{1,0:T(8,128)}, f32[640,6912]{1,0:T(8,128)}, f32[6912,256]{1,0:T(8,128)}) custom-call(s32[27]{0:T(128)S(1)} %stack.93.at, f32[512,256]{1,0:T(8,128)S(1)} %collective-permute-done.29.refs_0_, f32[512,256]{1,0:T(8,128)S(1)} %collective-permute-done.30.refs_1_, ...), custom_call_target="tpu_custom_call", output_to_operand_aliasing={{0}: (10, {}), {1}: (11, {}), {2}: (12, {})} | custom-call | flops 4026531840 | bytes 10485760 | tf_op jit(solution)/shard_map/final/pallas_call | solution.py:494
  187.6 6.5 %final.7 = (f32[640,6912]{1,0:T(8,128)}, f32[640,6912]{1,0:T(8,128)}, f32[6912,256]{1,0:T(8,128)}) custom-call(s32[27]{0:T(128)S(1)} %stack.93.at, f32[384,256]{1,0:T(8,128)S(1)} %collective-permute-done.17.refs_0_, f32[384,256]{1,0:T(8,128)S(1)} %collective-permute-done.19.refs_1_, ...), custom_call_target="tpu_custom_call", output_to_operand_aliasing={{0}: (10, {}), {1}: (11, {}), {2}: (12, {})} | custom-call | flops 3019898880 | bytes 7864320 | tf_op jit(solution)/shard_map/final/pallas_call | solution.py:494
  (41 shorter events, 0.4 us)
Async XLA Ops:
  10.4 12.7 %collective-permute-start = (f32[320,256]{1,0:T(8,128)S(1)}, f32[320,256]{1,0:T(8,128)S(1)}, u32[]{:S(2)}, u32[]{:S(2)}) collective-permute-start(f32[320,256]{1,0:T(8,128)S(1)} %get-tuple-element.46), channel_id=1, source_target_pairs={{0,1},{1,0},{2,3},{3,2},{4,5},{5,4},{6,7},{7,6},{8,9},{9,8},{10,11... | collective-permute-start | bytes 983048 | tf_op jit(solution)/shard_map/ppermute | solution.py:531
  23.1 37.8 %copy-start = (f32[320,7168]{1,0:T(8,128)}, f32[320,7168]{1,0:T(8,128)S(1)}, u32[]{:S(2)}) copy-start(f32[320,7168]{1,0:T(8,128)S(1)} %get-tuple-element.43.own.refs_5_.refs_7_) | copy-start | bytes 27525124
  23.2 13.6 %collective-permute-start.2 = (f32[160,256]{1,0:T(8,128)S(1)}, f32[160,256]{1,0:T(8,128)S(1)}, u32[]{:S(2)}, u32[]{:S(2)}) collective-permute-start(f32[160,256]{1,0:T(8,128)S(1)} %get-tuple-element.48.refs_0_), channel_id=1, source_target_pairs={{0,2},{1,3},{2,0},{3,1},{4,6},{5,7},{6,4},{7,5},{8,10},{9,11},{10,... | collective-permute-start | bytes 491528 | tf_op jit(solution)/shard_map/ppermute | solution.py:531
  25.8 14.4 %collective-permute-start.1 = (f32[160,256]{1,0:T(8,128)S(1)}, f32[160,256]{1,0:T(8,128)S(1)}, u32[]{:S(2)}, u32[]{:S(2)}) collective-permute-start(f32[160,256]{1,0:T(8,128)S(1)} %get-tuple-element.47.refs_0_), channel_id=1, source_target_pairs={{0,2},{1,3},{2,0},{3,1},{4,6},{5,7},{6,4},{7,5},{8,10},{9,11},{10,... | collective-permute-start | bytes 491528 | tf_op jit(solution)/shard_map/ppermute | solution.py:531
  36.8 7.1 %collective-permute-start.4 = (f32[160,256]{1,0:T(8,128)S(1)}, f32[160,256]{1,0:T(8,128)S(1)}, u32[]{:S(2)}, u32[]{:S(2)}) collective-permute-start(f32[160,256]{1,0:T(8,128)S(1)} %total.10.refs_1_), channel_id=1, source_target_pairs={{0,1},{1,0},{2,3},{3,2},{4,5},{5,4},{6,7},{7,6},{8,9},{9,8},{10,11... | collective-permute-start | bytes 491528 | tf_op jit(solution)/shard_map/ppermute | solution.py:531
  40.3 6.9 %collective-permute-start.3 = (f32[160,256]{1,0:T(8,128)S(1)}, f32[160,256]{1,0:T(8,128)S(1)}, u32[]{:S(2)}, u32[]{:S(2)}) collective-permute-start(f32[160,256]{1,0:T(8,128)S(1)} %total.9.refs_0_), channel_id=1, source_target_pairs={{0,1},{1,0},{2,3},{3,2},{4,5},{5,4},{6,7},{7,6},{8,9},{9,8},{10,11... | collective-permute-start | bytes 491528 | tf_op jit(solution)/shard_map/ppermute | solution.py:531
  52.1 3.9 %collective-permute-start.8 = (f32[1792,256]{1,0:T(8,128)S(1)}, f32[1792,256]{1,0:T(8,128)S(1)}, u32[]{:S(2)}, u32[]{:S(2)}) collective-permute-start(f32[1792,256]{1,0:T(8,128)S(1)} %w_send.3), channel_id=1, source_target_pairs={{0,4},{4,0},{8,12},{12,8},{16,20},{20,16},{24,28},{28,24},{1,5},{5... | collective-permute-start | bytes 5505032 | tf_op jit(solution)/shard_map/ppermute | solution.py:531
  55.4 5.5 %collective-permute-start.5 = (f32[1792,256]{1,0:T(8,128)S(1)}, f32[1792,256]{1,0:T(8,128)S(1)}, u32[]{:S(2)}, u32[]{:S(2)}) collective-permute-start(f32[1792,256]{1,0:T(8,128)S(1)} %w_send.2), channel_id=1, source_target_pairs={{0,4},{4,0},{8,12},{12,8},{16,20},{20,16},{24,28},{28,24},{1,5},{5... | collective-permute-start | bytes 5505032 | tf_op jit(solution)/shard_map/ppermute | solution.py:531
  59.2 32.8 %collective-permute-start.9 = (f32[896,256]{1,0:T(8,128)S(1)}, f32[896,256]{1,0:T(8,128)S(1)}, u32[]{:S(2)}, u32[]{:S(2)}) collective-permute-start(f32[896,256]{1,0:T(8,128)S(1)} %get-tuple-element.56), channel_id=1, source_target_pairs={{0,16},{4,20},{8,24},{12,28},{16,0},{20,4},{24,8},{28,12},{1,17},{... | collective-permute-start | bytes 2752520 | tf_op jit(solution)/shard_map/ppermute | solution.py:531
  64.1 30.1 %collective-permute-start.6 = (f32[896,256]{1,0:T(8,128)S(1)}, f32[896,256]{1,0:T(8,128)S(1)}, u32[]{:S(2)}, u32[]{:S(2)}) collective-permute-start(f32[896,256]{1,0:T(8,128)S(1)} %get-tuple-element.52), channel_id=1, source_target_pairs={{0,8},{4,12},{8,0},{12,4},{16,24},{20,28},{24,16},{28,20},{1,9},{5... | collective-permute-start | bytes 2752520 | tf_op jit(solution)/shard_map/ppermute | solution.py:531
  65.7 1.3 collective-permute-start.11
  67.1 23.2 %collective-permute-start.12 = (f32[128,256]{1,0:T(8,128)S(1)}, f32[128,256]{1,0:T(8,128)S(1)}, u32[]{:S(2)}, u32[]{:S(2)}) collective-permute-start(f32[128,256]{1,0:T(8,128)S(1)} %total.11.refs_0_), channel_id=1, source_target_pairs={{0,8},{4,12},{8,0},{12,4},{16,24},{20,28},{24,16},{28,20},{1,9},{5... | collective-permute-start | bytes 393224 | tf_op jit(solution)/shard_map/ppermute | solution.py:531
  67.7 22.6 %collective-permute-start.13 = (f32[128,256]{1,0:T(8,128)S(1)}, f32[128,256]{1,0:T(8,128)S(1)}, u32[]{:S(2)}, u32[]{:S(2)}) collective-permute-start(f32[128,256]{1,0:T(8,128)S(1)} %total.11.refs_0_), channel_id=1, source_target_pairs={{0,16},{4,20},{8,24},{12,28},{16,0},{20,4},{24,8},{28,12},{1,17},{... | collective-permute-start | bytes 393224 | tf_op jit(solution)/shard_map/ppermute | solution.py:531
  68.1 23.8 %collective-permute-start.14 = (f32[128,256]{1,0:T(8,128)S(1)}, f32[128,256]{1,0:T(8,128)S(1)}, u32[]{:S(2)}, u32[]{:S(2)}) collective-permute-start(f32[128,256]{1,0:T(8,128)S(1)} %total.11.refs_0_), channel_id=1, source_target_pairs={{0,24},{4,28},{8,16},{12,20},{16,8},{20,12},{24,0},{28,4},{1,25},{... | collective-permute-start | bytes 393224 | tf_op jit(solution)/shard_map/ppermute | solution.py:531
  92.0 4.5 %collective-permute-start.15 = (f32[128,256]{1,0:T(8,128)S(1)}, f32[128,256]{1,0:T(8,128)S(1)}, u32[]{:S(2)}, u32[]{:S(2)}) collective-permute-start(f32[128,256]{1,0:T(8,128)S(1)} %total.12.mine), channel_id=1, source_target_pairs={{0,4},{4,0},{8,12},{12,8},{16,20},{20,16},{24,28},{28,24},{1,5},{5... | collective-permute-start | bytes 393224 | tf_op jit(solution)/shard_map/ppermute | solution.py:531
  92.7 17.1 %collective-permute-start.10 = (f32[448,256]{1,0:T(8,128)S(1)}, f32[448,256]{1,0:T(8,128)S(1)}, u32[]{:S(2)}, u32[]{:S(2)}) collective-permute-start(f32[448,256]{1,0:T(8,128)S(1)} %get-tuple-element.58), channel_id=1, source_target_pairs={{0,8},{4,12},{8,0},{12,4},{16,24},{20,28},{24,16},{28,20},{1,9},{5... | collective-permute-start | bytes 1376264 | tf_op jit(solution)/shard_map/ppermute | solution.py:531
  94.9 14.9 %collective-permute-start.7 = (f32[448,256]{1,0:T(8,128)S(1)}, f32[448,256]{1,0:T(8,128)S(1)}, u32[]{:S(2)}, u32[]{:S(2)}) collective-permute-start(f32[448,256]{1,0:T(8,128)S(1)} %get-tuple-element.54), channel_id=1, source_target_pairs={{0,16},{4,20},{8,24},{12,28},{16,0},{20,4},{24,8},{28,12},{1,17},{... | collective-permute-start | bytes 1376264 | tf_op jit(solution)/shard_map/ppermute | solution.py:531
  96.5 66.9 %slice-start = ((s8[9175040]{0:T(1024)(128)(4,1)}), s8[4194304]{0:T(1024)(128)(4,1)S(1)}, s32[]{:S(2)}) async-start(s8[9175040]{0:T(1024)(128)(4,1)} %bitcast.21), calls=%async_computation | async-start | bytes 8388608
  96.5 66.9 %slice-start.1 = ((s8[9175040]{0:T(1024)(128)(4,1)}), s8[4194304]{0:T(1024)(128)(4,1)S(1)}, s32[]{:S(2)}) async-start(s8[9175040]{0:T(1024)(128)(4,1)} %bitcast.21), calls=%async_computation.1 | async-start | bytes 8388608
  96.5 66.9 %slice-start.2 = ((s8[9175040]{0:T(1024)(128)(4,1)}), s8[786432]{0:T(1024)(128)(4,1)S(1)}, s32[]{:S(2)}) async-start(s8[9175040]{0:T(1024)(128)(4,1)} %bitcast.21), calls=%async_computation.2 | async-start | bytes 1572864
  111.3 12.4 %collective-permute-start.18 = (f32[448,256]{1,0:T(8,128)S(1)}, f32[448,256]{1,0:T(8,128)S(1)}, u32[]{:S(2)}, u32[]{:S(2)}) collective-permute-start(f32[448,256]{1,0:T(8,128)S(1)} %get-tuple-element.65.x), channel_id=1, source_target_pairs={{0,8},{4,12},{8,0},{12,4},{16,24},{20,28},{24,16},{28,20},{1,9},{5... | collective-permute-start | bytes 1376264 | tf_op jit(solution)/shard_map/ppermute | solution.py:531
  111.9 12.6 %collective-permute-start.16 = (f32[448,256]{1,0:T(8,128)S(1)}, f32[448,256]{1,0:T(8,128)S(1)}, u32[]{:S(2)}, u32[]{:S(2)}) collective-permute-start(f32[448,256]{1,0:T(8,128)S(1)} %get-tuple-element.63.x), channel_id=1, source_target_pairs={{0,16},{4,20},{8,24},{12,28},{16,0},{20,4},{24,8},{28,12},{1,17},{... | collective-permute-start | bytes 1376264 | tf_op jit(solution)/shard_map/ppermute | solution.py:531
  124.4 47.1 %collective-permute-start.34 = (f32[896,256]{1,0:T(8,128)S(1)}, f32[896,256]{1,0:T(8,128)S(1)}, u32[]{:S(2)}, u32[]{:S(2)}) collective-permute-start(f32[896,256]{1,0:T(8,128)S(1)} %get-tuple-element.73.refs_1_), channel_id=1, source_target_pairs={{0,4},{4,0},{8,12},{12,8},{16,20},{20,16},{24,28},{28,24},{1,5},{5... | collective-permute-start | bytes 2752520 | tf_op jit(solution)/shard_map/ppermute | solution.py:531
  125.2 46.8 %collective-permute-start.33 = (f32[896,256]{1,0:T(8,128)S(1)}, f32[896,256]{1,0:T(8,128)S(1)}, u32[]{:S(2)}, u32[]{:S(2)}) collective-permute-start(f32[896,256]{1,0:T(8,128)S(1)} %get-tuple-element.72.refs_0_), channel_id=1, source_target_pairs={{0,4},{4,0},{8,12},{12,8},{16,20},{20,16},{24,28},{28,24},{1,5},{5... | collective-permute-start | bytes 2752520 | tf_op jit(solution)/shard_map/ppermute | solution.py:531
  125.7 37.1 %collective-permute-start.30 = (f32[512,256]{1,0:T(8,128)S(1)}, f32[512,256]{1,0:T(8,128)S(1)}, u32[]{:S(2)}, u32[]{:S(2)}) collective-permute-start(f32[512,256]{1,0:T(8,128)S(1)} %get-tuple-element.71), channel_id=1, source_target_pairs={{0,16},{4,20},{8,24},{12,28},{16,0},{20,4},{24,8},{28,12},{1,17},{... | collective-permute-start | bytes 1572872 | tf_op jit(solution)/shard_map/ppermute | solution.py:531
  126.2 36.7 %collective-permute-start.29 = (f32[512,256]{1,0:T(8,128)S(1)}, f32[512,256]{1,0:T(8,128)S(1)}, u32[]{:S(2)}, u32[]{:S(2)}) collective-permute-start(f32[512,256]{1,0:T(8,128)S(1)} %get-tuple-element.70), channel_id=1, source_target_pairs={{0,8},{4,12},{8,0},{12,4},{16,24},{20,28},{24,16},{28,20},{1,9},{5... | collective-permute-start | bytes 1572872 | tf_op jit(solution)/shard_map/ppermute | solution.py:531
  126.8 3.7 %collective-permute-start.22 = (f32[8,256]{1,0:T(8,128)S(1)}, f32[8,256]{1,0:T(8,128)S(1)}, u32[]{:S(2)}, u32[]{:S(2)}) collective-permute-start(f32[8,256]{1,0:T(8,128)S(1)} %get-tuple-element.67.refs_0_), channel_id=1, source_target_pairs={{0,1},{1,0},{2,3},{3,2},{4,5},{5,4},{6,7},{7,6},{8,9},{9,8},{10,11... | collective-permute-start | bytes 24584 | tf_op jit(solution)/shard_map/ppermute | solution.py:531
  130.5 4.5 %collective-permute-start.23 = (f32[8,256]{1,0:T(8,128)S(1)}, f32[8,256]{1,0:T(8,128)S(1)}, u32[]{:S(2)}, u32[]{:S(2)}) collective-permute-start(f32[8,256]{1,0:T(8,128)S(1)} %get-tuple-element.67.refs_0_), channel_id=1, source_target_pairs={{0,2},{1,3},{2,0},{3,1},{4,6},{5,7},{6,4},{7,5},{8,10},{9,11},{10,... | collective-permute-start | bytes 24584 | tf_op jit(solution)/shard_map/ppermute | solution.py:531
  135.0 5.4 %collective-permute-start.24 = (f32[8,256]{1,0:T(8,128)S(1)}, f32[8,256]{1,0:T(8,128)S(1)}, u32[]{:S(2)}, u32[]{:S(2)}) collective-permute-start(f32[8,256]{1,0:T(8,128)S(1)} %get-tuple-element.67.refs_0_), channel_id=1, source_target_pairs={{0,3},{1,2},{2,1},{3,0},{4,7},{5,6},{6,5},{7,4},{8,11},{9,10},{10,... | collective-permute-start | bytes 24584 | tf_op jit(solution)/shard_map/ppermute | solution.py:531
  140.5 1.2 collective-permute-start.25
  141.6 3.7 %collective-permute-start.26 = (f32[8,256]{1,0:T(8,128)S(1)}, f32[8,256]{1,0:T(8,128)S(1)}, u32[]{:S(2)}, u32[]{:S(2)}) collective-permute-start(f32[8,256]{1,0:T(8,128)S(1)} %total.14.refs_0_), channel_id=1, source_target_pairs={{0,8},{4,12},{8,0},{12,4},{16,24},{20,28},{24,16},{28,20},{1,9},{5... | collective-permute-start | bytes 24584 | tf_op jit(solution)/shard_map/ppermute | solution.py:531
  145.3 3.7 %collective-permute-start.27 = (f32[8,256]{1,0:T(8,128)S(1)}, f32[8,256]{1,0:T(8,128)S(1)}, u32[]{:S(2)}, u32[]{:S(2)}) collective-permute-start(f32[8,256]{1,0:T(8,128)S(1)} %total.14.refs_0_), channel_id=1, source_target_pairs={{0,16},{4,20},{8,24},{12,28},{16,0},{20,4},{24,8},{28,12},{1,17},{... | collective-permute-start | bytes 24584 | tf_op jit(solution)/shard_map/ppermute | solution.py:531
  149.0 4.7 %collective-permute-start.28 = (f32[8,256]{1,0:T(8,128)S(1)}, f32[8,256]{1,0:T(8,128)S(1)}, u32[]{:S(2)}, u32[]{:S(2)}) collective-permute-start(f32[8,256]{1,0:T(8,128)S(1)} %total.14.refs_0_), channel_id=1, source_target_pairs={{0,24},{4,28},{8,16},{12,20},{16,8},{20,12},{24,0},{28,4},{1,25},{... | collective-permute-start | bytes 24584 | tf_op jit(solution)/shard_map/ppermute | solution.py:531
  153.6 7.8 %collective-permute-start.19 = (f32[384,256]{1,0:T(8,128)S(1)}, f32[384,256]{1,0:T(8,128)S(1)}, u32[]{:S(2)}, u32[]{:S(2)}) collective-permute-start(f32[384,256]{1,0:T(8,128)S(1)} %get-tuple-element.66), channel_id=1, source_target_pairs={{0,16},{4,20},{8,24},{12,28},{16,0},{20,4},{24,8},{28,12},{1,17},{... | collective-permute-start | bytes 1179656 | tf_op jit(solution)/shard_map/ppermute | solution.py:531
  161.4 10.0 %collective-permute-start.17 = (f32[384,256]{1,0:T(8,128)S(1)}, f32[384,256]{1,0:T(8,128)S(1)}, u32[]{:S(2)}, u32[]{:S(2)}) collective-permute-start(f32[384,256]{1,0:T(8,128)S(1)} %get-tuple-element.64), channel_id=1, source_target_pairs={{0,8},{4,12},{8,0},{12,4},{16,24},{20,28},{24,16},{28,20},{1,9},{5... | collective-permute-start | bytes 1179656 | tf_op jit(solution)/shard_map/ppermute | solution.py:531
  162.8 17.1 %collective-permute-start.32 = (f32[512,256]{1,0:T(8,128)S(1)}, f32[512,256]{1,0:T(8,128)S(1)}, u32[]{:S(2)}, u32[]{:S(2)}) collective-permute-start(f32[512,256]{1,0:T(8,128)S(1)} %collective-permute-done.30.refs_1_), channel_id=1, source_target_pairs={{0,4},{4,0},{8,12},{12,8},{16,20},{20,16},{24,28},{28,24},{1,5},{5... | collective-permute-start | bytes 1572872 | tf_op jit(solution)/shard_map/ppermute | solution.py:531
  162.9 17.0 %collective-permute-start.31 = (f32[512,256]{1,0:T(8,128)S(1)}, f32[512,256]{1,0:T(8,128)S(1)}, u32[]{:S(2)}, u32[]{:S(2)}) collective-permute-start(f32[512,256]{1,0:T(8,128)S(1)} %collective-permute-done.29.refs_0_), channel_id=1, source_target_pairs={{0,4},{4,0},{8,12},{12,8},{16,20},{20,16},{24,28},{28,24},{1,5},{5... | collective-permute-start | bytes 1572872 | tf_op jit(solution)/shard_map/ppermute | solution.py:531
  171.4 16.2 %collective-permute-start.21 = (f32[384,256]{1,0:T(8,128)S(1)}, f32[384,256]{1,0:T(8,128)S(1)}, u32[]{:S(2)}, u32[]{:S(2)}) collective-permute-start(f32[384,256]{1,0:T(8,128)S(1)} %collective-permute-done.19.refs_1_), channel_id=1, source_target_pairs={{0,4},{4,0},{8,12},{12,8},{16,20},{20,16},{24,28},{28,24},{1,5},{5... | collective-permute-start | bytes 1179656 | tf_op jit(solution)/shard_map/ppermute | solution.py:531
  171.5 16.1 %collective-permute-start.20 = (f32[384,256]{1,0:T(8,128)S(1)}, f32[384,256]{1,0:T(8,128)S(1)}, u32[]{:S(2)}, u32[]{:S(2)}) collective-permute-start(f32[384,256]{1,0:T(8,128)S(1)} %collective-permute-done.17.refs_0_), channel_id=1, source_target_pairs={{0,4},{4,0},{8,12},{12,8},{16,20},{20,16},{24,28},{28,24},{1,5},{5... | collective-permute-start | bytes 1179656 | tf_op jit(solution)/shard_map/ppermute | solution.py:531
